TPU v7x, 32 devices: a whole 2x2x4 slice. The times are simulated.
32 devices in a mesh: dp: 8 (over y, x, core), blk: 4 (over z).
Axes of the slice: x: 2, y: 2, z: 4, core: 2. Of those that a mesh axis runs over, the one named last changes fastest.
Arguments:
- cell_states: bfloat16 [12288, 1024], P(('dp', 'blk')), may hold values from -16 to 16
- slide_lengths: int32 [8, 4], P('dp'), may hold values from 1 to 1024, 1536 in all within a row
- cell_mask: int32 [12288], P(('dp', 'blk')), may hold values from 0 to 1, as said below
- latent_noise: bfloat16 [12288, 512], P(('dp', 'blk')), may hold values from -4 to 4
- train_step: int32 [1], replicated, may hold values from 0 to 1999
- attn_gain: float32 [1024], replicated, may hold values from 0.5 to 1.5
- attn_shift: float32 [1024], replicated, may hold values from -0.3125 to 0.3125
- query_weight: bfloat16 [1024, 1024], replicated, may hold values from -0.1875 to 0.1875
- key_weight: bfloat16 [1024, 1024], replicated, may hold values from -0.1875 to 0.1875
- value_weight: bfloat16 [1024, 1024], replicated, may hold values from -0.1875 to 0.1875
- out_weight: bfloat16 [1024, 1024], replicated, may hold values from -3 to 3
- ffn_gain: float32 [1024], replicated, may hold values from 0.5 to 1.5
- ffn_shift: float32 [1024], replicated, may hold values from -1.75 to 1.75
- up_weight: bfloat16 [1024, 4096], replicated, may hold values from -0.1875 to 0.1875
- up_bias: float32 [4096], replicated, may hold values from -3 to 3
- down_weight: bfloat16 [4096, 1024], replicated, may hold values from -0.09375 to 0.09375
- down_bias: float32 [1024], replicated, may hold values from -1.75 to 1.75
- encode_weight: bfloat16 [1024, 1024], replicated, may hold values from -0.046875 to 0.046875
- encode_bias: float32 [1024], replicated, may hold values from -2 to 2
- decode_weight: bfloat16 [512, 1024], replicated, may hold values from -0.25 to 0.25
- prior_means: float32 [16, 512], replicated, may hold values from -6 to 6
- prior_logits: float32 [16], replicated, may hold values from -6 to 6
- out_grad: bfloat16 [12288, 1024], P(('dp', 'blk')), may hold values from -6 to 6
Outputs:
- layer_out: bfloat16 [12288, 1024], P(('dp', 'blk'))
- states_grad: float32 [12288, 1024], P(('dp', 'blk'))
- kl_per_dim: float32 [1], replicated
- attn_gain_grad: float32 [1024], P('blk')
- attn_shift_grad: float32 [1024], P('blk')
- query_weight_grad: float32 [1024, 1024], P('blk')
- key_weight_grad: float32 [1024, 1024], P('blk')
- value_weight_grad: float32 [1024, 1024], P('blk')
- out_weight_grad: float32 [1024, 1024], P('blk')
- ffn_gain_grad: float32 [1024], P('blk')
- ffn_shift_grad: float32 [1024], P('blk')
- up_weight_grad: float32 [1024, 4096], P('blk')
- up_bias_grad: float32 [4096], P('blk')
- down_weight_grad: float32 [4096, 1024], P('blk')
- down_bias_grad: float32 [1024], P('blk')
- encode_weight_grad: float32 [1024, 1024], P('blk')
- encode_bias_grad: float32 [1024], P('blk')
- decode_weight_grad: float32 [512, 1024], P('blk')
- prior_means_grad: float32 [16, 512], P(None, 'blk')
- prior_logits_grad: float32 [16], P('blk')
Inputs may be any that keep to these rules, and one draw needn't show every extreme that they name: `slide_lengths`: row g holds the lengths of the 4 slides of group g in order; they sum to 1536, and the longest is exactly 1024. `cell_mask`: the last cell, 12287, is real.
All inputs are finite; a program needn't handle non-finite values.
Results may differ from a plain program's by a relative error of at most 0.035.
Values may be sent and summed in bfloat16 or wider, within the bound.
No kernel may reach another device: no remote copies, remote signals or barrier semaphores. Data moves between devices by JAX's collectives and lax.ppermute only.
A program may use at most 192 MiB of HBM per device.

v0:
```python
from functools import partial

import jax
import jax.numpy as jnp
from jax import lax
from jax.sharding import PartitionSpec as P

D = 1024
H = 16
HD = 64
LAT = 512
WARM = 2000


ln_eps = 1e-05
free_floor = 1.3
neg_fill = -1e30


def shortened(array):

    def short(part):
        return part.astype(jnp.bfloat16) if part.dtype == jnp.float32 else part

    return jax.tree.map(short, array)


def passed_along(value, axis, steps):
    count = lax.axis_size(axis)
    pairs = [(source, (source + steps) % count) for source in range(count)]
    return lax.ppermute(value, axis, pairs)


def layer_norm(values, gain, shift):
    center = values - jnp.mean(values, axis=-1, keepdims=True)
    spread = jnp.mean(center * center, axis=-1, keepdims=True)
    return center * lax.rsqrt(spread + ln_eps) * gain + shift


def slide_index(position, lengths_row):
    ends = jnp.cumsum(lengths_row)
    return jnp.sum((position[:, None] >= ends[None, :]).astype(jnp.int32), axis=1)


def exact_dot(left, right):
    return jnp.dot(left, right, precision=lax.Precision.HIGHEST, preferred_element_type=jnp.float32)


def kl_terms(latent_mean, latent_logvar, prior_means, prior_logits):
    log_prior = jax.nn.log_softmax(prior_logits)
    logits = exact_dot(latent_mean, prior_means.T) * LAT ** (-0.5) + log_prior[None, :]
    resp = jax.nn.softmax(logits, axis=-1)
    log_resp = jax.nn.log_softmax(logits, axis=-1)
    mixed_mean = exact_dot(resp, prior_means)
    mixed_square = exact_dot(resp, prior_means * prior_means)
    kl_dim = 0.5 * (
        jnp.exp(latent_logvar)
        + latent_mean * latent_mean
        - 2.0 * latent_mean * mixed_mean
        + mixed_square
        - 1.0
        - latent_logvar
    )
    categorical = jnp.sum(resp * (log_resp - log_prior[None, :]), axis=-1)
    return (kl_dim, categorical)


def plain_dot(left, right):
    return jnp.dot(left, right, preferred_element_type=jnp.float32)


def rows_dot(left, right):
    return lax.dot_general(
        left, right, (((0,), (0,)), ((), ())), preferred_element_type=jnp.float32
    )


def cols_dot(left, right):
    return lax.dot_general(
        left, right, (((1,), (1,)), ((), ())), preferred_element_type=jnp.float32
    )


def pair_mask(query_slide, query_pos, key_slide, key_pos, key_live):
    same = query_slide[:, None] == key_slide[None, :]
    open_key = (key_live[None, :] > 0.5) | (query_pos[:, None] == key_pos[None, :])
    return (same & open_key)[None]


def forward_update(
    state, heads_q, query_slide, query_pos, heads_k, heads_v, key_live, key_pos, key_slide
):
    peak, total, running = state
    allowed = pair_mask(query_slide, query_pos, key_slide, key_pos, key_live)
    scores = jnp.einsum(
        "qhd,khd->hqk", heads_q, heads_k, preferred_element_type=jnp.float32
    ) * HD ** (-0.5)
    scores = jnp.where(allowed, scores, neg_fill)
    new_peak = jnp.maximum(peak, jnp.max(scores, axis=-1))
    weights = jnp.where(allowed, jnp.exp(scores - new_peak[:, :, None]), 0.0)
    rescale = jnp.exp(peak - new_peak)
    total = total * rescale + jnp.sum(weights, axis=-1)
    running = running * rescale.T[:, :, None] + jnp.einsum(
        "hqk,khd->qhd", weights.astype(jnp.bfloat16), heads_v, preferred_element_type=jnp.float32
    )
    return (new_peak, total, running)


def forward_visit(
    state, heads_q, query_slide, query_pos, heads_k, heads_v, key_live, key_pos, lengths_row
):
    key_slide = slide_index(key_pos, lengths_row)
    return forward_update(
        state, heads_q, query_slide, query_pos, heads_k, heads_v, key_live, key_pos, key_slide
    )


def backward_update(
    heads_q,
    heads_o,
    log_total,
    delta,
    query_slide,
    query_pos,
    heads_k,
    heads_v,
    key_live,
    key_pos,
    key_slide,
):
    allowed = pair_mask(query_slide, query_pos, key_slide, key_pos, key_live)
    scores = jnp.einsum(
        "qhd,khd->hqk", heads_q, heads_k, preferred_element_type=jnp.float32
    ) * HD ** (-0.5)
    probs = jnp.where(allowed, jnp.exp(scores - log_total[:, :, None]), 0.0)
    dprobs = jnp.einsum("qhd,khd->hqk", heads_o, heads_v, preferred_element_type=jnp.float32)
    dscores = (probs * (dprobs - delta[:, :, None])).astype(jnp.bfloat16)
    grad_q = jnp.einsum(
        "hqk,khd->qhd", dscores, heads_k, preferred_element_type=jnp.float32
    ) * HD ** (-0.5)
    grad_k = jnp.einsum(
        "hqk,qhd->khd", dscores, heads_q, preferred_element_type=jnp.float32
    ) * HD ** (-0.5)
    grad_v = jnp.einsum(
        "hqk,qhd->khd", probs.astype(jnp.bfloat16), heads_o, preferred_element_type=jnp.float32
    )
    return (grad_q, grad_k, grad_v)


def backward_visit(
    heads_q,
    heads_o,
    log_total,
    delta,
    query_slide,
    query_pos,
    heads_k,
    heads_v,
    key_live,
    key_pos,
    key_slide,
):
    return backward_update(
        heads_q,
        heads_o,
        log_total,
        delta,
        query_slide,
        query_pos,
        heads_k,
        heads_v,
        key_live,
        key_pos,
        key_slide,
    )


def local(
    cell_states,
    slide_lengths,
    cell_mask,
    latent_noise,
    train_step,
    attn_gain,
    attn_shift,
    query_weight,
    key_weight,
    value_weight,
    out_weight,
    ffn_gain,
    ffn_shift,
    up_weight,
    up_bias,
    down_weight,
    down_bias,
    encode_weight,
    encode_bias,
    decode_weight,
    prior_means,
    prior_logits,
    out_grad,
):
    rows_here = cell_states.shape[0]
    blocks = lax.axis_size("blk")
    my_index = lax.axis_index("blk")
    lengths_row = slide_lengths[0]
    local_range = jnp.arange(rows_here, dtype=jnp.int32)
    local_pos = my_index * rows_here + local_range
    local_slide = slide_index(local_pos, lengths_row)
    live = cell_mask.astype(jnp.bfloat16)
    x_float = cell_states.astype(jnp.float32)
    normed, norm_back = jax.vjp(layer_norm, x_float, attn_gain, attn_shift)
    normed_b = normed.astype(jnp.bfloat16)
    queries = plain_dot(normed_b, query_weight).astype(jnp.bfloat16)
    keys = plain_dot(normed_b, key_weight).astype(jnp.bfloat16)
    values = plain_dot(normed_b, value_weight).astype(jnp.bfloat16)
    heads_q = queries.reshape(rows_here, H, HD)
    start_state = (
        jnp.full((H, rows_here), neg_fill, jnp.float32),
        jnp.zeros((H, rows_here), jnp.float32),
        jnp.zeros((rows_here, H, HD), jnp.float32),
    )
    state = start_state
    piece_keys = lax.all_gather(keys, "blk", axis=0, tiled=True)
    piece_values = lax.all_gather(values, "blk", axis=0, tiled=True)
    piece_live = lax.all_gather(live, "blk", axis=0, tiled=True)
    rows = piece_keys.shape[0]
    width = min(rows, rows_here)

    def one_block(carry, index):
        offset = index * width
        block_keys = lax.dynamic_slice_in_dim(piece_keys, offset, width, 0).reshape(width, H, HD)
        block_values = lax.dynamic_slice_in_dim(piece_values, offset, width, 0).reshape(
            width, H, HD
        )
        block_live = lax.dynamic_slice_in_dim(piece_live, offset, width, 0)
        key_pos = offset + jnp.arange(width, dtype=jnp.int32)
        return (
            forward_visit(
                carry,
                heads_q,
                local_slide,
                local_pos,
                block_keys,
                block_values,
                block_live,
                key_pos,
                lengths_row,
            ),
            None,
        )

    state, _ = lax.scan(one_block, state, jnp.arange(rows // width, dtype=jnp.int32))
    peak, total, running = state
    context = running / total.T[:, :, None]
    log_total = peak + jnp.log(total)
    context_b = context.reshape(rows_here, D).astype(jnp.bfloat16)
    hidden = x_float + plain_dot(context_b, out_weight)
    normed_two, norm_two_back = jax.vjp(layer_norm, hidden, ffn_gain, ffn_shift)
    normed_two_b = normed_two.astype(jnp.bfloat16)
    inner = plain_dot(normed_two_b, up_weight) + up_bias
    activated, gelu_back = jax.vjp(partial(jax.nn.gelu, approximate=False), inner)
    activated_b = activated.astype(jnp.bfloat16)
    hidden_two = hidden + plain_dot(activated_b, down_weight) + down_bias
    hidden_two_b = hidden_two.astype(jnp.bfloat16)
    encoded = plain_dot(hidden_two_b, encode_weight) + encode_bias
    latent_mean = encoded[:, :LAT]
    latent_logvar = encoded[:, LAT:]
    spread = jnp.exp(0.5 * latent_logvar)
    noise_float = latent_noise.astype(jnp.float32)
    latent_b = (latent_mean + spread * noise_float).astype(jnp.bfloat16)
    output = hidden_two + plain_dot(latent_b, decode_weight)
    (kl_dim, categorical), kl_back = jax.vjp(
        kl_terms, latent_mean, latent_logvar, prior_means, prior_logits
    )
    real = cell_mask.astype(jnp.float32)
    kl_sum, cat_sum, count = lax.psum(
        (jnp.sum(kl_dim * real[:, None], axis=0), jnp.sum(categorical * real), jnp.sum(real)),
        ("dp", "blk"),
    )
    kbar = kl_sum / count
    floored = jnp.sum(jnp.maximum(kbar, free_floor))
    cat_mean = cat_sum / count
    beta = jnp.minimum(1.0, (train_step[0].astype(jnp.float32) + 1.0) / WARM)
    active = (kbar > free_floor).astype(jnp.float32)
    grad_decode = rows_dot(latent_b, out_grad)
    grad_latent = cols_dot(out_grad, decode_weight)
    grad_mean, grad_logvar, grad_means, grad_prior = kl_back(
        (beta * real[:, None] * active[None, :], beta * real)
    )
    grad_mean = grad_mean + grad_latent
    grad_logvar = grad_logvar + grad_latent * 0.5 * spread * noise_float
    grad_encoded_b = jnp.concatenate([grad_mean, grad_logvar], axis=1).astype(jnp.bfloat16)
    grad_encode = rows_dot(hidden_two_b, grad_encoded_b)
    grad_encode_bias = jnp.sum(grad_encoded_b.astype(jnp.float32), axis=0)
    grad_two = out_grad.astype(jnp.float32) + cols_dot(grad_encoded_b, encode_weight)
    grad_down_bias = jnp.sum(grad_two, axis=0)
    grad_branch_b = grad_two.astype(jnp.bfloat16)
    grad_down = rows_dot(activated_b, grad_branch_b)
    (grad_inner,) = gelu_back(cols_dot(grad_branch_b, down_weight))
    grad_inner_b = grad_inner.astype(jnp.bfloat16)
    grad_up_bias = jnp.sum(grad_inner_b.astype(jnp.float32), axis=0)
    grad_up = rows_dot(normed_two_b, grad_inner_b)
    grad_hidden, grad_ffn_gain, grad_ffn_shift = norm_two_back(cols_dot(grad_inner_b, up_weight))
    grad_hidden = grad_hidden + grad_two
    grad_attn_b = grad_hidden.astype(jnp.bfloat16)
    grad_out = rows_dot(context_b, grad_attn_b)
    grad_context_b = cols_dot(grad_attn_b, out_weight).astype(jnp.bfloat16)
    heads_o = grad_context_b.reshape(rows_here, H, HD)
    delta = jnp.sum(heads_o.astype(jnp.float32) * context, axis=-1).T
    zero_heads = jnp.zeros((rows_here, H, HD), jnp.float32)

    def key_turn(turn, carry):
        travel, grads_travel, grad_q = carry
        held_keys, held_values, held_live = travel
        anchor = (my_index + turn) % blocks
        key_pos = anchor * rows_here + local_range
        key_slide = slide_index(key_pos, lengths_row)
        part_q, part_k, part_v = backward_visit(
            heads_q,
            heads_o,
            log_total,
            delta,
            local_slide,
            local_pos,
            held_keys.reshape(rows_here, H, HD),
            held_values.reshape(rows_here, H, HD),
            held_live,
            key_pos,
            key_slide,
        )
        grads_travel = (grads_travel[0] + part_k, grads_travel[1] + part_v)
        travel = jax.tree.map(
            lambda part, own: part.astype(own.dtype),
            passed_along(shortened(travel), "blk", -1),
            travel,
        )
        grads_travel = (
            passed_along(grads_travel[0].astype(jnp.bfloat16), "blk", -1).astype(jnp.float32),
            passed_along(grads_travel[1].astype(jnp.bfloat16), "blk", -1).astype(jnp.float32),
        )
        return (travel, grads_travel, grad_q + part_q)

    _, (grad_k, grad_v), grad_q = lax.fori_loop(
        0, blocks, key_turn, ((keys, values, live), (zero_heads, zero_heads), zero_heads)
    )
    grad_q_b = grad_q.reshape(rows_here, D).astype(jnp.bfloat16)
    grad_k_b = grad_k.reshape(rows_here, D).astype(jnp.bfloat16)
    grad_v_b = grad_v.reshape(rows_here, D).astype(jnp.bfloat16)
    grad_query = rows_dot(normed_b, grad_q_b)
    grad_key = rows_dot(normed_b, grad_k_b)
    grad_value = rows_dot(normed_b, grad_v_b)
    grad_normed = (
        cols_dot(grad_q_b, query_weight)
        + cols_dot(grad_k_b, key_weight)
        + cols_dot(grad_v_b, value_weight)
    )
    grad_from_norm, grad_attn_gain, grad_attn_shift = norm_back(grad_normed)
    states_grad = grad_hidden + grad_from_norm
    shares = (
        lax.psum_scatter(
            grad_attn_gain.astype(jnp.bfloat16), "blk", scatter_dimension=0, tiled=True
        ).astype(jnp.float32),
        lax.psum_scatter(
            grad_attn_shift.astype(jnp.bfloat16), "blk", scatter_dimension=0, tiled=True
        ).astype(jnp.float32),
        lax.psum_scatter(
            grad_query.astype(jnp.bfloat16), "blk", scatter_dimension=0, tiled=True
        ).astype(jnp.float32),
        lax.psum_scatter(
            grad_key.astype(jnp.bfloat16), "blk", scatter_dimension=0, tiled=True
        ).astype(jnp.float32),
        lax.psum_scatter(
            grad_value.astype(jnp.bfloat16), "blk", scatter_dimension=0, tiled=True
        ).astype(jnp.float32),
        lax.psum_scatter(
            grad_out.astype(jnp.bfloat16), "blk", scatter_dimension=0, tiled=True
        ).astype(jnp.float32),
        lax.psum_scatter(
            grad_ffn_gain.astype(jnp.bfloat16), "blk", scatter_dimension=0, tiled=True
        ).astype(jnp.float32),
        lax.psum_scatter(
            grad_ffn_shift.astype(jnp.bfloat16), "blk", scatter_dimension=0, tiled=True
        ).astype(jnp.float32),
        lax.psum_scatter(
            grad_up.astype(jnp.bfloat16), "blk", scatter_dimension=0, tiled=True
        ).astype(jnp.float32),
        lax.psum_scatter(
            grad_up_bias.astype(jnp.bfloat16), "blk", scatter_dimension=0, tiled=True
        ).astype(jnp.float32),
        lax.psum_scatter(
            grad_down.astype(jnp.bfloat16), "blk", scatter_dimension=0, tiled=True
        ).astype(jnp.float32),
        lax.psum_scatter(
            grad_down_bias.astype(jnp.bfloat16), "blk", scatter_dimension=0, tiled=True
        ).astype(jnp.float32),
        lax.psum_scatter(
            grad_encode.astype(jnp.bfloat16), "blk", scatter_dimension=0, tiled=True
        ).astype(jnp.float32),
        lax.psum_scatter(
            grad_encode_bias.astype(jnp.bfloat16), "blk", scatter_dimension=0, tiled=True
        ).astype(jnp.float32),
        lax.psum_scatter(
            grad_decode.astype(jnp.bfloat16), "blk", scatter_dimension=0, tiled=True
        ).astype(jnp.float32),
        lax.psum_scatter(
            grad_means.astype(jnp.bfloat16), "blk", scatter_dimension=1, tiled=True
        ).astype(jnp.float32),
        lax.psum_scatter(
            grad_prior.astype(jnp.bfloat16), "blk", scatter_dimension=0, tiled=True
        ).astype(jnp.float32),
    )
    totals = (
        lax.psum(shares[0].astype(jnp.bfloat16), "dp").astype(jnp.float32),
        lax.psum(shares[1].astype(jnp.bfloat16), "dp").astype(jnp.float32),
        lax.psum(shares[2].astype(jnp.bfloat16), "dp").astype(jnp.float32),
        lax.psum(shares[3].astype(jnp.bfloat16), "dp").astype(jnp.float32),
        lax.psum(shares[4].astype(jnp.bfloat16), "dp").astype(jnp.float32),
        lax.psum(shares[5].astype(jnp.bfloat16), "dp").astype(jnp.float32),
        lax.psum(shares[6].astype(jnp.bfloat16), "dp").astype(jnp.float32),
        lax.psum(shares[7].astype(jnp.bfloat16), "dp").astype(jnp.float32),
        lax.psum(shares[8].astype(jnp.bfloat16), "dp").astype(jnp.float32),
        lax.psum(shares[9].astype(jnp.bfloat16), "dp").astype(jnp.float32),
        lax.psum(shares[10].astype(jnp.bfloat16), "dp").astype(jnp.float32),
        lax.psum(shares[11].astype(jnp.bfloat16), "dp").astype(jnp.float32),
        lax.psum(shares[12].astype(jnp.bfloat16), "dp").astype(jnp.float32),
        lax.psum(shares[13].astype(jnp.bfloat16), "dp").astype(jnp.float32),
        lax.psum(shares[14].astype(jnp.bfloat16), "dp").astype(jnp.float32),
        lax.psum(shares[15].astype(jnp.bfloat16), "dp").astype(jnp.float32),
        lax.psum(shares[16].astype(jnp.bfloat16), "dp").astype(jnp.float32),
    )
    kl_out = (floored / LAT + cat_mean).reshape(1)
    return (output.astype(jnp.bfloat16), states_grad, kl_out) + tuple(totals)


def solution(mesh):
    in_specs = (
        P(("dp", "blk"), None),
        P("dp", None),
        P(("dp", "blk")),
        P(("dp", "blk"), None),
        P(),
        P(),
        P(),
        P(),
        P(),
        P(),
        P(),
        P(),
        P(),
        P(),
        P(),
        P(),
        P(),
        P(),
        P(),
        P(),
        P(),
        P(),
        P(("dp", "blk"), None),
    )
    out_specs = (
        P(("dp", "blk"), None),
        P(("dp", "blk"), None),
        P(),
        P("blk"),
        P("blk"),
        P("blk", None),
        P("blk", None),
        P("blk", None),
        P("blk", None),
        P("blk"),
        P("blk"),
        P("blk", None),
        P("blk"),
        P("blk", None),
        P("blk"),
        P("blk", None),
        P("blk"),
        P("blk", None),
        P(None, "blk"),
        P("blk"),
    )
    return jax.shard_map(local, mesh=mesh, in_specs=in_specs, out_specs=out_specs, check_vma=False)
```

profile of v0, /device:TPU:17, one launch (start us, length us, event | category | flops | bytes accessed | tf_op | source)
XLA Modules:
  0.0 1377.0 jit_solution(9813630006612648483)
XLA Ops:
  27.8 9.4 all-gather
  41.8 36.4 %all-gather.4.cloned.1.call-done = bf16[1536,1024]{1,0:T(8,128)(2,1)} async-done(((bf16[384,1024]{1,0:T(8,128)(2,1)}), bf16[1536,1024]{1,0:T(8,128)(2,1)}) %all-gather.4.cloned.1.call-update) | async-done | bytes 3145744 | tf_op jit(solution)/shard_map/all_gather | solution.py:224
  78.2 64.3 %all-gather.6.cloned.1.call-done = bf16[1536,1024]{1,0:T(8,128)(2,1)} async-done(((bf16[384,1024]{1,0:T(8,128)(2,1)}), bf16[1536,1024]{1,0:T(8,128)(2,1)}) %all-gather.6.cloned.1.call-update) | async-done | bytes 3145744 | tf_op jit(solution)/shard_map/all_gather | solution.py:225
  142.5 100.3 %while.43 = (s32[]{:T(128)}, f32[16,384]{1,0:T(8,128)S(1)}, f32[16,384]{1,0:T(8,128)S(1)}, f32[384,16,64]{0,2,1:T(8,128)}, s32[384]{0:T(512)S(1)}, /*index=5*/s3...) while((s32[]{:T(128)}, f32[16,384]{1,0:T(8,128)S(1)}, ...), condition=%wide.region_9.10_spmd.clone, body=%wide.region_5.9_spmd.clone.sunk | while | flops 636463104 | bytes 69416768 | solution.py:253
  148.3 6.3 fusion.208
  157.1 8.0 bitcast_add_fusion.6
  173.1 6.3 fusion.208
  181.8 8.4 bitcast_add_fusion.6
  198.3 6.3 fusion.208
  207.0 8.4 bitcast_add_fusion.6
  223.5 6.3 fusion.208
  232.2 8.4 bitcast_add_fusion.6
  248.0 22.1 %multiply_convert_fusion.1 = (bf16[384,4096]{1,0:T(8,128)(2,1)S(1)}, f32[384,4096]{1,0:T(8,128)}, f32[384,4096]{1,0:T(8,128)}) fusion(f32[4096]{0:T(1024)S(1)} %copy-done.67, bf16[1024,4096]{1,0:T(8,128)(2,1)} %param.40, f32[384,1024]{1,0:T(8,128)S(1)} %get-tuple-element.864, f32[1024]{0:T(1024)S(1)} %copy-done.72, f32[1024]{0:T(1024)S(1)} %copy-done.58, ...), kind=kOutput, calls=%fused_computation.49 | convolution fusion | flops 3327000576 | bytes 25717760 | tf_op jit(solution)/shard_map/dot_general | solution.py:69
  277.6 39.8 %all-reduce.8 = (f32[512]{0:T(512)S(1)}, f32[]{:T(128)}) all-reduce(f32[512]{0:T(512)S(1)} %fusion.51, f32[]{:T(128)} %get-tuple-element.862), channel_id=1, replica_groups=mesh['dp'=8,'blk'=4] {'dp','blk'}, use_global_device_ids=true, to_apply=%region_17.18 | all-reduce | flops 513 | bytes 4104 | tf_op jit(solution)/shard_map/psum | solution.py:277
  327.8 13.6 fusion.131
  341.5 4.9 multiply_reduce_fusion
  363.3 365.2 %while.44 = (s32[]{:T(128)}, bf16[384,1024]{0,1:T(8,128)(2,1)}, bf16[384,1024]{0,1:T(8,128)(2,1)}, bf16[384]{0:T(512)(128)(2,1)S(1)}, f32[384,16,64]{0,2,1:T(8,1...) while((s32[]{:T(128)}, bf16[384,1024]{0,1:T(8,128)(2,1)}, ...), condition=%wide.region_27.28_spmd.clone, body=%wide.region_25.27_spmd.clone.sunk | while | flops 1538856192 | bytes 89401944 | solution.py:344
  369.6 5.2 multiply_convert_fusion.3
  390.1 22.5 %collective-permute-done.3 = bf16[384,16,64]{0,2,1:T(8,128)(2,1)} collective-permute-done((bf16[384,16,64]{0,2,1:T(8,128)(2,1)}, bf16[384,16,64]{0,2,1:T(8,128)(2,1)}, u32[]{:S(2)}, u32[]{:S(2)}) %collective-permute-start.3) | collective-permute-done | bytes 786464 | tf_op jit(solution)/shard_map/while/body/eval_jaxpr/ppermute | solution.py:31
  415.0 28.4 %collective-permute-done.4 = bf16[384,16,64]{0,2,1:T(8,128)(2,1)} collective-permute-done((bf16[384,16,64]{0,2,1:T(8,128)(2,1)}, bf16[384,16,64]{0,2,1:T(8,128)(2,1)}, u32[]{:S(2)}, u32[]{:S(2)}) %collective-permute-start.4) | collective-permute-done | bytes 786464 | tf_op jit(solution)/shard_map/while/body/eval_jaxpr/ppermute | solution.py:31
  445.9 34.3 %collective-permute-done.2 = bf16[384]{0:T(512)(128)(2,1)S(1)} collective-permute-done((bf16[384]{0:T(512)(128)(2,1)S(1)}, bf16[384]{0:T(512)(128)(2,1)S(1)}, u32[]{:S(2)}, u32[]{:S(2)}) %collective-permute-start.2) | collective-permute-done | bytes 800 | tf_op jit(solution)/shard_map/while/body/eval_jaxpr/ppermute | solution.py:31
  486.4 5.2 multiply_convert_fusion.3
  503.9 4.4 bitcast_add_fusion.7
  508.3 4.7 collective-permute-done.3
  515.4 14.4 %collective-permute-done.4 = bf16[384,16,64]{0,2,1:T(8,128)(2,1)} collective-permute-done((bf16[384,16,64]{0,2,1:T(8,128)(2,1)}, bf16[384,16,64]{0,2,1:T(8,128)(2,1)}, u32[]{:S(2)}, u32[]{:S(2)}) %collective-permute-start.4) | collective-permute-done | bytes 786464 | tf_op jit(solution)/shard_map/while/body/eval_jaxpr/ppermute | solution.py:31
  532.3 31.3 %collective-permute-done.2 = bf16[384]{0:T(512)(128)(2,1)S(1)} collective-permute-done((bf16[384]{0:T(512)(128)(2,1)S(1)}, bf16[384]{0:T(512)(128)(2,1)S(1)}, u32[]{:S(2)}, u32[]{:S(2)}) %collective-permute-start.2) | collective-permute-done | bytes 800 | tf_op jit(solution)/shard_map/while/body/eval_jaxpr/ppermute | solution.py:31
  569.7 5.2 multiply_convert_fusion.3
  578.0 4.3 fusion.224
  587.7 4.4 bitcast_add_fusion.7
  598.4 14.4 %collective-permute-done.4 = bf16[384,16,64]{0,2,1:T(8,128)(2,1)} collective-permute-done((bf16[384,16,64]{0,2,1:T(8,128)(2,1)}, bf16[384,16,64]{0,2,1:T(8,128)(2,1)}, u32[]{:S(2)}, u32[]{:S(2)}) %collective-permute-start.4) | collective-permute-done | bytes 786464 | tf_op jit(solution)/shard_map/while/body/eval_jaxpr/ppermute | solution.py:31
  615.2 31.3 %collective-permute-done.2 = bf16[384]{0:T(512)(128)(2,1)S(1)} collective-permute-done((bf16[384]{0:T(512)(128)(2,1)S(1)}, bf16[384]{0:T(512)(128)(2,1)S(1)}, u32[]{:S(2)}, u32[]{:S(2)}) %collective-permute-start.2) | collective-permute-done | bytes 800 | tf_op jit(solution)/shard_map/while/body/eval_jaxpr/ppermute | solution.py:31
  652.7 5.2 multiply_convert_fusion.3
  661.0 4.3 fusion.224
  670.7 4.4 bitcast_add_fusion.7
  680.4 14.4 %collective-permute-done.4 = bf16[384,16,64]{0,2,1:T(8,128)(2,1)} collective-permute-done((bf16[384,16,64]{0,2,1:T(8,128)(2,1)}, bf16[384,16,64]{0,2,1:T(8,128)(2,1)}, u32[]{:S(2)}, u32[]{:S(2)}) %collective-permute-start.4) | collective-permute-done | bytes 786464 | tf_op jit(solution)/shard_map/while/body/eval_jaxpr/ppermute | solution.py:31
  697.2 31.3 %collective-permute-done.2 = bf16[384]{0:T(512)(128)(2,1)S(1)} collective-permute-done((bf16[384]{0:T(512)(128)(2,1)S(1)}, bf16[384]{0:T(512)(128)(2,1)S(1)}, u32[]{:S(2)}, u32[]{:S(2)}) %collective-permute-start.2) | collective-permute-done | bytes 800 | tf_op jit(solution)/shard_map/while/body/eval_jaxpr/ppermute | solution.py:31
  749.7 10.3 convolution_convert_fusion.1
  760.4 10.2 convolution_convert_fusion
  775.1 8.7 reduce-scatter.12.cloned.1.call-done
  783.8 45.5 %reduce-scatter.14.cloned.1.call-done = bf16[256,1024]{1,0:T(8,128)(2,1)} async-done(((bf16[1024,1024]{1,0:T(8,128)(2,1)}), bf16[256,1024]{1,0:T(8,128)(2,1)}) %reduce-scatter.14.cloned.1.call-update) | async-done | bytes 524304 | tf_op jit(solution)/shard_map/reduce_scatter | solution.py:370
  829.3 45.5 %reduce-scatter.16.cloned.1.call-done = bf16[256,1024]{1,0:T(8,128)(2,1)} async-done(((bf16[1024,1024]{1,0:T(8,128)(2,1)}), bf16[256,1024]{1,0:T(8,128)(2,1)}) %reduce-scatter.16.cloned.1.call-update) | async-done | bytes 524304 | tf_op jit(solution)/shard_map/reduce_scatter | solution.py:373
  874.8 45.6 %reduce-scatter.18.cloned.1.call-done = bf16[256,1024]{1,0:T(8,128)(2,1)} async-done(((bf16[1024,1024]{1,0:T(8,128)(2,1)}), bf16[256,1024]{1,0:T(8,128)(2,1)}) %reduce-scatter.18.cloned.1.call-update) | async-done | bytes 524304 | tf_op jit(solution)/shard_map/reduce_scatter | solution.py:376
  920.4 147.6 %reduce-scatter.20.cloned.1.call-done = bf16[256,4096]{1,0:T(8,128)(2,1)} async-done(((bf16[1024,4096]{1,0:T(8,128)(2,1)}), bf16[256,4096]{1,0:T(8,128)(2,1)}) %reduce-scatter.20.cloned.1.call-update) | async-done | bytes 2097168 | tf_op jit(solution)/shard_map/reduce_scatter | solution.py:385
  1068.0 147.4 %reduce-scatter.22.cloned.1.call-done = bf16[1024,1024]{1,0:T(8,128)(2,1)} async-done(((bf16[4096,1024]{1,0:T(8,128)(2,1)}), bf16[1024,1024]{1,0:T(8,128)(2,1)}) %reduce-scatter.22.cloned.1.call-update) | async-done | bytes 2097168 | tf_op jit(solution)/shard_map/reduce_scatter | solution.py:391
  1219.3 39.8 %psum.142 = f32[]{:T(128)} all-reduce(f32[]{:T(128)} %multiply_reduce_fusion.8), channel_id=1, replica_groups=mesh['dp'=8,'blk'=4] {'dp','blk'}, use_global_device_ids=true, to_apply=%region_33.34 | all-reduce | flops 1 | bytes 8 | tf_op jit(solution)/shard_map/psum | solution.py:277
  1270.4 13.9 %all-reduce.11 = (bf16[1024]{0:T(1024)(128)(2,1)S(1)}, bf16[1024]{0:T(1024)(128)(2,1)S(1)}, bf16[1024]{0:T(1024)(128)(2,1)S(1)}, bf16[1024]{0:T(1024)(128)(2,1)S...) all-reduce(bf16[1024]{0:T(1024)(128)(2,1)S(1)} %get-tuple-element.7, ...), channel_id=2, replica_groups=mesh['dp'=8,'blk'=4] {'blk'}, use_global_device_ids=true, to_apply=%region_35.36.clone | all-reduce | flops 10256 | bytes 41024
  1294.0 16.1 %all-reduce.9 = (bf16[256]{0:T(256)(128)(2,1)S(1)}, bf16[256]{0:T(256)(128)(2,1)S(1)}, bf16[256]{0:T(256)(128)(2,1)S(1)}, bf16[256]{0:T(256)(128)(2,1)S(1)}, bf1...) all-reduce(bf16[256]{0:T(256)(128)(2,1)S(1)} %dynamic-slice.1, ...), channel_id=1, replica_groups=mesh['dp'=8,'blk'=4] {'dp'}, use_global_device_ids=true, to_apply=%region_36.37 | all-reduce | flops 4612 | bytes 18448 | tf_op jit(solution)/shard_map/psum | solution.py:414
  1315.2 40.3 %all-reduce.14.cloned.1.call-done = (bf16[256,1024]{1,0:T(8,128)(2,1)}, bf16[256,1024]{1,0:T(8,128)(2,1)}, bf16[256,1024]{1,0:T(8,128)(2,1)}, bf16[256,1024]{1,0...) async-done(((bf16[256,1024]{1,0:T(8,128)(2,1)}, bf16[256,1024]{1,0:T(8,128)(2,1)}, ...) | async-done | bytes 7077904 | tf_op jit(solution)/shard_map/psum | solution.py:416
  (473 shorter events, 260.8 us)
Async XLA Ops:
  7.2 71.0 %all-gather.4.cloned.1.call-start = ((), (), s32[]{:S(2)}) async-start(), calls=%async_computation.9 | async-start | bytes 3932160 | tf_op jit(solution)/shard_map/all_gather | solution.py:224
  14.7 127.8 %all-gather.6.cloned.1.call-start = ((), (), s32[]{:S(2)}) async-start(), calls=%async_computation.10 | async-start | bytes 3932160 | tf_op jit(solution)/shard_map/all_gather | solution.py:225
  16.8 758.3 %reduce-scatter.26.cloned.1.call-start = ((), (), s32[]{:S(2)}) async-start(), calls=%async_computation.18 | async-start | bytes 1310720 | tf_op jit(solution)/shard_map/reduce_scatter | solution.py:403
  21.5 15.8 %copy-start.61 = (f32[16]{0:T(128)S(1)}, f32[16]{0:T(128)}, u32[]{:S(2)}) copy-start(f32[16]{0:T(128)} %param.48) | copy-start | bytes 196
  27.8 114.7 %copy-start.44 = (bf16[384]{0:T(512)(128)(2,1)}, bf16[384]{0:T(512)(128)(2,1)S(1)}, u32[]{:S(2)}) copy-start(bf16[384]{0:T(512)(128)(2,1)S(1)} %convert_element_type.308) | copy-start | bytes 2308
  244.6 25.5 %slice-start.3 = ((s8[8388608]{0:T(1024)(128)(4,1)}), s8[4194304]{0:T(1024)(128)(4,1)S(1)}, s32[]{:S(2)}) async-start(s8[8388608]{0:T(1024)(128)(4,1)} %bitcast.174), calls=%async_computation.24 | async-start | bytes 8388608
  247.6 22.5 %copy-start.7 = (f32[384,1024]{1,0:T(8,128)}, f32[384,1024]{1,0:T(8,128)S(1)}, u32[]{:S(2)}) copy-start(f32[384,1024]{1,0:T(8,128)S(1)} %get-tuple-element.864) | copy-start | bytes 4718596
  247.9 22.2 %slice-start.4 = ((s8[8388608]{0:T(1024)(128)(4,1)}), s8[4194304]{0:T(1024)(128)(4,1)S(1)}, s32[]{:S(2)}) async-start(s8[8388608]{0:T(1024)(128)(4,1)} %bitcast.174), calls=%async_computation.25 | async-start | bytes 8388608
  248.0 22.2 %copy-start.68 = (f32[1024]{0:T(1024)S(1)}, f32[1024]{0:T(1024)}, u32[]{:S(2)}) copy-start(f32[1024]{0:T(1024)} %param.43) | copy-start | bytes 12292
  275.6 46.3 %copy-start.36 = (f32[384,16]{0,1:T(8,128)}, f32[384,16]{0,1:T(8,128)S(1)}, u32[]{:S(2)}) copy-start(f32[384,16]{0,1:T(8,128)S(1)} %get-tuple-element.867) | copy-start | bytes 73732
  275.6 46.3 %copy-start.48 = (f32[384]{0:T(512)}, f32[384]{0:T(512)S(1)}, u32[]{:S(2)}) copy-start(f32[384]{0:T(512)S(1)} %get-tuple-element.866) | copy-start | bytes 4612
  275.6 46.3 %copy-start.40 = (f32[384]{0:T(512)}, f32[384]{0:T(512)S(1)}, u32[]{:S(2)}) copy-start(f32[384]{0:T(512)S(1)} %fusion.96) | copy-start | bytes 4612
  324.8 21.6 %copy-start.25 = (bf16[384,512]{1,0:T(8,128)(2,1)}, bf16[384,512]{1,0:T(8,128)(2,1)S(1)}, u32[]{:S(2)}) copy-start(bf16[384,512]{1,0:T(8,128)(2,1)S(1)} %get-tuple-element.855) | copy-start | bytes 1179652
  326.7 14.7 %slice-start.5 = ((s8[8388608]{0:T(1024)(128)(4,1)}), s8[4194304]{0:T(1024)(128)(4,1)S(1)}, s32[]{:S(2)}) async-start(s8[8388608]{0:T(1024)(128)(4,1)} %bitcast.176), calls=%async_computation.26 | async-start | bytes 8388608
  348.1 427.0 %reduce-scatter.24.cloned.1.call-start = ((), (), s32[]{:S(2)}) async-start(), calls=%async_computation.17 | async-start | bytes 2621440 | tf_op jit(solution)/shard_map/reduce_scatter | solution.py:397
  363.3 420.5 %reduce-scatter.12.cloned.1.call-start = ((), (), s32[]{:S(2)}) async-start(), calls=%async_computation.11 | async-start | bytes 2621440 | tf_op jit(solution)/shard_map/reduce_scatter | solution.py:367
  377.9 34.7 %collective-permute-start.3 = (bf16[384,16,64]{0,2,1:T(8,128)(2,1)}, bf16[384,16,64]{0,2,1:T(8,128)(2,1)}, u32[]{:S(2)}, u32[]{:S(2)}) collective-permute-start(bf16[384,16,64]{0,2,1:T(8,128)(2,1)} %fusion.223), channel_id=1, source_target_pairs={{0,3},{1,0},{2,1},{3,2},{4,7},{5,4},{6,5},{7,6},{8,11},{9,8},{10,9... | collective-permute-start | bytes 2359304 | tf_op jit(solution)/shard_map/while/body/eval_jaxpr/ppermute | solution.py:31
  383.2 60.2 %collective-permute-start.4 = (bf16[384,16,64]{0,2,1:T(8,128)(2,1)}, bf16[384,16,64]{0,2,1:T(8,128)(2,1)}, u32[]{:S(2)}, u32[]{:S(2)}) collective-permute-start(bf16[384,16,64]{0,2,1:T(8,128)(2,1)} %fusion.224), channel_id=1, source_target_pairs={{0,3},{1,0},{2,1},{3,2},{4,7},{5,4},{6,5},{7,6},{8,11},{9,8},{10,9... | collective-permute-start | bytes 2359304 | tf_op jit(solution)/shard_map/while/body/eval_jaxpr/ppermute | solution.py:31
  383.3 97.0 %collective-permute-start = (bf16[384,1024]{0,1:T(8,128)(2,1)S(1)}, bf16[384,1024]{0,1:T(8,128)(2,1)}, u32[]{:S(2)}, u32[]{:S(2)}) collective-permute-start(bf16[384,1024]{0,1:T(8,128)(2,1)S(1)} %copy.102), channel_id=1, source_target_pairs={{0,3},{1,0},{2,1},{3,2},{4,7},{5,4},{6,5},{7,6},{8,11},{9,8},{10,9... | collective-permute-start | bytes 2359304 | tf_op jit(solution)/shard_map/while/body/eval_jaxpr/ppermute | solution.py:31
  385.2 95.0 %collective-permute-start.1 = (bf16[384,1024]{0,1:T(8,128)(2,1)}, bf16[384,1024]{0,1:T(8,128)(2,1)}, u32[]{:S(2)}, u32[]{:S(2)}) collective-permute-start(bf16[384,1024]{0,1:T(8,128)(2,1)} %copy.103), channel_id=1, source_target_pairs={{0,3},{1,0},{2,1},{3,2},{4,7},{5,4},{6,5},{7,6},{8,11},{9,8},{10,9... | collective-permute-start | bytes 2359304 | tf_op jit(solution)/shard_map/while/body/eval_jaxpr/ppermute | solution.py:31
  386.0 94.2 %collective-permute-start.2 = (bf16[384]{0:T(512)(128)(2,1)S(1)}, bf16[384]{0:T(512)(128)(2,1)S(1)}, u32[]{:S(2)}, u32[]{:S(2)}) collective-permute-start(bf16[384]{0:T(512)(128)(2,1)S(1)} %copy.104), channel_id=1, source_target_pairs={{0,3},{1,0},{2,1},{3,2},{4,7},{5,4},{6,5},{7,6},{8,11},{9,8},{10,9... | collective-permute-start | bytes 2312 | tf_op jit(solution)/shard_map/while/body/eval_jaxpr/ppermute | solution.py:31
  494.7 18.3 %collective-permute-start.3 = (bf16[384,16,64]{0,2,1:T(8,128)(2,1)}, bf16[384,16,64]{0,2,1:T(8,128)(2,1)}, u32[]{:S(2)}, u32[]{:S(2)}) collective-permute-start(bf16[384,16,64]{0,2,1:T(8,128)(2,1)} %fusion.223), channel_id=1, source_target_pairs={{0,3},{1,0},{2,1},{3,2},{4,7},{5,4},{6,5},{7,6},{8,11},{9,8},{10,9... | collective-permute-start | bytes 2359304 | tf_op jit(solution)/shard_map/while/body/eval_jaxpr/ppermute | solution.py:31
  500.0 29.8 %collective-permute-start.4 = (bf16[384,16,64]{0,2,1:T(8,128)(2,1)}, bf16[384,16,64]{0,2,1:T(8,128)(2,1)}, u32[]{:S(2)}, u32[]{:S(2)}) collective-permute-start(bf16[384,16,64]{0,2,1:T(8,128)(2,1)} %fusion.224), channel_id=1, source_target_pairs={{0,3},{1,0},{2,1},{3,2},{4,7},{5,4},{6,5},{7,6},{8,11},{9,8},{10,9... | collective-permute-start | bytes 2359304 | tf_op jit(solution)/shard_map/while/body/eval_jaxpr/ppermute | solution.py:31
  500.1 63.5 %collective-permute-start = (bf16[384,1024]{0,1:T(8,128)(2,1)S(1)}, bf16[384,1024]{0,1:T(8,128)(2,1)}, u32[]{:S(2)}, u32[]{:S(2)}) collective-permute-start(bf16[384,1024]{0,1:T(8,128)(2,1)S(1)} %copy.102), channel_id=1, source_target_pairs={{0,3},{1,0},{2,1},{3,2},{4,7},{5,4},{6,5},{7,6},{8,11},{9,8},{10,9... | collective-permute-start | bytes 2359304 | tf_op jit(solution)/shard_map/while/body/eval_jaxpr/ppermute | solution.py:31
  503.8 59.8 %collective-permute-start.1 = (bf16[384,1024]{0,1:T(8,128)(2,1)}, bf16[384,1024]{0,1:T(8,128)(2,1)}, u32[]{:S(2)}, u32[]{:S(2)}) collective-permute-start(bf16[384,1024]{0,1:T(8,128)(2,1)} %copy.103), channel_id=1, source_target_pairs={{0,3},{1,0},{2,1},{3,2},{4,7},{5,4},{6,5},{7,6},{8,11},{9,8},{10,9... | collective-permute-start | bytes 2359304 | tf_op jit(solution)/shard_map/while/body/eval_jaxpr/ppermute | solution.py:31
  503.9 59.7 %collective-permute-start.2 = (bf16[384]{0:T(512)(128)(2,1)S(1)}, bf16[384]{0:T(512)(128)(2,1)S(1)}, u32[]{:S(2)}, u32[]{:S(2)}) collective-permute-start(bf16[384]{0:T(512)(128)(2,1)S(1)} %copy.104), channel_id=1, source_target_pairs={{0,3},{1,0},{2,1},{3,2},{4,7},{5,4},{6,5},{7,6},{8,11},{9,8},{10,9... | collective-permute-start | bytes 2312 | tf_op jit(solution)/shard_map/while/body/eval_jaxpr/ppermute | solution.py:31
  578.0 17.9 %collective-permute-start.3 = (bf16[384,16,64]{0,2,1:T(8,128)(2,1)}, bf16[384,16,64]{0,2,1:T(8,128)(2,1)}, u32[]{:S(2)}, u32[]{:S(2)}) collective-permute-start(bf16[384,16,64]{0,2,1:T(8,128)(2,1)} %fusion.223), channel_id=1, source_target_pairs={{0,3},{1,0},{2,1},{3,2},{4,7},{5,4},{6,5},{7,6},{8,11},{9,8},{10,9... | collective-permute-start | bytes 2359304 | tf_op jit(solution)/shard_map/while/body/eval_jaxpr/ppermute | solution.py:31
  582.3 30.4 %collective-permute-start.4 = (bf16[384,16,64]{0,2,1:T(8,128)(2,1)}, bf16[384,16,64]{0,2,1:T(8,128)(2,1)}, u32[]{:S(2)}, u32[]{:S(2)}) collective-permute-start(bf16[384,16,64]{0,2,1:T(8,128)(2,1)} %fusion.224), channel_id=1, source_target_pairs={{0,3},{1,0},{2,1},{3,2},{4,7},{5,4},{6,5},{7,6},{8,11},{9,8},{10,9... | collective-permute-start | bytes 2359304 | tf_op jit(solution)/shard_map/while/body/eval_jaxpr/ppermute | solution.py:31
  583.6 62.9 %collective-permute-start = (bf16[384,1024]{0,1:T(8,128)(2,1)S(1)}, bf16[384,1024]{0,1:T(8,128)(2,1)}, u32[]{:S(2)}, u32[]{:S(2)}) collective-permute-start(bf16[384,1024]{0,1:T(8,128)(2,1)S(1)} %copy.102), channel_id=1, source_target_pairs={{0,3},{1,0},{2,1},{3,2},{4,7},{5,4},{6,5},{7,6},{8,11},{9,8},{10,9... | collective-permute-start | bytes 2359304 | tf_op jit(solution)/shard_map/while/body/eval_jaxpr/ppermute | solution.py:31
  587.7 58.8 %collective-permute-start.1 = (bf16[384,1024]{0,1:T(8,128)(2,1)}, bf16[384,1024]{0,1:T(8,128)(2,1)}, u32[]{:S(2)}, u32[]{:S(2)}) collective-permute-start(bf16[384,1024]{0,1:T(8,128)(2,1)} %copy.103), channel_id=1, source_target_pairs={{0,3},{1,0},{2,1},{3,2},{4,7},{5,4},{6,5},{7,6},{8,11},{9,8},{10,9... | collective-permute-start | bytes 2359304 | tf_op jit(solution)/shard_map/while/body/eval_jaxpr/ppermute | solution.py:31
  587.7 58.8 %collective-permute-start.2 = (bf16[384]{0:T(512)(128)(2,1)S(1)}, bf16[384]{0:T(512)(128)(2,1)S(1)}, u32[]{:S(2)}, u32[]{:S(2)}) collective-permute-start(bf16[384]{0:T(512)(128)(2,1)S(1)} %copy.104), channel_id=1, source_target_pairs={{0,3},{1,0},{2,1},{3,2},{4,7},{5,4},{6,5},{7,6},{8,11},{9,8},{10,9... | collective-permute-start | bytes 2312 | tf_op jit(solution)/shard_map/while/body/eval_jaxpr/ppermute | solution.py:31
  661.0 17.0 %collective-permute-start.3 = (bf16[384,16,64]{0,2,1:T(8,128)(2,1)}, bf16[384,16,64]{0,2,1:T(8,128)(2,1)}, u32[]{:S(2)}, u32[]{:S(2)}) collective-permute-start(bf16[384,16,64]{0,2,1:T(8,128)(2,1)} %fusion.223), channel_id=1, source_target_pairs={{0,3},{1,0},{2,1},{3,2},{4,7},{5,4},{6,5},{7,6},{8,11},{9,8},{10,9... | collective-permute-start | bytes 2359304 | tf_op jit(solution)/shard_map/while/body/eval_jaxpr/ppermute | solution.py:31
  665.3 29.5 %collective-permute-start.4 = (bf16[384,16,64]{0,2,1:T(8,128)(2,1)}, bf16[384,16,64]{0,2,1:T(8,128)(2,1)}, u32[]{:S(2)}, u32[]{:S(2)}) collective-permute-start(bf16[384,16,64]{0,2,1:T(8,128)(2,1)} %fusion.224), channel_id=1, source_target_pairs={{0,3},{1,0},{2,1},{3,2},{4,7},{5,4},{6,5},{7,6},{8,11},{9,8},{10,9... | collective-permute-start | bytes 2359304 | tf_op jit(solution)/shard_map/while/body/eval_jaxpr/ppermute | solution.py:31
  666.6 61.9 %collective-permute-start = (bf16[384,1024]{0,1:T(8,128)(2,1)S(1)}, bf16[384,1024]{0,1:T(8,128)(2,1)}, u32[]{:S(2)}, u32[]{:S(2)}) collective-permute-start(bf16[384,1024]{0,1:T(8,128)(2,1)S(1)} %copy.102), channel_id=1, source_target_pairs={{0,3},{1,0},{2,1},{3,2},{4,7},{5,4},{6,5},{7,6},{8,11},{9,8},{10,9... | collective-permute-start | bytes 2359304 | tf_op jit(solution)/shard_map/while/body/eval_jaxpr/ppermute | solution.py:31
  670.6 57.9 %collective-permute-start.1 = (bf16[384,1024]{0,1:T(8,128)(2,1)}, bf16[384,1024]{0,1:T(8,128)(2,1)}, u32[]{:S(2)}, u32[]{:S(2)}) collective-permute-start(bf16[384,1024]{0,1:T(8,128)(2,1)} %copy.103), channel_id=1, source_target_pairs={{0,3},{1,0},{2,1},{3,2},{4,7},{5,4},{6,5},{7,6},{8,11},{9,8},{10,9... | collective-permute-start | bytes 2359304 | tf_op jit(solution)/shard_map/while/body/eval_jaxpr/ppermute | solution.py:31
  670.6 57.9 %collective-permute-start.2 = (bf16[384]{0:T(512)(128)(2,1)S(1)}, bf16[384]{0:T(512)(128)(2,1)S(1)}, u32[]{:S(2)}, u32[]{:S(2)}) collective-permute-start(bf16[384]{0:T(512)(128)(2,1)S(1)} %copy.104), channel_id=1, source_target_pairs={{0,3},{1,0},{2,1},{3,2},{4,7},{5,4},{6,5},{7,6},{8,11},{9,8},{10,9... | collective-permute-start | bytes 2312 | tf_op jit(solution)/shard_map/while/body/eval_jaxpr/ppermute | solution.py:31
  733.9 95.4 %reduce-scatter.14.cloned.1.call-start = ((), (), s32[]{:S(2)}) async-start(), calls=%async_computation.12 | async-start | bytes 2621440 | tf_op jit(solution)/shard_map/reduce_scatter | solution.py:370
  739.5 135.3 %reduce-scatter.16.cloned.1.call-start = ((), (), s32[]{:S(2)}) async-start(), calls=%async_computation.13 | async-start | bytes 2621440 | tf_op jit(solution)/shard_map/reduce_scatter | solution.py:373
  744.8 175.7 %reduce-scatter.18.cloned.1.call-start = ((), (), s32[]{:S(2)}) async-start(), calls=%async_computation.14 | async-start | bytes 2621440 | tf_op jit(solution)/shard_map/reduce_scatter | solution.py:376
  749.1 318.9 %reduce-scatter.20.cloned.1.call-start = ((), (), s32[]{:S(2)}) async-start(), calls=%async_computation.15 | async-start | bytes 10485760 | tf_op jit(solution)/shard_map/reduce_scatter | solution.py:385
  760.1 455.4 %reduce-scatter.22.cloned.1.call-start = ((), (), s32[]{:S(2)}) async-start(), calls=%async_computation.16 | async-start | bytes 10485760 | tf_op jit(solution)/shard_map/reduce_scatter | solution.py:391
  770.6 522.6 %reduce-scatter.28.cloned.1.call-start = ((), (), s32[]{:S(2)}) async-start(), calls=%async_computation.19 | async-start | bytes 163840
  775.0 580.4 %all-reduce.14.cloned.1.call-start = ((), (), s32[]{:S(2)}) async-start(), calls=%async_computation.20 | async-start | bytes 14155776 | tf_op jit(solution)/shard_map/psum | solution.py:416
  1215.5 43.6 %copy-start.59 = (f32[16]{0:T(128)S(1)}, f32[16]{0:T(128)}, u32[]{:S(2)}) copy-start(f32[16]{0:T(128)} %get-tuple-element.842) | copy-start | bytes 196
  1215.5 43.6 %copy-start.63 = (f32[16]{0:T(128)S(1)}, f32[16]{0:T(128)}, u32[]{:S(2)}) copy-start(f32[16]{0:T(128)} %get-tuple-element.755) | copy-start | bytes 196
  1215.5 46.7 %copy-start.62 = (f32[16]{0:T(128)S(1)}, f32[16]{0:T(128)}, u32[]{:S(2)}) copy-start(f32[16]{0:T(128)} %param.48) | copy-start | bytes 196
  1268.4 17.7 %copy-start.57 = (f32[512]{0:T(512)S(1)}, f32[512]{0:T(512)}, u32[]{:S(2)}) copy-start(f32[512]{0:T(512)} %copy-done.56) | copy-start | bytes 6148
  1268.4 19.7 %copy-start.26 = (bf16[384,512]{1,0:T(8,128)(2,1)S(1)}, bf16[384,512]{1,0:T(8,128)(2,1)}, u32[]{:S(2)}) copy-start(bf16[384,512]{1,0:T(8,128)(2,1)} %copy-done.25) | copy-start | bytes 1179652
  (84 other events, 376.2 us)
Sparse Core Ops, SparseCore 0:
  14.8 63.3 all-gather.3
  80.4 62.1 all-gather.5
  348.3 26.9 reduce-scatter.25
  377.5 76.8 reduce-scatter.23
  734.1 49.7 reduce-scatter.11
  786.1 43.1 reduce-scatter.13
  831.6 43.1 reduce-scatter.15
  877.2 43.1 reduce-scatter.17
  922.8 145.1 reduce-scatter.19
  1070.2 145.1 reduce-scatter.21
  1218.3 14.9 reduce-scatter.27
  1237.9 117.5 all-reduce.13
where the time goes:
time: 1390 us; the launch traced here: 1380 us
  waiting for transfers between devices  815 us (59%)
  matrix products  256 us (18%)
  blocking collectives  119 us (9%)
  other arithmetic  75.6 us (5%)
  local copies, waits for them, and re-layouts  62.8 us (5%)
  between operations  23.6 us (2%)
  starting transfers between devices  21.8 us (2%)
    ppermute x20, waiting for transfers between devices, passed_along(): return lax.ppermute(value, axis, pairs)  234 us
    reduce_scatter x1, waiting for transfers between devices, local(): lax.psum_scatter(grad_up.astype(jnp.bfloat16), 'blk', scatter_dimension=0...  148 us
    reduce_scatter x1, waiting for transfers between devices, local(): lax.psum_scatter(grad_down.astype(jnp.bfloat16), 'blk', scatter_dimension...  147 us
    psum x2, blocking collectives, local(): lax.psum((jnp.sum(kl_dim * real[:, None], axis=0), jnp.sum(categorical *...  79.6 us
    all_gather x1, waiting for transfers between devices, local(): piece_values = lax.all_gather(values, 'blk', axis=0, tiled=True)  64.3 us
    reduce_scatter x1, waiting for transfers between devices, local(): lax.psum_scatter(grad_out.astype(jnp.bfloat16), 'blk', scatter_dimension=...  45.6 us
    reduce_scatter x1, waiting for transfers between devices, local(): lax.psum_scatter(grad_value.astype(jnp.bfloat16), 'blk', scatter_dimensio...  45.5 us
    reduce_scatter x1, waiting for transfers between devices, local(): lax.psum_scatter(grad_key.astype(jnp.bfloat16), 'blk', scatter_dimension=...  45.5 us
  transfers between devices with their start and end apart: 32, of which 21 were waited for; matrix products, arithmetic and copies ran while one was open for 15% of the time, Pallas kernels for 0%

commit v1 on v0

--- a/solution.py
+++ b/solution.py
@@ -9,6 +9,7 @@
 H = 16
 HD = 64
 LAT = 512
+K = 16
 WARM = 2000
 
 
@@ -173,6 +174,115 @@
         key_pos,
         key_slide,
     )
+
+
+MESH_AXES = ("dp", "blk")
+
+
+def swapped(value, dp_mask, blk_mask):
+    groups, blocks = lax.axis_size("dp"), lax.axis_size("blk")
+    pairs = [
+        (g * blocks + b, (g ^ dp_mask) * blocks + (b ^ blk_mask))
+        for g in range(groups)
+        for b in range(blocks)
+    ]
+    return lax.ppermute(value, MESH_AXES, pairs)
+
+
+def bits_of(count):
+    return count.bit_length() - 1
+
+
+def dp_masks():
+    return [1 << t for t in range(bits_of(lax.axis_size("dp")))]
+
+
+def blk_masks():
+    return [(2 << t) - 1 for t in range(bits_of(lax.axis_size("blk")))]
+
+
+def blk_sides(index):
+    count = bits_of(lax.axis_size("blk"))
+    return [((index >> t) ^ (index >> (t + 1))) & 1 for t in range(count)]
+
+
+def blk_leaf_order():
+    blocks = lax.axis_size("blk")
+    order = [0] * blocks
+    for index in range(blocks):
+        leaf = 0
+        for side in blk_sides(index):
+            leaf = 2 * leaf + side
+        order[leaf] = index
+    return order
+
+
+def summed_everywhere(value):
+    for mask in dp_masks():
+        value = value + swapped(value, mask, 0)
+    for mask in blk_masks():
+        value = value + swapped(value, 0, mask)
+    return value
+
+
+def halves(value, side, axis):
+    size = value.shape[axis] // 2
+    keep = lax.dynamic_slice_in_dim(value, side * size, size, axis)
+    send = lax.dynamic_slice_in_dim(value, (1 - side) * size, size, axis)
+    return keep, send
+
+
+def added(left, right):
+    return (left.astype(jnp.float32) + right.astype(jnp.float32)).astype(jnp.bfloat16)
+
+
+def joined(mine, other, side, axis):
+    first = jnp.where(side == 0, mine, other)
+    second = jnp.where(side == 0, other, mine)
+    return jnp.concatenate([first, second], axis=axis)
+
+
+def reduced(grad, flipped):
+    blocks = lax.axis_size("blk")
+    group, block = lax.axis_index("dp"), lax.axis_index("blk")
+    rows, cols = grad.shape
+    value = grad.astype(jnp.bfloat16).reshape(blocks, rows // blocks, cols)
+    steps = dp_masks()
+    if flipped:
+        steps = steps[:1] + steps[1:][::-1]
+    sides = [(group // mask) % 2 for mask in steps]
+    for mask, side in zip(steps, sides):
+        keep, send = halves(value, side, 1)
+        value = added(keep, swapped(send, mask, 0))
+    value = jnp.stack([value[index] for index in blk_leaf_order()])
+    for mask, side in zip(blk_masks(), blk_sides(block)):
+        keep, send = halves(value, side, 0)
+        value = added(keep, swapped(send, 0, mask))
+    value = value[0]
+    for mask, side in reversed(list(zip(steps, sides))):
+        value = joined(value, swapped(value, mask, 0), side, 0)
+    return value.astype(jnp.float32)
+
+
+def reduced_small(parts):
+    block = lax.axis_index("blk")
+    sizes = [part.shape[1] for part in parts]
+    total = sum(sizes)
+    padded = -(-total // 1024) * 1024
+    value = jnp.concatenate(parts, axis=1)
+    value = jnp.pad(value, ((0, 0), (0, padded - total)))
+    value = jnp.stack([value[index] for index in blk_leaf_order()])
+    for mask, side in zip(blk_masks(), blk_sides(block)):
+        keep, send = halves(value, side, 0)
+        value = keep + swapped(send, 0, mask)
+    value = value[0]
+    for mask in dp_masks():
+        value = value + swapped(value, mask, 0)
+    pieces, start = [], 0
+    for size in sizes:
+        pieces.append(value[start : start + size])
+        start += size
+    return pieces
 
 
 def local(
@@ -274,10 +384,16 @@
         kl_terms, latent_mean, latent_logvar, prior_means, prior_logits
     )
     real = cell_mask.astype(jnp.float32)
-    kl_sum, cat_sum, count = lax.psum(
-        (jnp.sum(kl_dim * real[:, None], axis=0), jnp.sum(categorical * real), jnp.sum(real)),
-        ("dp", "blk"),
-    )
+    sums = jnp.concatenate(
+        [
+            jnp.sum(kl_dim * real[:, None], axis=0),
+            jnp.sum(categorical * real)[None],
+            jnp.sum(real)[None],
+            jnp.zeros((126,), jnp.float32),
+        ]
+    )
+    sums = summed_everywhere(sums)
+    kl_sum, cat_sum, count = sums[:LAT], sums[LAT], sums[LAT + 1]
     kbar = kl_sum / count
     floored = jnp.sum(jnp.maximum(kbar, free_floor))
     cat_mean = cat_sum / count
@@ -357,77 +473,39 @@
     )
     grad_from_norm, grad_attn_gain, grad_attn_shift = norm_back(grad_normed)
     states_grad = grad_hidden + grad_from_norm
-    shares = (
-        lax.psum_scatter(
-            grad_attn_gain.astype(jnp.bfloat16), "blk", scatter_dimension=0, tiled=True
-        ).astype(jnp.float32),
-        lax.psum_scatter(
-            grad_attn_shift.astype(jnp.bfloat16), "blk", scatter_dimension=0, tiled=True
-        ).astype(jnp.float32),
-        lax.psum_scatter(
-            grad_query.astype(jnp.bfloat16), "blk", scatter_dimension=0, tiled=True
-        ).astype(jnp.float32),
-        lax.psum_scatter(
-            grad_key.astype(jnp.bfloat16), "blk", scatter_dimension=0, tiled=True
-        ).astype(jnp.float32),
-        lax.psum_scatter(
-            grad_value.astype(jnp.bfloat16), "blk", scatter_dimension=0, tiled=True
-        ).astype(jnp.float32),
-        lax.psum_scatter(
-            grad_out.astype(jnp.bfloat16), "blk", scatter_dimension=0, tiled=True
-        ).astype(jnp.float32),
-        lax.psum_scatter(
-            grad_ffn_gain.astype(jnp.bfloat16), "blk", scatter_dimension=0, tiled=True
-        ).astype(jnp.float32),
-        lax.psum_scatter(
-            grad_ffn_shift.astype(jnp.bfloat16), "blk", scatter_dimension=0, tiled=True
-        ).astype(jnp.float32),
-        lax.psum_scatter(
-            grad_up.astype(jnp.bfloat16), "blk", scatter_dimension=0, tiled=True
-        ).astype(jnp.float32),
-        lax.psum_scatter(
-            grad_up_bias.astype(jnp.bfloat16), "blk", scatter_dimension=0, tiled=True
-        ).astype(jnp.float32),
-        lax.psum_scatter(
-            grad_down.astype(jnp.bfloat16), "blk", scatter_dimension=0, tiled=True
-        ).astype(jnp.float32),
-        lax.psum_scatter(
-            grad_down_bias.astype(jnp.bfloat16), "blk", scatter_dimension=0, tiled=True
-        ).astype(jnp.float32),
-        lax.psum_scatter(
-            grad_encode.astype(jnp.bfloat16), "blk", scatter_dimension=0, tiled=True
-        ).astype(jnp.float32),
-        lax.psum_scatter(
-            grad_encode_bias.astype(jnp.bfloat16), "blk", scatter_dimension=0, tiled=True
-        ).astype(jnp.float32),
-        lax.psum_scatter(
-            grad_decode.astype(jnp.bfloat16), "blk", scatter_dimension=0, tiled=True
-        ).astype(jnp.float32),
-        lax.psum_scatter(
-            grad_means.astype(jnp.bfloat16), "blk", scatter_dimension=1, tiled=True
-        ).astype(jnp.float32),
-        lax.psum_scatter(
-            grad_prior.astype(jnp.bfloat16), "blk", scatter_dimension=0, tiled=True
-        ).astype(jnp.float32),
+    by_block = lambda part: part.reshape(blocks, -1)
+    means_block = jnp.moveaxis(grad_means.reshape(K, blocks, LAT // blocks), 1, 0)
+    small = reduced_small(
+        [
+            by_block(grad_attn_gain),
+            by_block(grad_attn_shift),
+            by_block(grad_ffn_gain),
+            by_block(grad_ffn_shift),
+            by_block(grad_up_bias),
+            by_block(grad_down_bias),
+            by_block(grad_encode_bias),
+            by_block(means_block),
+            by_block(grad_prior),
+        ]
     )
     totals = (
-        lax.psum(shares[0].astype(jnp.bfloat16), "dp").astype(jnp.float32),
-        lax.psum(shares[1].astype(jnp.bfloat16), "dp").astype(jnp.float32),
-        lax.psum(shares[2].astype(jnp.bfloat16), "dp").astype(jnp.float32),
-        lax.psum(shares[3].astype(jnp.bfloat16), "dp").astype(jnp.float32),
-        lax.psum(shares[4].astype(jnp.bfloat16), "dp").astype(jnp.float32),
-        lax.psum(shares[5].astype(jnp.bfloat16), "dp").astype(jnp.float32),
-        lax.psum(shares[6].astype(jnp.bfloat16), "dp").astype(jnp.float32),
-        lax.psum(shares[7].astype(jnp.bfloat16), "dp").astype(jnp.float32),
-        lax.psum(shares[8].astype(jnp.bfloat16), "dp").astype(jnp.float32),
-        lax.psum(shares[9].astype(jnp.bfloat16), "dp").astype(jnp.float32),
-        lax.psum(shares[10].astype(jnp.bfloat16), "dp").astype(jnp.float32),
-        lax.psum(shares[11].astype(jnp.bfloat16), "dp").astype(jnp.float32),
-        lax.psum(shares[12].astype(jnp.bfloat16), "dp").astype(jnp.float32),
-        lax.psum(shares[13].astype(jnp.bfloat16), "dp").astype(jnp.float32),
-        lax.psum(shares[14].astype(jnp.bfloat16), "dp").astype(jnp.float32),
-        lax.psum(shares[15].astype(jnp.bfloat16), "dp").astype(jnp.float32),
-        lax.psum(shares[16].astype(jnp.bfloat16), "dp").astype(jnp.float32),
+        small[0],
+        small[1],
+        reduced(grad_query, False),
+        reduced(grad_key, True),
+        reduced(grad_value, False),
+        reduced(grad_out, True),
+        small[2],
+        small[3],
+        reduced(grad_up, True),
+        small[4],
+        reduced(grad_down, False),
+        small[5],
+        reduced(grad_encode, True),
+        small[6],
+        reduced(grad_decode, False),
+        small[7].reshape(K, LAT // blocks),
+        small[8],
     )
     kl_out = (floored / LAT + cat_mean).reshape(1)
     return (output.astype(jnp.bfloat16), states_grad, kl_out) + tuple(totals)

time: 1390 us -> 1020 us (0.73)
  waiting for transfers between devices: 815 us -> 442 us
  starting transfers between devices: 21.8 us -> 131 us
  blocking collectives: 119 us -> 10.3 us
  matrix products: 256 us -> 208 us
  other arithmetic: 75.6 us -> 105 us
  local copies, waits for them, and re-layouts: 62.8 us -> 85.9 us
    reduce_scatter x8 -> x0, waiting for transfers between devices: 440 us -> none  [the longest x1 148 us: local(): lax.psum_scatter(grad_up.astype(jnp.bfloat16), 'blk', scatter_dimension=0...]
    ppermute x0 -> x74, waiting for transfers between devices: none -> 146 us  [swapped(): return lax.ppermute(value, MESH_AXES, pairs)]
    ppermute x0 -> x74, starting transfers between devices: none -> 110 us  [swapped(): return lax.ppermute(value, MESH_AXES, pairs)]
    psum x3 -> x0, blocking collectives: 95.7 us -> none  [the longest x2 79.6 us: local(): lax.psum((jnp.sum(kl_dim * real[:, None], axis=0), jnp.sum(categorical *...]
    ppermute x20, waiting for transfers between devices: 234 us -> 191 us  [passed_along(): return lax.ppermute(value, axis, pairs)]
    psum x1 -> x0, waiting for transfers between devices: 40.3 us -> none  [local(): lax.psum(shares[2].astype(jnp.bfloat16), 'dp').astype(jnp.float32)]
    all_gather x1, waiting for transfers between devices: 36.4 us -> 64.3 us  [local(): piece_keys = lax.all_gather(keys, 'blk', axis=0, tiled=True)]
    all_gather x1, waiting for transfers between devices: 64.3 us -> 40 us  [local(): piece_values = lax.all_gather(values, 'blk', axis=0, tiled=True)]
  transfers between devices with their start and end apart: 32 -> 96, of which waited for: 21 -> 47; matrix products, arithmetic and copies ran while one was open for 15% -> 13% of each run, Pallas kernels for 0% -> 0%
where the time goes in v1:
time: 1020 us; the launch traced here: 1010 us
  waiting for transfers between devices  442 us (43%)
  matrix products  208 us (20%)
  starting transfers between devices  131 us (13%)
  other arithmetic  105 us (10%)
  local copies, waits for them, and re-layouts  85.9 us (8%)
  between operations  22.5 us (2%)
  blocking collectives  10.3 us (1%)
    ppermute x20, waiting for transfers between devices, passed_along(): return lax.ppermute(value, axis, pairs)  191 us
    ppermute x74, waiting for transfers between devices, swapped(): return lax.ppermute(value, MESH_AXES, pairs)  146 us
    ppermute x74, starting transfers between devices, swapped(): return lax.ppermute(value, MESH_AXES, pairs)  110 us
    all_gather x1, waiting for transfers between devices, local(): piece_keys = lax.all_gather(keys, 'blk', axis=0, tiled=True)  64.3 us
    dot_general x8, matrix products, plain_dot(): return jnp.dot(left, right, preferred_element_type=jnp.float32)  41.4 us
    all_gather x1, waiting for transfers between devices, local(): piece_values = lax.all_gather(values, 'blk', axis=0, tiled=True)  40 us
    dot_general x8, matrix products, cols_dot(): lax.dot_general(left, right, (((1,), (1,)), ((), ())), preferred_element_...  31.2 us
    dot_general x8, matrix products, rows_dot(): lax.dot_general(left, right, (((0,), (0,)), ((), ())), preferred_element_...  31.2 us
  transfers between devices with their start and end apart: 96, of which 47 were waited for; matrix products, arithmetic and copies ran while one was open for 13% of the time, Pallas kernels for 0%

profile of v1, /device:TPU:17, one launch (start us, length us, event | category | flops | bytes accessed | tf_op | source)
XLA Modules:
  0.0 1006.9 jit_solution(8252428241828500659)
XLA Ops:
  21.3 10.3 %all-gather = bf16[4,1,384]{2,1,0:T(2,128)(2,1)S(1)} all-gather(bf16[1,1,384]{2,1,0:T(2,128)(2,1)S(1)} %reshape.510), channel_id=1, replica_groups=mesh['dp'=8,'blk'=4] {'blk'}, dimensions={0}, use_global_device_ids=true | all-gather | bytes 3840 | tf_op jit(solution)/shard_map/all_gather | solution.py:336
  37.5 40.0 %all-gather.6.cloned.1.call-done = bf16[1536,1024]{1,0:T(8,128)(2,1)} async-done(((bf16[384,1024]{1,0:T(8,128)(2,1)}), bf16[1536,1024]{1,0:T(8,128)(2,1)}) %all-gather.6.cloned.1.call-update) | async-done | bytes 3145744 | tf_op jit(solution)/shard_map/all_gather | solution.py:335
  77.5 64.3 %all-gather.4.cloned.1.call-done = bf16[1536,1024]{1,0:T(8,128)(2,1)} async-done(((bf16[384,1024]{1,0:T(8,128)(2,1)}), bf16[1536,1024]{1,0:T(8,128)(2,1)}) %all-gather.4.cloned.1.call-update) | async-done | bytes 3145744 | tf_op jit(solution)/shard_map/all_gather | solution.py:334
  141.8 71.5 %while.43 = (s32[]{:T(128)}, f32[16,384]{1,0:T(8,128)S(1)}, f32[16,384]{1,0:T(8,128)S(1)}, f32[384,16,64]{0,2,1:T(8,128)}, s32[384]{0:T(512)S(1)}, /*index=5*/s3...) while((s32[]{:T(128)}, f32[16,384]{1,0:T(8,128)S(1)}, ...), condition=%wide.region_9.10_spmd.clone, body=%wide.region_5.9_spmd.clone.sunk | while | flops 636463104 | bytes 56833876 | solution.py:363
  218.4 22.4 %multiply_convert_fusion.1 = (bf16[384,4096]{1,0:T(8,128)(2,1)S(1)}, f32[384,4096]{1,0:T(8,128)}, f32[384,4096]{1,0:T(8,128)}) fusion(f32[4096]{0:T(1024)S(1)} %copy-done.71, bf16[1024,4096]{1,0:T(8,128)(2,1)} %param.40, f32[384,1024]{1,0:T(8,128)S(1)} %get-tuple-element.910, f32[1024]{0:T(1024)S(1)} %copy-done.76, f32[1024]{0:T(1024)S(1)} %copy-done.63, ...), kind=kOutput, calls=%fused_computation.52 | convolution fusion | flops 3327000576 | bytes 25717760 | tf_op jit(solution)/shard_map/dot_general | solution.py:70
  282.2 14.8 %convert_reduce_fusion.2 = (f32[4096]{0:T(1024)S(1)}, bf16[384,4096]{1,0:T(8,128)(2,1)}) fusion(f32[384,4096]{1,0:T(8,128)} %get-tuple-element.821, f32[384,4096]{1,0:T(8,128)} %get-tuple-element.911, bf16[4096,1024]{1,0:T(8,128)(2,1)} %param.42, f32[384,1024]{1,0:T(8,128)S(1)} %convert_add_fusion.1), kind=kOutput, calls=%fused_computation.50 | convolution fusion | flops 3246780416 | bytes 25706496 | tf_op jit(solution)/shard_map/dot_general | solution.py:80
  297.0 5.7 multiply_reduce_fusion
  314.2 321.3 %while.44 = (s32[]{:T(128)}, bf16[384,1024]{0,1:T(8,128)(2,1)}, bf16[384,1024]{0,1:T(8,128)(2,1)}, bf16[384]{0:T(512)(128)(2,1)S(1)}, f32[384,16,64]{0,2,1:T(8,1...) while((s32[]{:T(128)}, bf16[384,1024]{0,1:T(8,128)(2,1)}, ...), condition=%wide.region_27.28_spmd.clone, body=%wide.region_25.27_spmd.clone.sunk | while | flops 1538856192 | bytes 92547696 | solution.py:460
  321.8 5.1 multiply_convert_fusion.3
  336.8 4.1 bitcast_add_fusion.7
  340.9 3.9 collective-permute-done.3
  347.3 14.4 %collective-permute-done.4 = bf16[384,16,64]{0,2,1:T(8,128)(2,1)} collective-permute-done((bf16[384,16,64]{0,2,1:T(8,128)(2,1)}, bf16[384,16,64]{0,2,1:T(8,128)(2,1)}, u32[]{:S(2)}, u32[]{:S(2)}) %collective-permute-start.4) | collective-permute-done | bytes 786464 | tf_op jit(solution)/shard_map/while/body/eval_jaxpr/ppermute | solution.py:32
  364.2 31.2 %collective-permute-done.2 = bf16[384]{0:T(512)(128)(2,1)S(1)} collective-permute-done((bf16[384]{0:T(512)(128)(2,1)S(1)}, bf16[384]{0:T(512)(128)(2,1)S(1)}, u32[]{:S(2)}, u32[]{:S(2)}) %collective-permute-start.2) | collective-permute-done | bytes 800 | tf_op jit(solution)/shard_map/while/body/eval_jaxpr/ppermute | solution.py:32
  402.6 5.1 multiply_convert_fusion.3
  418.7 4.6 bitcast_add_fusion.7
  428.2 14.4 %collective-permute-done.4 = bf16[384,16,64]{0,2,1:T(8,128)(2,1)} collective-permute-done((bf16[384,16,64]{0,2,1:T(8,128)(2,1)}, bf16[384,16,64]{0,2,1:T(8,128)(2,1)}, u32[]{:S(2)}, u32[]{:S(2)}) %collective-permute-start.4) | collective-permute-done | bytes 786464 | tf_op jit(solution)/shard_map/while/body/eval_jaxpr/ppermute | solution.py:32
  445.2 31.2 %collective-permute-done.2 = bf16[384]{0:T(512)(128)(2,1)S(1)} collective-permute-done((bf16[384]{0:T(512)(128)(2,1)S(1)}, bf16[384]{0:T(512)(128)(2,1)S(1)}, u32[]{:S(2)}, u32[]{:S(2)}) %collective-permute-start.2) | collective-permute-done | bytes 800 | tf_op jit(solution)/shard_map/while/body/eval_jaxpr/ppermute | solution.py:32
  483.6 5.1 multiply_convert_fusion.3
  495.5 4.0 collective-permute-start
  499.6 4.6 bitcast_add_fusion.7
  508.3 14.4 %collective-permute-done.4 = bf16[384,16,64]{0,2,1:T(8,128)(2,1)} collective-permute-done((bf16[384,16,64]{0,2,1:T(8,128)(2,1)}, bf16[384,16,64]{0,2,1:T(8,128)(2,1)}, u32[]{:S(2)}, u32[]{:S(2)}) %collective-permute-start.4) | collective-permute-done | bytes 786464 | tf_op jit(solution)/shard_map/while/body/eval_jaxpr/ppermute | solution.py:32
  525.2 31.2 %collective-permute-done.2 = bf16[384]{0:T(512)(128)(2,1)S(1)} collective-permute-done((bf16[384]{0:T(512)(128)(2,1)S(1)}, bf16[384]{0:T(512)(128)(2,1)S(1)}, u32[]{:S(2)}, u32[]{:S(2)}) %collective-permute-start.2) | collective-permute-done | bytes 800 | tf_op jit(solution)/shard_map/while/body/eval_jaxpr/ppermute | solution.py:32
  563.6 5.1 multiply_convert_fusion.3
  575.6 4.0 collective-permute-start
  579.7 4.6 bitcast_add_fusion.7
  587.4 14.4 %collective-permute-done.4 = bf16[384,16,64]{0,2,1:T(8,128)(2,1)} collective-permute-done((bf16[384,16,64]{0,2,1:T(8,128)(2,1)}, bf16[384,16,64]{0,2,1:T(8,128)(2,1)}, u32[]{:S(2)}, u32[]{:S(2)}) %collective-permute-start.4) | collective-permute-done | bytes 786464 | tf_op jit(solution)/shard_map/while/body/eval_jaxpr/ppermute | solution.py:32
  604.3 31.2 %collective-permute-done.2 = bf16[384]{0:T(512)(128)(2,1)S(1)} collective-permute-done((bf16[384]{0:T(512)(128)(2,1)S(1)}, bf16[384]{0:T(512)(128)(2,1)S(1)}, u32[]{:S(2)}, u32[]{:S(2)}) %collective-permute-start.2) | collective-permute-done | bytes 800 | tf_op jit(solution)/shard_map/while/body/eval_jaxpr/ppermute | solution.py:32
  657.7 4.0 convolution_convert_fusion.4
  664.6 5.2 convolution_convert_fusion.1
  669.8 9.4 convolution_convert_fusion
  679.3 7.5 collective-permute-start.71
  742.2 4.1 collective-permute-done.78
  752.0 10.3 %collective-permute-done.40 = bf16[4,64,1024]{2,1,0:T(8,128)(2,1)S(1)} collective-permute-done((bf16[4,64,1024]{2,1,0:T(8,128)(2,1)S(1)}, bf16[4,64,1024]{2,1,0:T(8,128)(2,1)S(1)}, u32[]{:S(2)}, u32[]{:S(2)}) %collective-permute-start.40) | collective-permute-done | bytes 524320 | tf_op jit(solution)/shard_map/ppermute | solution.py:189
  763.2 10.3 %collective-permute-done.24 = bf16[4,64,1024]{2,1,0:T(8,128)(2,1)S(1)} collective-permute-done((bf16[4,64,1024]{2,1,0:T(8,128)(2,1)S(1)}, bf16[4,64,1024]{2,1,0:T(8,128)(2,1)S(1)}, u32[]{:S(2)}, u32[]{:S(2)}) %collective-permute-start.24) | collective-permute-done | bytes 524320 | tf_op jit(solution)/shard_map/ppermute | solution.py:189
  780.3 5.0 collective-permute-done.41
  786.0 5.0 collective-permute-done.25
  828.8 5.9 add_convert_fusion.1
  838.6 8.4 collective-permute-start.70
  853.8 4.3 add_convert_fusion
  858.3 16.7 %collective-permute-done.48 = bf16[4,64,4096]{2,1,0:T(8,128)(2,1)S(1)} collective-permute-done((bf16[4,64,4096]{2,1,0:T(8,128)(2,1)}, bf16[4,64,4096]{2,1,0:T(8,128)(2,1)S(1)}, u32[]{:S(2)}, u32[]{:S(2)}) %collective-permute-start.48) | collective-permute-done | bytes 2097184 | tf_op jit(solution)/shard_map/ppermute | solution.py:189
  878.6 10.2 %collective-permute-start.22 = (bf16[128,1024]{1,0:T(8,128)(2,1)S(1)}, bf16[128,1024]{1,0:T(8,128)(2,1)S(1)}, u32[]{:S(2)}, u32[]{:S(2)}) collective-permute-start(bf16[128,1024]{1,0:T(8,128)(2,1)S(1)} %pad_maximum_fusion.8), channel_id=1, source_target_pairs={{0,4},{1,5},{2,6},{3,7},{4,0},{5,1},{6,2},{7,3},{8,12},{9,13},{10,... | collective-permute-start | bytes 786440 | tf_op jit(solution)/shard_map/ppermute | solution.py:189
  890.9 21.6 %collective-permute-done.56 = bf16[4,256,1024]{2,1,0:T(8,128)(2,1)S(1)} collective-permute-done((bf16[4,256,1024]{2,1,0:T(8,128)(2,1)S(1)}, bf16[4,256,1024]{2,1,0:T(8,128)(2,1)S(1)}, u32[]{:S(2)}, u32[]{:S(2)}) %collective-permute-start.56) | collective-permute-done | bytes 2097184 | tf_op jit(solution)/shard_map/ppermute | solution.py:189
  915.6 19.4 %collective-permute-done.49 = bf16[4,32,4096]{2,1,0:T(8,128)(2,1)S(1)} collective-permute-done((bf16[4,32,4096]{2,1,0:T(8,128)(2,1)S(1)}, bf16[4,32,4096]{2,1,0:T(8,128)(2,1)S(1)}, u32[]{:S(2)}, u32[]{:S(2)}) %collective-permute-start.49) | collective-permute-done | bytes 1048608 | tf_op jit(solution)/shard_map/ppermute | solution.py:189
  937.8 6.1 collective-permute-done.50
  944.3 5.5 collective-permute-done.58
  952.0 6.4 collective-permute-done.59
  965.1 5.5 collective-permute-done.53
  970.9 18.0 %collective-permute-start.54 = (bf16[128,4096]{1,0:T(8,128)(2,1)S(1)}, bf16[128,4096]{1,0:T(8,128)(2,1)S(1)}, u32[]{:S(2)}, u32[]{:S(2)}) collective-permute-start(bf16[128,4096]{1,0:T(8,128)(2,1)S(1)} %pad_maximum_fusion.1), channel_id=1, source_target_pairs={{0,4},{1,5},{2,6},{3,7},{4,0},{5,1},{6,2},{7,3},{8,12},{9,13},{10,... | collective-permute-start | bytes 3145736 | tf_op jit(solution)/shard_map/ppermute | solution.py:189
  (759 shorter events, 401.5 us)
Async XLA Ops:
  7.2 70.2 %all-gather.6.cloned.1.call-start = ((), (), s32[]{:S(2)}) async-start(), calls=%async_computation.1 | async-start | bytes 3932160 | tf_op jit(solution)/shard_map/all_gather | solution.py:335
  14.0 127.8 %all-gather.4.cloned.1.call-start = ((), (), s32[]{:S(2)}) async-start(), calls=%async_computation | async-start | bytes 3932160 | tf_op jit(solution)/shard_map/all_gather | solution.py:334
  328.8 16.0 %collective-permute-start.3 = (bf16[384,16,64]{0,2,1:T(8,128)(2,1)}, bf16[384,16,64]{0,2,1:T(8,128)(2,1)}, u32[]{:S(2)}, u32[]{:S(2)}) collective-permute-start(bf16[384,16,64]{0,2,1:T(8,128)(2,1)} %fusion.240), channel_id=1, source_target_pairs={{0,3},{1,0},{2,1},{3,2},{4,7},{5,4},{6,5},{7,6},{8,11},{9,8},{10,9... | collective-permute-start | bytes 2359304 | tf_op jit(solution)/shard_map/while/body/eval_jaxpr/ppermute | solution.py:32
  332.8 28.9 %collective-permute-start.4 = (bf16[384,16,64]{0,2,1:T(8,128)(2,1)}, bf16[384,16,64]{0,2,1:T(8,128)(2,1)}, u32[]{:S(2)}, u32[]{:S(2)}) collective-permute-start(bf16[384,16,64]{0,2,1:T(8,128)(2,1)} %fusion.241), channel_id=1, source_target_pairs={{0,3},{1,0},{2,1},{3,2},{4,7},{5,4},{6,5},{7,6},{8,11},{9,8},{10,9... | collective-permute-start | bytes 2359304 | tf_op jit(solution)/shard_map/while/body/eval_jaxpr/ppermute | solution.py:32
  336.1 59.4 %collective-permute-start = (bf16[384,1024]{0,1:T(8,128)(2,1)}, bf16[384,1024]{0,1:T(8,128)(2,1)}, u32[]{:S(2)}, u32[]{:S(2)}) collective-permute-start(bf16[384,1024]{0,1:T(8,128)(2,1)} %copy.100), channel_id=1, source_target_pairs={{0,3},{1,0},{2,1},{3,2},{4,7},{5,4},{6,5},{7,6},{8,11},{9,8},{10,9... | collective-permute-start | bytes 2359304 | tf_op jit(solution)/shard_map/while/body/eval_jaxpr/ppermute | solution.py:32
  336.7 58.7 %collective-permute-start.1 = (bf16[384,1024]{0,1:T(8,128)(2,1)}, bf16[384,1024]{0,1:T(8,128)(2,1)}, u32[]{:S(2)}, u32[]{:S(2)}) collective-permute-start(bf16[384,1024]{0,1:T(8,128)(2,1)} %copy.101), channel_id=1, source_target_pairs={{0,3},{1,0},{2,1},{3,2},{4,7},{5,4},{6,5},{7,6},{8,11},{9,8},{10,9... | collective-permute-start | bytes 2359304 | tf_op jit(solution)/shard_map/while/body/eval_jaxpr/ppermute | solution.py:32
  336.8 58.6 %collective-permute-start.2 = (bf16[384]{0:T(512)(128)(2,1)S(1)}, bf16[384]{0:T(512)(128)(2,1)S(1)}, u32[]{:S(2)}, u32[]{:S(2)}) collective-permute-start(bf16[384]{0:T(512)(128)(2,1)S(1)} %copy.102), channel_id=1, source_target_pairs={{0,3},{1,0},{2,1},{3,2},{4,7},{5,4},{6,5},{7,6},{8,11},{9,8},{10,9... | collective-permute-start | bytes 2312 | tf_op jit(solution)/shard_map/while/body/eval_jaxpr/ppermute | solution.py:32
  409.6 16.2 %collective-permute-start.3 = (bf16[384,16,64]{0,2,1:T(8,128)(2,1)}, bf16[384,16,64]{0,2,1:T(8,128)(2,1)}, u32[]{:S(2)}, u32[]{:S(2)}) collective-permute-start(bf16[384,16,64]{0,2,1:T(8,128)(2,1)} %fusion.240), channel_id=1, source_target_pairs={{0,3},{1,0},{2,1},{3,2},{4,7},{5,4},{6,5},{7,6},{8,11},{9,8},{10,9... | collective-permute-start | bytes 2359304 | tf_op jit(solution)/shard_map/while/body/eval_jaxpr/ppermute | solution.py:32
  413.9 28.7 %collective-permute-start.4 = (bf16[384,16,64]{0,2,1:T(8,128)(2,1)}, bf16[384,16,64]{0,2,1:T(8,128)(2,1)}, u32[]{:S(2)}, u32[]{:S(2)}) collective-permute-start(bf16[384,16,64]{0,2,1:T(8,128)(2,1)} %fusion.241), channel_id=1, source_target_pairs={{0,3},{1,0},{2,1},{3,2},{4,7},{5,4},{6,5},{7,6},{8,11},{9,8},{10,9... | collective-permute-start | bytes 2359304 | tf_op jit(solution)/shard_map/while/body/eval_jaxpr/ppermute | solution.py:32
  416.1 60.2 %collective-permute-start = (bf16[384,1024]{0,1:T(8,128)(2,1)}, bf16[384,1024]{0,1:T(8,128)(2,1)}, u32[]{:S(2)}, u32[]{:S(2)}) collective-permute-start(bf16[384,1024]{0,1:T(8,128)(2,1)} %copy.100), channel_id=1, source_target_pairs={{0,3},{1,0},{2,1},{3,2},{4,7},{5,4},{6,5},{7,6},{8,11},{9,8},{10,9... | collective-permute-start | bytes 2359304 | tf_op jit(solution)/shard_map/while/body/eval_jaxpr/ppermute | solution.py:32
  418.6 57.8 %collective-permute-start.1 = (bf16[384,1024]{0,1:T(8,128)(2,1)}, bf16[384,1024]{0,1:T(8,128)(2,1)}, u32[]{:S(2)}, u32[]{:S(2)}) collective-permute-start(bf16[384,1024]{0,1:T(8,128)(2,1)} %copy.101), channel_id=1, source_target_pairs={{0,3},{1,0},{2,1},{3,2},{4,7},{5,4},{6,5},{7,6},{8,11},{9,8},{10,9... | collective-permute-start | bytes 2359304 | tf_op jit(solution)/shard_map/while/body/eval_jaxpr/ppermute | solution.py:32
  418.7 57.7 %collective-permute-start.2 = (bf16[384]{0:T(512)(128)(2,1)S(1)}, bf16[384]{0:T(512)(128)(2,1)S(1)}, u32[]{:S(2)}, u32[]{:S(2)}) collective-permute-start(bf16[384]{0:T(512)(128)(2,1)S(1)} %copy.102), channel_id=1, source_target_pairs={{0,3},{1,0},{2,1},{3,2},{4,7},{5,4},{6,5},{7,6},{8,11},{9,8},{10,9... | collective-permute-start | bytes 2312 | tf_op jit(solution)/shard_map/while/body/eval_jaxpr/ppermute | solution.py:32
  490.6 15.2 %collective-permute-start.3 = (bf16[384,16,64]{0,2,1:T(8,128)(2,1)}, bf16[384,16,64]{0,2,1:T(8,128)(2,1)}, u32[]{:S(2)}, u32[]{:S(2)}) collective-permute-start(bf16[384,16,64]{0,2,1:T(8,128)(2,1)} %fusion.240), channel_id=1, source_target_pairs={{0,3},{1,0},{2,1},{3,2},{4,7},{5,4},{6,5},{7,6},{8,11},{9,8},{10,9... | collective-permute-start | bytes 2359304 | tf_op jit(solution)/shard_map/while/body/eval_jaxpr/ppermute | solution.py:32
  494.2 28.4 %collective-permute-start.4 = (bf16[384,16,64]{0,2,1:T(8,128)(2,1)}, bf16[384,16,64]{0,2,1:T(8,128)(2,1)}, u32[]{:S(2)}, u32[]{:S(2)}) collective-permute-start(bf16[384,16,64]{0,2,1:T(8,128)(2,1)} %fusion.241), channel_id=1, source_target_pairs={{0,3},{1,0},{2,1},{3,2},{4,7},{5,4},{6,5},{7,6},{8,11},{9,8},{10,9... | collective-permute-start | bytes 2359304 | tf_op jit(solution)/shard_map/while/body/eval_jaxpr/ppermute | solution.py:32
  495.5 60.9 %collective-permute-start = (bf16[384,1024]{0,1:T(8,128)(2,1)}, bf16[384,1024]{0,1:T(8,128)(2,1)}, u32[]{:S(2)}, u32[]{:S(2)}) collective-permute-start(bf16[384,1024]{0,1:T(8,128)(2,1)} %copy.100), channel_id=1, source_target_pairs={{0,3},{1,0},{2,1},{3,2},{4,7},{5,4},{6,5},{7,6},{8,11},{9,8},{10,9... | collective-permute-start | bytes 2359304 | tf_op jit(solution)/shard_map/while/body/eval_jaxpr/ppermute | solution.py:32
  499.6 56.9 %collective-permute-start.1 = (bf16[384,1024]{0,1:T(8,128)(2,1)}, bf16[384,1024]{0,1:T(8,128)(2,1)}, u32[]{:S(2)}, u32[]{:S(2)}) collective-permute-start(bf16[384,1024]{0,1:T(8,128)(2,1)} %copy.101), channel_id=1, source_target_pairs={{0,3},{1,0},{2,1},{3,2},{4,7},{5,4},{6,5},{7,6},{8,11},{9,8},{10,9... | collective-permute-start | bytes 2359304 | tf_op jit(solution)/shard_map/while/body/eval_jaxpr/ppermute | solution.py:32
  499.6 56.8 %collective-permute-start.2 = (bf16[384]{0:T(512)(128)(2,1)S(1)}, bf16[384]{0:T(512)(128)(2,1)S(1)}, u32[]{:S(2)}, u32[]{:S(2)}) collective-permute-start(bf16[384]{0:T(512)(128)(2,1)S(1)} %copy.102), channel_id=1, source_target_pairs={{0,3},{1,0},{2,1},{3,2},{4,7},{5,4},{6,5},{7,6},{8,11},{9,8},{10,9... | collective-permute-start | bytes 2312 | tf_op jit(solution)/shard_map/while/body/eval_jaxpr/ppermute | solution.py:32
  570.6 14.3 %collective-permute-start.3 = (bf16[384,16,64]{0,2,1:T(8,128)(2,1)}, bf16[384,16,64]{0,2,1:T(8,128)(2,1)}, u32[]{:S(2)}, u32[]{:S(2)}) collective-permute-start(bf16[384,16,64]{0,2,1:T(8,128)(2,1)} %fusion.240), channel_id=1, source_target_pairs={{0,3},{1,0},{2,1},{3,2},{4,7},{5,4},{6,5},{7,6},{8,11},{9,8},{10,9... | collective-permute-start | bytes 2359304 | tf_op jit(solution)/shard_map/while/body/eval_jaxpr/ppermute | solution.py:32
  574.3 27.5 %collective-permute-start.4 = (bf16[384,16,64]{0,2,1:T(8,128)(2,1)}, bf16[384,16,64]{0,2,1:T(8,128)(2,1)}, u32[]{:S(2)}, u32[]{:S(2)}) collective-permute-start(bf16[384,16,64]{0,2,1:T(8,128)(2,1)} %fusion.241), channel_id=1, source_target_pairs={{0,3},{1,0},{2,1},{3,2},{4,7},{5,4},{6,5},{7,6},{8,11},{9,8},{10,9... | collective-permute-start | bytes 2359304 | tf_op jit(solution)/shard_map/while/body/eval_jaxpr/ppermute | solution.py:32
  575.6 59.9 %collective-permute-start = (bf16[384,1024]{0,1:T(8,128)(2,1)}, bf16[384,1024]{0,1:T(8,128)(2,1)}, u32[]{:S(2)}, u32[]{:S(2)}) collective-permute-start(bf16[384,1024]{0,1:T(8,128)(2,1)} %copy.100), channel_id=1, source_target_pairs={{0,3},{1,0},{2,1},{3,2},{4,7},{5,4},{6,5},{7,6},{8,11},{9,8},{10,9... | collective-permute-start | bytes 2359304 | tf_op jit(solution)/shard_map/while/body/eval_jaxpr/ppermute | solution.py:32
  579.6 55.9 %collective-permute-start.1 = (bf16[384,1024]{0,1:T(8,128)(2,1)}, bf16[384,1024]{0,1:T(8,128)(2,1)}, u32[]{:S(2)}, u32[]{:S(2)}) collective-permute-start(bf16[384,1024]{0,1:T(8,128)(2,1)} %copy.101), channel_id=1, source_target_pairs={{0,3},{1,0},{2,1},{3,2},{4,7},{5,4},{6,5},{7,6},{8,11},{9,8},{10,9... | collective-permute-start | bytes 2359304 | tf_op jit(solution)/shard_map/while/body/eval_jaxpr/ppermute | solution.py:32
  579.6 55.9 %collective-permute-start.2 = (bf16[384]{0:T(512)(128)(2,1)S(1)}, bf16[384]{0:T(512)(128)(2,1)S(1)}, u32[]{:S(2)}, u32[]{:S(2)}) collective-permute-start(bf16[384]{0:T(512)(128)(2,1)S(1)} %copy.102), channel_id=1, source_target_pairs={{0,3},{1,0},{2,1},{3,2},{4,7},{5,4},{6,5},{7,6},{8,11},{9,8},{10,9... | collective-permute-start | bytes 2312 | tf_op jit(solution)/shard_map/while/body/eval_jaxpr/ppermute | solution.py:32
  679.3 23.7 %collective-permute-start.71 = (bf16[4,64,1024]{2,1,0:T(8,128)(2,1)S(1)}, bf16[4,64,1024]{2,1,0:T(8,128)(2,1)S(1)}, u32[]{:S(2)}, u32[]{:S(2)}) collective-permute-start(bf16[4,64,1024]{2,1,0:T(8,128)(2,1)S(1)} %constant_dynamic-slice_fusion.6), channel_id=1, source_target_pairs={{0,4},{1,5},{2,6},{3,7},{4,0},{5,1},{6,2},{7,3},{8,12},{9,13},{10,... | collective-permute-start | bytes 1572872 | tf_op jit(solution)/shard_map/ppermute | solution.py:189
  687.9 41.5 %collective-permute-start.63 = (bf16[4,128,1024]{2,1,0:T(8,128)(2,1)}, bf16[4,128,1024]{2,1,0:T(8,128)(2,1)}, u32[]{:S(2)}, u32[]{:S(2)}) collective-permute-start(bf16[4,128,1024]{2,1,0:T(8,128)(2,1)} %constant_dynamic-slice_fusion.11), channel_id=1, source_target_pairs={{0,4},{1,5},{2,6},{3,7},{4,0},{5,1},{6,2},{7,3},{8,12},{9,13},{10,... | collective-permute-start | bytes 3145736 | tf_op jit(solution)/shard_map/ppermute | solution.py:189
  688.9 44.4 %collective-permute-start.39 = (bf16[4,128,1024]{2,1,0:T(8,128)(2,1)}, bf16[4,128,1024]{2,1,0:T(8,128)(2,1)}, u32[]{:S(2)}, u32[]{:S(2)}) collective-permute-start(bf16[4,128,1024]{2,1,0:T(8,128)(2,1)} %constant_dynamic-slice_fusion.26), channel_id=1, source_target_pairs={{0,4},{1,5},{2,6},{3,7},{4,0},{5,1},{6,2},{7,3},{8,12},{9,13},{10,... | collective-permute-start | bytes 3145736 | tf_op jit(solution)/shard_map/ppermute | solution.py:189
  691.9 43.4 %collective-permute-start.23 = (bf16[4,128,1024]{2,1,0:T(8,128)(2,1)}, bf16[4,128,1024]{2,1,0:T(8,128)(2,1)}, u32[]{:S(2)}, u32[]{:S(2)}) collective-permute-start(bf16[4,128,1024]{2,1,0:T(8,128)(2,1)} %constant_dynamic-slice_fusion.36), channel_id=1, source_target_pairs={{0,4},{1,5},{2,6},{3,7},{4,0},{5,1},{6,2},{7,3},{8,12},{9,13},{10,... | collective-permute-start | bytes 3145736 | tf_op jit(solution)/shard_map/ppermute | solution.py:189
  717.2 20.9 %collective-permute-start.31 = (bf16[4,128,1024]{2,1,0:T(8,128)(2,1)S(1)}, bf16[4,128,1024]{2,1,0:T(8,128)(2,1)S(1)}, u32[]{:S(2)}, u32[]{:S(2)}) collective-permute-start(bf16[4,128,1024]{2,1,0:T(8,128)(2,1)S(1)} %constant_dynamic-slice_fusion.31), channel_id=1, source_target_pairs={{0,4},{1,5},{2,6},{3,7},{4,0},{5,1},{6,2},{7,3},{8,12},{9,13},{10,... | collective-permute-start | bytes 3145736 | tf_op jit(solution)/shard_map/ppermute | solution.py:189
  732.2 93.7 %collective-permute-start.47 = (bf16[4,128,4096]{2,1,0:T(8,128)(2,1)}, bf16[4,128,4096]{2,1,0:T(8,128)(2,1)S(1)}, u32[]{:S(2)}, u32[]{:S(2)}) collective-permute-start(bf16[4,128,4096]{2,1,0:T(8,128)(2,1)} %constant_dynamic-slice_fusion.21), channel_id=1, source_target_pairs={{0,4},{1,5},{2,6},{3,7},{4,0},{5,1},{6,2},{7,3},{8,12},{9,13},{10,... | collective-permute-start | bytes 12582920 | tf_op jit(solution)/shard_map/ppermute | solution.py:189
  733.4 118.4 %collective-permute-start.55 = (bf16[4,512,1024]{2,1,0:T(8,128)(2,1)}, bf16[4,512,1024]{2,1,0:T(8,128)(2,1)S(1)}, u32[]{:S(2)}, u32[]{:S(2)}) collective-permute-start(bf16[4,512,1024]{2,1,0:T(8,128)(2,1)} %constant_dynamic-slice_fusion.16), channel_id=1, source_target_pairs={{0,4},{1,5},{2,6},{3,7},{4,0},{5,1},{6,2},{7,3},{8,12},{9,13},{10,... | collective-permute-start | bytes 12582920 | tf_op jit(solution)/shard_map/ppermute | solution.py:189
  739.2 23.1 %collective-permute-start.40 = (bf16[4,64,1024]{2,1,0:T(8,128)(2,1)S(1)}, bf16[4,64,1024]{2,1,0:T(8,128)(2,1)S(1)}, u32[]{:S(2)}, u32[]{:S(2)}) collective-permute-start(bf16[4,64,1024]{2,1,0:T(8,128)(2,1)S(1)} %constant_dynamic-slice_fusion.25), channel_id=1, source_target_pairs={{0,16},{1,17},{2,18},{3,19},{4,20},{5,21},{6,22},{7,23},{8,24},{9,... | collective-permute-start | bytes 1572872 | tf_op jit(solution)/shard_map/ppermute | solution.py:189
  746.3 27.2 %collective-permute-start.24 = (bf16[4,64,1024]{2,1,0:T(8,128)(2,1)S(1)}, bf16[4,64,1024]{2,1,0:T(8,128)(2,1)S(1)}, u32[]{:S(2)}, u32[]{:S(2)}) collective-permute-start(bf16[4,64,1024]{2,1,0:T(8,128)(2,1)S(1)} %constant_dynamic-slice_fusion.35), channel_id=1, source_target_pairs={{0,16},{1,17},{2,18},{3,19},{4,20},{5,21},{6,22},{7,23},{8,24},{9,... | collective-permute-start | bytes 1572872 | tf_op jit(solution)/shard_map/ppermute | solution.py:189
  751.0 23.5 %collective-permute-start.32 = (bf16[4,64,1024]{2,1,0:T(8,128)(2,1)S(1)}, bf16[4,64,1024]{2,1,0:T(8,128)(2,1)S(1)}, u32[]{:S(2)}, u32[]{:S(2)}) collective-permute-start(bf16[4,64,1024]{2,1,0:T(8,128)(2,1)S(1)} %constant_dynamic-slice_fusion.30), channel_id=1, source_target_pairs={{0,8},{1,9},{2,10},{3,11},{4,12},{5,13},{6,14},{7,15},{8,0},{9,1},... | collective-permute-start | bytes 1572872 | tf_op jit(solution)/shard_map/ppermute | solution.py:189
  775.5 15.5 %collective-permute-start.25 = (bf16[4,32,1024]{2,1,0:T(8,128)(2,1)S(1)}, bf16[4,32,1024]{2,1,0:T(8,128)(2,1)S(1)}, u32[]{:S(2)}, u32[]{:S(2)}) collective-permute-start(bf16[4,32,1024]{2,1,0:T(8,128)(2,1)S(1)} %constant_dynamic-slice_fusion.34), channel_id=1, source_target_pairs={{0,8},{1,9},{2,10},{3,11},{4,12},{5,13},{6,14},{7,15},{8,0},{9,1},... | collective-permute-start | bytes 786440 | tf_op jit(solution)/shard_map/ppermute | solution.py:189
  821.6 14.6 %collective-permute-start.45 = (bf16[64,1024]{1,0:T(8,128)(2,1)S(1)}, bf16[64,1024]{1,0:T(8,128)(2,1)S(1)}, u32[]{:S(2)}, u32[]{:S(2)}) collective-permute-start(bf16[64,1024]{1,0:T(8,128)(2,1)S(1)} %pad_maximum_fusion.22), channel_id=1, source_target_pairs={{0,16},{1,17},{2,18},{3,19},{4,20},{5,21},{6,22},{7,23},{8,24},{9,... | collective-permute-start | bytes 393224 | tf_op jit(solution)/shard_map/ppermute | solution.py:189
  823.3 14.7 %collective-permute-start.29 = (bf16[64,1024]{1,0:T(8,128)(2,1)}, bf16[64,1024]{1,0:T(8,128)(2,1)S(1)}, u32[]{:S(2)}, u32[]{:S(2)}) collective-permute-start(bf16[64,1024]{1,0:T(8,128)(2,1)} %pad_maximum_fusion.20), channel_id=1, source_target_pairs={{0,16},{1,17},{2,18},{3,19},{4,20},{5,21},{6,22},{7,23},{8,24},{9,... | collective-permute-start | bytes 393224 | tf_op jit(solution)/shard_map/ppermute | solution.py:189
  825.1 23.6 %collective-permute-start.37 = (bf16[64,1024]{1,0:T(8,128)(2,1)}, bf16[64,1024]{1,0:T(8,128)(2,1)}, u32[]{:S(2)}, u32[]{:S(2)}) collective-permute-start(bf16[64,1024]{1,0:T(8,128)(2,1)} %pad_maximum_fusion.21), channel_id=1, source_target_pairs={{0,8},{1,9},{2,10},{3,11},{4,12},{5,13},{6,14},{7,15},{8,0},{9,1},... | collective-permute-start | bytes 393224 | tf_op jit(solution)/shard_map/ppermute | solution.py:189
  828.0 23.1 %collective-permute-start.21 = (bf16[64,1024]{1,0:T(8,128)(2,1)}, bf16[64,1024]{1,0:T(8,128)(2,1)S(1)}, u32[]{:S(2)}, u32[]{:S(2)}) collective-permute-start(bf16[64,1024]{1,0:T(8,128)(2,1)} %pad_maximum_fusion.19), channel_id=1, source_target_pairs={{0,8},{1,9},{2,10},{3,11},{4,12},{5,13},{6,14},{7,15},{8,0},{9,1},... | collective-permute-start | bytes 393224 | tf_op jit(solution)/shard_map/ppermute | solution.py:189
  836.2 38.7 %collective-permute-start.48 = (bf16[4,64,4096]{2,1,0:T(8,128)(2,1)}, bf16[4,64,4096]{2,1,0:T(8,128)(2,1)S(1)}, u32[]{:S(2)}, u32[]{:S(2)}) collective-permute-start(bf16[4,64,4096]{2,1,0:T(8,128)(2,1)} %constant_dynamic-slice_fusion.20), channel_id=1, source_target_pairs={{0,16},{1,17},{2,18},{3,19},{4,20},{5,21},{6,22},{7,23},{8,24},{9,... | collective-permute-start | bytes 6291464 | tf_op jit(solution)/shard_map/ppermute | solution.py:189
  838.6 38.0 %collective-permute-start.70 = (bf16[128,1024]{1,0:T(8,128)(2,1)}, bf16[128,1024]{1,0:T(8,128)(2,1)}, u32[]{:S(2)}, u32[]{:S(2)}) collective-permute-start(bf16[128,1024]{1,0:T(8,128)(2,1)} %pad_maximum_fusion.16), channel_id=1, source_target_pairs={{0,4},{1,5},{2,6},{3,7},{4,0},{5,1},{6,2},{7,3},{8,12},{9,13},{10,... | collective-permute-start | bytes 786440 | tf_op jit(solution)/shard_map/ppermute | solution.py:189
  848.7 29.9 %collective-permute-start.46 = (bf16[128,1024]{1,0:T(8,128)(2,1)}, bf16[128,1024]{1,0:T(8,128)(2,1)}, u32[]{:S(2)}, u32[]{:S(2)}) collective-permute-start(bf16[128,1024]{1,0:T(8,128)(2,1)} %pad_maximum_fusion.14), channel_id=1, source_target_pairs={{0,4},{1,5},{2,6},{3,7},{4,0},{5,1},{6,2},{7,3},{8,12},{9,13},{10,... | collective-permute-start | bytes 786440 | tf_op jit(solution)/shard_map/ppermute | solution.py:189
  851.1 38.7 %collective-permute-start.30 = (bf16[128,1024]{1,0:T(8,128)(2,1)}, bf16[128,1024]{1,0:T(8,128)(2,1)}, u32[]{:S(2)}, u32[]{:S(2)}) collective-permute-start(bf16[128,1024]{1,0:T(8,128)(2,1)} %pad_maximum_fusion.10), channel_id=1, source_target_pairs={{0,4},{1,5},{2,6},{3,7},{4,0},{5,1},{6,2},{7,3},{8,12},{9,13},{10,... | collective-permute-start | bytes 786440 | tf_op jit(solution)/shard_map/ppermute | solution.py:189
  853.8 97.2 %collective-permute-start.38 = (bf16[128,1024]{1,0:T(8,128)(2,1)}, bf16[128,1024]{1,0:T(8,128)(2,1)}, u32[]{:S(2)}, u32[]{:S(2)}) collective-permute-start(bf16[128,1024]{1,0:T(8,128)(2,1)} %pad_maximum_fusion.12), channel_id=1, source_target_pairs={{0,4},{1,5},{2,6},{3,7},{4,0},{5,1},{6,2},{7,3},{8,12},{9,13},{10,... | collective-permute-start | bytes 786440 | tf_op jit(solution)/shard_map/ppermute | solution.py:189
  874.9 37.6 %collective-permute-start.56 = (bf16[4,256,1024]{2,1,0:T(8,128)(2,1)S(1)}, bf16[4,256,1024]{2,1,0:T(8,128)(2,1)S(1)}, u32[]{:S(2)}, u32[]{:S(2)}) collective-permute-start(bf16[4,256,1024]{2,1,0:T(8,128)(2,1)S(1)} %constant_dynamic-slice_fusion.15), channel_id=1, source_target_pairs={{0,8},{1,9},{2,10},{3,11},{4,12},{5,13},{6,14},{7,15},{8,0},{9,1},... | collective-permute-start | bytes 6291464 | tf_op jit(solution)/shard_map/ppermute | solution.py:189
  876.6 58.4 %collective-permute-start.49 = (bf16[4,32,4096]{2,1,0:T(8,128)(2,1)S(1)}, bf16[4,32,4096]{2,1,0:T(8,128)(2,1)S(1)}, u32[]{:S(2)}, u32[]{:S(2)}) collective-permute-start(bf16[4,32,4096]{2,1,0:T(8,128)(2,1)S(1)} %constant_dynamic-slice_fusion.19), channel_id=1, source_target_pairs={{0,8},{1,9},{2,10},{3,11},{4,12},{5,13},{6,14},{7,15},{8,0},{9,1},... | collective-permute-start | bytes 3145736 | tf_op jit(solution)/shard_map/ppermute | solution.py:189
  878.6 112.5 %collective-permute-start.22 = (bf16[128,1024]{1,0:T(8,128)(2,1)S(1)}, bf16[128,1024]{1,0:T(8,128)(2,1)S(1)}, u32[]{:S(2)}, u32[]{:S(2)}) collective-permute-start(bf16[128,1024]{1,0:T(8,128)(2,1)S(1)} %pad_maximum_fusion.8), channel_id=1, source_target_pairs={{0,4},{1,5},{2,6},{3,7},{4,0},{5,1},{6,2},{7,3},{8,12},{9,13},{10,... | collective-permute-start | bytes 786440 | tf_op jit(solution)/shard_map/ppermute | solution.py:189
  913.6 22.0 %collective-permute-start.57 = (bf16[4,128,1024]{2,1,0:T(8,128)(2,1)S(1)}, bf16[4,128,1024]{2,1,0:T(8,128)(2,1)S(1)}, u32[]{:S(2)}, u32[]{:S(2)}) collective-permute-start(bf16[4,128,1024]{2,1,0:T(8,128)(2,1)S(1)} %constant_dynamic-slice_fusion.14), channel_id=1, source_target_pairs={{0,16},{1,17},{2,18},{3,19},{4,20},{5,21},{6,22},{7,23},{8,24},{9,... | collective-permute-start | bytes 3145736 | tf_op jit(solution)/shard_map/ppermute | solution.py:189
  965.0 27.2 %collective-permute-start.61 = (bf16[256,1024]{1,0:T(8,128)(2,1)S(1)}, bf16[256,1024]{1,0:T(8,128)(2,1)S(1)}, u32[]{:S(2)}, u32[]{:S(2)}) collective-permute-start(bf16[256,1024]{1,0:T(8,128)(2,1)S(1)} %pad_maximum_fusion.6), channel_id=1, source_target_pairs={{0,8},{1,9},{2,10},{3,11},{4,12},{5,13},{6,14},{7,15},{8,0},{9,1},... | collective-permute-start | bytes 1572872 | tf_op jit(solution)/shard_map/ppermute | solution.py:189
  970.9 21.8 %collective-permute-start.54 = (bf16[128,4096]{1,0:T(8,128)(2,1)S(1)}, bf16[128,4096]{1,0:T(8,128)(2,1)S(1)}, u32[]{:S(2)}, u32[]{:S(2)}) collective-permute-start(bf16[128,4096]{1,0:T(8,128)(2,1)S(1)} %pad_maximum_fusion.1), channel_id=1, source_target_pairs={{0,4},{1,5},{2,6},{3,7},{4,0},{5,1},{6,2},{7,3},{8,12},{9,13},{10,... | collective-permute-start | bytes 3145736 | tf_op jit(solution)/shard_map/ppermute | solution.py:189
  (153 other events, 943.3 us)
Sparse Core Ops, SparseCore 0:
  14.1 63.2 all-gather.5
  79.6 62.1 all-gather.3

commit v2 on v1

--- a/solution.py
+++ b/solution.py
@@ -1,8 +1,11 @@
+import math
 from functools import partial
 
 import jax
 import jax.numpy as jnp
 from jax import lax
+from jax.experimental import pallas as pl
+from jax.experimental.pallas import tpu as pltpu
 from jax.sharding import PartitionSpec as P
 
 D = 1024
@@ -17,19 +20,9 @@
 free_floor = 1.3
 neg_fill = -1e30
 
-
-def shortened(array):
-
-    def short(part):
-        return part.astype(jnp.bfloat16) if part.dtype == jnp.float32 else part
-
-    return jax.tree.map(short, array)
-
-
-def passed_along(value, axis, steps):
-    count = lax.axis_size(axis)
-    pairs = [(source, (source + steps) % count) for source in range(count)]
-    return lax.ppermute(value, axis, pairs)
+QUERY_TILE = 512
+KEY_TILE = 512
+KEY_UNIT = 128
 
 
 def layer_norm(values, gain, shift):
@@ -79,100 +72,6 @@
 def cols_dot(left, right):
     return lax.dot_general(
         left, right, (((1,), (1,)), ((), ())), preferred_element_type=jnp.float32
-    )
-
-
-def pair_mask(query_slide, query_pos, key_slide, key_pos, key_live):
-    same = query_slide[:, None] == key_slide[None, :]
-    open_key = (key_live[None, :] > 0.5) | (query_pos[:, None] == key_pos[None, :])
-    return (same & open_key)[None]
-
-
-def forward_update(
-    state, heads_q, query_slide, query_pos, heads_k, heads_v, key_live, key_pos, key_slide
-):
-    peak, total, running = state
-    allowed = pair_mask(query_slide, query_pos, key_slide, key_pos, key_live)
-    scores = jnp.einsum(
-        "qhd,khd->hqk", heads_q, heads_k, preferred_element_type=jnp.float32
-    ) * HD ** (-0.5)
-    scores = jnp.where(allowed, scores, neg_fill)
-    new_peak = jnp.maximum(peak, jnp.max(scores, axis=-1))
-    weights = jnp.where(allowed, jnp.exp(scores - new_peak[:, :, None]), 0.0)
-    rescale = jnp.exp(peak - new_peak)
-    total = total * rescale + jnp.sum(weights, axis=-1)
-    running = running * rescale.T[:, :, None] + jnp.einsum(
-        "hqk,khd->qhd", weights.astype(jnp.bfloat16), heads_v, preferred_element_type=jnp.float32
-    )
-    return (new_peak, total, running)
-
-
-def forward_visit(
-    state, heads_q, query_slide, query_pos, heads_k, heads_v, key_live, key_pos, lengths_row
-):
-    key_slide = slide_index(key_pos, lengths_row)
-    return forward_update(
-        state, heads_q, query_slide, query_pos, heads_k, heads_v, key_live, key_pos, key_slide
-    )
-
-
-def backward_update(
-    heads_q,
-    heads_o,
-    log_total,
-    delta,
-    query_slide,
-    query_pos,
-    heads_k,
-    heads_v,
-    key_live,
-    key_pos,
-    key_slide,
-):
-    allowed = pair_mask(query_slide, query_pos, key_slide, key_pos, key_live)
-    scores = jnp.einsum(
-        "qhd,khd->hqk", heads_q, heads_k, preferred_element_type=jnp.float32
-    ) * HD ** (-0.5)
-    probs = jnp.where(allowed, jnp.exp(scores - log_total[:, :, None]), 0.0)
-    dprobs = jnp.einsum("qhd,khd->hqk", heads_o, heads_v, preferred_element_type=jnp.float32)
-    dscores = (probs * (dprobs - delta[:, :, None])).astype(jnp.bfloat16)
-    grad_q = jnp.einsum(
-        "hqk,khd->qhd", dscores, heads_k, preferred_element_type=jnp.float32
-    ) * HD ** (-0.5)
-    grad_k = jnp.einsum(
-        "hqk,qhd->khd", dscores, heads_q, preferred_element_type=jnp.float32
-    ) * HD ** (-0.5)
-    grad_v = jnp.einsum(
-        "hqk,qhd->khd", probs.astype(jnp.bfloat16), heads_o, preferred_element_type=jnp.float32
-    )
-    return (grad_q, grad_k, grad_v)
-
-
-def backward_visit(
-    heads_q,
-    heads_o,
-    log_total,
-    delta,
-    query_slide,
-    query_pos,
-    heads_k,
-    heads_v,
-    key_live,
-    key_pos,
-    key_slide,
-):
-    return backward_update(
-        heads_q,
-        heads_o,
-        log_total,
-        delta,
-        query_slide,
-        query_pos,
-        heads_k,
-        heads_v,
-        key_live,
-        key_pos,
-        key_slide,
     )
 
 
@@ -283,6 +182,310 @@
         pieces.append(value[start : start + size])
         start += size
     return pieces
+
+
+def head_lanes(value, head):
+    lane = lax.broadcasted_iota(jnp.int32, value.shape, 1) // HD
+    return jnp.where(lane == head, value, jnp.zeros_like(value))
+
+def nt_dot(left, right):
+    return lax.dot_general(left, right, (((1,),(1,)),((),())), preferred_element_type=jnp.float32)
+
+def nn_dot(left, right):
+    return lax.dot_general(left, right, (((1,),(0,)),((),())), preferred_element_type=jnp.float32)
+
+def allowed_pairs(code_k, code_q, block_k, tile):
+    key_pos = block_k + lax.broadcasted_iota(jnp.int32, tile, 0)
+    query_pos = pl.program_id(0) * QUERY_TILE + lax.broadcasted_iota(jnp.int32, tile, 1)
+    return (code_k == code_q) | (key_pos == query_pos)
+
+def forward_kernel(range_ref, q_ref, k_ref, vt_ref, cq_ref, ck_ref, ctx_ref, lse_ref, m_ref, l_ref, acc_ref):
+    nh = q_ref.shape[1] // HD
+    step = pl.program_id(0)
+    m_ref[...] = jnp.full(m_ref.shape, neg_fill, jnp.float32)
+    l_ref[...] = jnp.zeros(l_ref.shape, jnp.float32)
+    acc_ref[...] = jnp.zeros(acc_ref.shape, jnp.float32)
+    code_q = cq_ref[...]
+    scaled = (q_ref[...].astype(jnp.float32) * HD ** (-0.5)).astype(jnp.bfloat16)
+    def body(kb, _):
+        start = pl.multiple_of(range_ref[step, 0] * KEY_UNIT + kb * KEY_TILE, KEY_UNIT)
+        keys = k_ref[pl.ds(start, KEY_TILE), :]
+        open_pair = allowed_pairs(ck_ref[pl.ds(start, KEY_TILE), :], code_q, start, (KEY_TILE, QUERY_TILE))
+        for h in range(nh):
+            s = nt_dot(keys, head_lanes(scaled, h))
+            s = jnp.where(open_pair, s, neg_fill)
+            m_old = m_ref[h:h+1, :]
+            m_new = jnp.maximum(m_old, jnp.max(s, axis=0, keepdims=True))
+            p = jnp.exp(s - m_new)
+            alpha = jnp.exp(m_old - m_new)
+            l_ref[h:h+1, :] = l_ref[h:h+1, :] * alpha + jnp.sum(p, axis=0, keepdims=True)
+            m_ref[h:h+1, :] = m_new
+            rows = slice(h*HD, (h+1)*HD)
+            acc_ref[rows, :] = acc_ref[rows, :] * alpha + nn_dot(vt_ref[rows, pl.ds(start, KEY_TILE)], p.astype(jnp.bfloat16))
+        return 0
+    lax.fori_loop(0, range_ref[step, 1], body, 0)
+    for h in range(nh):
+        rows = slice(h*HD, (h+1)*HD)
+        acc_ref[rows, :] = acc_ref[rows, :] / l_ref[h:h+1, :]
+    ctx_ref[...] = acc_ref[...].T.astype(jnp.bfloat16)
+    lse_ref[...] = m_ref[...] + jnp.log(l_ref[...])
+
+def attention_forward(ranges, q, k, vt, code_q, code_k):
+    N, W = q.shape
+    nh = W // HD
+    full = lambda shape: pl.BlockSpec(shape, lambda i, r: (0,)*len(shape))
+    return pl.pallas_call(
+        forward_kernel,
+        out_shape=(jax.ShapeDtypeStruct((N, W), jnp.bfloat16), jax.ShapeDtypeStruct((nh, N), jnp.float32)),
+        grid_spec=pltpu.PrefetchScalarGridSpec(
+            num_scalar_prefetch=1, grid=(N//QUERY_TILE,),
+            in_specs=[pl.BlockSpec((QUERY_TILE, W), lambda i, r: (i, 0)), full((N, W)), full((W, N)),
+                      pl.BlockSpec((1, QUERY_TILE), lambda i, r: (0, i)), full((N, 1))],
+            out_specs=[pl.BlockSpec((QUERY_TILE, W), lambda i, r: (i, 0)), pl.BlockSpec((nh, QUERY_TILE), lambda i, r: (0, i))],
+            scratch_shapes=[pltpu.VMEM((nh, QUERY_TILE), jnp.float32), pltpu.VMEM((nh, QUERY_TILE), jnp.float32), pltpu.VMEM((W, QUERY_TILE), jnp.float32)]),
+        name="attention_forward",
+    )(ranges, q, k, vt, code_q, code_k)
+
+def backward_kernel(range_ref, q_ref, do_ref, ctx_ref, lse_ref, k_ref, v_ref, kt_ref, cq_ref, ck_ref,
+                    dq_ref, dk_ref, dv_ref, dqt_ref, dk_acc, dv_acc):
+    nh = q_ref.shape[1] // HD
+    step = pl.program_id(0)
+    @pl.when(step == 0)
+    def _():
+        dk_acc[...] = jnp.zeros(dk_acc.shape, jnp.float32)
+        dv_acc[...] = jnp.zeros(dv_acc.shape, jnp.float32)
+    dqt_ref[...] = jnp.zeros(dqt_ref.shape, jnp.float32)
+    code_q = cq_ref[...]
+    scaled = (q_ref[...].astype(jnp.float32) * HD ** (-0.5)).astype(jnp.bfloat16)
+    grads = do_ref[...]
+    product = (grads.astype(jnp.float32) * ctx_ref[...].astype(jnp.float32)).T
+    deltas = [jnp.sum(product[h*HD:(h+1)*HD, :], axis=0, keepdims=True) for h in range(nh)]
+    q_all = jnp.concatenate([head_lanes(scaled, h) for h in range(nh)], axis=0)
+    do_all = jnp.concatenate([head_lanes(grads, h) for h in range(nh)], axis=0)
+    def body(kb, _):
+        start = pl.multiple_of(range_ref[step, 0] * KEY_UNIT + kb * KEY_TILE, KEY_UNIT)
+        keys = k_ref[pl.ds(start, KEY_TILE), :]
+        values = v_ref[pl.ds(start, KEY_TILE), :]
+        open_pair = allowed_pairs(ck_ref[pl.ds(start, KEY_TILE), :], code_q, start, (KEY_TILE, QUERY_TILE))
+        ps, dss = [], []
+        for h in range(nh):
+            cols = slice(h*QUERY_TILE, (h+1)*QUERY_TILE)
+            rows = slice(h*HD, (h+1)*HD)
+            s = nt_dot(keys, q_all[cols, :])
+            p = jnp.where(open_pair, jnp.exp(s - lse_ref[h:h+1, :]), 0.0)
+            dp = nt_dot(values, do_all[cols, :])
+            ds = (p * (dp - deltas[h])).astype(jnp.bfloat16)
+            ps.append(p.astype(jnp.bfloat16))
+            dss.append(ds)
+            dqt_ref[rows, :] += nn_dot(kt_ref[rows, pl.ds(start, KEY_TILE)], ds)
+        dv_acc[pl.ds(start, KEY_TILE), :] += nn_dot(jnp.concatenate(ps, axis=1), do_all)
+        dk_acc[pl.ds(start, KEY_TILE), :] += nn_dot(jnp.concatenate(dss, axis=1), q_all)
+        return 0
+    lax.fori_loop(0, range_ref[step, 1], body, 0)
+    dq_ref[...] = (dqt_ref[...] * HD ** (-0.5)).T.astype(jnp.bfloat16)
+    @pl.when(step == pl.num_programs(0) - 1)
+    def _():
+        dk_ref[...] = dk_acc[...].astype(jnp.bfloat16)
+        dv_ref[...] = dv_acc[...].astype(jnp.bfloat16)
+
+def attention_backward(ranges, q, do, ctx, lse, k, v, kt, code_q, code_k):
+    N, W = q.shape
+    nh = W // HD
+    full = lambda shape: pl.BlockSpec(shape, lambda i, r: (0,)*len(shape))
+    row = lambda: pl.BlockSpec((QUERY_TILE, W), lambda i, r: (i, 0))
+    out = jax.ShapeDtypeStruct((N, W), jnp.bfloat16)
+    return pl.pallas_call(
+        backward_kernel,
+        out_shape=(out, out, out),
+        grid_spec=pltpu.PrefetchScalarGridSpec(
+            num_scalar_prefetch=1, grid=(N//QUERY_TILE,),
+            in_specs=[row(), row(), row(), pl.BlockSpec((nh, QUERY_TILE), lambda i, r: (0, i)), full((N, W)), full((N, W)), full((W, N)),
+                      pl.BlockSpec((1, QUERY_TILE), lambda i, r: (0, i)), full((N, 1))],
+            out_specs=[row(), full((N, W)), full((N, W))],
+            scratch_shapes=[pltpu.VMEM((W, QUERY_TILE), jnp.float32), pltpu.VMEM((N, W), jnp.float32), pltpu.VMEM((N, W), jnp.float32)]),
+        name="attention_backward",
+    )(ranges, q, do, ctx, lse, k, v, kt, code_q, code_k)
+
+def slide_tables(lengths_row, mask_all):
+    cells = mask_all.shape[0]
+    ends = jnp.cumsum(lengths_row)
+    starts = ends - lengths_row
+    slide = slide_index(jnp.arange(cells, dtype=jnp.int32), lengths_row)
+    first = jnp.arange(cells // QUERY_TILE, dtype=jnp.int32) * QUERY_TILE
+    first_slide = slide_index(first, lengths_row)
+    last_slide = slide_index(first + (QUERY_TILE - 1), lengths_row)
+    order = jnp.arange(lengths_row.shape[0], dtype=jnp.int32)
+
+    def picked(table, index):
+        return jnp.sum(jnp.where(index[:, None] == order[None, :], table[None, :], 0), axis=1)
+
+    low = picked(starts, first_slide) // KEY_UNIT
+    high = picked(ends, last_slide)
+    tiles = (high - low * KEY_UNIT + KEY_TILE - 1) // KEY_TILE
+    low = jnp.minimum(low, (cells - tiles * KEY_TILE) // KEY_UNIT)
+    ranges = jnp.stack([low, tiles], axis=1).astype(jnp.int32)
+    open_code = jnp.where(mask_all == 1, slide, -1)
+    return ranges, slide[None, :], open_code[:, None]
+
+
+def moved(value, target):
+    groups, blocks = lax.axis_size("dp"), lax.axis_size("blk")
+    pairs = []
+    for g in range(groups):
+        for b in range(blocks):
+            there = target(g, b)
+            if there is not None:
+                pairs.append((g * blocks + b, there[0] * blocks + there[1]))
+    return lax.ppermute(value, MESH_AXES, pairs)
+
+
+def at_home(g, b):
+    return g % 2 == b // (lax.axis_size("blk") // 2)
+
+
+def head_block(g, b):
+    return (b % (lax.axis_size("blk") // 2)) * 2 + g % 2
+
+
+def worker_of(g, block_of_heads):
+    half = lax.axis_size("blk") // 2
+    return (g - g % 2) + block_of_heads % 2, (g % 2) * half + block_of_heads // 2
+
+
+def owner_of(g, b, index):
+    return (g - g % 2) + b // (lax.axis_size("blk") // 2), index
+
+
+def pair_masks():
+    return [1 << t for t in range(bits_of(lax.axis_size("blk")) - 1)]
+
+
+def group_meta(meta):
+    blocks = lax.axis_size("blk")
+    group, block = lax.axis_index("dp"), lax.axis_index("blk")
+    other = swapped(meta, 1, 0)
+    both = jnp.where(group % 2 == 0, jnp.stack([meta, other]), jnp.stack([other, meta]))
+    pieces = jnp.stack([both] + [swapped(both, 0, mask) for mask in range(1, blocks)])
+    half = block // (blocks // 2)
+    mine = jnp.where(half == 0, pieces[:, 0], pieces[:, 1])
+    order = jnp.arange(blocks, dtype=jnp.int32) ^ block
+    chosen = order[:, None] == jnp.arange(blocks, dtype=jnp.int32)[None, :]
+    return jnp.sum(jnp.where(chosen[:, :, None], mine[None], 0), axis=1)
+
+
+def group_rows(own):
+    blocks = lax.axis_size("blk")
+    group, block = lax.axis_index("dp"), lax.axis_index("blk")
+    home = at_home(group, block)
+    rows, cols = own.shape
+    mirror = moved(own, lambda g, b: None if at_home(g, b) else (g, blocks - 1 - b))
+    pieces = [(own, lambda b: b), (mirror, lambda b: blocks - 1 - b)]
+    for mask in pair_masks():
+        more = []
+        for value, place in pieces:
+            value = moved(value, lambda g, b: (g, b ^ mask) if at_home(g, b) else None)
+            more.append((value, lambda b, place=place, mask=mask: place(b ^ mask)))
+        pieces = pieces + more
+    whole = jnp.zeros((blocks * rows, cols), own.dtype)
+    for value, place in pieces:
+        other = moved(value, lambda g, b: (g ^ 1, b) if at_home(g, b) else None)
+        value = jnp.where(home, value, other)
+        whole = lax.dynamic_update_slice_in_dim(whole, value, place(block) * rows, 0)
+    return whole
+
+
+def rows_to_owners(context):
+    blocks = lax.axis_size("blk")
+    group, block = lax.axis_index("dp"), lax.axis_index("blk")
+    mine = head_block(group, block)
+    cells, width = context.shape
+    rows = cells // blocks
+    whole = jnp.zeros((rows, blocks * width), context.dtype)
+    for k in range(blocks):
+        piece = lax.dynamic_slice_in_dim(context, (mine + k) % blocks * rows, rows, 0)
+        piece = moved(piece, lambda g, b: owner_of(g, b, (head_block(g, b) + k) % blocks))
+        whole = lax.dynamic_update_slice_in_dim(whole, piece, (block - k) % blocks * width, 1)
+    return whole
+
+
+def heads_to_workers(value):
+    blocks = lax.axis_size("blk")
+    group, block = lax.axis_index("dp"), lax.axis_index("blk")
+    mine = head_block(group, block)
+    rows, cols = value.shape
+    width = cols // blocks
+    whole = jnp.zeros((blocks * rows, width), value.dtype)
+    for k in range(blocks):
+        piece = lax.dynamic_slice_in_dim(value, (block - k) % blocks * width, width, 1)
+        piece = moved(piece, lambda g, b: worker_of(g, (b - k) % blocks))
+        whole = lax.dynamic_update_slice_in_dim(whole, piece, (mine + k) % blocks * rows, 0)
+    return whole
+
+
+def rows_summed(partial_rows):
+    blocks = lax.axis_size("blk")
+    group, block = lax.axis_index("dp"), lax.axis_index("blk")
+    rows = partial_rows.shape[0] // blocks
+    home = at_home(group, block)
+    other = moved(partial_rows, lambda g, b: None if at_home(g, b) else (g ^ 1, b))
+    total = added(partial_rows, other)
+
+    def taken(place):
+        return lax.dynamic_slice_in_dim(total, place * rows, rows, 0)
+
+    mine = {r: [taken(block ^ r), taken(blocks - 1 - (block ^ r))] for r in range(blocks // 2)}
+    for mask in reversed(pair_masks()):
+        kept = {r: mine[r] for r in range(mask)}
+        for r in range(mask):
+            came = [
+                moved(part, lambda g, b: (g, b ^ mask) if at_home(g, b) else None)
+                for part in mine[r + mask]
+            ]
+            kept[r] = [added(here, there) for here, there in zip(kept[r], came)]
+        mine = kept
+    own, mirror = mine[0]
+    far = moved(mirror, lambda g, b: (g, blocks - 1 - b) if at_home(g, b) else None)
+    return jnp.where(home, own, far)
+
+
+def reduced_heads(grad):
+    blocks = lax.axis_size("blk")
+    group, block = lax.axis_index("dp"), lax.axis_index("blk")
+    half = blocks // 2
+    rows, cols = grad.shape
+    width = cols // 3
+    value = grad.astype(jnp.bfloat16).reshape(blocks, rows // blocks, cols)
+    steps = dp_masks()[1:]
+    sides = [(group // mask) % 2 for mask in steps]
+    for mask, side in zip(steps, sides):
+        keep, send = halves(value, side, 1)
+        value = added(keep, swapped(send, mask, 0))
+    keep, send = halves(value, block // half, 0)
+    value = added(keep, swapped(send, 0, half))
+    place = block % half
+    pieces = [
+        (
+            lax.dynamic_index_in_dim(value, place ^ k, 0, keepdims=False)
+            if k == 0
+            else swapped(
+                lax.dynamic_index_in_dim(value, place ^ k, 0, keepdims=False), 0, k
+            )
+        )
+        for k in range(half)
+    ]
+    order = [place ^ k for k in range(half)]
+    value = jnp.zeros((half,) + pieces[0].shape, pieces[0].dtype)
+    for piece, index in zip(pieces, order):
+        value = lax.dynamic_update_slice_in_dim(value, piece[None], index, 0)
+    for mask, side in reversed(list(zip(steps, sides))):
+        value = joined(value, swapped(value, mask, 0), side, 1)
+    core = group % 2
+    other = swapped(value, 1, 0)
+    both = jnp.stack([jnp.where(core == 0, value, other), jnp.where(core == 0, other, value)])
+    both = both.reshape(2, half, rows // blocks, 3, width)
+    both = jnp.transpose(both, (3, 2, 1, 0, 4)).reshape(3, rows // blocks, blocks * width)
+    both = both.astype(jnp.float32)
+    return both[0], both[1], both[2]
 
 
 def local(
@@ -312,59 +515,31 @@
 ):
     rows_here = cell_states.shape[0]
     blocks = lax.axis_size("blk")
-    my_index = lax.axis_index("blk")
-    lengths_row = slide_lengths[0]
-    local_range = jnp.arange(rows_here, dtype=jnp.int32)
-    local_pos = my_index * rows_here + local_range
-    local_slide = slide_index(local_pos, lengths_row)
-    live = cell_mask.astype(jnp.bfloat16)
+    group, block = lax.axis_index("dp"), lax.axis_index("blk")
+    width = D // blocks
+    my_heads = head_block(group, block) * width
+    meta = group_meta(jnp.concatenate([cell_mask, slide_lengths[0]]))
+    mask_all = meta[:, :rows_here].reshape(-1)
+    ranges, query_code, key_code = slide_tables(meta[0, rows_here:], mask_all)
     x_float = cell_states.astype(jnp.float32)
-    normed, norm_back = jax.vjp(layer_norm, x_float, attn_gain, attn_shift)
-    normed_b = normed.astype(jnp.bfloat16)
-    queries = plain_dot(normed_b, query_weight).astype(jnp.bfloat16)
-    keys = plain_dot(normed_b, key_weight).astype(jnp.bfloat16)
-    values = plain_dot(normed_b, value_weight).astype(jnp.bfloat16)
-    heads_q = queries.reshape(rows_here, H, HD)
-    start_state = (
-        jnp.full((H, rows_here), neg_fill, jnp.float32),
-        jnp.zeros((H, rows_here), jnp.float32),
-        jnp.zeros((rows_here, H, HD), jnp.float32),
-    )
-    state = start_state
-    piece_keys = lax.all_gather(keys, "blk", axis=0, tiled=True)
-    piece_values = lax.all_gather(values, "blk", axis=0, tiled=True)
-    piece_live = lax.all_gather(live, "blk", axis=0, tiled=True)
-    rows = piece_keys.shape[0]
-    width = min(rows, rows_here)
-
-    def one_block(carry, index):
-        offset = index * width
-        block_keys = lax.dynamic_slice_in_dim(piece_keys, offset, width, 0).reshape(width, H, HD)
-        block_values = lax.dynamic_slice_in_dim(piece_values, offset, width, 0).reshape(
-            width, H, HD
-        )
-        block_live = lax.dynamic_slice_in_dim(piece_live, offset, width, 0)
-        key_pos = offset + jnp.arange(width, dtype=jnp.int32)
-        return (
-            forward_visit(
-                carry,
-                heads_q,
-                local_slide,
-                local_pos,
-                block_keys,
-                block_values,
-                block_live,
-                key_pos,
-                lengths_row,
-            ),
-            None,
-        )
-
-    state, _ = lax.scan(one_block, state, jnp.arange(rows // width, dtype=jnp.int32))
-    peak, total, running = state
-    context = running / total.T[:, :, None]
-    log_total = peak + jnp.log(total)
-    context_b = context.reshape(rows_here, D).astype(jnp.bfloat16)
+    _, norm_back = jax.vjp(layer_norm, x_float, attn_gain, attn_shift)
+    x_all = group_rows(cell_states)
+    normed_b = layer_norm(x_all.astype(jnp.float32), attn_gain, attn_shift).astype(jnp.bfloat16)
+    weight_here = jnp.concatenate(
+        [
+            lax.dynamic_slice_in_dim(weight, my_heads, width, 1)
+            for weight in (query_weight, key_weight, value_weight)
+        ],
+        axis=1,
+    )
+    projected = plain_dot(normed_b, weight_here).astype(jnp.bfloat16)
+    queries = projected[:, :width]
+    keys = projected[:, width : 2 * width]
+    values = projected[:, 2 * width :]
+    context_here, log_total = attention_forward(
+        ranges, queries, keys, values.T, query_code, key_code
+    )
+    context_b = rows_to_owners(context_here)
     hidden = x_float + plain_dot(context_b, out_weight)
     normed_two, norm_two_back = jax.vjp(layer_norm, hidden, ffn_gain, ffn_shift)
     normed_two_b = normed_two.astype(jnp.bfloat16)
@@ -422,55 +597,14 @@
     grad_attn_b = grad_hidden.astype(jnp.bfloat16)
     grad_out = rows_dot(context_b, grad_attn_b)
     grad_context_b = cols_dot(grad_attn_b, out_weight).astype(jnp.bfloat16)
-    heads_o = grad_context_b.reshape(rows_here, H, HD)
-    delta = jnp.sum(heads_o.astype(jnp.float32) * context, axis=-1).T
-    zero_heads = jnp.zeros((rows_here, H, HD), jnp.float32)
-
-    def key_turn(turn, carry):
-        travel, grads_travel, grad_q = carry
-        held_keys, held_values, held_live = travel
-        anchor = (my_index + turn) % blocks
-        key_pos = anchor * rows_here + local_range
-        key_slide = slide_index(key_pos, lengths_row)
-        part_q, part_k, part_v = backward_visit(
-            heads_q,
-            heads_o,
-            log_total,
-            delta,
-            local_slide,
-            local_pos,
-            held_keys.reshape(rows_here, H, HD),
-            held_values.reshape(rows_here, H, HD),
-            held_live,
-            key_pos,
-            key_slide,
-        )
-        grads_travel = (grads_travel[0] + part_k, grads_travel[1] + part_v)
-        travel = jax.tree.map(
-            lambda part, own: part.astype(own.dtype),
-            passed_along(shortened(travel), "blk", -1),
-            travel,
-        )
-        grads_travel = (
-            passed_along(grads_travel[0].astype(jnp.bfloat16), "blk", -1).astype(jnp.float32),
-            passed_along(grads_travel[1].astype(jnp.bfloat16), "blk", -1).astype(jnp.float32),
-        )
-        return (travel, grads_travel, grad_q + part_q)
-
-    _, (grad_k, grad_v), grad_q = lax.fori_loop(
-        0, blocks, key_turn, ((keys, values, live), (zero_heads, zero_heads), zero_heads)
-    )
-    grad_q_b = grad_q.reshape(rows_here, D).astype(jnp.bfloat16)
-    grad_k_b = grad_k.reshape(rows_here, D).astype(jnp.bfloat16)
-    grad_v_b = grad_v.reshape(rows_here, D).astype(jnp.bfloat16)
-    grad_query = rows_dot(normed_b, grad_q_b)
-    grad_key = rows_dot(normed_b, grad_k_b)
-    grad_value = rows_dot(normed_b, grad_v_b)
-    grad_normed = (
-        cols_dot(grad_q_b, query_weight)
-        + cols_dot(grad_k_b, key_weight)
-        + cols_dot(grad_v_b, value_weight)
-    )
+    grad_here = heads_to_workers(grad_context_b)
+    grad_q, grad_k, grad_v = attention_backward(
+        ranges, queries, grad_here, context_here, log_total, keys, values, keys.T, query_code, key_code
+    )
+    grad_projected = jnp.concatenate([grad_q, grad_k, grad_v], axis=1)
+    grad_query, grad_key, grad_value = reduced_heads(rows_dot(normed_b, grad_projected))
+    grad_normed = rows_summed(cols_dot(grad_projected, weight_here).astype(jnp.bfloat16))
+    grad_normed = grad_normed.astype(jnp.float32)
     grad_from_norm, grad_attn_gain, grad_attn_shift = norm_back(grad_normed)
     states_grad = grad_hidden + grad_from_norm
     by_block = lambda part: part.reshape(blocks, -1)
@@ -491,9 +625,9 @@
     totals = (
         small[0],
         small[1],
-        reduced(grad_query, False),
-        reduced(grad_key, True),
-        reduced(grad_value, False),
+        grad_query,
+        grad_key,
+        grad_value,
         reduced(grad_out, True),
         small[2],
         small[3],

time: 1020 us -> 647 us (0.63)
  waiting for transfers between devices: 442 us -> 168 us
  matrix products: 208 us -> 94.6 us
  Pallas kernels: 0 us -> 65.8 us
  other arithmetic: 105 us -> 71.7 us
  starting transfers between devices: 131 us -> 153 us
  local copies, waits for them, and re-layouts: 85.9 us -> 72.1 us
  between operations: 22.5 us -> 9.15 us
  blocking collectives: 10.3 us -> 0 us
    ppermute x20 -> x19, waiting for transfers between devices: 191 us -> 19.5 us  [moved(): return lax.ppermute(value, MESH_AXES, pairs)]
    all_gather x2 -> x0, waiting for transfers between devices: 104 us -> none  [the longest x1 64.3 us: local(): piece_keys = lax.all_gather(keys, 'blk', axis=0, tiled=True)]
    dot_general x28 -> x0, matrix products: 93 us -> none  [the longest x4 20.4 us: backward_update(): jnp.einsum('qhd,khd->hqk', heads_o, heads_v, preferred_element_type=jnp.f...]
    pallas_call x0 -> x2, Pallas kernels: none -> 65.8 us  [the longest x1 38.1 us: attention_backward(): pl.pallas_call(backward_kernel, out_shape=(out, out, out), grid_spec=pltp...]
    ppermute x20 -> x19, starting transfers between devices: 20.6 us -> 54.3 us  [moved(): return lax.ppermute(value, MESH_AXES, pairs)]
    dynamic_slice x16 -> x6, local copies, waits for them, and re-layouts: 31.2 us -> 8.02 us  [the longest x2 4.1 us: local(): lax.dynamic_slice_in_dim(weight, my_heads, width, 1)]
    convert_element_type x13 -> x1, other arithmetic: 25 us -> 1.87 us  [reduced_heads(): both = both.astype(jnp.float32)]
    while x64 -> x0, local copies, waits for them, and re-layouts: 21.3 us -> none
  transfers between devices with their start and end apart: 96 -> 80, of which waited for: 47 -> 38; matrix products, arithmetic and copies ran while one was open for 13% -> 21% of each run, Pallas kernels for 0% -> 6%
where the time goes in v2:
time: 647 us; the launch traced here: 634 us
  waiting for transfers between devices  168 us (26%)
  starting transfers between devices  153 us (24%)
  matrix products  94.6 us (15%)
  local copies, waits for them, and re-layouts  72.1 us (11%)
  other arithmetic  71.7 us (11%)
  Pallas kernels  65.8 us (10%)
  between operations  9.15 us (1%)
    ppermute x61, waiting for transfers between devices, swapped(): return lax.ppermute(value, MESH_AXES, pairs)  148 us
    ppermute x61, starting transfers between devices, swapped(): return lax.ppermute(value, MESH_AXES, pairs)  98.4 us
    ppermute x19, starting transfers between devices, moved(): return lax.ppermute(value, MESH_AXES, pairs)  54.3 us
    pallas_call x1, Pallas kernels, attention_backward(): pl.pallas_call(backward_kernel, out_shape=(out, out, out), grid_spec=pltp...  38.1 us
    dot_general x6, matrix products, plain_dot(): return jnp.dot(left, right, preferred_element_type=jnp.float32)  32.4 us
    convert_element_type x25, other arithmetic, added(): (left.astype(jnp.float32) + right.astype(jnp.float32)).astype(jnp.bfloat16)  30 us
    dot_general x6, matrix products, cols_dot(): lax.dot_general(left, right, (((1,), (1,)), ((), ())), preferred_element_...  28.5 us
    pallas_call x1, Pallas kernels, attention_forward(): pl.pallas_call(forward_kernel, out_shape=(jax.ShapeDtypeStruct((N, W), jn...  27.7 us
  transfers between devices with their start and end apart: 80, of which 38 were waited for; matrix products, arithmetic and copies ran while one was open for 21% of the time, Pallas kernels for 6%

profile of v2, /device:TPU:17, one launch (start us, length us, event | category | flops | bytes accessed | tf_op | source)
XLA Modules:
  0.0 634.0 jit_solution(10017209474161722374)
XLA Ops:
  0.7 3.8 collective-permute-start.4
  22.4 6.8 %collective-permute-start.7 = (bf16[384,1024]{1,0:T(8,128)(2,1)S(1)}, bf16[384,1024]{1,0:T(8,128)(2,1)}, u32[]{:S(2)}, u32[]{:S(2)}) collective-permute-start(bf16[384,1024]{1,0:T(8,128)(2,1)S(1)} %copy-done.4), channel_id=1, source_target_pairs={{0,1},{1,0},{6,7},{7,6},{8,9},{9,8},{14,15},{15,14},{16,17},{17,16... | collective-permute-start | bytes 2359304 | tf_op jit(solution)/shard_map/ppermute | solution.py:339
  41.3 5.8 collective-permute-done.9
  56.1 3.2 convolution_convert_fusion.3
  65.9 27.7 %attention_forward.1 = (bf16[1536,256]{1,0:T(8,128)(2,1)}, f32[4,1536]{1,0:T(4,128)}) custom-call(s32[3,2]{1,0:T(4,128)} %pad_add_fusion.2.range_ref, bf16[1536,256]{1,0:T(8,128)(2,1)} %copy.131.q_ref, bf16[1536,256]{1,0:T(8,128)(2,1)} %copy.132.k_ref, bf16[256,1536]{1,0:T(8,128)(2,1)} %get-tuple-element.120.vt_ref, s32[1,1536]{1,0:T(1,128)} %broadcast_in_dim.153.cq_ref, ...), custom_call_target="tpu_custom_call" | custom-call | tf_op jit(solution)/shard_map/attention_forward/pallas_call | solution.py:237
  99.5 3.8 collective-permute-start.13
  103.3 4.4 collective-permute-start.14
  108.8 5.8 collective-permute-done.14
  116.1 22.2 %multiply_convert_fusion = (bf16[384,4096]{1,0:T(8,128)(2,1)S(1)}, f32[384,4096]{1,0:T(8,128)}, f32[384,4096]{1,0:T(8,128)}) fusion(f32[4096]{0:T(1024)S(1)} %copy-done.42, bf16[1024,4096]{1,0:T(8,128)(2,1)} %param.36, f32[384,1024]{1,0:T(8,128)S(1)} %get-tuple-element.202, f32[1024]{0:T(1024)S(1)} %copy-done.45, f32[1024]{0:T(1024)S(1)} %copy-done.38, ...), kind=kOutput, calls=%fused_computation.17 | convolution fusion | flops 3327000576 | bytes 25717760 | tf_op jit(solution)/shard_map/dot_general | solution.py:63
  138.4 3.4 add_add_fusion.4
  168.2 3.1 fusion.31
  175.6 13.1 %convert_reduce_fusion.1 = (f32[4096]{0:T(1024)S(1)}, bf16[384,4096]{1,0:T(8,128)(2,1)S(1)}) fusion(f32[384,4096]{1,0:T(8,128)} %get-tuple-element.111, f32[384,4096]{1,0:T(8,128)} %get-tuple-element.203, bf16[4096,1024]{1,0:T(8,128)(2,1)} %param.38, f32[384,1024]{1,0:T(8,128)S(1)} %convert_add_fusion.1), kind=kOutput, calls=%fused_computation.14 | convolution fusion | flops 3246780416 | bytes 25706496 | tf_op jit(solution)/shard_map/dot_general | solution.py:73
  188.8 3.8 multiply_reduce_fusion
  197.8 7.1 %convolution_convert_fusion.1 = bf16[1024,4096]{1,0:T(8,128)(2,1)} fusion(bf16[384,4096]{1,0:T(8,128)(2,1)S(1)} %get-tuple-element.211, f32[384,1024]{1,0:T(8,128)S(1)} %copy-done.15, f32[1024]{0:T(1024)S(1)} %copy-done.45, f32[1024]{0:T(1024)S(1)} %copy-done.38, f32[384]{0:T(512)S(1)} %fusion.87, f32[384]{0:T(512)S(1)} %broadcast_multiply_fusion.2), kind=kOutput, calls=%fused_computation.6 | convolution fusion | flops 3227385856 | bytes 13118464 | tf_op jit(solution)/shard_map/dot_general | solution.py:67
  204.9 7.2 %convolution_convert_fusion = bf16[4096,1024]{1,0:T(8,128)(2,1)} fusion(bf16[384,4096]{1,0:T(8,128)(2,1)S(1)} %copy-done.48, f32[384,1024]{1,0:T(8,128)S(1)} %convert_add_fusion.1), kind=kOutput, calls=%fused_computation.5 | convolution fusion | flops 3225812992 | bytes 13107200 | tf_op jit(solution)/shard_map/dot_general | solution.py:67
  216.4 8.2 %collective-permute-start.20 = (bf16[384,256]{1,0:T(8,128)(2,1)}, bf16[384,256]{1,0:T(8,128)(2,1)}, u32[]{:S(2)}, u32[]{:S(2)}) collective-permute-start(bf16[384,256]{1,0:T(8,128)(2,1)} %get-tuple-element.151), channel_id=1, source_target_pairs={{0,0},{1,4},{2,1},{3,5},{4,2},{5,6},{6,3},{7,7},{8,8},{9,12},{10,9... | collective-permute-start | bytes 589832 | tf_op jit(solution)/shard_map/ppermute | solution.py:339
  227.6 3.4 collective-permute-start.23
  240.8 4.7 constant_dynamic-slice_fusion.19
  246.2 4.7 constant_dynamic-slice_fusion.14
  261.2 38.1 %attention_backward.1 = (bf16[1536,256]{1,0:T(8,128)(2,1)}, bf16[1536,256]{1,0:T(8,128)(2,1)}, bf16[1536,256]{1,0:T(8,128)(2,1)}) custom-call(s32[3,2]{1,0:T(4,128)} %pad_add_fusion.2.range_ref, bf16[1536,256]{1,0:T(8,128)(2,1)} %copy.131.q_ref, bf16[1536,256]{1,0:T(8,128)(2,1)} %constant_dynamic-update-slice_fusion.11.do_ref, ...), custom_call_target="tpu_custom_call" | custom-call | tf_op jit(solution)/shard_map/attention_backward/pallas_call | solution.py:297
  305.5 3.3 convolution_convert_fusion.6
  308.8 3.3 collective-permute-done.73
  320.1 6.4 %convolution_convert_fusion.2 = bf16[1536,1024]{1,0:T(8,128)(2,1)} fusion(bf16[1536,768]{1,0:T(8,128)(2,1)} %copy-done.35, bf16[1024,256]{1,0:T(8,128)(2,1)} %get-tuple-element.214, bf16[1024,256]{1,0:T(8,128)(2,1)} %get-tuple-element.215, bf16[1024,256]{1,0:T(8,128)(2,1)} %constant_dynamic-slice_fusion.44), kind=kOutput, calls=%fused_computation.34 | convolution fusion | flops 2422210560 | bytes 7077888 | tf_op jit(solution)/shard_map/dot_general | solution.py:73
  329.9 5.9 collective-permute-done.33
  349.8 5.6 collective-permute-start.79
  363.4 7.6 %collective-permute-done.41 = bf16[4,64,1024]{2,1,0:T(8,128)(2,1)S(1)} collective-permute-done((bf16[4,64,1024]{2,1,0:T(8,128)(2,1)}, bf16[4,64,1024]{2,1,0:T(8,128)(2,1)S(1)}, u32[]{:S(2)}, u32[]{:S(2)}) %collective-permute-start.41) | collective-permute-done | bytes 524320 | tf_op jit(solution)/shard_map/ppermute | solution.py:88
  371.0 4.5 collective-permute-start.35
  375.8 6.6 %collective-permute-done.65 = bf16[4,64,1024]{2,1,0:T(8,128)(2,1)} collective-permute-done((bf16[4,64,1024]{2,1,0:T(8,128)(2,1)}, bf16[4,64,1024]{2,1,0:T(8,128)(2,1)}, u32[]{:S(2)}, u32[]{:S(2)}) %collective-permute-start.65) | collective-permute-done | bytes 524320 | tf_op jit(solution)/shard_map/ppermute | solution.py:88
  384.9 6.4 %collective-permute-done.35 = bf16[2,64,768]{1,2,0:T(8,128)(2,1)S(1)} collective-permute-done((bf16[2,64,768]{1,2,0:T(8,128)(2,1)S(1)}, bf16[2,64,768]{1,2,0:T(8,128)(2,1)S(1)}, u32[]{:S(2)}, u32[]{:S(2)}) %collective-permute-start.35) | collective-permute-done | bytes 196640 | tf_op jit(solution)/shard_map/ppermute | solution.py:88
  392.0 5.8 collective-permute-done.36
  400.6 3.9 collective-permute-done.66
  404.7 3.4 collective-permute-done.37
  427.2 3.1 collective-permute-done.46
  431.1 3.1 collective-permute-done.70
  434.2 10.3 %collective-permute-start.47 = (bf16[128,1024]{1,0:T(8,128)(2,1)S(1)}, bf16[128,1024]{1,0:T(8,128)(2,1)S(1)}, u32[]{:S(2)}, u32[]{:S(2)}) collective-permute-start(bf16[128,1024]{1,0:T(8,128)(2,1)S(1)} %pad_maximum_fusion.13), channel_id=1, source_target_pairs={{0,4},{1,5},{2,6},{3,7},{4,0},{5,1},{6,2},{7,3},{8,12},{9,13},{10,... | collective-permute-start | bytes 786440 | tf_op jit(solution)/shard_map/ppermute | solution.py:88
  446.4 3.4 add_convert_fusion.2
  450.0 4.8 collective-permute-start.26
  466.3 5.3 add_convert_fusion.1
  474.6 6.3 add_convert_fusion
  491.3 22.1 %collective-permute-done.49 = bf16[4,64,4096]{2,1,0:T(8,128)(2,1)} collective-permute-done((bf16[4,64,4096]{2,1,0:T(8,128)(2,1)}, bf16[4,64,4096]{2,1,0:T(8,128)(2,1)}, u32[]{:S(2)}, u32[]{:S(2)}) %collective-permute-start.49) | collective-permute-done | bytes 2097184 | tf_op jit(solution)/shard_map/ppermute | solution.py:88
  516.2 14.2 %collective-permute-done.57 = bf16[4,256,1024]{2,1,0:T(8,128)(2,1)S(1)} collective-permute-done((bf16[4,256,1024]{2,1,0:T(8,128)(2,1)S(1)}, bf16[4,256,1024]{2,1,0:T(8,128)(2,1)S(1)}, u32[]{:S(2)}, u32[]{:S(2)}) %collective-permute-start.57) | collective-permute-done | bytes 2097184 | tf_op jit(solution)/shard_map/ppermute | solution.py:88
  534.3 18.6 %collective-permute-done.50 = bf16[4,32,4096]{2,1,0:T(8,128)(2,1)S(1)} collective-permute-done((bf16[4,32,4096]{2,1,0:T(8,128)(2,1)S(1)}, bf16[4,32,4096]{2,1,0:T(8,128)(2,1)S(1)}, u32[]{:S(2)}, u32[]{:S(2)}) %collective-permute-start.50) | collective-permute-done | bytes 1048608 | tf_op jit(solution)/shard_map/ppermute | solution.py:88
  555.7 5.8 collective-permute-done.51
  561.6 8.6 %collective-permute-start.52 = (bf16[1,32,4096]{2,1,0:T(8,128)(2,1)S(1)}, bf16[1,32,4096]{2,1,0:T(8,128)(2,1)S(1)}, u32[]{:S(2)}, u32[]{:S(2)}) collective-permute-start(bf16[1,32,4096]{2,1,0:T(8,128)(2,1)S(1)} %constant_dynamic-slice_fusion.15), channel_id=1, source_target_pairs={{0,3},{1,2},{2,1},{3,0},{4,7},{5,6},{6,5},{7,4},{8,11},{9,10},{10,... | collective-permute-start | bytes 786440 | tf_op jit(solution)/shard_map/ppermute | solution.py:88
  573.8 12.5 %collective-permute-start.60 = (bf16[1,128,1024]{2,1,0:T(8,128)(2,1)}, bf16[1,128,1024]{2,1,0:T(8,128)(2,1)}, u32[]{:S(2)}, u32[]{:S(2)}) collective-permute-start(bf16[1,128,1024]{2,1,0:T(8,128)(2,1)} %constant_dynamic-slice_fusion.10), channel_id=1, source_target_pairs={{0,3},{1,2},{2,1},{3,0},{4,7},{5,6},{6,5},{7,4},{8,11},{9,10},{10,... | collective-permute-start | bytes 786440 | tf_op jit(solution)/shard_map/ppermute | solution.py:88
  596.3 3.9 collective-permute-done.60
  607.6 10.9 %collective-permute-done.54 = bf16[64,4096]{1,0:T(8,128)(2,1)S(1)} collective-permute-done((bf16[64,4096]{1,0:T(8,128)(2,1)S(1)}, bf16[64,4096]{1,0:T(8,128)(2,1)S(1)}, u32[]{:S(2)}, u32[]{:S(2)}) %collective-permute-start.54) | collective-permute-done | bytes 524320 | tf_op jit(solution)/shard_map/ppermute | solution.py:88
  618.8 3.2 collective-permute-start.55
  (508 shorter events, 245.7 us)
Async XLA Ops:
  0.7 47.8 %collective-permute-start.4 = (bf16[384,1024]{1,0:T(8,128)(2,1)}, bf16[384,1024]{1,0:T(8,128)(2,1)}, u32[]{:S(2)}, u32[]{:S(2)}) collective-permute-start(bf16[384,1024]{1,0:T(8,128)(2,1)} %param.23), channel_id=1, source_target_pairs={{0,4},{1,5},{6,2},{7,3},{8,12},{9,13},{14,10},{15,11},{16,20},{17,... | collective-permute-start | bytes 2359304 | tf_op jit(solution)/shard_map/ppermute | solution.py:339
  4.5 26.9 %collective-permute-start.5 = (bf16[384,1024]{1,0:T(8,128)(2,1)}, bf16[384,1024]{1,0:T(8,128)(2,1)}, u32[]{:S(2)}, u32[]{:S(2)}) collective-permute-start(bf16[384,1024]{1,0:T(8,128)(2,1)} %param.23), channel_id=1, source_target_pairs={{2,1},{3,0},{4,7},{5,6},{10,9},{11,8},{12,15},{13,14},{18,17},{19,... | collective-permute-start | bytes 2359304 | tf_op jit(solution)/shard_map/ppermute | solution.py:339
  6.4 11.3 %collective-permute-start = (s32[388]{0:T(512)S(1)}, s32[388]{0:T(512)S(1)}, u32[]{:S(2)}, u32[]{:S(2)}) collective-permute-start(s32[388]{0:T(512)S(1)} %pad_add_fusion.1), channel_id=1, source_target_pairs={{0,4},{1,5},{2,6},{3,7},{4,0},{5,1},{6,2},{7,3},{8,12},{9,13},{10,... | collective-permute-start | bytes 4664 | tf_op jit(solution)/shard_map/ppermute | solution.py:88
  17.8 11.5 %collective-permute-start.3 = (s32[2,388]{1,0:T(2,128)S(1)}, s32[2,388]{1,0:T(2,128)S(1)}, u32[]{:S(2)}, u32[]{:S(2)}) collective-permute-start(s32[2,388]{1,0:T(2,128)S(1)} %add_select_fusion), channel_id=1, source_target_pairs={{0,3},{1,2},{2,1},{3,0},{4,7},{5,6},{6,5},{7,4},{8,11},{9,10},{10,... | collective-permute-start | bytes 9320 | tf_op jit(solution)/shard_map/ppermute | solution.py:88
  22.4 16.3 %collective-permute-start.7 = (bf16[384,1024]{1,0:T(8,128)(2,1)S(1)}, bf16[384,1024]{1,0:T(8,128)(2,1)}, u32[]{:S(2)}, u32[]{:S(2)}) collective-permute-start(bf16[384,1024]{1,0:T(8,128)(2,1)S(1)} %copy-done.4), channel_id=1, source_target_pairs={{0,1},{1,0},{6,7},{7,6},{8,9},{9,8},{14,15},{15,14},{16,17},{17,16... | collective-permute-start | bytes 2359304 | tf_op jit(solution)/shard_map/ppermute | solution.py:339
  31.4 15.8 %collective-permute-start.9 = (bf16[384,1024]{1,0:T(8,128)(2,1)}, bf16[384,1024]{1,0:T(8,128)(2,1)}, u32[]{:S(2)}, u32[]{:S(2)}) collective-permute-start(bf16[384,1024]{1,0:T(8,128)(2,1)} %collective-permute-done.5), channel_id=1, source_target_pairs={{0,1},{1,0},{6,7},{7,6},{8,9},{9,8},{14,15},{15,14},{16,17},{17,16... | collective-permute-start | bytes 2359304 | tf_op jit(solution)/shard_map/ppermute | solution.py:339
  33.3 15.9 %collective-permute-start.6 = (bf16[384,1024]{1,0:T(8,128)(2,1)}, bf16[384,1024]{1,0:T(8,128)(2,1)}, u32[]{:S(2)}, u32[]{:S(2)}) collective-permute-start(bf16[384,1024]{1,0:T(8,128)(2,1)} %collective-permute-done.5), channel_id=1, source_target_pairs={{0,4},{1,5},{6,2},{7,3},{8,12},{9,13},{14,10},{15,11},{16,20},{17,... | collective-permute-start | bytes 2359304 | tf_op jit(solution)/shard_map/ppermute | solution.py:339
  38.7 12.0 %collective-permute-start.8 = (bf16[384,1024]{1,0:T(8,128)(2,1)}, bf16[384,1024]{1,0:T(8,128)(2,1)S(1)}, u32[]{:S(2)}, u32[]{:S(2)}) collective-permute-start(bf16[384,1024]{1,0:T(8,128)(2,1)} %collective-permute-done.7), channel_id=1, source_target_pairs={{0,4},{1,5},{6,2},{7,3},{8,12},{9,13},{14,10},{15,11},{16,20},{17,... | collective-permute-start | bytes 2359304 | tf_op jit(solution)/shard_map/ppermute | solution.py:339
  95.6 12.1 %collective-permute-start.11 = (bf16[384,256]{1,0:T(8,128)(2,1)}, bf16[384,256]{1,0:T(8,128)(2,1)}, u32[]{:S(2)}, u32[]{:S(2)}) collective-permute-start(bf16[384,256]{1,0:T(8,128)(2,1)} %get-tuple-element.155), channel_id=1, source_target_pairs={{0,0},{1,2},{2,4},{3,6},{4,1},{5,3},{6,5},{7,7},{8,8},{9,10},{10,1... | collective-permute-start | bytes 589832 | tf_op jit(solution)/shard_map/ppermute | solution.py:339
  98.3 10.4 %collective-permute-start.12 = (bf16[384,256]{1,0:T(8,128)(2,1)S(1)}, bf16[384,256]{1,0:T(8,128)(2,1)S(1)}, u32[]{:S(2)}, u32[]{:S(2)}) collective-permute-start(bf16[384,256]{1,0:T(8,128)(2,1)S(1)} %get-tuple-element.154), channel_id=1, source_target_pairs={{0,1},{1,3},{2,5},{3,7},{4,2},{5,0},{6,6},{7,4},{8,9},{9,11},{10,1... | collective-permute-start | bytes 589832 | tf_op jit(solution)/shard_map/ppermute | solution.py:339
  99.5 9.3 %collective-permute-start.13 = (bf16[384,256]{1,0:T(8,128)(2,1)S(1)}, bf16[384,256]{1,0:T(8,128)(2,1)S(1)}, u32[]{:S(2)}, u32[]{:S(2)}) collective-permute-start(bf16[384,256]{1,0:T(8,128)(2,1)S(1)} %get-tuple-element.153), channel_id=1, source_target_pairs={{0,2},{1,0},{2,6},{3,4},{4,3},{5,1},{6,7},{7,5},{8,10},{9,8},{10,1... | collective-permute-start | bytes 589832 | tf_op jit(solution)/shard_map/ppermute | solution.py:339
  103.3 11.3 %collective-permute-start.14 = (bf16[384,256]{1,0:T(8,128)(2,1)S(1)}, bf16[384,256]{1,0:T(8,128)(2,1)S(1)}, u32[]{:S(2)}, u32[]{:S(2)}) collective-permute-start(bf16[384,256]{1,0:T(8,128)(2,1)S(1)} %get-tuple-element.152), channel_id=1, source_target_pairs={{0,3},{1,1},{2,7},{3,5},{4,0},{5,2},{6,4},{7,6},{8,11},{9,9},{10,1... | collective-permute-start | bytes 589832 | tf_op jit(solution)/shard_map/ppermute | solution.py:339
  216.4 36.3 %collective-permute-start.20 = (bf16[384,256]{1,0:T(8,128)(2,1)}, bf16[384,256]{1,0:T(8,128)(2,1)}, u32[]{:S(2)}, u32[]{:S(2)}) collective-permute-start(bf16[384,256]{1,0:T(8,128)(2,1)} %get-tuple-element.151), channel_id=1, source_target_pairs={{0,0},{1,4},{2,1},{3,5},{4,2},{5,6},{6,3},{7,7},{8,8},{9,12},{10,9... | collective-permute-start | bytes 589832 | tf_op jit(solution)/shard_map/ppermute | solution.py:339
  224.6 31.2 %collective-permute-start.21 = (bf16[384,256]{1,0:T(8,128)(2,1)}, bf16[384,256]{1,0:T(8,128)(2,1)}, u32[]{:S(2)}, u32[]{:S(2)}) collective-permute-start(bf16[384,256]{1,0:T(8,128)(2,1)} %get-tuple-element.150), channel_id=1, source_target_pairs={{0,5},{1,0},{2,4},{3,1},{4,7},{5,2},{6,6},{7,3},{8,13},{9,8},{10,1... | collective-permute-start | bytes 589832 | tf_op jit(solution)/shard_map/ppermute | solution.py:339
  227.6 29.8 %collective-permute-start.22 = (bf16[384,256]{1,0:T(8,128)(2,1)}, bf16[384,256]{1,0:T(8,128)(2,1)}, u32[]{:S(2)}, u32[]{:S(2)}) collective-permute-start(bf16[384,256]{1,0:T(8,128)(2,1)} %get-tuple-element.149), channel_id=1, source_target_pairs={{0,1},{1,5},{2,0},{3,4},{4,3},{5,7},{6,2},{7,6},{8,9},{9,13},{10,8... | collective-permute-start | bytes 589832 | tf_op jit(solution)/shard_map/ppermute | solution.py:339
  227.6 31.9 %collective-permute-start.23 = (bf16[384,256]{1,0:T(8,128)(2,1)S(1)}, bf16[384,256]{1,0:T(8,128)(2,1)}, u32[]{:S(2)}, u32[]{:S(2)}) collective-permute-start(bf16[384,256]{1,0:T(8,128)(2,1)S(1)} %get-tuple-element.148), channel_id=1, source_target_pairs={{0,4},{1,1},{2,5},{3,0},{4,6},{5,3},{6,7},{7,2},{8,12},{9,9},{10,1... | collective-permute-start | bytes 589832 | tf_op jit(solution)/shard_map/ppermute | solution.py:339
  240.8 101.9 %collective-permute-start.40 = (bf16[4,128,1024]{2,1,0:T(8,128)(2,1)}, bf16[4,128,1024]{2,1,0:T(8,128)(2,1)}, u32[]{:S(2)}, u32[]{:S(2)}) collective-permute-start(bf16[4,128,1024]{2,1,0:T(8,128)(2,1)} %constant_dynamic-slice_fusion.24), channel_id=1, source_target_pairs={{0,4},{1,5},{2,6},{3,7},{4,0},{5,1},{6,2},{7,3},{8,12},{9,13},{10,... | collective-permute-start | bytes 3145736 | tf_op jit(solution)/shard_map/ppermute | solution.py:88
  252.7 213.6 %collective-permute-start.48 = (bf16[4,128,4096]{2,1,0:T(8,128)(2,1)}, bf16[4,128,4096]{2,1,0:T(8,128)(2,1)}, u32[]{:S(2)}, u32[]{:S(2)}) collective-permute-start(bf16[4,128,4096]{2,1,0:T(8,128)(2,1)} %constant_dynamic-slice_fusion.19), channel_id=1, source_target_pairs={{0,4},{1,5},{2,6},{3,7},{4,0},{5,1},{6,2},{7,3},{8,12},{9,13},{10,... | collective-permute-start | bytes 12582920 | tf_op jit(solution)/shard_map/ppermute | solution.py:88
  255.8 218.8 %collective-permute-start.56 = (bf16[4,512,1024]{2,1,0:T(8,128)(2,1)}, bf16[4,512,1024]{2,1,0:T(8,128)(2,1)}, u32[]{:S(2)}, u32[]{:S(2)}) collective-permute-start(bf16[4,512,1024]{2,1,0:T(8,128)(2,1)} %constant_dynamic-slice_fusion.14), channel_id=1, source_target_pairs={{0,4},{1,5},{2,6},{3,7},{4,0},{5,1},{6,2},{7,3},{8,12},{9,13},{10,... | collective-permute-start | bytes 12582920 | tf_op jit(solution)/shard_map/ppermute | solution.py:88
  257.4 44.6 %collective-permute-start.72 = (bf16[4,64,1024]{2,1,0:T(8,128)(2,1)}, bf16[4,64,1024]{2,1,0:T(8,128)(2,1)}, u32[]{:S(2)}, u32[]{:S(2)}) collective-permute-start(bf16[4,64,1024]{2,1,0:T(8,128)(2,1)} %constant_dynamic-slice_fusion.4), channel_id=1, source_target_pairs={{0,4},{1,5},{2,6},{3,7},{4,0},{5,1},{6,2},{7,3},{8,12},{9,13},{10,... | collective-permute-start | bytes 1572872 | tf_op jit(solution)/shard_map/ppermute | solution.py:88
  317.4 18.5 %collective-permute-start.33 = (bf16[4,128,768]{1,2,0:T(8,128)(2,1)}, bf16[4,128,768]{1,2,0:T(8,128)(2,1)}, u32[]{:S(2)}, u32[]{:S(2)}) collective-permute-start(bf16[4,128,768]{1,2,0:T(8,128)(2,1)} %copy.148), channel_id=1, source_target_pairs={{0,8},{1,9},{2,10},{3,11},{4,12},{5,13},{6,14},{7,15},{8,0},{9,1},... | collective-permute-start | bytes 2359304 | tf_op jit(solution)/shard_map/ppermute | solution.py:88
  327.7 18.6 %collective-permute-start.64 = (bf16[4,128,1024]{2,1,0:T(8,128)(2,1)}, bf16[4,128,1024]{2,1,0:T(8,128)(2,1)}, u32[]{:S(2)}, u32[]{:S(2)}) collective-permute-start(bf16[4,128,1024]{2,1,0:T(8,128)(2,1)} %constant_dynamic-slice_fusion.9), channel_id=1, source_target_pairs={{0,4},{1,5},{2,6},{3,7},{4,0},{5,1},{6,2},{7,3},{8,12},{9,13},{10,... | collective-permute-start | bytes 3145736 | tf_op jit(solution)/shard_map/ppermute | solution.py:88
  341.2 104.9 %collective-permute-start.24 = (bf16[1536,1024]{1,0:T(8,128)(2,1)}, bf16[1536,1024]{1,0:T(8,128)(2,1)}, u32[]{:S(2)}, u32[]{:S(2)}) collective-permute-start(bf16[1536,1024]{1,0:T(8,128)(2,1)} %convolution_convert_fusion.2), channel_id=1, source_target_pairs={{2,6},{3,7},{4,0},{5,1},{10,14},{11,15},{12,8},{13,9},{18,22},{19,... | collective-permute-start | bytes 9437192 | tf_op jit(solution)/shard_map/ppermute | solution.py:339
  345.5 14.0 %collective-permute-start.34 = (bf16[4,64,768]{2,1,0:T(8,128)(2,1)}, bf16[4,64,768]{2,1,0:T(8,128)(2,1)}, u32[]{:S(2)}, u32[]{:S(2)}) collective-permute-start(bf16[4,64,768]{2,1,0:T(8,128)(2,1)} %copy.138), channel_id=1, source_target_pairs={{0,16},{1,17},{2,18},{3,19},{4,20},{5,21},{6,22},{7,23},{8,24},{9,... | collective-permute-start | bytes 1179656 | tf_op jit(solution)/shard_map/ppermute | solution.py:88
  357.1 13.9 %collective-permute-start.41 = (bf16[4,64,1024]{2,1,0:T(8,128)(2,1)}, bf16[4,64,1024]{2,1,0:T(8,128)(2,1)S(1)}, u32[]{:S(2)}, u32[]{:S(2)}) collective-permute-start(bf16[4,64,1024]{2,1,0:T(8,128)(2,1)} %constant_dynamic-slice_fusion.23), channel_id=1, source_target_pairs={{0,16},{1,17},{2,18},{3,19},{4,20},{5,21},{6,22},{7,23},{8,24},{9,... | collective-permute-start | bytes 1572872 | tf_op jit(solution)/shard_map/ppermute | solution.py:88
  359.6 22.8 %collective-permute-start.65 = (bf16[4,64,1024]{2,1,0:T(8,128)(2,1)}, bf16[4,64,1024]{2,1,0:T(8,128)(2,1)}, u32[]{:S(2)}, u32[]{:S(2)}) collective-permute-start(bf16[4,64,1024]{2,1,0:T(8,128)(2,1)} %constant_dynamic-slice_fusion.8), channel_id=1, source_target_pairs={{0,16},{1,17},{2,18},{3,19},{4,20},{5,21},{6,22},{7,23},{8,24},{9,... | collective-permute-start | bytes 1572872 | tf_op jit(solution)/shard_map/ppermute | solution.py:88
  371.0 20.3 %collective-permute-start.35 = (bf16[2,64,768]{1,2,0:T(8,128)(2,1)S(1)}, bf16[2,64,768]{1,2,0:T(8,128)(2,1)S(1)}, u32[]{:S(2)}, u32[]{:S(2)}) collective-permute-start(bf16[2,64,768]{1,2,0:T(8,128)(2,1)S(1)} %constant_dynamic-slice_fusion.25), channel_id=1, source_target_pairs={{0,2},{1,3},{2,0},{3,1},{4,6},{5,7},{6,4},{7,5},{8,10},{9,11},{10,... | collective-permute-start | bytes 589832 | tf_op jit(solution)/shard_map/ppermute | solution.py:88
  382.4 16.6 %collective-permute-start.42 = (bf16[4,32,1024]{2,1,0:T(8,128)(2,1)S(1)}, bf16[4,32,1024]{2,1,0:T(8,128)(2,1)S(1)}, u32[]{:S(2)}, u32[]{:S(2)}) collective-permute-start(bf16[4,32,1024]{2,1,0:T(8,128)(2,1)S(1)} %constant_dynamic-slice_fusion.22), channel_id=1, source_target_pairs={{0,8},{1,9},{2,10},{3,11},{4,12},{5,13},{6,14},{7,15},{8,0},{9,1},... | collective-permute-start | bytes 786440 | tf_op jit(solution)/shard_map/ppermute | solution.py:88
  409.7 34.8 %collective-permute-start.38 = (bf16[2,128,768]{1,2,0:T(8,128)(2,1)S(1)}, bf16[2,128,768]{1,2,0:T(8,128)(2,1)S(1)}, u32[]{:S(2)}, u32[]{:S(2)}) collective-permute-start(bf16[2,128,768]{1,2,0:T(8,128)(2,1)S(1)} %pad_maximum_fusion.11), channel_id=1, source_target_pairs={{0,8},{1,9},{2,10},{3,11},{4,12},{5,13},{6,14},{7,15},{8,0},{9,1},... | collective-permute-start | bytes 1179656 | tf_op jit(solution)/shard_map/ppermute | solution.py:88
  434.2 11.4 %collective-permute-start.47 = (bf16[128,1024]{1,0:T(8,128)(2,1)S(1)}, bf16[128,1024]{1,0:T(8,128)(2,1)S(1)}, u32[]{:S(2)}, u32[]{:S(2)}) collective-permute-start(bf16[128,1024]{1,0:T(8,128)(2,1)S(1)} %pad_maximum_fusion.13), channel_id=1, source_target_pairs={{0,4},{1,5},{2,6},{3,7},{4,0},{5,1},{6,2},{7,3},{8,12},{9,13},{10,... | collective-permute-start | bytes 786440 | tf_op jit(solution)/shard_map/ppermute | solution.py:88
  444.5 10.3 %collective-permute-start.71 = (bf16[128,1024]{1,0:T(8,128)(2,1)S(1)}, bf16[128,1024]{1,0:T(8,128)(2,1)S(1)}, u32[]{:S(2)}, u32[]{:S(2)}) collective-permute-start(bf16[128,1024]{1,0:T(8,128)(2,1)S(1)} %pad_maximum_fusion.15), channel_id=1, source_target_pairs={{0,4},{1,5},{2,6},{3,7},{4,0},{5,1},{6,2},{7,3},{8,12},{9,13},{10,... | collective-permute-start | bytes 786440 | tf_op jit(solution)/shard_map/ppermute | solution.py:88
  445.6 11.5 %collective-permute-start.39 = (bf16[2,256,768]{1,2,0:T(8,128)(2,1)S(1)}, bf16[2,256,768]{1,2,0:T(8,128)(2,1)S(1)}, u32[]{:S(2)}, u32[]{:S(2)}) collective-permute-start(bf16[2,256,768]{1,2,0:T(8,128)(2,1)S(1)} %pad_maximum_fusion.6), channel_id=1, source_target_pairs={{0,4},{1,5},{2,6},{3,7},{4,0},{5,1},{6,2},{7,3},{8,12},{9,13},{10,... | collective-permute-start | bytes 2359304 | tf_op jit(solution)/shard_map/ppermute | solution.py:88
  450.0 14.2 %collective-permute-start.26 = (bf16[384,1024]{1,0:T(8,128)(2,1)S(1)}, bf16[384,1024]{1,0:T(8,128)(2,1)S(1)}, u32[]{:S(2)}, u32[]{:S(2)}) collective-permute-start(bf16[384,1024]{1,0:T(8,128)(2,1)S(1)} %get-tuple-element.118), channel_id=1, source_target_pairs={{0,1},{1,0},{6,7},{7,6},{8,9},{9,8},{14,15},{15,14},{16,17},{17,16... | collective-permute-start | bytes 2359304 | tf_op jit(solution)/shard_map/ppermute | solution.py:339
  459.4 21.6 %collective-permute-start.25 = (bf16[384,1024]{1,0:T(8,128)(2,1)S(1)}, bf16[384,1024]{1,0:T(8,128)(2,1)S(1)}, u32[]{:S(2)}, u32[]{:S(2)}) collective-permute-start(bf16[384,1024]{1,0:T(8,128)(2,1)S(1)} %get-tuple-element.117), channel_id=1, source_target_pairs={{0,1},{1,0},{6,7},{7,6},{8,9},{9,8},{14,15},{15,14},{16,17},{17,16... | collective-permute-start | bytes 2359304 | tf_op jit(solution)/shard_map/ppermute | solution.py:339
  464.5 18.9 %collective-permute-start.27 = (bf16[384,1024]{1,0:T(8,128)(2,1)S(1)}, bf16[384,1024]{1,0:T(8,128)(2,1)S(1)}, u32[]{:S(2)}, u32[]{:S(2)}) collective-permute-start(bf16[384,1024]{1,0:T(8,128)(2,1)S(1)} %add_convert_fusion.12), channel_id=1, source_target_pairs={{0,3},{1,2},{6,5},{7,4},{8,11},{9,10},{14,13},{15,12},{16,19},{17,... | collective-permute-start | bytes 2359304 | tf_op jit(solution)/shard_map/ppermute | solution.py:339
  473.3 40.1 %collective-permute-start.49 = (bf16[4,64,4096]{2,1,0:T(8,128)(2,1)}, bf16[4,64,4096]{2,1,0:T(8,128)(2,1)}, u32[]{:S(2)}, u32[]{:S(2)}) collective-permute-start(bf16[4,64,4096]{2,1,0:T(8,128)(2,1)} %constant_dynamic-slice_fusion.18), channel_id=1, source_target_pairs={{0,16},{1,17},{2,18},{3,19},{4,20},{5,21},{6,22},{7,23},{8,24},{9,... | collective-permute-start | bytes 6291464 | tf_op jit(solution)/shard_map/ppermute | solution.py:88
  487.5 42.9 %collective-permute-start.57 = (bf16[4,256,1024]{2,1,0:T(8,128)(2,1)S(1)}, bf16[4,256,1024]{2,1,0:T(8,128)(2,1)S(1)}, u32[]{:S(2)}, u32[]{:S(2)}) collective-permute-start(bf16[4,256,1024]{2,1,0:T(8,128)(2,1)S(1)} %constant_dynamic-slice_fusion.13), channel_id=1, source_target_pairs={{0,8},{1,9},{2,10},{3,11},{4,12},{5,13},{6,14},{7,15},{8,0},{9,1},... | collective-permute-start | bytes 6291464 | tf_op jit(solution)/shard_map/ppermute | solution.py:88
  488.9 27.2 %collective-permute-start.29 = (f32[1,5120]{1,0:T(1,128)S(1)}, f32[1,5120]{1,0:T(1,128)S(1)}, u32[]{:S(2)}, u32[]{:S(2)}) collective-permute-start(f32[1,5120]{1,0:T(1,128)S(1)} %constant_dynamic-slice_fusion.29), channel_id=1, source_target_pairs={{0,3},{1,2},{2,1},{3,0},{4,7},{5,6},{6,5},{7,4},{8,11},{9,10},{10,... | collective-permute-start | bytes 61448 | tf_op jit(solution)/shard_map/ppermute | solution.py:88
  516.0 36.9 %collective-permute-start.50 = (bf16[4,32,4096]{2,1,0:T(8,128)(2,1)S(1)}, bf16[4,32,4096]{2,1,0:T(8,128)(2,1)S(1)}, u32[]{:S(2)}, u32[]{:S(2)}) collective-permute-start(bf16[4,32,4096]{2,1,0:T(8,128)(2,1)S(1)} %constant_dynamic-slice_fusion.17), channel_id=1, source_target_pairs={{0,8},{1,9},{2,10},{3,11},{4,12},{5,13},{6,14},{7,15},{8,0},{9,1},... | collective-permute-start | bytes 3145736 | tf_op jit(solution)/shard_map/ppermute | solution.py:88
  516.1 78.8 %collective-permute-start.30 = (f32[5120]{0:T(1024)S(1)}, f32[5120]{0:T(1024)S(1)}, u32[]{:S(2)}, u32[]{:S(2)}) collective-permute-start(f32[5120]{0:T(1024)S(1)} %bitcast.114), channel_id=1, source_target_pairs={{0,4},{1,5},{2,6},{3,7},{4,0},{5,1},{6,2},{7,3},{8,12},{9,13},{10,... | collective-permute-start | bytes 61448 | tf_op jit(solution)/shard_map/ppermute | solution.py:88
  531.5 23.0 %collective-permute-start.58 = (bf16[4,128,1024]{2,1,0:T(8,128)(2,1)S(1)}, bf16[4,128,1024]{2,1,0:T(8,128)(2,1)S(1)}, u32[]{:S(2)}, u32[]{:S(2)}) collective-permute-start(bf16[4,128,1024]{2,1,0:T(8,128)(2,1)S(1)} %constant_dynamic-slice_fusion.12), channel_id=1, source_target_pairs={{0,16},{1,17},{2,18},{3,19},{4,20},{5,21},{6,22},{7,23},{8,24},{9,... | collective-permute-start | bytes 3145736 | tf_op jit(solution)/shard_map/ppermute | solution.py:88
  555.1 17.7 %collective-permute-start.59 = (bf16[2,128,1024]{2,1,0:T(8,128)(2,1)S(1)}, bf16[2,128,1024]{2,1,0:T(8,128)(2,1)S(1)}, u32[]{:S(2)}, u32[]{:S(2)}) collective-permute-start(bf16[2,128,1024]{2,1,0:T(8,128)(2,1)S(1)} %constant_dynamic-slice_fusion.11), channel_id=1, source_target_pairs={{0,1},{1,0},{2,3},{3,2},{4,5},{5,4},{6,7},{7,6},{8,9},{9,8},{10,11... | collective-permute-start | bytes 1572872 | tf_op jit(solution)/shard_map/ppermute | solution.py:88
  561.6 24.7 %collective-permute-start.52 = (bf16[1,32,4096]{2,1,0:T(8,128)(2,1)S(1)}, bf16[1,32,4096]{2,1,0:T(8,128)(2,1)S(1)}, u32[]{:S(2)}, u32[]{:S(2)}) collective-permute-start(bf16[1,32,4096]{2,1,0:T(8,128)(2,1)S(1)} %constant_dynamic-slice_fusion.15), channel_id=1, source_target_pairs={{0,3},{1,2},{2,1},{3,0},{4,7},{5,6},{6,5},{7,4},{8,11},{9,10},{10,... | collective-permute-start | bytes 786440 | tf_op jit(solution)/shard_map/ppermute | solution.py:88
  573.8 26.3 %collective-permute-start.60 = (bf16[1,128,1024]{2,1,0:T(8,128)(2,1)}, bf16[1,128,1024]{2,1,0:T(8,128)(2,1)}, u32[]{:S(2)}, u32[]{:S(2)}) collective-permute-start(bf16[1,128,1024]{2,1,0:T(8,128)(2,1)} %constant_dynamic-slice_fusion.10), channel_id=1, source_target_pairs={{0,3},{1,2},{2,1},{3,0},{4,7},{5,6},{6,5},{7,4},{8,11},{9,10},{10,... | collective-permute-start | bytes 786440 | tf_op jit(solution)/shard_map/ppermute | solution.py:88
  586.4 16.5 %collective-permute-start.53 = (bf16[32,4096]{1,0:T(8,128)(2,1)S(1)}, bf16[32,4096]{1,0:T(8,128)(2,1)}, u32[]{:S(2)}, u32[]{:S(2)}) collective-permute-start(bf16[32,4096]{1,0:T(8,128)(2,1)S(1)} %fusion.64), channel_id=1, source_target_pairs={{0,8},{1,9},{2,10},{3,11},{4,12},{5,13},{6,14},{7,15},{8,0},{9,1},... | collective-permute-start | bytes 786440 | tf_op jit(solution)/shard_map/ppermute | solution.py:88
  603.9 14.6 %collective-permute-start.54 = (bf16[64,4096]{1,0:T(8,128)(2,1)S(1)}, bf16[64,4096]{1,0:T(8,128)(2,1)S(1)}, u32[]{:S(2)}, u32[]{:S(2)}) collective-permute-start(bf16[64,4096]{1,0:T(8,128)(2,1)S(1)} %pad_maximum_fusion.9), channel_id=1, source_target_pairs={{0,16},{1,17},{2,18},{3,19},{4,20},{5,21},{6,22},{7,23},{8,24},{9,... | collective-permute-start | bytes 1572872 | tf_op jit(solution)/shard_map/ppermute | solution.py:88
  604.1 19.7 %collective-permute-start.32 = (f32[5120]{0:T(1024)S(1)}, f32[5120]{0:T(1024)S(1)}, u32[]{:S(2)}, u32[]{:S(2)}) collective-permute-start(f32[5120]{0:T(1024)S(1)} %add.637), channel_id=1, source_target_pairs={{0,16},{1,17},{2,18},{3,19},{4,20},{5,21},{6,22},{7,23},{8,24},{9,... | collective-permute-start | bytes 61448 | tf_op jit(solution)/shard_map/ppermute | solution.py:88
  607.3 18.7 %collective-permute-start.62 = (bf16[256,1024]{1,0:T(8,128)(2,1)S(1)}, bf16[256,1024]{1,0:T(8,128)(2,1)S(1)}, u32[]{:S(2)}, u32[]{:S(2)}) collective-permute-start(bf16[256,1024]{1,0:T(8,128)(2,1)S(1)} %pad_maximum_fusion.10), channel_id=1, source_target_pairs={{0,8},{1,9},{2,10},{3,11},{4,12},{5,13},{6,14},{7,15},{8,0},{9,1},... | collective-permute-start | bytes 1572872 | tf_op jit(solution)/shard_map/ppermute | solution.py:88
  (88 other events, 769.1 us)

commit v3 on v2

v3 whole, which is shorter than its diff:
```python
import math
from functools import partial

import jax
import jax.numpy as jnp
from jax import lax
from jax.experimental import pallas as pl
from jax.experimental.pallas import tpu as pltpu
from jax.sharding import PartitionSpec as P

D = 1024
H = 16
HD = 64
LAT = 512
K = 16
WARM = 2000


ln_eps = 1e-05
free_floor = 1.3
neg_fill = -1e30

QUERY_TILE = 512
KEY_TILE = 512
KEY_UNIT = 128
FEED_TILE = 512


def layer_norm(values, gain, shift):
    center = values - jnp.mean(values, axis=-1, keepdims=True)
    spread = jnp.mean(center * center, axis=-1, keepdims=True)
    return center * lax.rsqrt(spread + ln_eps) * gain + shift


def slide_index(position, lengths_row):
    ends = jnp.cumsum(lengths_row)
    return jnp.sum((position[:, None] >= ends[None, :]).astype(jnp.int32), axis=1)


def exact_dot(left, right):
    return jnp.dot(left, right, precision=lax.Precision.HIGHEST, preferred_element_type=jnp.float32)


def kl_terms(latent_mean, latent_logvar, prior_means, prior_logits):
    log_prior = jax.nn.log_softmax(prior_logits)
    logits = exact_dot(latent_mean, prior_means.T) * LAT ** (-0.5) + log_prior[None, :]
    resp = jax.nn.softmax(logits, axis=-1)
    log_resp = jax.nn.log_softmax(logits, axis=-1)
    mixed_mean = exact_dot(resp, prior_means)
    mixed_square = exact_dot(resp, prior_means * prior_means)
    kl_dim = 0.5 * (
        jnp.exp(latent_logvar)
        + latent_mean * latent_mean
        - 2.0 * latent_mean * mixed_mean
        + mixed_square
        - 1.0
        - latent_logvar
    )
    categorical = jnp.sum(resp * (log_resp - log_prior[None, :]), axis=-1)
    return (kl_dim, categorical)


def plain_dot(left, right):
    return jnp.dot(left, right, preferred_element_type=jnp.float32)


def rows_dot(left, right):
    return lax.dot_general(
        left, right, (((0,), (0,)), ((), ())), preferred_element_type=jnp.float32
    )


def cols_dot(left, right):
    return lax.dot_general(
        left, right, (((1,), (1,)), ((), ())), preferred_element_type=jnp.float32
    )


MESH_AXES = ("dp", "blk")


def swapped(value, dp_mask, blk_mask):
    groups, blocks = lax.axis_size("dp"), lax.axis_size("blk")
    pairs = [
        (g * blocks + b, (g ^ dp_mask) * blocks + (b ^ blk_mask))
        for g in range(groups)
        for b in range(blocks)
    ]
    return lax.ppermute(value, MESH_AXES, pairs)


def bits_of(count):
    return count.bit_length() - 1


def dp_masks():
    return [1 << t for t in range(bits_of(lax.axis_size("dp")))]


def blk_masks():
    return [(2 << t) - 1 for t in range(bits_of(lax.axis_size("blk")))]


def summed_everywhere(value):
    for mask in dp_masks():
        value = value + swapped(value, mask, 0)
    for mask in blk_masks():
        value = value + swapped(value, 0, mask)
    return value


def added(left, right):
    return (left.astype(jnp.float32) + right.astype(jnp.float32)).astype(jnp.bfloat16)


def summed(terms):
    total = terms[0].astype(jnp.float32)
    for term in terms[1:]:
        total = total + term.astype(jnp.float32)
    return total.astype(jnp.bfloat16)


def chunk(value, start, size, axis):
    return lax.dynamic_slice_in_dim(value, start, size, axis)


def tied(value, other):
    return lax.optimization_barrier((value, other))[0]


class Exchange:
    def __init__(self, steps):
        self.steps = steps
        self.result = None
        self.last = None
        self.flight = None
        self._take(lambda: next(self.steps))

    def _take(self, step):
        try:
            values, permute = step()
            self.last = values
            self.flight = [permute(value) for value in values]
        except StopIteration as end:
            self.result = end.value
            self.last = end.value
            self.flight = None

    def advance(self, token):
        came = tied(self.flight, token)
        self._take(lambda: self.steps.send(came))
        return self.last


def by_mask(dp_mask, blk_mask):
    return lambda value: swapped(value, dp_mask, blk_mask)


def dp_order(flipped):
    masks = dp_masks()
    return masks[:1] + masks[1:][::-1] if flipped else masks


def relative_masks(steps):
    places = [0]
    for step in steps[::-1]:
        places = places + [place ^ step for place in places]
    return places


def relative_table(steps, mine):
    masks = relative_masks(steps)
    inverse = [masks.index(place) for place in range(len(masks))]
    order = jnp.arange(len(masks), dtype=jnp.int32)
    wanted = order ^ mine
    return sum(jnp.where(wanted == place, inverse[place], 0) for place in range(len(masks)))


def spread_kernel(parts, table_ref, mine_ref, other_ref, *out_refs):
    held, _, width = mine_ref.shape
    cols = 2 * held * width
    for place in range(2 * held):
        index = table_ref[place]
        piece = jnp.where(index < held, mine_ref[index & (held - 1)], other_ref[index & (held - 1)])
        piece = piece.astype(jnp.float32)
        for out_ref, (begin, count, times) in zip(out_refs, parts):
            for time in range(times):
                row, column = begin + time * count, time * cols + place * width
                out_ref[:, column : column + width] = piece[row : row + count]


def spread_columns(mine, other, table, parts):
    held, rows, width = mine.shape
    cols = 2 * held * width
    begin, placed, shapes = 0, [], []
    for count, times in parts:
        placed.append((begin, count, times))
        shapes.append(jax.ShapeDtypeStruct((count, times * cols), jnp.float32))
        begin += count * times
    return pl.pallas_call(
        partial(spread_kernel, placed),
        out_shape=shapes,
        grid_spec=pltpu.PrefetchScalarGridSpec(
            num_scalar_prefetch=1,
            grid=(1,),
            in_specs=[resident((held, rows, width))] * 2,
            out_specs=[resident(shape.shape) for shape in shapes],
        ),
        cost_estimate=nothing(),
        name="spread_columns",
    )(table, mine, other)


def head_steps(value):
    blocks = lax.axis_size("blk")
    group, block = lax.axis_index("dp"), lax.axis_index("blk")
    half = blocks // 2
    steps = dp_masks()[1:]
    masks = relative_masks([step >> 1 for step in steps])
    taken = [[chunk(value, (group >> 1) ^ mask, 1, 1)] for mask in masks]
    size = len(masks)
    for step in steps:
        size = size // 2
        send = jnp.concatenate([summed(taken[place]) for place in range(size, 2 * size)], axis=1)
        (came,) = yield [send], by_mask(step, 0)
        taken = [taken[place] + [came[:, place : place + 1]] for place in range(size)]
    side = block >> (bits_of(blocks) - 1)
    away = [chunk(term, (1 - side) * half, half, 0) for term in taken[0]]
    (came,) = yield [summed(away)], by_mask(0, half)
    terms = [chunk(term, side * half, half, 0) for term in taken[0]] + [came]
    place = block & (half - 1)
    pieces = [summed([chunk(term, place, 1, 0) for term in terms])]
    for k in range(1, half):
        send = summed([chunk(term, place ^ k, 1, 0) for term in terms])
        (came,) = yield [send], by_mask(0, k)
        pieces.append(came)
    value = jnp.concatenate(pieces, axis=1)
    for step in steps[::-1]:
        (came,) = yield [value], by_mask(step, 0)
        value = jnp.concatenate([value, came], axis=0)
    (other,) = yield [value], by_mask(1, 0)
    return value, other


def heads_kernel(table_ref, mine_ref, other_ref, *out_refs):
    pieces = pl.num_programs(0)
    place, core = table_ref[pieces], table_ref[pieces + 1]
    half = mine_ref.shape[1]
    rows = out_refs[0].shape[0]
    width = mine_ref.shape[3] // 3
    for chip in range(half):
        mine = mine_ref[0, chip ^ place].astype(jnp.float32)
        other = other_ref[0, chip ^ place].astype(jnp.float32)
        for c in range(2):
            value = jnp.where(core == c, mine, other)
            column = (2 * chip + c) * width
            for kind in range(3):
                out_refs[kind][:, column : column + width] = value[:rows, kind * width : (kind + 1) * width]


def spread_heads(mine, other, rows):
    blocks = lax.axis_size("blk")
    group, block = lax.axis_index("dp"), lax.axis_index("blk")
    pieces, half, held_rows, width = mine.shape
    table = relative_table([step >> 1 for step in dp_masks()[1:]], group >> 1)
    table = jnp.concatenate([table, jnp.stack([block & (half - 1), group & 1])])
    held = pl.BlockSpec((1, half, held_rows, width), lambda i, table: (table[i], 0, 0, 0))
    cols = 2 * half * width // 3
    return pl.pallas_call(
        heads_kernel,
        out_shape=(jax.ShapeDtypeStruct((pieces * rows, cols), jnp.float32),) * 3,
        grid_spec=pltpu.PrefetchScalarGridSpec(
            num_scalar_prefetch=1,
            grid=(pieces,),
            in_specs=[held, held],
            out_specs=[pl.BlockSpec((rows, cols), lambda i, table: (i, 0))] * 3,
        ),
        cost_estimate=nothing(),
        name="spread_heads",
    )(table, mine, other)


def head_lanes(value, head):
    lane = lax.broadcasted_iota(jnp.int32, value.shape, 1) // HD
    return jnp.where(lane == head, value, jnp.zeros_like(value))

def nt_dot(left, right):
    return lax.dot_general(left, right, (((1,),(1,)),((),())), preferred_element_type=jnp.float32)

def nn_dot(left, right):
    return lax.dot_general(left, right, (((1,),(0,)),((),())), preferred_element_type=jnp.float32)

def allowed_pairs(code_k, code_q, block_k, tile):
    key_pos = block_k + lax.broadcasted_iota(jnp.int32, tile, 0)
    query_pos = pl.program_id(0) * QUERY_TILE + lax.broadcasted_iota(jnp.int32, tile, 1)
    return (code_k == code_q) | (key_pos == query_pos)

def forward_kernel(range_ref, q_ref, k_ref, v_ref, cq_ref, ck_ref, ctx_ref, lse_ref, m_ref, l_ref, acc_ref, vt_ref):
    nh = q_ref.shape[1] // HD
    step = pl.program_id(0)

    @pl.when(step == 0)
    def _():
        vt_ref[...] = v_ref[...].T

    m_ref[...] = jnp.full(m_ref.shape, neg_fill, jnp.float32)
    l_ref[...] = jnp.zeros(l_ref.shape, jnp.float32)
    acc_ref[...] = jnp.zeros(acc_ref.shape, jnp.float32)
    code_q = cq_ref[...]
    scaled = (q_ref[...].astype(jnp.float32) * HD ** (-0.5)).astype(jnp.bfloat16)
    def body(kb, _):
        start = pl.multiple_of(range_ref[step, 0] * KEY_UNIT + kb * KEY_TILE, KEY_UNIT)
        keys = k_ref[pl.ds(start, KEY_TILE), :]
        open_pair = allowed_pairs(ck_ref[pl.ds(start, KEY_TILE), :], code_q, start, (KEY_TILE, QUERY_TILE))
        for h in range(nh):
            s = nt_dot(keys, head_lanes(scaled, h))
            s = jnp.where(open_pair, s, neg_fill)
            m_old = m_ref[h:h+1, :]
            m_new = jnp.maximum(m_old, jnp.max(s, axis=0, keepdims=True))
            p = jnp.exp(s - m_new)
            alpha = jnp.exp(m_old - m_new)
            l_ref[h:h+1, :] = l_ref[h:h+1, :] * alpha + jnp.sum(p, axis=0, keepdims=True)
            m_ref[h:h+1, :] = m_new
            rows = slice(h*HD, (h+1)*HD)
            acc_ref[rows, :] = acc_ref[rows, :] * alpha + nn_dot(vt_ref[rows, pl.ds(start, KEY_TILE)], p.astype(jnp.bfloat16))
        return 0
    lax.fori_loop(0, range_ref[step, 1], body, 0)
    for h in range(nh):
        rows = slice(h*HD, (h+1)*HD)
        acc_ref[rows, :] = acc_ref[rows, :] / l_ref[h:h+1, :]
    ctx_ref[...] = acc_ref[...].T.astype(jnp.bfloat16)
    lse_ref[...] = m_ref[...] + jnp.log(l_ref[...])

def attention_forward(ranges, q, k, v, code_q, code_k):
    N, W = q.shape
    nh = W // HD
    full = lambda shape: pl.BlockSpec(shape, lambda i, r: (0,)*len(shape))
    return pl.pallas_call(
        forward_kernel,
        out_shape=(jax.ShapeDtypeStruct((N, W), jnp.bfloat16), jax.ShapeDtypeStruct((nh, N), jnp.float32)),
        grid_spec=pltpu.PrefetchScalarGridSpec(
            num_scalar_prefetch=1, grid=(N//QUERY_TILE,),
            in_specs=[pl.BlockSpec((QUERY_TILE, W), lambda i, r: (i, 0)), full((N, W)), full((N, W)),
                      pl.BlockSpec((1, QUERY_TILE), lambda i, r: (0, i)), full((N, 1))],
            out_specs=[pl.BlockSpec((QUERY_TILE, W), lambda i, r: (i, 0)), pl.BlockSpec((nh, QUERY_TILE), lambda i, r: (0, i))],
            scratch_shapes=[pltpu.VMEM((nh, QUERY_TILE), jnp.float32), pltpu.VMEM((nh, QUERY_TILE), jnp.float32), pltpu.VMEM((W, QUERY_TILE), jnp.float32), pltpu.VMEM((W, N), jnp.bfloat16)]),
        cost_estimate=nothing(),
        name="attention_forward",
    )(ranges, q, k, v, code_q, code_k)

def backward_kernel(range_ref, row_ref, q_ref, ctx_ref, lse_ref, k_ref, v_ref, cq_ref, ck_ref,
                    *refs):
    pieces = row_ref.shape[0]
    do_refs, (dq_ref, dk_ref, dv_ref, dqt_ref, dk_acc, dv_acc, kt_ref, do_ref) = refs[:pieces], refs[pieces:]
    nh = q_ref.shape[1] // HD
    step = pl.program_id(0)
    @pl.when(step == 0)
    def _():
        dk_acc[...] = jnp.zeros(dk_acc.shape, jnp.float32)
        dv_acc[...] = jnp.zeros(dv_acc.shape, jnp.float32)
        kt_ref[...] = k_ref[...].T
        for k, piece_ref in enumerate(do_refs):
            rows = piece_ref.shape[0]
            do_ref[pl.ds(pl.multiple_of(row_ref[k] * rows, rows), rows), :] = piece_ref[...]

    dqt_ref[...] = jnp.zeros(dqt_ref.shape, jnp.float32)
    code_q = cq_ref[...]
    scaled = (q_ref[...].astype(jnp.float32) * HD ** (-0.5)).astype(jnp.bfloat16)
    grads = do_ref[pl.ds(pl.multiple_of(step * QUERY_TILE, QUERY_TILE), QUERY_TILE), :]
    product = (grads.astype(jnp.float32) * ctx_ref[...].astype(jnp.float32)).T
    deltas = [jnp.sum(product[h*HD:(h+1)*HD, :], axis=0, keepdims=True) for h in range(nh)]
    q_all = jnp.concatenate([head_lanes(scaled, h) for h in range(nh)], axis=0)
    do_all = jnp.concatenate([head_lanes(grads, h) for h in range(nh)], axis=0)
    def body(kb, _):
        start = pl.multiple_of(range_ref[step, 0] * KEY_UNIT + kb * KEY_TILE, KEY_UNIT)
        keys = k_ref[pl.ds(start, KEY_TILE), :]
        values = v_ref[pl.ds(start, KEY_TILE), :]
        open_pair = allowed_pairs(ck_ref[pl.ds(start, KEY_TILE), :], code_q, start, (KEY_TILE, QUERY_TILE))
        ps, dss = [], []
        for h in range(nh):
            cols = slice(h*QUERY_TILE, (h+1)*QUERY_TILE)
            rows = slice(h*HD, (h+1)*HD)
            s = nt_dot(keys, q_all[cols, :])
            p = jnp.where(open_pair, jnp.exp(s - lse_ref[h:h+1, :]), 0.0)
            dp = nt_dot(values, do_all[cols, :])
            ds = (p * (dp - deltas[h])).astype(jnp.bfloat16)
            ps.append(p.astype(jnp.bfloat16))
            dss.append(ds)
            dqt_ref[rows, :] += nn_dot(kt_ref[rows, pl.ds(start, KEY_TILE)], ds)
        dv_acc[pl.ds(start, KEY_TILE), :] += nn_dot(jnp.concatenate(ps, axis=1), do_all)
        dk_acc[pl.ds(start, KEY_TILE), :] += nn_dot(jnp.concatenate(dss, axis=1), q_all)
        return 0
    lax.fori_loop(0, range_ref[step, 1], body, 0)
    dq_ref[...] = (dqt_ref[...] * HD ** (-0.5)).T.astype(jnp.bfloat16)
    @pl.when(step == pl.num_programs(0) - 1)
    def _():
        dk_ref[...] = dk_acc[...].astype(jnp.bfloat16)
        dv_ref[...] = dv_acc[...].astype(jnp.bfloat16)

def attention_backward(ranges, places, q, pieces, ctx, lse, k, v, code_q, code_k):
    cells, width = q.shape
    heads = width // HD

    def row():
        return pl.BlockSpec((QUERY_TILE, width), lambda i, *_: (i, 0))

    out = jax.ShapeDtypeStruct((cells, width), jnp.bfloat16)
    return pl.pallas_call(
        backward_kernel,
        out_shape=(out, out, out),
        grid_spec=pltpu.PrefetchScalarGridSpec(
            num_scalar_prefetch=2,
            grid=(cells // QUERY_TILE,),
            in_specs=[
                row(),
                row(),
                pl.BlockSpec((heads, QUERY_TILE), lambda i, *_: (0, i)),
                resident((cells, width)),
                resident((cells, width)),
                pl.BlockSpec((1, QUERY_TILE), lambda i, *_: (0, i)),
                resident((cells, 1)),
            ]
            + [resident(piece.shape) for piece in pieces],
            out_specs=[row(), resident((cells, width)), resident((cells, width))],
            scratch_shapes=[
                pltpu.VMEM((width, QUERY_TILE), jnp.float32),
                pltpu.VMEM((cells, width), jnp.float32),
                pltpu.VMEM((cells, width), jnp.float32),
                pltpu.VMEM((width, cells), jnp.bfloat16),
                pltpu.VMEM((cells, width), jnp.bfloat16),
            ],
        ),
        cost_estimate=nothing(),
        name="attention_backward",
    )(ranges, places, q, ctx, lse, k, v, code_q, code_k, *pieces)


def slide_tables(lengths_row, mask_all):
    cells = mask_all.shape[0]
    ends = jnp.cumsum(lengths_row)
    starts = ends - lengths_row
    slide = slide_index(jnp.arange(cells, dtype=jnp.int32), lengths_row)
    first = jnp.arange(cells // QUERY_TILE, dtype=jnp.int32) * QUERY_TILE
    first_slide = slide_index(first, lengths_row)
    last_slide = slide_index(first + (QUERY_TILE - 1), lengths_row)
    order = jnp.arange(lengths_row.shape[0], dtype=jnp.int32)

    def picked(table, index):
        return jnp.sum(jnp.where(index[:, None] == order[None, :], table[None, :], 0), axis=1)

    low = picked(starts, first_slide) // KEY_UNIT
    high = picked(ends, last_slide)
    tiles = (high - low * KEY_UNIT + KEY_TILE - 1) // KEY_TILE
    low = jnp.minimum(low, (cells - tiles * KEY_TILE) // KEY_UNIT)
    ranges = jnp.stack([low, tiles], axis=1).astype(jnp.int32)
    open_code = jnp.where(mask_all == 1, slide, -1)
    return ranges, slide[None, :], open_code[:, None]


def moved(value, target):
    groups, blocks = lax.axis_size("dp"), lax.axis_size("blk")
    pairs = []
    for g in range(groups):
        for b in range(blocks):
            there = target(g, b)
            if there is not None:
                pairs.append((g * blocks + b, there[0] * blocks + there[1]))
    return lax.ppermute(value, MESH_AXES, pairs)


def at_home(g, b):
    return (g & 1) == b >> (bits_of(lax.axis_size("blk")) - 1)


def head_block(g, b):
    return (b & (lax.axis_size("blk") // 2 - 1)) * 2 + (g & 1)


def worker_of(g, block_of_heads):
    half = lax.axis_size("blk") // 2
    return (g - g % 2) + block_of_heads % 2, (g % 2) * half + block_of_heads // 2


def owner_of(g, b, index):
    return (g - g % 2) + b // (lax.axis_size("blk") // 2), index


def pair_masks():
    return [1 << t for t in range(bits_of(lax.axis_size("blk")) - 1)]


def with_meta(cells, mask, lengths):
    count = lengths.shape[0]
    meta = jnp.concatenate([mask, lengths >> 7, lengths & 127]).astype(cells.dtype)
    meta = jnp.pad(meta, (0, cells.shape[1] - mask.shape[0] - 2 * count))
    return jnp.concatenate([cells, jnp.pad(meta[None], ((0, 7), (0, 0)))], axis=0)


def from_meta(meta, rows, count):
    meta = meta.astype(jnp.int32)
    high = meta[0, rows : rows + count]
    return meta[:, :rows].reshape(-1), high * 128 + meta[0, rows + count : rows + 2 * count]


def from_home(value):
    return moved(value, lambda g, b: (g ^ 1, b) if at_home(g, b) else None)


def paired(value, mask):
    return moved(value, lambda g, b: (g, b ^ mask) if at_home(g, b) else None)


def group_rows(own, use):
    blocks = lax.axis_size("blk")
    block = lax.axis_index("blk")
    mirror = moved(own, lambda g, b: None if at_home(g, b) else (g, blocks - 1 - b))
    held, rows = None, []
    for mirrored in (False, True):
        pieces = [(mirror if mirrored else own, 0)]
        for mask in pair_masks():
            pieces += [(paired(piece, mask), place ^ mask) for piece, place in pieces]
        pieces = [
            (piece, from_home(tied(piece, held) if mirrored else piece), blocks - 1 - (block ^ place) if mirrored else block ^ place)
            for piece, place in pieces
        ]
        held = use(pieces, held)
        rows += pieces
    return held, rows


def entry_kernel(count, place_ref, *refs):
    pieces, refs = refs[: 2 * count], refs[2 * count :]
    gain_ref, shift_ref = refs[:2]
    weights = refs[2:5]
    normed_ref, *out_refs = refs[-4:]
    step, home = pl.program_id(0), place_ref[count]
    rows = normed_ref.shape[0]
    for k in range(count):

        @pl.when(step == k)
        def _(k=k):
            value = jnp.where(home == 1, pieces[2 * k][:rows], pieces[2 * k + 1][:rows])
            unit, _ = norm_parts(value.astype(jnp.float32))
            normed_ref[...] = (unit * gain_ref[...] + shift_ref[...]).astype(jnp.bfloat16)

    for weight_ref, out_ref in zip(weights, out_refs):
        out_ref[...] = nn_dot(normed_ref[...], weight_ref[...]).astype(jnp.bfloat16)


def head_columns(weight):
    width = weight.shape[1] // lax.axis_size("blk")
    if width % 128 == 0:
        return weight, pl.BlockSpec((weight.shape[0], width), lambda i, place: (0, place[place.shape[0] - 1]))
    mine = head_block(lax.axis_index("dp"), lax.axis_index("blk")) * width
    return lax.dynamic_slice_in_dim(weight, mine, width, 1), resident((weight.shape[0], width))


def entry(pieces, gain, shift, weights, held):
    blocks, count = lax.axis_size("blk"), len(pieces)
    group, block = lax.axis_index("dp"), lax.axis_index("blk")
    rows, model = pieces[0][0].shape[0] - 8, pieces[0][0].shape[1]
    width = model // blocks
    home = at_home(group, block).astype(jnp.int32)
    table = jnp.stack([place for _, _, place in pieces] + [home, head_block(group, block)])
    narrow = pl.BlockSpec((rows, width), lambda i, place: (place[i], 0))
    shapes = [jax.ShapeDtypeStruct((blocks * rows, cols), jnp.bfloat16) for cols in (model,) + (width,) * 3]
    operands = [value for mine, other, _ in pieces for value in (mine, other)]
    specs = [resident(value.shape) for value in operands] + [resident((1, model))] * 2
    operands += [gain[None], shift[None]]
    for weight in weights:
        weight, spec = head_columns(weight)
        operands.append(weight)
        specs.append(spec)
    aliases = {}
    if held is not None:
        aliases = {1 + len(operands) + i: i for i in range(4)}
        operands += list(held)
        specs += [pl.BlockSpec(memory_space=pl.ANY)] * 4
    return pl.pallas_call(
        partial(entry_kernel, count),
        grid_spec=pltpu.PrefetchScalarGridSpec(
            num_scalar_prefetch=1,
            grid=(count,),
            in_specs=specs,
            out_specs=[pl.BlockSpec((rows, model), lambda i, place: (place[i], 0)), narrow, narrow, narrow],
        ),
        out_shape=shapes,
        input_output_aliases=aliases,
        cost_estimate=nothing(),
        name="entry",
    )(table, *operands)


def project_back_kernel(place_ref, normed_ref, dq_ref, dk_ref, dv_ref, wq_ref, wk_ref, wv_ref,
                        rows_ref, grad_ref, gain_ref, shift_ref, acc_ref, sum_ref):
    step = pl.program_id(0)
    width = dq_ref.shape[1]

    @pl.when(step == 0)
    def _():
        acc_ref[...] = jnp.zeros(acc_ref.shape, jnp.float32)
        sum_ref[...] = jnp.zeros(sum_ref.shape, jnp.float32)

    total = jnp.zeros(rows_ref.shape, jnp.float32)
    for kind, (grad, weight_ref) in enumerate(((dq_ref, wq_ref), (dk_ref, wk_ref), (dv_ref, wv_ref))):
        cols = slice(kind * width, (kind + 1) * width)
        total += nt_dot(grad[...], weight_ref[...])
        acc_ref[:, cols] += tn_dot(normed_ref[...], grad[...])
        sum_ref[:1, cols] += jnp.sum(grad[...].astype(jnp.float32), axis=0, keepdims=True)
    rows_ref[...] = total.astype(jnp.bfloat16)

    @pl.when(step == pl.num_programs(0) - 1)
    def _():
        grad_ref[...] = acc_ref[...].astype(jnp.bfloat16)
        ones = jnp.ones((8, width), jnp.float32)
        gain = jnp.zeros(gain_ref.shape, jnp.float32)
        shift = jnp.zeros(shift_ref.shape, jnp.float32)
        for kind, weight_ref in enumerate((wq_ref, wk_ref, wv_ref)):
            cols = slice(kind * width, (kind + 1) * width)
            weight = weight_ref[...].astype(jnp.float32)
            gain += exact_nt_dot(ones, weight * acc_ref[:, cols])
            shift += exact_nt_dot(sum_ref[:, cols], weight)
        gain_ref[...] = gain
        shift_ref[...] = shift


def exact_nt_dot(left, right):
    return lax.dot_general(
        left,
        right,
        (((1,), (1,)), ((), ())),
        precision=lax.Precision.HIGHEST,
        preferred_element_type=jnp.float32,
    )


def project_back(normed, grads, weights):
    cells, width = grads[0].shape
    model = weights[0].shape[0]
    columns = [head_columns(weight) for weight in weights]
    table = head_block(lax.axis_index("dp"), lax.axis_index("blk"))[None]
    wide = pl.BlockSpec((QUERY_TILE, model), lambda i, place: (i, 0))
    return pl.pallas_call(
        project_back_kernel,
        grid_spec=pltpu.PrefetchScalarGridSpec(
            num_scalar_prefetch=1,
            grid=(cells // QUERY_TILE,),
            in_specs=[wide]
            + [pl.BlockSpec((QUERY_TILE, width), lambda i, place: (i, 0))] * 3
            + [spec for _, spec in columns],
            out_specs=[wide, resident((model, 3 * width)), resident((8, model)), resident((8, model))],
            scratch_shapes=[pltpu.VMEM((model, 3 * width), jnp.float32), pltpu.VMEM((8, 3 * width), jnp.float32)],
        ),
        out_shape=[
            jax.ShapeDtypeStruct((cells, model), jnp.bfloat16),
            jax.ShapeDtypeStruct((model, 3 * width), jnp.bfloat16),
            jax.ShapeDtypeStruct((8, model), jnp.float32),
            jax.ShapeDtypeStruct((8, model), jnp.float32),
        ],
        cost_estimate=nothing(),
        name="project_back",
    )(table, normed, *grads, *[weight for weight, _ in columns])


def heads_at_owner():
    blocks, block = lax.axis_size("blk"), lax.axis_index("blk")
    return jnp.stack([(block - k) & (blocks - 1) for k in range(blocks)])


def rows_at_worker():
    blocks = lax.axis_size("blk")
    mine = head_block(lax.axis_index("dp"), lax.axis_index("blk"))
    return jnp.stack([(mine + k) & (blocks - 1) for k in range(blocks)])


def rows_to_owners(context):
    blocks = lax.axis_size("blk")
    places = rows_at_worker()
    rows = context.shape[0] // blocks
    return [
        moved(
            chunk(context, places[k] * rows, rows, 0),
            lambda g, b: owner_of(g, b, (head_block(g, b) + k) % blocks),
        )
        for k in range(blocks)
    ]


def heads_to_workers(pieces):
    blocks = lax.axis_size("blk")
    return [
        moved(piece, lambda g, b: worker_of(g, (b - k) % blocks)) for k, piece in enumerate(pieces)
    ]


def row_steps(partial_rows):
    blocks = lax.axis_size("blk")
    group, block = lax.axis_index("dp"), lax.axis_index("blk")
    rows = partial_rows.shape[0] // blocks
    home = at_home(group, block)
    (other,) = yield [partial_rows], lambda value: moved(
        value, lambda g, b: None if at_home(g, b) else (g ^ 1, b)
    )

    def taken(place):
        return [chunk(part, place * rows, rows, 0)[None] for part in (partial_rows, other)]

    mine = {r: (taken(block ^ r), taken(blocks - 1 - (block ^ r))) for r in range(blocks // 2)}
    for mask in reversed(pair_masks()):
        send = jnp.concatenate([summed(part) for r in range(mask) for part in mine[r + mask]], axis=0)
        (came,) = yield [send], lambda value, mask=mask: moved(
            value, lambda g, b: (g, b ^ mask) if at_home(g, b) else None
        )
        mine = {
            r: tuple(mine[r][k] + [came[2 * r + k : 2 * r + k + 1]] for k in range(2))
            for r in range(mask)
        }
    own, mirror = mine[0]
    (far,) = yield [summed(mirror)], lambda value: moved(
        value, lambda g, b: (g, blocks - 1 - b) if at_home(g, b) else None
    )
    return jnp.where(home, summed(own), far)[0]


def norm_parts(values):
    center = values - jnp.mean(values, axis=-1, keepdims=True)
    spread = jnp.mean(center * center, axis=-1, keepdims=True)
    scale = lax.rsqrt(spread + ln_eps)
    return center * scale, scale


def nothing():
    return pl.CostEstimate(flops=0, bytes_accessed=0, transcendentals=0)


def resident(shape):
    return pl.BlockSpec(shape, lambda *_: (0,) * len(shape))


def feed_kernel(head_ref, *refs):
    pieces = head_ref.shape[0]
    context_refs, (cell_ref, weight_ref), refs = refs[:pieces], refs[pieces : pieces + 2], refs[pieces + 2 :]
    context_ref, hidden_ref, refs = refs[6], refs[7], refs[:6] + refs[8:]

    @pl.when(pl.program_id(0) == 0)
    def _():
        width = weight_ref.shape[0] // pieces
        total = cell_ref[...].astype(jnp.float32)
        for k in range(pieces):
            begin = head_ref[k] * width
            piece = context_refs[k][...]
            total += nn_dot(piece, weight_ref[pl.ds(pl.multiple_of(begin, width), width), :])
            if width % 128 == 0:
                context_ref[:, pl.ds(pl.multiple_of(begin, width), width)] = piece
        hidden_ref[...] = total

    feed_body(hidden_ref, *refs)


def feed_body(hidden_ref, gain_ref, shift_ref, up_ref, up_bias_ref, down_ref, down_bias_ref,
                normed_ref, active_ref, slope_ref, two_ref, two_b_ref, acc_ref):
    step = pl.program_id(0)

    @pl.when(step == 0)
    def _():
        unit, _ = norm_parts(hidden_ref[...])
        normed_ref[...] = (unit * gain_ref[...] + shift_ref[...]).astype(jnp.bfloat16)
        acc_ref[...] = hidden_ref[...] + down_bias_ref[...]

    inner = nn_dot(normed_ref[...], up_ref[...]) + up_bias_ref[...]
    chance = 0.5 + 0.5 * lax.erf(inner * 2.0**-0.5)
    active = (inner * chance).astype(jnp.bfloat16)
    active_ref[...] = active
    slope = chance + inner * jnp.exp(-0.5 * inner * inner) * (2.0 * math.pi) ** -0.5
    slope_ref[...] = slope.astype(jnp.bfloat16)
    acc_ref[...] += nn_dot(active, down_ref[...])

    @pl.when(step == pl.num_programs(0) - 1)
    def _():
        two_ref[...] = acc_ref[...]
        two_b_ref[...] = acc_ref[...].astype(jnp.bfloat16)


def feed_forward(heads, contexts, cells, out_weight, gain, shift, up_weight, up_bias, down_weight, down_bias):
    rows, model = cells.shape
    inner = up_weight.shape[1]
    tile = FEED_TILE
    across = pl.BlockSpec((rows, tile), lambda j, heads: (0, j))
    return pl.pallas_call(
        feed_kernel,
        grid_spec=pltpu.PrefetchScalarGridSpec(
            num_scalar_prefetch=1,
            grid=(inner // tile,),
            in_specs=[resident(part.shape) for part in contexts]
            + [
                resident((rows, model)),
                resident((model, model)),
                resident((1, model)),
                resident((1, model)),
                pl.BlockSpec((model, tile), lambda j, heads: (0, j)),
                pl.BlockSpec((1, tile), lambda j, heads: (0, j)),
                pl.BlockSpec((tile, model), lambda j, heads: (j, 0)),
                resident((1, model)),
            ],
            out_specs=[
                resident((rows, model)),
                resident((rows, model)),
                resident((rows, model)),
                across,
                across,
                resident((rows, model)),
                resident((rows, model)),
            ],
            scratch_shapes=[pltpu.VMEM((rows, model), jnp.float32)],
        ),
        out_shape=[
            jax.ShapeDtypeStruct((rows, model), jnp.bfloat16),
            jax.ShapeDtypeStruct((rows, model), jnp.float32),
            jax.ShapeDtypeStruct((rows, model), jnp.bfloat16),
            jax.ShapeDtypeStruct((rows, inner), jnp.bfloat16),
            jax.ShapeDtypeStruct((rows, inner), jnp.bfloat16),
            jax.ShapeDtypeStruct((rows, model), jnp.float32),
            jax.ShapeDtypeStruct((rows, model), jnp.bfloat16),
        ],
        cost_estimate=nothing(),
        name="feed_forward",
    )(
        heads, *contexts, cells, out_weight, gain[None], shift[None], up_weight, up_bias[None], down_weight,
        down_bias[None],
    )


def feed_back_kernel(head_ref, two_ref, branch_ref, slope_ref, down_ref, up_ref, hidden_ref, gain_ref, weight_ref,
                     inner_ref, bias_ref, hidden_grad_ref, hidden_grad_b_ref, gain_grad_ref, shift_grad_ref,
                     *rest):
    piece_refs, acc_ref = rest[:-1], rest[-1]
    step = pl.program_id(0)

    @pl.when(step == 0)
    def _():
        acc_ref[...] = jnp.zeros(acc_ref.shape, jnp.float32)

    inner = (nt_dot(branch_ref[...], down_ref[...]) * slope_ref[...].astype(jnp.float32)).astype(jnp.bfloat16)
    inner_ref[...] = inner
    bias_ref[...] = jnp.sum(inner.astype(jnp.float32), axis=0, keepdims=True)
    acc_ref[...] += nt_dot(inner, up_ref[...])

    @pl.when(step == pl.num_programs(0) - 1)
    def _():
        unit, scale = norm_parts(hidden_ref[...])
        grad = acc_ref[...]
        gain_grad_ref[...] = jnp.sum(grad * unit, axis=0, keepdims=True)
        shift_grad_ref[...] = jnp.sum(grad, axis=0, keepdims=True)
        grad = grad * gain_ref[...]
        mean = jnp.mean(grad, axis=-1, keepdims=True)
        slant = jnp.mean(grad * unit, axis=-1, keepdims=True)
        total = two_ref[...] + scale * (grad - mean - unit * slant)
        hidden_grad_ref[...] = total
        total = total.astype(jnp.bfloat16)
        hidden_grad_b_ref[...] = total
        for k, piece_ref in enumerate(piece_refs):
            width = piece_ref.shape[1]
            begin = pl.multiple_of(head_ref[k] * width, width)
            piece_ref[...] = nt_dot(total, weight_ref[pl.ds(begin, width), :]).astype(jnp.bfloat16)


def feed_back(heads, grad_two, grad_branch, slope, down_weight, up_weight, hidden, gain, out_weight):
    rows, model = hidden.shape
    inner = up_weight.shape[1]
    tile = FEED_TILE
    count = heads.shape[0]
    return pl.pallas_call(
        feed_back_kernel,
        grid_spec=pltpu.PrefetchScalarGridSpec(
            num_scalar_prefetch=1,
            grid=(inner // tile,),
            in_specs=[
                resident((rows, model)),
                resident((rows, model)),
                pl.BlockSpec((rows, tile), lambda j, heads: (0, j)),
                pl.BlockSpec((tile, model), lambda j, heads: (j, 0)),
                pl.BlockSpec((model, tile), lambda j, heads: (0, j)),
                resident((rows, model)),
                resident((1, model)),
                resident((model, model)),
            ],
            out_specs=[
                pl.BlockSpec((rows, tile), lambda j, heads: (0, j)),
                pl.BlockSpec((1, tile), lambda j, heads: (0, j)),
                resident((rows, model)),
                resident((rows, model)),
                resident((1, model)),
                resident((1, model)),
            ]
            + [resident((rows, model // count))] * count,
            scratch_shapes=[pltpu.VMEM((rows, model), jnp.float32)],
        ),
        out_shape=[
            jax.ShapeDtypeStruct((rows, inner), jnp.bfloat16),
            jax.ShapeDtypeStruct((1, inner), jnp.float32),
            jax.ShapeDtypeStruct((rows, model), jnp.float32),
            jax.ShapeDtypeStruct((rows, model), jnp.bfloat16),
            jax.ShapeDtypeStruct((1, model), jnp.float32),
            jax.ShapeDtypeStruct((1, model), jnp.float32),
        ]
        + [jax.ShapeDtypeStruct((rows, model // count), jnp.bfloat16)] * count,
        cost_estimate=nothing(),
        name="feed_back",
    )(heads, grad_two, grad_branch, slope, down_weight, up_weight, hidden, gain[None], out_weight)


def tn_dot(left, right):
    return lax.dot_general(left, right, (((0,), (0,)), ((), ())), preferred_element_type=jnp.float32)


def weights_kernel(lefts_at, ready, place_ref, column_ref, *refs):
    count = len(lefts_at)
    scratch = 0 if ready else count
    lefts = refs[: max(lefts_at) + 1]
    rights = refs[len(lefts) : len(lefts) + count]
    refs, ordered = refs[len(lefts) + count : len(refs) - scratch], refs[len(refs) - scratch :]
    vector_ref, (keep_ref, send_ref) = refs[:-2], refs[-2:]
    held, grouped, _, width = keep_ref.shape
    if ready:
        ordered = rights
    else:

        @pl.when(pl.program_id(0) == 0)
        def _():
            for right_ref, ordered_ref in zip(rights, ordered):
                for piece in range(2 * held):
                    begin = pl.multiple_of(column_ref[piece] * width, width)
                    ordered_ref[:, piece * width : (piece + 1) * width] = right_ref[:, pl.ds(begin, width)]

    begin = 0
    for at, ordered_ref in zip(lefts_at, ordered):
        total = lefts[at].shape[1]
        tile = min(total, 256)
        rows = min(tile, total // grouped)
        for first in range(0, total, tile):
            value = tn_dot(lefts[at][:, first : first + tile], ordered_ref[...]).astype(jnp.bfloat16)
            for inside in range(0, tile, rows):
                z, row = divmod(first + inside, total // grouped)
                part = value[inside : inside + rows]
                place = slice(begin + row, begin + row + rows)
                for piece in range(held):
                    keep_ref[piece, z, place, :] = part[:, piece * width : (piece + 1) * width]
                    other = held + piece
                    send_ref[piece, z, place, :] = part[:, other * width : (other + 1) * width]
        begin += total // grouped

    if vector_ref:
        keep_ref[:, :, begin:, :] = vector_ref[0][0]
        send_ref[:, :, begin:, :] = vector_ref[0][1]


def relative_columns(value, steps):
    group = lax.axis_index("dp")
    masks = relative_masks(steps)
    size = value.shape[1] // len(masks)
    return jnp.concatenate([chunk(value, (group ^ mask) * size, size, 1) for mask in masks], axis=1)


def weight_pieces(pairs, steps, vector=None):
    blocks, block = lax.axis_size("blk"), lax.axis_index("blk")
    pieces, group = lax.axis_size("dp"), lax.axis_index("dp")
    width = D // pieces
    masks = relative_masks(blk_masks())
    sizes = [left.shape[1] // blocks for left, _, _ in pairs]
    places = jnp.stack([block ^ mask for mask in masks])
    columns = jnp.stack([group ^ mask for mask in relative_masks(steps)])
    cells = pairs[0][1].shape[0]
    lefts, lefts_at = [], []
    for left, _, _ in pairs:
        if not any(left is seen for seen in lefts):
            lefts.append(left)
        lefts_at.append(next(i for i, seen in enumerate(lefts) if left is seen))
    rights = [right for _, right, _ in pairs]
    parts = [part for _, _, part in pairs]
    grouped = max(1, 128 // min(sizes))
    ready = grouped > 1 or width % 128 != 0
    if ready:
        rights = [
            relative_columns(right[:, part * D : (part + 1) * D], steps) for right, part in zip(rights, parts)
        ]
        parts = [0] * len(parts)
        lefts = [
            jnp.concatenate(
                [chunk(left, (block ^ mask) * (left.shape[1] // blocks), left.shape[1] // blocks, 1) for mask in masks],
                axis=1,
            )
            for left in lefts
        ]
        places = jnp.arange(blocks, dtype=jnp.int32)
    rows = sum(sizes) + (0 if vector is None else vector.shape[3])
    out = pl.BlockSpec((pieces // 2, grouped, rows, width), lambda z, place, column: (0, z, 0, 0))
    specs = [
        pl.BlockSpec((cells, left.shape[1] // blocks * grouped), lambda z, place, column: (0, place[z]))
        for left in lefts
    ]
    specs += [pl.BlockSpec((cells, D), lambda z, place, column, part=part: (0, part)) for part in parts]
    operands = lefts + rights
    if vector is not None:
        specs.append(
            pl.BlockSpec(
                (2, pieces // 2, grouped, vector.shape[3], width), lambda z, place, column: (0, 0, z, 0, 0)
            )
        )
        operands.append(vector)
    shape = jax.ShapeDtypeStruct((pieces // 2, blocks, rows, width), jnp.bfloat16)
    return pl.pallas_call(
        partial(weights_kernel, lefts_at, ready),
        grid_spec=pltpu.PrefetchScalarGridSpec(
            num_scalar_prefetch=2,
            grid=(blocks // grouped,),
            in_specs=specs,
            out_specs=[out, out],
            scratch_shapes=[pltpu.VMEM((cells, D), jnp.bfloat16) for _ in pairs if not ready],
        ),
        out_shape=[shape, shape],
        cost_estimate=nothing(),
        name="weight_pieces",
    )(places, columns, *operands)


def weight_steps(keep, send, flipped, parts):
    steps = dp_order(flipped)
    (came,) = yield [send], by_mask(steps[0], 0)
    size = keep.shape[0]
    terms = [[keep[place], came[place]] for place in range(size)]
    for mask in steps[1:]:
        size = size // 2
        came = yield [summed(terms[place]) for place in range(size, 2 * size)], by_mask(mask, 0)
        terms = [terms[place] + [came[place]] for place in range(size)]
    terms = terms[0]
    size = keep.shape[1]
    for mask in blk_masks():
        size = size // 2
        (came,) = yield [summed([term[size : 2 * size] for term in terms])], by_mask(0, mask)
        terms = [term[:size] for term in terms] + [came]
    value = summed(terms)
    for mask in steps[:0:-1]:
        (came,) = yield [value], by_mask(mask, 0)
        value = jnp.concatenate([value, came], axis=0)
    (came,) = yield [value], by_mask(steps[0], 0)
    return spread_columns(value, came, relative_table(steps, lax.axis_index("dp")), parts)


def local(
    cell_states,
    slide_lengths,
    cell_mask,
    latent_noise,
    train_step,
    attn_gain,
    attn_shift,
    query_weight,
    key_weight,
    value_weight,
    out_weight,
    ffn_gain,
    ffn_shift,
    up_weight,
    up_bias,
    down_weight,
    down_bias,
    encode_weight,
    encode_bias,
    decode_weight,
    prior_means,
    prior_logits,
    out_grad,
):
    rows_here = cell_states.shape[0]
    blocks = lax.axis_size("blk")
    group, block = lax.axis_index("dp"), lax.axis_index("blk")
    width = D // blocks
    x_float = cell_states.astype(jnp.float32)
    _, norm_back = jax.vjp(layer_norm, x_float, attn_gain, attn_shift)
    weights = (query_weight, key_weight, value_weight)
    held, pieces = group_rows(
        with_meta(cell_states, cell_mask, slide_lengths[0]),
        lambda pieces, held: entry(pieces, attn_gain, attn_shift, weights, held),
    )
    normed_b, queries, keys, values = held
    meta = jnp.zeros((blocks, D), jnp.bfloat16)
    order = jnp.arange(blocks, dtype=jnp.int32)
    for mine, other, place in pieces:
        row = jnp.where(at_home(group, block), mine[rows_here], other[rows_here])
        meta = jnp.where(order[:, None] == place, row[None], meta)
    mask_all, lengths_row = from_meta(meta, rows_here, slide_lengths.shape[1])
    ranges, query_code, key_code = slide_tables(lengths_row, mask_all)
    context_here, log_total = attention_forward(ranges, queries, keys, values, query_code, key_code)
    contexts = rows_to_owners(context_here)
    owner_heads = heads_at_owner()
    context_b, hidden, normed_two_b, activated_b, slope_b, hidden_two, hidden_two_b = feed_forward(
        owner_heads, contexts, cell_states, out_weight, ffn_gain, ffn_shift, up_weight, up_bias, down_weight,
        down_bias,
    )
    if width % 128:
        context_b = jnp.zeros((rows_here, D), jnp.bfloat16)
        for k in range(blocks):
            context_b = lax.dynamic_update_slice_in_dim(context_b, contexts[k], owner_heads[k] * width, 1)
    encoded = plain_dot(hidden_two_b, encode_weight) + encode_bias
    latent_mean = encoded[:, :LAT]
    latent_logvar = encoded[:, LAT:]
    spread = jnp.exp(0.5 * latent_logvar)
    noise_float = latent_noise.astype(jnp.float32)
    latent_b = (latent_mean + spread * noise_float).astype(jnp.bfloat16)
    output = hidden_two + plain_dot(latent_b, decode_weight)
    (kl_dim, categorical), kl_back = jax.vjp(
        kl_terms, latent_mean, latent_logvar, prior_means, prior_logits
    )
    real = cell_mask.astype(jnp.float32)
    sums = jnp.concatenate(
        [
            jnp.sum(kl_dim * real[:, None], axis=0),
            jnp.sum(categorical * real)[None],
            jnp.sum(real)[None],
            jnp.zeros((126,), jnp.float32),
        ]
    )
    sums = summed_everywhere(sums)
    kl_sum, cat_sum, count = sums[:LAT], sums[LAT], sums[LAT + 1]
    kbar = kl_sum / count
    floored = jnp.sum(jnp.maximum(kbar, free_floor))
    cat_mean = cat_sum / count
    beta = jnp.minimum(1.0, (train_step[0].astype(jnp.float32) + 1.0) / WARM)
    active = (kbar > free_floor).astype(jnp.float32)
    grad_latent = cols_dot(out_grad, decode_weight)
    grad_mean, grad_logvar, grad_means, grad_prior = kl_back(
        (beta * real[:, None] * active[None, :], beta * real)
    )
    grad_mean = grad_mean + grad_latent
    grad_logvar = grad_logvar + grad_latent * 0.5 * spread * noise_float
    grad_encoded_b = jnp.concatenate([grad_mean, grad_logvar], axis=1).astype(jnp.bfloat16)
    grad_encode_bias = jnp.sum(grad_encoded_b.astype(jnp.float32), axis=0)
    grad_two = out_grad.astype(jnp.float32) + cols_dot(grad_encoded_b, encode_weight)
    grad_down_bias = jnp.sum(grad_two, axis=0)
    grad_branch_b = grad_two.astype(jnp.bfloat16)

    straight, flipped = dp_order(False), dp_order(True)
    block_rows = D // blocks
    down = Exchange(
        weight_steps(
            *weight_pieces(
                [(activated_b, grad_branch_b, 0), (hidden_two_b, grad_encoded_b, 0), (latent_b, out_grad, 0)],
                straight,
            ),
            False,
            [(4 * block_rows, 1), (block_rows, 1), (block_rows // 2, 1)],
        )
    )
    back = feed_back(
        owner_heads, grad_two, tied(grad_branch_b, down.last), slope_b, down_weight, up_weight, hidden, ffn_gain,
        out_weight,
    )
    grad_inner_b, grad_up_bias, grad_hidden, grad_attn_b, grad_ffn_gain, grad_ffn_shift = back[:6]
    grads_here = heads_to_workers(back[6:])
    token = grads_here
    by_block = lambda part: part.reshape(blocks, -1)
    means_block = jnp.moveaxis(grad_means.reshape(K, blocks, LAT // blocks), 1, 0)
    vectors = [
        by_block(grad_ffn_gain),
        by_block(grad_ffn_shift),
        by_block(grad_up_bias),
        by_block(grad_down_bias),
        by_block(grad_encode_bias),
        by_block(means_block),
        by_block(grad_prior),
    ]
    sizes = [part.shape[1] for part in vectors]
    vector = jnp.concatenate([part.astype(jnp.bfloat16) for part in vectors], axis=1)
    vector_rows = -(-sum(sizes) // (8 * D)) * 8
    vector = jnp.pad(vector, ((0, 0), (0, vector_rows * D - sum(sizes))))
    vector = relative_columns(vector.reshape(blocks * vector_rows, D), flipped)
    devices_along = lax.axis_size("dp")
    vector = vector.reshape(blocks, vector_rows, 2, devices_along // 2, D // devices_along)
    vector = jnp.transpose(vector, (2, 3, 0, 1, 4))
    vector = jnp.concatenate([chunk(vector, block ^ mask, 1, 2) for mask in relative_masks(blk_masks())], axis=2)
    up = Exchange(
        weight_steps(
            *weight_pieces(
                [(normed_two_b, tied(grad_inner_b, token), part) for part in range(4)]
                + [(context_b, grad_attn_b, 0)],
                flipped,
                vector,
            ),
            True,
            [(block_rows, 4), (block_rows, 1), (vector_rows, 1)],
        )
    )
    token = down.advance(up.last)
    token = up.advance(token)
    grads = attention_backward(
        ranges, rows_at_worker(), tied(queries, token), grads_here, context_here, log_total, keys, values, query_code,
        key_code,
    )
    grads = tied(grads, (down.flight[0], up.flight[0]))
    partial_rows, grad_heads, part_gain, part_shift = project_back(normed_b, grads, weights)
    partial_rows, grad_heads = tied((partial_rows, grad_heads), (down.flight, up.flight))
    row_sum = Exchange(row_steps(partial_rows))
    part_shift = part_shift[0]
    part_gain = (part_gain[0] - attn_shift * part_shift) / attn_gain
    token = down.advance(grad_heads)
    token = up.advance(token)
    extra = jnp.concatenate([by_block(part_gain), by_block(part_shift)], axis=1)
    extra_size = extra.shape[1]
    extra = jnp.pad(extra, ((0, 0), (0, 3 * width - extra_size))).astype(jnp.bfloat16)
    pieces = lax.axis_size("dp") // 2
    piece_rows = block_rows // pieces
    grad_heads = grad_heads.reshape(blocks, pieces, piece_rows, 3 * width)
    extra = jnp.broadcast_to(extra[:, None, None, :], (blocks, pieces, 8, 3 * width))
    attn = Exchange(head_steps(jnp.concatenate([grad_heads, extra], axis=2)))
    token = attn.last
    order = [row_sum, attn, down, up, row_sum, attn]
    live = [down, row_sum, up, attn]
    for bundle in order:
        token = bundle.advance(token)
    while any(bundle.result is None for bundle in live):
        for bundle in live:
            if bundle.result is None:
                token = bundle.advance(token)
    grad_normed = row_sum.result.astype(jnp.float32)
    grad_from_norm, _, _ = norm_back(grad_normed)
    states_grad = grad_hidden + grad_from_norm
    mine, other = attn.result
    attn_vector = jnp.sum((mine[0].astype(jnp.float32) + other[0].astype(jnp.float32)), axis=0)[piece_rows]
    main = spread_heads(mine, other, piece_rows)
    down_sum, encode_sum, decode_sum = down.result
    up_sum, out_sum, vector_sum = up.result
    flat = vector_sum.reshape(-1)
    small, begin = [], 0
    for size in sizes:
        small.append(flat[begin : begin + size])
        begin += size
    totals = (
        attn_vector[: extra_size // 2],
        attn_vector[extra_size // 2 : extra_size],
        main[0],
        main[1],
        main[2],
        out_sum,
        small[0],
        small[1],
        up_sum,
        small[2],
        down_sum,
        small[3],
        encode_sum,
        small[4],
        decode_sum,
        small[5].reshape(K, LAT // blocks),
        small[6],
    )
    kl_out = (floored / LAT + cat_mean).reshape(1)
    return (output.astype(jnp.bfloat16), states_grad, kl_out) + tuple(totals)


def solution(mesh):
    in_specs = (
        P(("dp", "blk"), None),
        P("dp", None),
        P(("dp", "blk")),
        P(("dp", "blk"), None),
        P(),
        P(),
        P(),
        P(),
        P(),
        P(),
        P(),
        P(),
        P(),
        P(),
        P(),
        P(),
        P(),
        P(),
        P(),
        P(),
        P(),
        P(),
        P(("dp", "blk"), None),
    )
    out_specs = (
        P(("dp", "blk"), None),
        P(("dp", "blk"), None),
        P(),
        P("blk"),
        P("blk"),
        P("blk", None),
        P("blk", None),
        P("blk", None),
        P("blk", None),
        P("blk"),
        P("blk"),
        P("blk", None),
        P("blk"),
        P("blk", None),
        P("blk"),
        P("blk", None),
        P("blk"),
        P("blk", None),
        P(None, "blk"),
        P("blk"),
    )
    return jax.shard_map(local, mesh=mesh, in_specs=in_specs, out_specs=out_specs, check_vma=False)
```

time: 647 us -> 524 us (0.81)
  Pallas kernels: 65.8 us -> 175 us
  matrix products: 94.6 us -> 15.3 us
  starting transfers between devices: 153 us -> 86.2 us
  local copies, waits for them, and re-layouts: 72.1 us -> 15.9 us
  waiting for transfers between devices: 168 us -> 143 us
    pallas_call x0 -> x10, Pallas kernels: none -> 109 us  [the longest x2 24.9 us: weight_pieces(): pl.pallas_call(partial(weights_kernel, lefts_at, ready), grid_spec=pltpu....]
    ppermute x61 -> x30, starting transfers between devices: 98.4 us -> 37.8 us  [swapped(): return lax.ppermute(value, MESH_AXES, pairs)]
    ppermute x61 -> x30, waiting for transfers between devices: 148 us -> 93.1 us  [swapped(): return lax.ppermute(value, MESH_AXES, pairs)]
    ppermute x19 -> x18, waiting for transfers between devices: 19.5 us -> 50.1 us  [moved(): return lax.ppermute(value, MESH_AXES, pairs)]
    dynamic_slice x36 -> x2, local copies, waits for them, and re-layouts: 31.3 us -> 1.29 us  [chunk(): return lax.dynamic_slice_in_dim(value, start, size, axis)]
    dot_general x6 -> x2, matrix products: 32.4 us -> 2.68 us  [plain_dot(): return jnp.dot(left, right, preferred_element_type=jnp.float32)]
    dot_general x6 -> x2, matrix products: 28.5 us -> 5.24 us  [cols_dot(): lax.dot_general(left, right, (((1,), (1,)), ((), ())), preferred_element_...]
    dot_general x6 -> x0, matrix products: 22.3 us -> none  [rows_dot(): lax.dot_general(left, right, (((0,), (0,)), ((), ())), preferred_element_...]
  transfers between devices with their start and end apart: 80 -> 48, of which waited for: 38 -> 24; matrix products, arithmetic and copies ran while one was open for 21% -> 13% of each run, Pallas kernels for 6% -> 20%
where the time goes in v3:
time: 524 us; the launch traced here: 514 us
  Pallas kernels  175 us (33%)
  waiting for transfers between devices  143 us (27%)
  starting transfers between devices  86.2 us (16%)
  other arithmetic  71.3 us (14%)
  local copies, waits for them, and re-layouts  15.9 us (3%)
  matrix products  15.3 us (3%)
  between operations  7.68 us (1%)
    ppermute x30, waiting for transfers between devices, swapped(): return lax.ppermute(value, MESH_AXES, pairs)  93.1 us
    ppermute x18, waiting for transfers between devices, moved(): return lax.ppermute(value, MESH_AXES, pairs)  50.1 us
    ppermute x18, starting transfers between devices, moved(): return lax.ppermute(value, MESH_AXES, pairs)  48.4 us
    pallas_call x1, Pallas kernels, attention_backward(): pl.pallas_call(backward_kernel, out_shape=(out, out, out), grid_spec=pltp...  37.8 us
    ppermute x30, starting transfers between devices, swapped(): return lax.ppermute(value, MESH_AXES, pairs)  37.8 us
    convert_element_type x15, other arithmetic, summed(): return total.astype(jnp.bfloat16)  32.8 us
    pallas_call x1, Pallas kernels, attention_forward(): pl.pallas_call(forward_kernel, out_shape=(jax.ShapeDtypeStruct((N, W), jn...  27.9 us
    pallas_call x2, Pallas kernels, weight_pieces(): pl.pallas_call(partial(weights_kernel, lefts_at, ready), grid_spec=pltpu....  24.9 us
  transfers between devices with their start and end apart: 48, of which 24 were waited for; matrix products, arithmetic and copies ran while one was open for 13% of the time, Pallas kernels for 20%

profile of v3, /device:TPU:17, one launch (start us, length us, event | category | flops | bytes accessed | tf_op | source)
XLA Modules:
  0.0 514.3 jit_solution(13213372552031769863)
XLA Ops:
  3.5 3.2 collective-permute-start.3
  8.0 4.2 collective-permute-start.2
  12.2 8.5 %collective-permute-done.3.refs_2_ = bf16[392,1024]{1,0:T(8,128)(2,1)} collective-permute-done((bf16[392,1024]{1,0:T(8,128)(2,1)S(1)}, bf16[392,1024]{1,0:T(8,128)(2,1)}, u32[]{:S(2)}, u32[]{:S(2)}) %collective-permute-start.3) | collective-permute-done | bytes 802848 | tf_op jit(solution)/shard_map/ppermute | solution.py:468
  22.8 5.5 %collective-permute-done.refs_0_ = bf16[392,1024]{1,0:T(8,128)(2,1)} collective-permute-done((bf16[392,1024]{1,0:T(8,128)(2,1)S(1)}, bf16[392,1024]{1,0:T(8,128)(2,1)}, u32[]{:S(2)}, u32[]{:S(2)}) %collective-permute-start) | collective-permute-done | bytes 802848 | tf_op jit(solution)/shard_map/ppermute | solution.py:468
  32.9 6.7 %entry.2 = (bf16[1536,1024]{1,0:T(8,128)(2,1)}, bf16[1536,256]{1,0:T(8,128)(2,1)}, bf16[1536,256]{1,0:T(8,128)(2,1)}, bf16[1536,256]{1,0:T(8,128)(2,1)}) custom-call(s32[4]{0:T(128)} %add_add_fusion.3.place_ref, bf16[392,1024]{1,0:T(8,128)(2,1)} %copy-done.9, bf16[392,1024]{1,0:T(8,128)(2,1)} %collective-permute-done.2.refs_1_, ...), custom_call_target="tpu_custom_call" | custom-call | tf_op jit(solution)/shard_map/entry/pallas_call | solution.py:579
  54.7 6.7 %entry.3 = (bf16[1536,1024]{1,0:T(8,128)(2,1)}, bf16[1536,256]{1,0:T(8,128)(2,1)}, bf16[1536,256]{1,0:T(8,128)(2,1)}, bf16[1536,256]{1,0:T(8,128)(2,1)}) custom-call(s32[4]{0:T(128)} %add_add_fusion.4.place_ref, bf16[392,1024]{1,0:T(8,128)(2,1)} %collective-permute-done.refs_0_, ...), custom_call_target="tpu_custom_call", output_to_operand_aliasing={{0}: (10, {}), {1}: (11, {}), {2}: (12, {}), {3}: (13, {})} | custom-call | tf_op jit(solution)/shard_map/entry/pallas_call | solution.py:579
  61.4 27.9 %attention_forward.1 = (bf16[1536,256]{1,0:T(8,128)(2,1)}, f32[4,1536]{1,0:T(4,128)}) custom-call(s32[3,2]{1,0:T(4,128)} %pad_add_fusion.range_ref, bf16[1536,256]{1,0:T(8,128)(2,1)} %get-tuple-element.141.q_ref, bf16[1536,256]{1,0:T(8,128)(2,1)} %get-tuple-element.112.k_ref, bf16[1536,256]{1,0:T(8,128)(2,1)} %get-tuple-element.113.v_ref, ...), custom_call_target="tpu_custom_call" | custom-call | tf_op jit(solution)/shard_map/attention_forward/pallas_call | solution.py:338
  94.6 5.1 collective-permute-start.7
  100.5 4.8 collective-permute-done.7.refs_0_
  106.0 20.1 %feed_forward.1 = (bf16[384,1024]{1,0:T(8,128)(2,1)}, f32[384,1024]{1,0:T(8,128)}, bf16[384,1024]{1,0:T(8,128)(2,1)}, bf16[384,4096]{1,0:T(8,128)(2,1)}, bf16[38...) custom-call(s32[4]{0:T(128)} %get-tuple-element.251.head_ref, bf16[384,256]{1,0:T(8,128)(2,1)} %copy-done.34, ...), custom_call_target="tpu_custom_call" | custom-call | tf_op jit(solution)/shard_map/feed_forward/pallas_call | solution.py:789
  133.2 3.8 collective-permute-start.11
  139.2 2.4 collective-permute-done.12
  141.6 2.9 collective-permute-start.13
  154.3 2.9 fusion.31
  159.2 2.4 fusion.141
  161.6 12.5 %weight_pieces.2 = (bf16[4,4,1408,128]{3,2,1,0:T(8,128)(2,1)}, bf16[4,4,1408,128]{3,2,1,0:T(8,128)(2,1)}) custom-call(s32[4]{0:T(128)} %get-tuple-element.252.place_ref, s32[8]{0:T(128)} %stack.150.column_ref, bf16[384,4096]{1,0:T(8,128)(2,1)} %get-tuple-element.117.refs_0_, bf16[384,1024]{1,0:T(8,128)(2,1)} %get-tuple-element.116.refs_1_, ...), custom_call_target="tpu_custom_call" | custom-call | tf_op jit(solution)/shard_map/weight_pieces/pallas_call | solution.py:1011
  174.2 4.7 collective-permute-start.21
  182.7 19.7 %feed_back.1 = (bf16[384,4096]{1,0:T(8,128)(2,1)}, f32[1,4096]{1,0:T(1,128)}, f32[384,1024]{1,0:T(8,128)}, bf16[384,1024]{1,0:T(8,128)(2,1)}, f32[1,1024]{1,0:T(...) custom-call(s32[4]{0:T(128)} %get-tuple-element.251.head_ref, ...), custom_call_target="tpu_custom_call" | custom-call | tf_op jit(solution)/shard_map/feed_back/pallas_call | solution.py:872
  204.8 3.3 collective-permute-start.16
  209.7 2.7 collective-permute-start.18
  215.2 8.6 %collective-permute-done.19.refs_3_ = bf16[384,256]{1,0:T(8,128)(2,1)S(1)} collective-permute-done((bf16[384,256]{1,0:T(8,128)(2,1)}, bf16[384,256]{1,0:T(8,128)(2,1)S(1)}, u32[]{:S(2)}, u32[]{:S(2)}) %collective-permute-start.19) | collective-permute-done | bytes 196640 | tf_op jit(solution)/shard_map/ppermute | solution.py:468
  223.9 12.4 %weight_pieces.3 = (bf16[4,4,1288,128]{3,2,1,0:T(8,128)(2,1)}, bf16[4,4,1288,128]{3,2,1,0:T(8,128)(2,1)}) custom-call(s32[4]{0:T(128)} %get-tuple-element.252.place_ref, s32[8]{0:T(128)} %stack.156.column_ref, bf16[384,1024]{1,0:T(8,128)(2,1)} %get-tuple-element.124.refs_0_, bf16[384,1024]{1,0:T(8,128)(2,1)} %get-tuple-element.125.refs_1_, ...), custom_call_target="tpu_custom_call" | custom-call | tf_op jit(solution)/shard_map/weight_pieces/pallas_call | solution.py:1011
  236.3 2.6 collective-permute-start.20
  238.9 5.2 %fusion.11 = (bf16[4,1408,128]{2,1,0:T(8,128)(2,1)}, bf16[4,1408,128]{2,1,0:T(8,128)(2,1)}) fusion(bf16[4,4,1408,128]{3,2,1,0:T(8,128)(2,1)} %collective-permute-done.21, bf16[4,4,1408,128]{3,2,1,0:T(8,128)(2,1)} %get-tuple-element.138), kind=kLoop, calls=%fused_computation.37 | loop fusion | flops 5767168 | bytes 8650752 | tf_op jit(solution)/shard_map/convert_element_type | solution.py:120
  247.5 2.6 fusion.15
  253.0 37.8 %attention_backward.1 = (bf16[1536,256]{1,0:T(8,128)(2,1)}, bf16[1536,256]{1,0:T(8,128)(2,1)}, bf16[1536,256]{1,0:T(8,128)(2,1)}) custom-call(s32[3,2]{1,0:T(4,128)} %pad_add_fusion.range_ref, s32[4]{0:T(128)} %pad_add_fusion.3.row_ref, bf16[1536,256]{1,0:T(8,128)(2,1)} %get-tuple-element.141.q_ref, bf16[1536,256]{1,0:T(8,128)(2,1)} %get-tuple-element.114.ctx_ref, ...), custom_call_target="tpu_custom_call" | custom-call | tf_op jit(solution)/shard_map/attention_backward/pallas_call | solution.py:408
  290.8 18.2 %collective-permute-done.22 = bf16[4,1408,128]{2,1,0:T(8,128)(2,1)S(1)} collective-permute-done((bf16[4,1408,128]{2,1,0:T(8,128)(2,1)}, bf16[4,1408,128]{2,1,0:T(8,128)(2,1)S(1)}, u32[]{:S(2)}, u32[]{:S(2)}) %collective-permute-start.22) | collective-permute-done | bytes 1441824 | tf_op jit(solution)/shard_map/ppermute | solution.py:89
  310.1 14.9 %project_back.1 = (bf16[1536,1024]{1,0:T(8,128)(2,1)}, bf16[1024,768]{1,0:T(8,128)(2,1)}, f32[8,1024]{1,0:T(8,128)}, f32[8,1024]{1,0:T(8,128)}) custom-call(s32[1]{0:T(128)} %bitcast.9.place_ref, bf16[1536,1024]{1,0:T(8,128)(2,1)} %get-tuple-element.123.normed_ref, bf16[1536,256]{1,0:T(8,128)(2,1)} %get-tuple-element.146.dq_ref, ...), custom_call_target="tpu_custom_call" | custom-call | tf_op jit(solution)/shard_map/project_back/pallas_call | solution.py:643
  328.9 2.9 fusion
  335.2 2.6 fusion.1
  340.4 3.3 collective-permute-start.27
  343.7 8.3 %collective-permute-done.30 = bf16[4,2,72,768]{3,2,1,0:T(8,128)(2,1)S(1)} collective-permute-done((bf16[4,2,72,768]{3,2,1,0:T(8,128)(2,1)S(1)}, bf16[4,2,72,768]{3,2,1,0:T(8,128)(2,1)S(1)}, u32[]{:S(2)}, u32[]{:S(2)}) %collective-permute-start.30) | collective-permute-done | bytes 884768 | tf_op jit(solution)/shard_map/ppermute | solution.py:89
  353.4 9.4 %collective-permute-done.29 = bf16[4,1408,128]{2,1,0:T(8,128)(2,1)S(1)} collective-permute-done((bf16[4,1408,128]{2,1,0:T(8,128)(2,1)S(1)}, bf16[4,1408,128]{2,1,0:T(8,128)(2,1)S(1)}, u32[]{:S(2)}, u32[]{:S(2)}) %collective-permute-start.29) | collective-permute-done | bytes 1441824 | tf_op jit(solution)/shard_map/ppermute | solution.py:89
  362.8 3.1 fusion.13
  367.1 13.3 %collective-permute-done.28 = bf16[4,1288,128]{2,1,0:T(8,128)(2,1)S(1)} collective-permute-done((bf16[4,1288,128]{2,1,0:T(8,128)(2,1)S(1)}, bf16[4,1288,128]{2,1,0:T(8,128)(2,1)S(1)}, u32[]{:S(2)}, u32[]{:S(2)}) %collective-permute-start.28) | collective-permute-done | bytes 1318944 | tf_op jit(solution)/shard_map/ppermute | solution.py:89
  380.4 3.2 fusion.17
  385.7 8.9 %collective-permute-start.31 = (bf16[1,384,1024]{2,1,0:T(8,128)(2,1)S(1)}, bf16[1,384,1024]{2,1,0:T(8,128)(2,1)}, u32[]{:S(2)}, u32[]{:S(2)}) collective-permute-start(bf16[1,384,1024]{2,1,0:T(8,128)(2,1)S(1)} %fusion.8), channel_id=1, source_target_pairs={{0,3},{1,2},{6,5},{7,4},{8,11},{9,10},{14,13},{15,12},{16,19},{17,... | collective-permute-start | bytes 2359304 | tf_op jit(solution)/shard_map/ppermute | solution.py:468
  401.7 20.7 %collective-permute-done.31 = bf16[1,384,1024]{2,1,0:T(8,128)(2,1)} collective-permute-done((bf16[1,384,1024]{2,1,0:T(8,128)(2,1)S(1)}, bf16[1,384,1024]{2,1,0:T(8,128)(2,1)}, u32[]{:S(2)}, u32[]{:S(2)}) %collective-permute-start.31) | collective-permute-done | bytes 786464 | tf_op jit(solution)/shard_map/ppermute | solution.py:468
  422.5 2.3 fusion.6
  428.8 11.8 %collective-permute-done.34 = bf16[2,1,72,768]{3,2,1,0:T(8,128)(2,1)S(1)} collective-permute-done((bf16[2,1,72,768]{3,2,1,0:T(8,128)(2,1)S(1)}, bf16[2,1,72,768]{3,2,1,0:T(8,128)(2,1)S(1)}, u32[]{:S(2)}, u32[]{:S(2)}) %collective-permute-start.34) | collective-permute-done | bytes 221216 | tf_op jit(solution)/shard_map/ppermute | solution.py:89
  441.8 4.6 collective-permute-done.38
  452.9 3.9 collective-permute-done.41
  461.5 2.9 collective-permute-done.39
  465.9 9.5 %collective-permute-done.44 = bf16[2,1408,128]{2,1,0:T(8,128)(2,1)S(1)} collective-permute-done((bf16[2,1408,128]{2,1,0:T(8,128)(2,1)S(1)}, bf16[2,1408,128]{2,1,0:T(8,128)(2,1)S(1)}, u32[]{:S(2)}, u32[]{:S(2)}) %collective-permute-start.44) | collective-permute-done | bytes 720928 | tf_op jit(solution)/shard_map/ppermute | solution.py:89
  476.7 2.8 collective-permute-start.47
  491.5 5.8 %spread_columns.2 = (f32[1024,1024]{1,0:T(8,128)}, f32[256,1024]{1,0:T(8,128)}, f32[128,1024]{1,0:T(8,128)}) custom-call(s32[8]{0:T(128)} %get-tuple-element.253.table_ref, bf16[4,1408,128]{2,1,0:T(8,128)(2,1)} %pad_maximum_fusion.1.mine_ref, bf16[4,1408,128]{2,1,0:T(8,128)(2,1)} %collective-permute-done.47.other_ref), custom_call_target="tpu_custom_call" | custom-call | tf_op jit(solution)/shard_map/spread_columns/pallas_call | solution.py:200
  497.3 5.6 %spread_columns.3 = (f32[256,4096]{1,0:T(8,128)}, f32[256,1024]{1,0:T(8,128)}, f32[8,1024]{1,0:T(8,128)}) custom-call(s32[8]{0:T(128)} %get-tuple-element.254.table_ref, bf16[4,1288,128]{2,1,0:T(8,128)(2,1)} %pad_maximum_fusion.2.mine_ref, bf16[4,1288,128]{2,1,0:T(8,128)(2,1)} %collective-permute-done.46.other_ref), custom_call_target="tpu_custom_call" | custom-call | tf_op jit(solution)/shard_map/spread_columns/pallas_call | solution.py:200
  508.3 4.6 spread_heads.1
  (307 shorter events, 125.1 us)
Async XLA Ops:
  3.5 17.1 %collective-permute-start.3 = (bf16[392,1024]{1,0:T(8,128)(2,1)S(1)}, bf16[392,1024]{1,0:T(8,128)(2,1)}, u32[]{:S(2)}, u32[]{:S(2)}) collective-permute-start(bf16[392,1024]{1,0:T(8,128)(2,1)S(1)} %fusion.27.refs_0_), channel_id=1, source_target_pairs={{0,1},{1,0},{6,7},{7,6},{8,9},{9,8},{14,15},{15,14},{16,17},{17,16... | collective-permute-start | bytes 2408456 | tf_op jit(solution)/shard_map/ppermute | solution.py:468
  6.7 21.6 %collective-permute-start = (bf16[392,1024]{1,0:T(8,128)(2,1)S(1)}, bf16[392,1024]{1,0:T(8,128)(2,1)}, u32[]{:S(2)}, u32[]{:S(2)}) collective-permute-start(bf16[392,1024]{1,0:T(8,128)(2,1)S(1)} %fusion.27.refs_0_), channel_id=1, source_target_pairs={{2,1},{3,0},{4,7},{5,6},{10,9},{11,8},{12,15},{13,14},{18,17},{19,... | collective-permute-start | bytes 2408456 | tf_op jit(solution)/shard_map/ppermute | solution.py:468
  8.0 24.9 %collective-permute-start.2 = (bf16[392,1024]{1,0:T(8,128)(2,1)S(1)}, bf16[392,1024]{1,0:T(8,128)(2,1)}, u32[]{:S(2)}, u32[]{:S(2)}) collective-permute-start(bf16[392,1024]{1,0:T(8,128)(2,1)S(1)} %fusion.27.refs_0_), channel_id=1, source_target_pairs={{0,4},{1,5},{6,2},{7,3},{8,12},{9,13},{14,10},{15,11},{16,20},{17,... | collective-permute-start | bytes 2408456 | tf_op jit(solution)/shard_map/ppermute | solution.py:468
  20.6 12.3 %collective-permute-start.4 = (bf16[392,1024]{1,0:T(8,128)(2,1)}, bf16[392,1024]{1,0:T(8,128)(2,1)}, u32[]{:S(2)}, u32[]{:S(2)}) collective-permute-start(bf16[392,1024]{1,0:T(8,128)(2,1)} %collective-permute-done.3.refs_2_), channel_id=1, source_target_pairs={{0,4},{1,5},{6,2},{7,3},{8,12},{9,13},{14,10},{15,11},{16,20},{17,... | collective-permute-start | bytes 2408456 | tf_op jit(solution)/shard_map/ppermute | solution.py:468
  28.3 13.2 %collective-permute-start.1 = (bf16[392,1024]{1,0:T(8,128)(2,1)}, bf16[392,1024]{1,0:T(8,128)(2,1)}, u32[]{:S(2)}, u32[]{:S(2)}) collective-permute-start(bf16[392,1024]{1,0:T(8,128)(2,1)} %collective-permute-done.refs_0_), channel_id=1, source_target_pairs={{0,1},{1,0},{6,7},{7,6},{8,9},{9,8},{14,15},{15,14},{16,17},{17,16... | collective-permute-start | bytes 2408456 | tf_op jit(solution)/shard_map/ppermute | solution.py:468
  41.5 7.7 %collective-permute-start.5 = (bf16[392,1024]{1,0:T(8,128)(2,1)}, bf16[392,1024]{1,0:T(8,128)(2,1)S(1)}, u32[]{:S(2)}, u32[]{:S(2)}) collective-permute-start(bf16[392,1024]{1,0:T(8,128)(2,1)} %collective-permute-done.1.refs_2_), channel_id=1, source_target_pairs={{0,4},{1,5},{6,2},{7,3},{8,12},{9,13},{14,10},{15,11},{16,20},{17,... | collective-permute-start | bytes 2408456 | tf_op jit(solution)/shard_map/ppermute | solution.py:468
  42.9 7.1 %collective-permute-start.6 = (bf16[392,1024]{1,0:T(8,128)(2,1)}, bf16[392,1024]{1,0:T(8,128)(2,1)}, u32[]{:S(2)}, u32[]{:S(2)}) collective-permute-start(bf16[392,1024]{1,0:T(8,128)(2,1)} %collective-permute-done.refs_0_), channel_id=1, source_target_pairs={{0,4},{1,5},{6,2},{7,3},{8,12},{9,13},{14,10},{15,11},{16,20},{17,... | collective-permute-start | bytes 2408456 | tf_op jit(solution)/shard_map/ppermute | solution.py:468
  90.5 9.9 %collective-permute-start.10 = (bf16[384,256]{1,0:T(8,128)(2,1)S(1)}, bf16[384,256]{1,0:T(8,128)(2,1)S(1)}, u32[]{:S(2)}, u32[]{:S(2)}) collective-permute-start(bf16[384,256]{1,0:T(8,128)(2,1)S(1)} %get-tuple-element.220), channel_id=1, source_target_pairs={{0,3},{1,1},{2,7},{3,5},{4,0},{5,2},{6,4},{7,6},{8,11},{9,9},{10,1... | collective-permute-start | bytes 589832 | tf_op jit(solution)/shard_map/ppermute | solution.py:468
  92.4 8.1 %collective-permute-start.9 = (bf16[384,256]{1,0:T(8,128)(2,1)S(1)}, bf16[384,256]{1,0:T(8,128)(2,1)S(1)}, u32[]{:S(2)}, u32[]{:S(2)}) collective-permute-start(bf16[384,256]{1,0:T(8,128)(2,1)S(1)} %get-tuple-element.221), channel_id=1, source_target_pairs={{0,2},{1,0},{2,6},{3,4},{4,3},{5,1},{6,7},{7,5},{8,10},{9,8},{10,1... | collective-permute-start | bytes 589832 | tf_op jit(solution)/shard_map/ppermute | solution.py:468
  93.9 6.6 %collective-permute-start.8 = (bf16[384,256]{1,0:T(8,128)(2,1)S(1)}, bf16[384,256]{1,0:T(8,128)(2,1)S(1)}, u32[]{:S(2)}, u32[]{:S(2)}) collective-permute-start(bf16[384,256]{1,0:T(8,128)(2,1)S(1)} %get-tuple-element.222), channel_id=1, source_target_pairs={{0,1},{1,3},{2,5},{3,7},{4,2},{5,0},{6,6},{7,4},{8,9},{9,11},{10,1... | collective-permute-start | bytes 589832 | tf_op jit(solution)/shard_map/ppermute | solution.py:468
  94.6 10.7 %collective-permute-start.7 = (bf16[384,256]{1,0:T(8,128)(2,1)S(1)}, bf16[384,256]{1,0:T(8,128)(2,1)S(1)}, u32[]{:S(2)}, u32[]{:S(2)}) collective-permute-start(bf16[384,256]{1,0:T(8,128)(2,1)S(1)} %get-tuple-element.223), channel_id=1, source_target_pairs={{0,0},{1,2},{2,4},{3,6},{4,1},{5,3},{6,5},{7,7},{8,8},{9,10},{10,1... | collective-permute-start | bytes 589832 | tf_op jit(solution)/shard_map/ppermute | solution.py:468
  133.2 4.6 collective-permute-start.11
  139.1 2.5 collective-permute-start.12
  141.6 3.9 collective-permute-start.13
  145.5 2.5 collective-permute-start.14
  147.9 2.5 collective-permute-start.15
  174.2 64.8 %collective-permute-start.21 = (bf16[4,4,1408,128]{3,2,1,0:T(8,128)(2,1)}, bf16[4,4,1408,128]{3,2,1,0:T(8,128)(2,1)}, u32[]{:S(2)}, u32[]{:S(2)}) collective-permute-start(bf16[4,4,1408,128]{3,2,1,0:T(8,128)(2,1)} %get-tuple-element.118), channel_id=1, source_target_pairs={{0,4},{1,5},{2,6},{3,7},{4,0},{5,1},{6,2},{7,3},{8,12},{9,13},{10,... | collective-permute-start | bytes 17301512 | tf_op jit(solution)/shard_map/ppermute | solution.py:89
  204.8 10.4 %collective-permute-start.16 = (bf16[384,256]{1,0:T(8,128)(2,1)}, bf16[384,256]{1,0:T(8,128)(2,1)S(1)}, u32[]{:S(2)}, u32[]{:S(2)}) collective-permute-start(bf16[384,256]{1,0:T(8,128)(2,1)} %get-tuple-element.127), channel_id=1, source_target_pairs={{0,0},{1,4},{2,1},{3,5},{4,2},{5,6},{6,3},{7,7},{8,8},{9,12},{10,9... | collective-permute-start | bytes 589832 | tf_op jit(solution)/shard_map/ppermute | solution.py:468
  208.2 7.0 %collective-permute-start.17 = (bf16[384,256]{1,0:T(8,128)(2,1)}, bf16[384,256]{1,0:T(8,128)(2,1)S(1)}, u32[]{:S(2)}, u32[]{:S(2)}) collective-permute-start(bf16[384,256]{1,0:T(8,128)(2,1)} %get-tuple-element.128), channel_id=1, source_target_pairs={{0,5},{1,0},{2,4},{3,1},{4,7},{5,2},{6,6},{7,3},{8,13},{9,8},{10,1... | collective-permute-start | bytes 589832 | tf_op jit(solution)/shard_map/ppermute | solution.py:468
  209.7 5.5 %collective-permute-start.18 = (bf16[384,256]{1,0:T(8,128)(2,1)}, bf16[384,256]{1,0:T(8,128)(2,1)S(1)}, u32[]{:S(2)}, u32[]{:S(2)}) collective-permute-start(bf16[384,256]{1,0:T(8,128)(2,1)} %get-tuple-element.129), channel_id=1, source_target_pairs={{0,1},{1,5},{2,0},{3,4},{4,3},{5,7},{6,2},{7,6},{8,9},{9,13},{10,8... | collective-permute-start | bytes 589832 | tf_op jit(solution)/shard_map/ppermute | solution.py:468
  212.4 11.5 %collective-permute-start.19 = (bf16[384,256]{1,0:T(8,128)(2,1)}, bf16[384,256]{1,0:T(8,128)(2,1)S(1)}, u32[]{:S(2)}, u32[]{:S(2)}) collective-permute-start(bf16[384,256]{1,0:T(8,128)(2,1)} %get-tuple-element.130), channel_id=1, source_target_pairs={{0,4},{1,1},{2,5},{3,0},{4,6},{5,3},{6,7},{7,2},{8,12},{9,9},{10,1... | collective-permute-start | bytes 589832 | tf_op jit(solution)/shard_map/ppermute | solution.py:468
  236.3 11.2 %collective-permute-start.20 = (bf16[4,4,1288,128]{3,2,1,0:T(8,128)(2,1)}, bf16[4,4,1288,128]{3,2,1,0:T(8,128)(2,1)S(1)}, u32[]{:S(2)}, u32[]{:S(2)}) collective-permute-start(bf16[4,4,1288,128]{3,2,1,0:T(8,128)(2,1)} %get-tuple-element.137), channel_id=1, source_target_pairs={{0,4},{1,5},{2,6},{3,7},{4,0},{5,1},{6,2},{7,3},{8,12},{9,13},{10,... | collective-permute-start | bytes 15826952 | tf_op jit(solution)/shard_map/ppermute | solution.py:89
  244.1 80.9 %collective-permute-start.24 = (bf16[4,1408,128]{2,1,0:T(8,128)(2,1)}, bf16[4,1408,128]{2,1,0:T(8,128)(2,1)S(1)}, u32[]{:S(2)}, u32[]{:S(2)}) collective-permute-start(bf16[4,1408,128]{2,1,0:T(8,128)(2,1)} %get-tuple-element.204), channel_id=1, source_target_pairs={{0,8},{1,9},{2,10},{3,11},{4,12},{5,13},{6,14},{7,15},{8,0},{9,1},... | collective-permute-start | bytes 4325384 | tf_op jit(solution)/shard_map/ppermute | solution.py:89
  245.9 63.1 %collective-permute-start.22 = (bf16[4,1408,128]{2,1,0:T(8,128)(2,1)}, bf16[4,1408,128]{2,1,0:T(8,128)(2,1)S(1)}, u32[]{:S(2)}, u32[]{:S(2)}) collective-permute-start(bf16[4,1408,128]{2,1,0:T(8,128)(2,1)} %get-tuple-element.205), channel_id=1, source_target_pairs={{0,8},{1,9},{2,10},{3,11},{4,12},{5,13},{6,14},{7,15},{8,0},{9,1},... | collective-permute-start | bytes 4325384 | tf_op jit(solution)/shard_map/ppermute | solution.py:89
  250.7 40.2 %collective-permute-start.23 = (bf16[4,1288,128]{2,1,0:T(8,128)(2,1)}, bf16[4,1288,128]{2,1,0:T(8,128)(2,1)}, u32[]{:S(2)}, u32[]{:S(2)}) collective-permute-start(bf16[4,1288,128]{2,1,0:T(8,128)(2,1)} %get-tuple-element.207), channel_id=1, source_target_pairs={{0,16},{1,17},{2,18},{3,19},{4,20},{5,21},{6,22},{7,23},{8,24},{9,... | collective-permute-start | bytes 3956744 | tf_op jit(solution)/shard_map/ppermute | solution.py:89
  252.4 72.6 %collective-permute-start.25 = (bf16[4,1288,128]{2,1,0:T(8,128)(2,1)}, bf16[4,1288,128]{2,1,0:T(8,128)(2,1)}, u32[]{:S(2)}, u32[]{:S(2)}) collective-permute-start(bf16[4,1288,128]{2,1,0:T(8,128)(2,1)} %get-tuple-element.206), channel_id=1, source_target_pairs={{0,16},{1,17},{2,18},{3,19},{4,20},{5,21},{6,22},{7,23},{8,24},{9,... | collective-permute-start | bytes 3956744 | tf_op jit(solution)/shard_map/ppermute | solution.py:89
  325.0 13.2 %collective-permute-start.26 = (bf16[1536,1024]{1,0:T(8,128)(2,1)}, bf16[1536,1024]{1,0:T(8,128)(2,1)}, u32[]{:S(2)}, u32[]{:S(2)}) collective-permute-start(bf16[1536,1024]{1,0:T(8,128)(2,1)} %get-tuple-element.151), channel_id=1, source_target_pairs={{2,6},{3,7},{4,0},{5,1},{10,14},{11,15},{12,8},{13,9},{18,22},{19,... | collective-permute-start | bytes 9437192 | tf_op jit(solution)/shard_map/ppermute | solution.py:468
  331.8 30.9 %collective-permute-start.29 = (bf16[4,1408,128]{2,1,0:T(8,128)(2,1)S(1)}, bf16[4,1408,128]{2,1,0:T(8,128)(2,1)S(1)}, u32[]{:S(2)}, u32[]{:S(2)}) collective-permute-start(bf16[4,1408,128]{2,1,0:T(8,128)(2,1)S(1)} %fusion), channel_id=1, source_target_pairs={{0,16},{1,17},{2,18},{3,19},{4,20},{5,21},{6,22},{7,23},{8,24},{9,... | collective-permute-start | bytes 4325384 | tf_op jit(solution)/shard_map/ppermute | solution.py:89
  333.9 18.2 %collective-permute-start.30 = (bf16[4,2,72,768]{3,2,1,0:T(8,128)(2,1)S(1)}, bf16[4,2,72,768]{3,2,1,0:T(8,128)(2,1)S(1)}, u32[]{:S(2)}, u32[]{:S(2)}) collective-permute-start(bf16[4,2,72,768]{3,2,1,0:T(8,128)(2,1)S(1)} %pad_maximum_fusion.3), channel_id=1, source_target_pairs={{0,8},{1,9},{2,10},{3,11},{4,12},{5,13},{6,14},{7,15},{8,0},{9,1},... | collective-permute-start | bytes 2654216 | tf_op jit(solution)/shard_map/ppermute | solution.py:89
  337.8 42.6 %collective-permute-start.28 = (bf16[4,1288,128]{2,1,0:T(8,128)(2,1)S(1)}, bf16[4,1288,128]{2,1,0:T(8,128)(2,1)S(1)}, u32[]{:S(2)}, u32[]{:S(2)}) collective-permute-start(bf16[4,1288,128]{2,1,0:T(8,128)(2,1)S(1)} %fusion.1), channel_id=1, source_target_pairs={{0,8},{1,9},{2,10},{3,11},{4,12},{5,13},{6,14},{7,15},{8,0},{9,1},... | collective-permute-start | bytes 3956744 | tf_op jit(solution)/shard_map/ppermute | solution.py:89
  340.4 43.1 %collective-permute-start.27 = (bf16[2,384,1024]{2,1,0:T(8,128)(2,1)S(1)}, bf16[2,384,1024]{2,1,0:T(8,128)(2,1)S(1)}, u32[]{:S(2)}, u32[]{:S(2)}) collective-permute-start(bf16[2,384,1024]{2,1,0:T(8,128)(2,1)S(1)} %pad_maximum_fusion), channel_id=1, source_target_pairs={{0,1},{1,0},{6,7},{7,6},{8,9},{9,8},{14,15},{15,14},{16,17},{17,16... | collective-permute-start | bytes 4718600 | tf_op jit(solution)/shard_map/ppermute | solution.py:468
  353.1 44.0 %collective-permute-start.33 = (bf16[4,1,72,768]{3,2,1,0:T(8,128)(2,1)}, bf16[4,1,72,768]{3,2,1,0:T(8,128)(2,1)}, u32[]{:S(2)}, u32[]{:S(2)}) collective-permute-start(bf16[4,1,72,768]{3,2,1,0:T(8,128)(2,1)} %add_convert_fusion.7), channel_id=1, source_target_pairs={{0,16},{1,17},{2,18},{3,19},{4,20},{5,21},{6,22},{7,23},{8,24},{9,... | collective-permute-start | bytes 1327112 | tf_op jit(solution)/shard_map/ppermute | solution.py:89
  365.8 32.4 %collective-permute-start.32 = (bf16[2,1408,128]{2,1,0:T(8,128)(2,1)}, bf16[2,1408,128]{2,1,0:T(8,128)(2,1)}, u32[]{:S(2)}, u32[]{:S(2)}) collective-permute-start(bf16[2,1408,128]{2,1,0:T(8,128)(2,1)} %fusion.13), channel_id=1, source_target_pairs={{0,1},{1,0},{2,3},{3,2},{4,5},{5,4},{6,7},{7,6},{8,9},{9,8},{10,11... | collective-permute-start | bytes 2162696 | tf_op jit(solution)/shard_map/ppermute | solution.py:89
  385.7 36.7 %collective-permute-start.31 = (bf16[1,384,1024]{2,1,0:T(8,128)(2,1)S(1)}, bf16[1,384,1024]{2,1,0:T(8,128)(2,1)}, u32[]{:S(2)}, u32[]{:S(2)}) collective-permute-start(bf16[1,384,1024]{2,1,0:T(8,128)(2,1)S(1)} %fusion.8), channel_id=1, source_target_pairs={{0,3},{1,2},{6,5},{7,4},{8,11},{9,10},{14,13},{15,12},{16,19},{17,... | collective-permute-start | bytes 2359304 | tf_op jit(solution)/shard_map/ppermute | solution.py:468
  396.4 29.4 %collective-permute-start.35 = (bf16[2,1288,128]{2,1,0:T(8,128)(2,1)}, bf16[2,1288,128]{2,1,0:T(8,128)(2,1)S(1)}, u32[]{:S(2)}, u32[]{:S(2)}) collective-permute-start(bf16[2,1288,128]{2,1,0:T(8,128)(2,1)} %fusion.17), channel_id=1, source_target_pairs={{0,1},{1,0},{2,3},{3,2},{4,5},{5,4},{6,7},{7,6},{8,9},{9,8},{10,11... | collective-permute-start | bytes 1978376 | tf_op jit(solution)/shard_map/ppermute | solution.py:89
  398.2 42.5 %collective-permute-start.34 = (bf16[2,1,72,768]{3,2,1,0:T(8,128)(2,1)S(1)}, bf16[2,1,72,768]{3,2,1,0:T(8,128)(2,1)S(1)}, u32[]{:S(2)}, u32[]{:S(2)}) collective-permute-start(bf16[2,1,72,768]{3,2,1,0:T(8,128)(2,1)S(1)} %add_convert_fusion.8), channel_id=1, source_target_pairs={{0,2},{1,3},{2,0},{3,1},{4,6},{5,7},{6,4},{7,5},{8,10},{9,11},{10,... | collective-permute-start | bytes 663560 | tf_op jit(solution)/shard_map/ppermute | solution.py:89
  399.8 46.6 %collective-permute-start.38 = (bf16[1,1408,128]{2,1,0:T(8,128)(2,1)S(1)}, bf16[1,1408,128]{2,1,0:T(8,128)(2,1)S(1)}, u32[]{:S(2)}, u32[]{:S(2)}) collective-permute-start(bf16[1,1408,128]{2,1,0:T(8,128)(2,1)S(1)} %fusion.44), channel_id=1, source_target_pairs={{0,3},{1,2},{2,1},{3,0},{4,7},{5,6},{6,5},{7,4},{8,11},{9,10},{10,... | collective-permute-start | bytes 1081352 | tf_op jit(solution)/shard_map/ppermute | solution.py:89
  427.2 22.7 %collective-permute-start.37 = (bf16[1,1288,128]{2,1,0:T(8,128)(2,1)S(1)}, bf16[1,1288,128]{2,1,0:T(8,128)(2,1)S(1)}, u32[]{:S(2)}, u32[]{:S(2)}) collective-permute-start(bf16[1,1288,128]{2,1,0:T(8,128)(2,1)S(1)} %fusion.51), channel_id=1, source_target_pairs={{0,3},{1,2},{2,1},{3,0},{4,7},{5,6},{6,5},{7,4},{8,11},{9,10},{10,... | collective-permute-start | bytes 989192 | tf_op jit(solution)/shard_map/ppermute | solution.py:89
  441.7 11.2 %collective-permute-start.36 = (bf16[1,1,72,768]{3,2,1,0:T(8,128)(2,1)S(1)}, bf16[1,1,72,768]{3,2,1,0:T(8,128)(2,1)S(1)}, u32[]{:S(2)}, u32[]{:S(2)}) collective-permute-start(bf16[1,1,72,768]{3,2,1,0:T(8,128)(2,1)S(1)} %get-tuple-element.211), channel_id=1, source_target_pairs={{0,1},{1,0},{2,3},{3,2},{4,5},{5,4},{6,7},{7,6},{8,9},{9,8},{10,11... | collective-permute-start | bytes 331784 | tf_op jit(solution)/shard_map/ppermute | solution.py:89
  447.9 8.9 %collective-permute-start.41 = (bf16[1,1408,128]{2,1,0:T(8,128)(2,1)S(1)}, bf16[1,1408,128]{2,1,0:T(8,128)(2,1)S(1)}, u32[]{:S(2)}, u32[]{:S(2)}) collective-permute-start(bf16[1,1408,128]{2,1,0:T(8,128)(2,1)S(1)} %fusion.41), channel_id=1, source_target_pairs={{0,16},{1,17},{2,18},{3,19},{4,20},{5,21},{6,22},{7,23},{8,24},{9,... | collective-permute-start | bytes 1081352 | tf_op jit(solution)/shard_map/ppermute | solution.py:89
  451.3 8.3 %collective-permute-start.40 = (bf16[1,1288,128]{2,1,0:T(8,128)(2,1)S(1)}, bf16[1,1288,128]{2,1,0:T(8,128)(2,1)S(1)}, u32[]{:S(2)}, u32[]{:S(2)}) collective-permute-start(bf16[1,1288,128]{2,1,0:T(8,128)(2,1)S(1)} %fusion.48), channel_id=1, source_target_pairs={{0,8},{1,9},{2,10},{3,11},{4,12},{5,13},{6,14},{7,15},{8,0},{9,1},... | collective-permute-start | bytes 989192 | tf_op jit(solution)/shard_map/ppermute | solution.py:89
  456.9 18.6 %collective-permute-start.44 = (bf16[2,1408,128]{2,1,0:T(8,128)(2,1)S(1)}, bf16[2,1408,128]{2,1,0:T(8,128)(2,1)S(1)}, u32[]{:S(2)}, u32[]{:S(2)}) collective-permute-start(bf16[2,1408,128]{2,1,0:T(8,128)(2,1)S(1)} %pad_maximum_fusion.6), channel_id=1, source_target_pairs={{0,8},{1,9},{2,10},{3,11},{4,12},{5,13},{6,14},{7,15},{8,0},{9,1},... | collective-permute-start | bytes 2162696 | tf_op jit(solution)/shard_map/ppermute | solution.py:89
  459.4 5.1 collective-permute-start.39
  459.7 19.8 %collective-permute-start.43 = (bf16[2,1288,128]{2,1,0:T(8,128)(2,1)S(1)}, bf16[2,1288,128]{2,1,0:T(8,128)(2,1)S(1)}, u32[]{:S(2)}, u32[]{:S(2)}) collective-permute-start(bf16[2,1288,128]{2,1,0:T(8,128)(2,1)S(1)} %pad_maximum_fusion.7), channel_id=1, source_target_pairs={{0,16},{1,17},{2,18},{3,19},{4,20},{5,21},{6,22},{7,23},{8,24},{9,... | collective-permute-start | bytes 1978376 | tf_op jit(solution)/shard_map/ppermute | solution.py:89
  465.9 21.0 %collective-permute-start.42 = (bf16[2,2,72,768]{3,2,1,0:T(8,128)(2,1)}, bf16[2,2,72,768]{3,2,1,0:T(8,128)(2,1)}, u32[]{:S(2)}, u32[]{:S(2)}) collective-permute-start(bf16[2,2,72,768]{3,2,1,0:T(8,128)(2,1)} %pad_maximum_fusion.8), channel_id=1, source_target_pairs={{0,8},{1,9},{2,10},{3,11},{4,12},{5,13},{6,14},{7,15},{8,0},{9,1},... | collective-permute-start | bytes 1327112 | tf_op jit(solution)/shard_map/ppermute | solution.py:89
  476.7 14.8 %collective-permute-start.47 = (bf16[4,1408,128]{2,1,0:T(8,128)(2,1)}, bf16[4,1408,128]{2,1,0:T(8,128)(2,1)}, u32[]{:S(2)}, u32[]{:S(2)}) collective-permute-start(bf16[4,1408,128]{2,1,0:T(8,128)(2,1)} %pad_maximum_fusion.1.mine_ref), channel_id=1, source_target_pairs={{0,4},{1,5},{2,6},{3,7},{4,0},{5,1},{6,2},{7,3},{8,12},{9,13},{10,... | collective-permute-start | bytes 4325384 | tf_op jit(solution)/shard_map/ppermute | solution.py:89
  480.7 16.6 %collective-permute-start.46 = (bf16[4,1288,128]{2,1,0:T(8,128)(2,1)}, bf16[4,1288,128]{2,1,0:T(8,128)(2,1)}, u32[]{:S(2)}, u32[]{:S(2)}) collective-permute-start(bf16[4,1288,128]{2,1,0:T(8,128)(2,1)} %pad_maximum_fusion.2.mine_ref), channel_id=1, source_target_pairs={{0,4},{1,5},{2,6},{3,7},{4,0},{5,1},{6,2},{7,3},{8,12},{9,13},{10,... | collective-permute-start | bytes 3956744 | tf_op jit(solution)/shard_map/ppermute | solution.py:89
  489.2 17.0 %collective-permute-start.45 = (bf16[4,2,72,768]{3,2,1,0:T(8,128)(2,1)}, bf16[4,2,72,768]{3,2,1,0:T(8,128)(2,1)}, u32[]{:S(2)}, u32[]{:S(2)}) collective-permute-start(bf16[4,2,72,768]{3,2,1,0:T(8,128)(2,1)} %pad_maximum_fusion.4.mine_ref), channel_id=1, source_target_pairs={{0,4},{1,5},{2,6},{3,7},{4,0},{5,1},{6,2},{7,3},{8,12},{9,13},{10,... | collective-permute-start | bytes 2654216 | tf_op jit(solution)/shard_map/ppermute | solution.py:89
  (45 other events, 576.9 us)

commit v4 on v3

--- a/solution.py
+++ b/solution.py
@@ -20,8 +20,9 @@
 free_floor = 1.3
 neg_fill = -1e30
 
-QUERY_TILE = 512
-KEY_TILE = 512
+QUERY_TILE = 256
+KEY_TILE = 384
+ROW_TILE = 512
 KEY_UNIT = 128
 FEED_TILE = 512
 
@@ -101,12 +102,20 @@
     return [(2 << t) - 1 for t in range(bits_of(lax.axis_size("blk")))]
 
 
+def tree_sum(value, masks):
+    places = [(0, 0)]
+    for dp_mask, blk_mask in masks:
+        places = places + [(dp ^ dp_mask, blk ^ blk_mask) for dp, blk in places]
+    terms = [value] + [swapped(value, dp, blk) for dp, blk in places[1:]]
+    while len(terms) > 1:
+        terms = [terms[i] + terms[i + 1] for i in range(0, len(terms), 2)]
+    return terms[0]
+
+
 def summed_everywhere(value):
-    for mask in dp_masks():
-        value = value + swapped(value, mask, 0)
-    for mask in blk_masks():
-        value = value + swapped(value, 0, mask)
-    return value
+    value = tree_sum(value, [(1, 0)])
+    value = tree_sum(value, [(mask, 0) for mask in dp_masks()[1:]])
+    return tree_sum(value, [(0, mask) for mask in blk_masks()])
 
 
 def added(left, right):
@@ -136,20 +145,26 @@
         self.flight = None
         self._take(lambda: next(self.steps))
 
-    def _take(self, step):
+    def _take(self, step, hold=False):
         try:
             values, permute = step()
+            first = len(values) // 2 if hold else len(values)
             self.last = values
-            self.flight = [permute(value) for value in values]
+            self.flight = [permute(value) for value in values[:first]]
+            self.held = (values[first:], permute)
         except StopIteration as end:
             self.result = end.value
             self.last = end.value
             self.flight = None
 
-    def advance(self, token):
+    def advance(self, token, hold=False):
         came = tied(self.flight, token)
-        self._take(lambda: self.steps.send(came))
+        self._take(lambda: self.steps.send(came), hold)
         return self.last
+
+    def release(self, token):
+        values, permute = self.held
+        self.flight = self.flight + [permute(tied(value, token)) for value in values]
 
 
 def by_mask(dp_mask, blk_mask):
@@ -312,17 +327,22 @@
         start = pl.multiple_of(range_ref[step, 0] * KEY_UNIT + kb * KEY_TILE, KEY_UNIT)
         keys = k_ref[pl.ds(start, KEY_TILE), :]
         open_pair = allowed_pairs(ck_ref[pl.ds(start, KEY_TILE), :], code_q, start, (KEY_TILE, QUERY_TILE))
+        bias = jnp.where(open_pair, 0.0, neg_fill)
+        rows = [slice(h * HD, (h + 1) * HD) for h in range(nh)]
+        scores = [nt_dot(keys[:, rows[h]], scaled[:, rows[h]]) + bias for h in range(nh)]
+        probs, scales = [], []
         for h in range(nh):
-            s = nt_dot(keys, head_lanes(scaled, h))
-            s = jnp.where(open_pair, s, neg_fill)
-            m_old = m_ref[h:h+1, :]
-            m_new = jnp.maximum(m_old, jnp.max(s, axis=0, keepdims=True))
-            p = jnp.exp(s - m_new)
+            m_old = m_ref[h : h + 1, :]
+            m_new = jnp.maximum(m_old, jnp.max(scores[h], axis=0, keepdims=True))
+            p = jnp.exp(scores[h] - m_new)
             alpha = jnp.exp(m_old - m_new)
-            l_ref[h:h+1, :] = l_ref[h:h+1, :] * alpha + jnp.sum(p, axis=0, keepdims=True)
-            m_ref[h:h+1, :] = m_new
-            rows = slice(h*HD, (h+1)*HD)
-            acc_ref[rows, :] = acc_ref[rows, :] * alpha + nn_dot(vt_ref[rows, pl.ds(start, KEY_TILE)], p.astype(jnp.bfloat16))
+            l_ref[h : h + 1, :] = l_ref[h : h + 1, :] * alpha + jnp.sum(p, axis=0, keepdims=True)
+            m_ref[h : h + 1, :] = m_new
+            probs.append(p.astype(jnp.bfloat16))
+            scales.append(alpha)
+        for h in range(nh):
+            part = nn_dot(vt_ref[rows[h], pl.ds(start, KEY_TILE)], probs[h])
+            acc_ref[rows[h], :] = acc_ref[rows[h], :] * scales[h] + part
         return 0
     lax.fori_loop(0, range_ref[step, 1], body, 0)
     for h in range(nh):
@@ -376,17 +396,16 @@
         keys = k_ref[pl.ds(start, KEY_TILE), :]
         values = v_ref[pl.ds(start, KEY_TILE), :]
         open_pair = allowed_pairs(ck_ref[pl.ds(start, KEY_TILE), :], code_q, start, (KEY_TILE, QUERY_TILE))
-        ps, dss = [], []
+        bias = jnp.where(open_pair, 0.0, neg_fill)
+        cols = [slice(h * QUERY_TILE, (h + 1) * QUERY_TILE) for h in range(nh)]
+        scores = [nt_dot(keys, q_all[cols[h], :]) + bias for h in range(nh)]
+        dps = [nt_dot(values, do_all[cols[h], :]) for h in range(nh)]
+        ps = [jnp.exp(scores[h] - lse_ref[h : h + 1, :]) for h in range(nh)]
+        dss = [(ps[h] * (dps[h] - deltas[h])).astype(jnp.bfloat16) for h in range(nh)]
+        ps = [p.astype(jnp.bfloat16) for p in ps]
         for h in range(nh):
-            cols = slice(h*QUERY_TILE, (h+1)*QUERY_TILE)
-            rows = slice(h*HD, (h+1)*HD)
-            s = nt_dot(keys, q_all[cols, :])
-            p = jnp.where(open_pair, jnp.exp(s - lse_ref[h:h+1, :]), 0.0)
-            dp = nt_dot(values, do_all[cols, :])
-            ds = (p * (dp - deltas[h])).astype(jnp.bfloat16)
-            ps.append(p.astype(jnp.bfloat16))
-            dss.append(ds)
-            dqt_ref[rows, :] += nn_dot(kt_ref[rows, pl.ds(start, KEY_TILE)], ds)
+            rows = slice(h * HD, (h + 1) * HD)
+            dqt_ref[rows, :] += nn_dot(kt_ref[rows, pl.ds(start, KEY_TILE)], dss[h])
         dv_acc[pl.ds(start, KEY_TILE), :] += nn_dot(jnp.concatenate(ps, axis=1), do_all)
         dk_acc[pl.ds(start, KEY_TILE), :] += nn_dot(jnp.concatenate(dss, axis=1), q_all)
         return 0
@@ -639,14 +658,14 @@
     model = weights[0].shape[0]
     columns = [head_columns(weight) for weight in weights]
     table = head_block(lax.axis_index("dp"), lax.axis_index("blk"))[None]
-    wide = pl.BlockSpec((QUERY_TILE, model), lambda i, place: (i, 0))
+    wide = pl.BlockSpec((ROW_TILE, model), lambda i, place: (i, 0))
     return pl.pallas_call(
         project_back_kernel,
         grid_spec=pltpu.PrefetchScalarGridSpec(
             num_scalar_prefetch=1,
-            grid=(cells // QUERY_TILE,),
+            grid=(cells // ROW_TILE,),
             in_specs=[wide]
-            + [pl.BlockSpec((QUERY_TILE, width), lambda i, place: (i, 0))] * 3
+            + [pl.BlockSpec((ROW_TILE, width), lambda i, place: (i, 0))] * 3
             + [spec for _, spec in columns],
             out_specs=[wide, resident((model, 3 * width)), resident((8, model)), resident((8, model))],
             scratch_shapes=[pltpu.VMEM((model, 3 * width), jnp.float32), pltpu.VMEM((8, 3 * width), jnp.float32)],
@@ -1157,7 +1176,6 @@
     )
     grad_inner_b, grad_up_bias, grad_hidden, grad_attn_b, grad_ffn_gain, grad_ffn_shift = back[:6]
     grads_here = heads_to_workers(back[6:])
-    token = grads_here
     by_block = lambda part: part.reshape(blocks, -1)
     means_block = jnp.moveaxis(grad_means.reshape(K, blocks, LAT // blocks), 1, 0)
     vectors = [
@@ -1178,32 +1196,32 @@
     vector = vector.reshape(blocks, vector_rows, 2, devices_along // 2, D // devices_along)
     vector = jnp.transpose(vector, (2, 3, 0, 1, 4))
     vector = jnp.concatenate([chunk(vector, block ^ mask, 1, 2) for mask in relative_masks(blk_masks())], axis=2)
+    up_pieces = weight_pieces(
+        [(normed_two_b, tied(grad_inner_b, back[6:]), part) for part in range(4)] + [(context_b, grad_attn_b, 0)],
+        flipped,
+        vector,
+    )
     up = Exchange(
         weight_steps(
-            *weight_pieces(
-                [(normed_two_b, tied(grad_inner_b, token), part) for part in range(4)]
-                + [(context_b, grad_attn_b, 0)],
-                flipped,
-                vector,
-            ),
-            True,
-            [(block_rows, 4), (block_rows, 1), (vector_rows, 1)],
+            *tied(up_pieces, grads_here), True, [(block_rows, 4), (block_rows, 1), (vector_rows, 1)]
         )
     )
-    token = down.advance(up.last)
-    token = up.advance(token)
+    token = down.advance(up.last, hold=True)
+    token = up.advance(token, hold=True)
     grads = attention_backward(
         ranges, rows_at_worker(), tied(queries, token), grads_here, context_here, log_total, keys, values, query_code,
         key_code,
     )
-    grads = tied(grads, (down.flight[0], up.flight[0]))
+    grads = tied(grads, (down.flight, up.flight))
+    down.release(grads[0])
+    up.release(grads[0])
     partial_rows, grad_heads, part_gain, part_shift = project_back(normed_b, grads, weights)
     partial_rows, grad_heads = tied((partial_rows, grad_heads), (down.flight, up.flight))
     row_sum = Exchange(row_steps(partial_rows))
     part_shift = part_shift[0]
     part_gain = (part_gain[0] - attn_shift * part_shift) / attn_gain
-    token = down.advance(grad_heads)
-    token = up.advance(token)
+    token = up.advance(grad_heads)
+    token = down.advance(token)
     extra = jnp.concatenate([by_block(part_gain), by_block(part_shift)], axis=1)
     extra_size = extra.shape[1]
     extra = jnp.pad(extra, ((0, 0), (0, 3 * width - extra_size))).astype(jnp.bfloat16)
@@ -1213,7 +1231,7 @@
     extra = jnp.broadcast_to(extra[:, None, None, :], (blocks, pieces, 8, 3 * width))
     attn = Exchange(head_steps(jnp.concatenate([grad_heads, extra], axis=2)))
     token = attn.last
-    order = [row_sum, attn, down, up, row_sum, attn]
+    order = [row_sum, attn, down, row_sum, up, attn]
     live = [down, row_sum, up, attn]
     for bundle in order:
         token = bundle.advance(token)

time: 524 us -> 482 us (0.920)
  waiting for transfers between devices: 143 us -> 98.6 us
  starting transfers between devices: 86.2 us -> 110 us
  Pallas kernels: 175 us -> 158 us
    ppermute x18, waiting for transfers between devices: 50.1 us -> 23.6 us  [moved(): return lax.ppermute(value, MESH_AXES, pairs)]
    ppermute x30 -> x32, starting transfers between devices: 37.8 us -> 60.2 us  [swapped(): return lax.ppermute(value, MESH_AXES, pairs)]
    ppermute x30 -> x32, waiting for transfers between devices: 93.1 us -> 75 us  [swapped(): return lax.ppermute(value, MESH_AXES, pairs)]
    pallas_call x1, Pallas kernels: 27.9 us -> 19.3 us  [attention_forward(): pl.pallas_call(forward_kernel, out_shape=(jax.ShapeDtypeStruct((N, W), jn...]
    pallas_call x1, Pallas kernels: 37.8 us -> 29.9 us  [attention_backward(): pl.pallas_call(backward_kernel, out_shape=(out, out, out), grid_spec=pltp...]
  transfers between devices with their start and end apart: 48 -> 50, of which waited for: 24 -> 20; matrix products, arithmetic and copies ran while one was open for 13% -> 14% of each run, Pallas kernels for 20% -> 20%
where the time goes in v4:
time: 482 us; the launch traced here: 475 us
  Pallas kernels  158 us (33%)
  starting transfers between devices  110 us (23%)
  waiting for transfers between devices  98.6 us (20%)
  other arithmetic  69.6 us (14%)
  local copies, waits for them, and re-layouts  15.9 us (3%)
  matrix products  15.3 us (3%)
  between operations  7.64 us (2%)
    ppermute x32, waiting for transfers between devices, swapped(): return lax.ppermute(value, MESH_AXES, pairs)  75 us
    ppermute x32, starting transfers between devices, swapped(): return lax.ppermute(value, MESH_AXES, pairs)  60.2 us
    ppermute x18, starting transfers between devices, moved(): return lax.ppermute(value, MESH_AXES, pairs)  49.9 us
    convert_element_type x15, other arithmetic, summed(): return total.astype(jnp.bfloat16)  30.2 us
    pallas_call x1, Pallas kernels, attention_backward(): pl.pallas_call(backward_kernel, out_shape=(out, out, out), grid_spec=pltp...  29.9 us
    pallas_call x2, Pallas kernels, weight_pieces(): pl.pallas_call(partial(weights_kernel, lefts_at, ready), grid_spec=pltpu....  24.5 us
    ppermute x18, waiting for transfers between devices, moved(): return lax.ppermute(value, MESH_AXES, pairs)  23.6 us
    pallas_call x1, Pallas kernels, feed_forward(): pl.pallas_call(feed_kernel, grid_spec=pltpu.PrefetchScalarGridSpec(num_sc...  20.1 us
  transfers between devices with their start and end apart: 50, of which 20 were waited for; matrix products, arithmetic and copies ran while one was open for 14% of the time, Pallas kernels for 20%

profile of v4, /device:TPU:17, one launch (start us, length us, event | category | flops | bytes accessed | tf_op | source)
XLA Modules:
  0.0 475.1 jit_solution(13657658775782933135)
XLA Ops:
  3.5 3.2 collective-permute-start.3
  8.0 4.1 collective-permute-start.2
  12.1 8.5 %collective-permute-done.3.refs_2_ = bf16[392,1024]{1,0:T(8,128)(2,1)} collective-permute-done((bf16[392,1024]{1,0:T(8,128)(2,1)S(1)}, bf16[392,1024]{1,0:T(8,128)(2,1)}, u32[]{:S(2)}, u32[]{:S(2)}) %collective-permute-start.3) | collective-permute-done | bytes 802848 | tf_op jit(solution)/shard_map/ppermute | solution.py:487
  20.6 2.2 collective-permute-start.4
  22.8 5.5 %collective-permute-done.refs_0_ = bf16[392,1024]{1,0:T(8,128)(2,1)} collective-permute-done((bf16[392,1024]{1,0:T(8,128)(2,1)S(1)}, bf16[392,1024]{1,0:T(8,128)(2,1)}, u32[]{:S(2)}, u32[]{:S(2)}) %collective-permute-start) | collective-permute-done | bytes 802848 | tf_op jit(solution)/shard_map/ppermute | solution.py:487
  32.8 6.7 %entry.2 = (bf16[1536,1024]{1,0:T(8,128)(2,1)}, bf16[1536,256]{1,0:T(8,128)(2,1)}, bf16[1536,256]{1,0:T(8,128)(2,1)}, bf16[1536,256]{1,0:T(8,128)(2,1)}) custom-call(s32[4]{0:T(128)} %add_add_fusion.5.place_ref, bf16[392,1024]{1,0:T(8,128)(2,1)} %copy-done.9, bf16[392,1024]{1,0:T(8,128)(2,1)} %collective-permute-done.2.refs_1_, ...), custom_call_target="tpu_custom_call" | custom-call | tf_op jit(solution)/shard_map/entry/pallas_call | solution.py:598
  42.9 2.2 collective-permute-start.6
  54.2 6.7 %entry.3 = (bf16[1536,1024]{1,0:T(8,128)(2,1)}, bf16[1536,256]{1,0:T(8,128)(2,1)}, bf16[1536,256]{1,0:T(8,128)(2,1)}, bf16[1536,256]{1,0:T(8,128)(2,1)}) custom-call(s32[4]{0:T(128)} %add_add_fusion.6.place_ref, bf16[392,1024]{1,0:T(8,128)(2,1)} %collective-permute-done.refs_0_, ...), custom_call_target="tpu_custom_call", output_to_operand_aliasing={{0}: (10, {}), {1}: (11, {}), {2}: (12, {}), {3}: (13, {})} | custom-call | tf_op jit(solution)/shard_map/entry/pallas_call | solution.py:598
  60.9 19.3 %attention_forward.1 = (bf16[1536,256]{1,0:T(8,128)(2,1)}, f32[4,1536]{1,0:T(4,128)}) custom-call(s32[6,2]{1,0:T(8,128)} %copy.73.range_ref, bf16[1536,256]{1,0:T(8,128)(2,1)} %get-tuple-element.147.q_ref, bf16[1536,256]{1,0:T(8,128)(2,1)} %get-tuple-element.116.k_ref, bf16[1536,256]{1,0:T(8,128)(2,1)} %get-tuple-element.117.v_ref, ...), custom_call_target="tpu_custom_call" | custom-call | tf_op jit(solution)/shard_map/attention_forward/pallas_call | solution.py:358
  85.6 5.4 %collective-permute-start.7 = (bf16[384,256]{1,0:T(8,128)(2,1)S(1)}, bf16[384,256]{1,0:T(8,128)(2,1)S(1)}, u32[]{:S(2)}, u32[]{:S(2)}) collective-permute-start(bf16[384,256]{1,0:T(8,128)(2,1)S(1)} %get-tuple-element.229), channel_id=1, source_target_pairs={{0,0},{1,2},{2,4},{3,6},{4,1},{5,3},{6,5},{7,7},{8,8},{9,10},{10,1... | collective-permute-start | bytes 589832 | tf_op jit(solution)/shard_map/ppermute | solution.py:487
  93.0 6.3 %collective-permute-done.7.refs_0_ = bf16[384,256]{1,0:T(8,128)(2,1)S(1)} collective-permute-done((bf16[384,256]{1,0:T(8,128)(2,1)S(1)}, bf16[384,256]{1,0:T(8,128)(2,1)S(1)}, u32[]{:S(2)}, u32[]{:S(2)}) %collective-permute-start.7) | collective-permute-done | bytes 196640 | tf_op jit(solution)/shard_map/ppermute | solution.py:487
  100.0 20.1 %feed_forward.1 = (bf16[384,1024]{1,0:T(8,128)(2,1)}, f32[384,1024]{1,0:T(8,128)}, bf16[384,1024]{1,0:T(8,128)(2,1)}, bf16[384,4096]{1,0:T(8,128)(2,1)}, bf16[38...) custom-call(s32[4]{0:T(128)} %get-tuple-element.259.head_ref, bf16[384,256]{1,0:T(8,128)(2,1)} %copy-done.26, ...), custom_call_target="tpu_custom_call" | custom-call | tf_op jit(solution)/shard_map/feed_forward/pallas_call | solution.py:808
  120.1 2.1 convolution_add_fusion
  131.4 2.6 collective-permute-start.14
  136.4 2.2 collective-permute-start.17
  145.0 2.8 fusion.31
  149.9 2.5 fusion.136
  152.4 12.5 %weight_pieces.2 = (bf16[4,4,1408,128]{3,2,1,0:T(8,128)(2,1)}, bf16[4,4,1408,128]{3,2,1,0:T(8,128)(2,1)}) custom-call(s32[4]{0:T(128)} %get-tuple-element.260.place_ref, s32[8]{0:T(128)} %stack.150.column_ref, bf16[384,4096]{1,0:T(8,128)(2,1)} %get-tuple-element.121.refs_0_, bf16[384,1024]{1,0:T(8,128)(2,1)} %get-tuple-element.120.refs_1_, ...), custom_call_target="tpu_custom_call" | custom-call | tf_op jit(solution)/shard_map/weight_pieces/pallas_call | solution.py:1030
  164.9 3.2 collective-permute-start.23
  171.9 19.7 %feed_back.1 = (bf16[384,4096]{1,0:T(8,128)(2,1)}, f32[1,4096]{1,0:T(1,128)}, f32[384,1024]{1,0:T(8,128)}, bf16[384,1024]{1,0:T(8,128)(2,1)}, f32[1,1024]{1,0:T(...) custom-call(s32[4]{0:T(128)} %get-tuple-element.259.head_ref, ...), custom_call_target="tpu_custom_call" | custom-call | tf_op jit(solution)/shard_map/feed_back/pallas_call | solution.py:891
  193.8 3.5 collective-permute-start.18
  200.4 2.4 collective-permute-start.21
  203.8 12.0 %weight_pieces.3 = (bf16[4,4,1288,128]{3,2,1,0:T(8,128)(2,1)}, bf16[4,4,1288,128]{3,2,1,0:T(8,128)(2,1)}) custom-call(s32[4]{0:T(128)} %get-tuple-element.260.place_ref, s32[8]{0:T(128)} %stack.156.column_ref, bf16[384,1024]{1,0:T(8,128)(2,1)} %get-tuple-element.128.refs_0_, bf16[384,1024]{1,0:T(8,128)(2,1)} %get-tuple-element.129.refs_1_, ...), custom_call_target="tpu_custom_call" | custom-call | tf_op jit(solution)/shard_map/weight_pieces/pallas_call | solution.py:1030
  217.5 4.7 fusion.11
  222.8 3.3 collective-permute-done.22
  226.1 2.6 fusion.15
  231.5 29.9 %attention_backward.1 = (bf16[1536,256]{1,0:T(8,128)(2,1)}, bf16[1536,256]{1,0:T(8,128)(2,1)}, bf16[1536,256]{1,0:T(8,128)(2,1)}) custom-call(s32[6,2]{1,0:T(8,128)} %copy.73.range_ref, s32[4]{0:T(128)} %pad_add_fusion.3.row_ref, bf16[1536,256]{1,0:T(8,128)(2,1)} %get-tuple-element.147.q_ref, bf16[1536,256]{1,0:T(8,128)(2,1)} %get-tuple-element.118.ctx_ref, ...), custom_call_target="tpu_custom_call" | custom-call | tf_op jit(solution)/shard_map/attention_backward/pallas_call | solution.py:427
  261.7 14.9 %project_back.1 = (bf16[1536,1024]{1,0:T(8,128)(2,1)}, bf16[1024,768]{1,0:T(8,128)(2,1)}, f32[8,1024]{1,0:T(8,128)}, f32[8,1024]{1,0:T(8,128)}) custom-call(s32[1]{0:T(128)} %bitcast.9.place_ref, bf16[1536,1024]{1,0:T(8,128)(2,1)} %get-tuple-element.127.normed_ref, bf16[1536,256]{1,0:T(8,128)(2,1)} %get-tuple-element.152.dq_ref, ...), custom_call_target="tpu_custom_call" | custom-call | tf_op jit(solution)/shard_map/project_back/pallas_call | solution.py:662
  276.6 15.1 %collective-permute-done.27 = bf16[4,1288,128]{2,1,0:T(8,128)(2,1)} collective-permute-done((bf16[4,1288,128]{2,1,0:T(8,128)(2,1)}, bf16[4,1288,128]{2,1,0:T(8,128)(2,1)}, u32[]{:S(2)}, u32[]{:S(2)}) %collective-permute-start.27) | collective-permute-done | bytes 1318944 | tf_op jit(solution)/shard_map/ppermute | solution.py:90
  291.7 2.3 collective-permute-done.26
  297.7 3.7 fusion.1
  301.5 4.0 fusion
  311.1 2.8 collective-permute-start.29
  315.0 9.6 %collective-permute-done.31 = bf16[4,2,72,768]{3,2,1,0:T(8,128)(2,1)} collective-permute-done((bf16[4,2,72,768]{3,2,1,0:T(8,128)(2,1)}, bf16[4,2,72,768]{3,2,1,0:T(8,128)(2,1)}, u32[]{:S(2)}, u32[]{:S(2)}) %collective-permute-start.31) | collective-permute-done | bytes 884768 | tf_op jit(solution)/shard_map/ppermute | solution.py:90
  328.3 7.4 %collective-permute-done.30 = bf16[4,1408,128]{2,1,0:T(8,128)(2,1)} collective-permute-done((bf16[4,1408,128]{2,1,0:T(8,128)(2,1)}, bf16[4,1408,128]{2,1,0:T(8,128)(2,1)}, u32[]{:S(2)}, u32[]{:S(2)}) %collective-permute-start.30) | collective-permute-done | bytes 1441824 | tf_op jit(solution)/shard_map/ppermute | solution.py:90
  340.4 11.1 %collective-permute-start.32 = (bf16[1,384,1024]{2,1,0:T(8,128)(2,1)S(1)}, bf16[1,384,1024]{2,1,0:T(8,128)(2,1)S(1)}, u32[]{:S(2)}, u32[]{:S(2)}) collective-permute-start(bf16[1,384,1024]{2,1,0:T(8,128)(2,1)S(1)} %fusion.8), channel_id=1, source_target_pairs={{0,3},{1,2},{6,5},{7,4},{8,11},{9,10},{14,13},{15,12},{16,19},{17,... | collective-permute-start | bytes 2359304 | tf_op jit(solution)/shard_map/ppermute | solution.py:487
  356.0 8.1 %collective-permute-start.36 = (bf16[2,1,72,768]{3,2,1,0:T(8,128)(2,1)S(1)}, bf16[2,1,72,768]{3,2,1,0:T(8,128)(2,1)S(1)}, u32[]{:S(2)}, u32[]{:S(2)}) collective-permute-start(bf16[2,1,72,768]{3,2,1,0:T(8,128)(2,1)S(1)} %add_convert_fusion.8), channel_id=1, source_target_pairs={{0,2},{1,3},{2,0},{3,1},{4,6},{5,7},{6,4},{7,5},{8,10},{9,11},{10,... | collective-permute-start | bytes 663560 | tf_op jit(solution)/shard_map/ppermute | solution.py:90
  365.6 11.1 %collective-permute-start.40 = (bf16[1,1408,128]{2,1,0:T(8,128)(2,1)S(1)}, bf16[1,1408,128]{2,1,0:T(8,128)(2,1)S(1)}, u32[]{:S(2)}, u32[]{:S(2)}) collective-permute-start(bf16[1,1408,128]{2,1,0:T(8,128)(2,1)S(1)} %fusion.44), channel_id=1, source_target_pairs={{0,3},{1,2},{2,1},{3,0},{4,7},{5,6},{6,5},{7,4},{8,11},{9,10},{10,... | collective-permute-start | bytes 1081352 | tf_op jit(solution)/shard_map/ppermute | solution.py:90
  376.7 2.3 fusion.6
  382.6 14.5 %collective-permute-start.39 = (bf16[1,1288,128]{2,1,0:T(8,128)(2,1)S(1)}, bf16[1,1288,128]{2,1,0:T(8,128)(2,1)S(1)}, u32[]{:S(2)}, u32[]{:S(2)}) collective-permute-start(bf16[1,1288,128]{2,1,0:T(8,128)(2,1)S(1)} %fusion.51), channel_id=1, source_target_pairs={{0,3},{1,2},{2,1},{3,0},{4,7},{5,6},{6,5},{7,4},{8,11},{9,10},{10,... | collective-permute-start | bytes 989192 | tf_op jit(solution)/shard_map/ppermute | solution.py:90
  397.2 2.9 collective-permute-start.38
  401.7 9.1 %collective-permute-done.39 = bf16[1,1288,128]{2,1,0:T(8,128)(2,1)S(1)} collective-permute-done((bf16[1,1288,128]{2,1,0:T(8,128)(2,1)S(1)}, bf16[1,1288,128]{2,1,0:T(8,128)(2,1)S(1)}, u32[]{:S(2)}, u32[]{:S(2)}) %collective-permute-start.39) | collective-permute-done | bytes 329760 | tf_op jit(solution)/shard_map/ppermute | solution.py:90
  414.9 7.1 %collective-permute-done.42 = bf16[1,1288,128]{2,1,0:T(8,128)(2,1)S(1)} collective-permute-done((bf16[1,1288,128]{2,1,0:T(8,128)(2,1)S(1)}, bf16[1,1288,128]{2,1,0:T(8,128)(2,1)S(1)}, u32[]{:S(2)}, u32[]{:S(2)}) %collective-permute-start.42) | collective-permute-done | bytes 329760 | tf_op jit(solution)/shard_map/ppermute | solution.py:90
  424.6 12.9 %collective-permute-done.46 = bf16[2,1408,128]{2,1,0:T(8,128)(2,1)S(1)} collective-permute-done((bf16[2,1408,128]{2,1,0:T(8,128)(2,1)S(1)}, bf16[2,1408,128]{2,1,0:T(8,128)(2,1)S(1)}, u32[]{:S(2)}, u32[]{:S(2)}) %collective-permute-start.46) | collective-permute-done | bytes 720928 | tf_op jit(solution)/shard_map/ppermute | solution.py:90
  447.1 2.1 pad_maximum_fusion.4.mine_ref
  452.1 5.8 %spread_columns.2 = (f32[1024,1024]{1,0:T(8,128)}, f32[256,1024]{1,0:T(8,128)}, f32[128,1024]{1,0:T(8,128)}) custom-call(s32[8]{0:T(128)} %get-tuple-element.261.table_ref, bf16[4,1408,128]{2,1,0:T(8,128)(2,1)} %pad_maximum_fusion.1.mine_ref, bf16[4,1408,128]{2,1,0:T(8,128)(2,1)} %collective-permute-done.49.other_ref), custom_call_target="tpu_custom_call" | custom-call | tf_op jit(solution)/shard_map/spread_columns/pallas_call | solution.py:215
  457.9 5.6 %spread_columns.3 = (f32[256,4096]{1,0:T(8,128)}, f32[256,1024]{1,0:T(8,128)}, f32[8,1024]{1,0:T(8,128)}) custom-call(s32[8]{0:T(128)} %get-tuple-element.262.table_ref, bf16[4,1288,128]{2,1,0:T(8,128)(2,1)} %pad_maximum_fusion.2.mine_ref, bf16[4,1288,128]{2,1,0:T(8,128)(2,1)} %collective-permute-done.48.other_ref), custom_call_target="tpu_custom_call" | custom-call | tf_op jit(solution)/shard_map/spread_columns/pallas_call | solution.py:215
  468.9 4.6 spread_heads.1
  (292 shorter events, 114.1 us)
Async XLA Ops:
  3.5 17.1 %collective-permute-start.3 = (bf16[392,1024]{1,0:T(8,128)(2,1)S(1)}, bf16[392,1024]{1,0:T(8,128)(2,1)}, u32[]{:S(2)}, u32[]{:S(2)}) collective-permute-start(bf16[392,1024]{1,0:T(8,128)(2,1)S(1)} %fusion.27.refs_0_), channel_id=1, source_target_pairs={{0,1},{1,0},{6,7},{7,6},{8,9},{9,8},{14,15},{15,14},{16,17},{17,16... | collective-permute-start | bytes 2408456 | tf_op jit(solution)/shard_map/ppermute | solution.py:487
  6.7 21.6 %collective-permute-start = (bf16[392,1024]{1,0:T(8,128)(2,1)S(1)}, bf16[392,1024]{1,0:T(8,128)(2,1)}, u32[]{:S(2)}, u32[]{:S(2)}) collective-permute-start(bf16[392,1024]{1,0:T(8,128)(2,1)S(1)} %fusion.27.refs_0_), channel_id=1, source_target_pairs={{2,1},{3,0},{4,7},{5,6},{10,9},{11,8},{12,15},{13,14},{18,17},{19,... | collective-permute-start | bytes 2408456 | tf_op jit(solution)/shard_map/ppermute | solution.py:487
  8.0 24.8 %collective-permute-start.2 = (bf16[392,1024]{1,0:T(8,128)(2,1)S(1)}, bf16[392,1024]{1,0:T(8,128)(2,1)}, u32[]{:S(2)}, u32[]{:S(2)}) collective-permute-start(bf16[392,1024]{1,0:T(8,128)(2,1)S(1)} %fusion.27.refs_0_), channel_id=1, source_target_pairs={{0,4},{1,5},{6,2},{7,3},{8,12},{9,13},{14,10},{15,11},{16,20},{17,... | collective-permute-start | bytes 2408456 | tf_op jit(solution)/shard_map/ppermute | solution.py:487
  20.6 12.2 %collective-permute-start.4 = (bf16[392,1024]{1,0:T(8,128)(2,1)}, bf16[392,1024]{1,0:T(8,128)(2,1)}, u32[]{:S(2)}, u32[]{:S(2)}) collective-permute-start(bf16[392,1024]{1,0:T(8,128)(2,1)} %collective-permute-done.3.refs_2_), channel_id=1, source_target_pairs={{0,4},{1,5},{6,2},{7,3},{8,12},{9,13},{14,10},{15,11},{16,20},{17,... | collective-permute-start | bytes 2408456 | tf_op jit(solution)/shard_map/ppermute | solution.py:487
  28.3 13.2 %collective-permute-start.1 = (bf16[392,1024]{1,0:T(8,128)(2,1)}, bf16[392,1024]{1,0:T(8,128)(2,1)}, u32[]{:S(2)}, u32[]{:S(2)}) collective-permute-start(bf16[392,1024]{1,0:T(8,128)(2,1)} %collective-permute-done.refs_0_), channel_id=1, source_target_pairs={{0,1},{1,0},{6,7},{7,6},{8,9},{9,8},{14,15},{15,14},{16,17},{17,16... | collective-permute-start | bytes 2408456 | tf_op jit(solution)/shard_map/ppermute | solution.py:487
  41.5 7.6 %collective-permute-start.5 = (bf16[392,1024]{1,0:T(8,128)(2,1)}, bf16[392,1024]{1,0:T(8,128)(2,1)S(1)}, u32[]{:S(2)}, u32[]{:S(2)}) collective-permute-start(bf16[392,1024]{1,0:T(8,128)(2,1)} %collective-permute-done.1.refs_2_), channel_id=1, source_target_pairs={{0,4},{1,5},{6,2},{7,3},{8,12},{9,13},{14,10},{15,11},{16,20},{17,... | collective-permute-start | bytes 2408456 | tf_op jit(solution)/shard_map/ppermute | solution.py:487
  42.9 7.0 %collective-permute-start.6 = (bf16[392,1024]{1,0:T(8,128)(2,1)}, bf16[392,1024]{1,0:T(8,128)(2,1)}, u32[]{:S(2)}, u32[]{:S(2)}) collective-permute-start(bf16[392,1024]{1,0:T(8,128)(2,1)} %collective-permute-done.refs_0_), channel_id=1, source_target_pairs={{0,4},{1,5},{6,2},{7,3},{8,12},{9,13},{14,10},{15,11},{16,20},{17,... | collective-permute-start | bytes 2408456 | tf_op jit(solution)/shard_map/ppermute | solution.py:487
  81.5 10.8 %collective-permute-start.10 = (bf16[384,256]{1,0:T(8,128)(2,1)S(1)}, bf16[384,256]{1,0:T(8,128)(2,1)S(1)}, u32[]{:S(2)}, u32[]{:S(2)}) collective-permute-start(bf16[384,256]{1,0:T(8,128)(2,1)S(1)} %get-tuple-element.226), channel_id=1, source_target_pairs={{0,3},{1,1},{2,7},{3,5},{4,0},{5,2},{6,4},{7,6},{8,11},{9,9},{10,1... | collective-permute-start | bytes 589832 | tf_op jit(solution)/shard_map/ppermute | solution.py:487
  83.4 9.6 %collective-permute-start.9 = (bf16[384,256]{1,0:T(8,128)(2,1)S(1)}, bf16[384,256]{1,0:T(8,128)(2,1)S(1)}, u32[]{:S(2)}, u32[]{:S(2)}) collective-permute-start(bf16[384,256]{1,0:T(8,128)(2,1)S(1)} %get-tuple-element.227), channel_id=1, source_target_pairs={{0,2},{1,0},{2,6},{3,4},{4,3},{5,1},{6,7},{7,5},{8,10},{9,8},{10,1... | collective-permute-start | bytes 589832 | tf_op jit(solution)/shard_map/ppermute | solution.py:487
  85.0 8.1 %collective-permute-start.8 = (bf16[384,256]{1,0:T(8,128)(2,1)S(1)}, bf16[384,256]{1,0:T(8,128)(2,1)S(1)}, u32[]{:S(2)}, u32[]{:S(2)}) collective-permute-start(bf16[384,256]{1,0:T(8,128)(2,1)S(1)} %get-tuple-element.228), channel_id=1, source_target_pairs={{0,1},{1,3},{2,5},{3,7},{4,2},{5,0},{6,6},{7,4},{8,9},{9,11},{10,1... | collective-permute-start | bytes 589832 | tf_op jit(solution)/shard_map/ppermute | solution.py:487
  85.6 13.7 %collective-permute-start.7 = (bf16[384,256]{1,0:T(8,128)(2,1)S(1)}, bf16[384,256]{1,0:T(8,128)(2,1)S(1)}, u32[]{:S(2)}, u32[]{:S(2)}) collective-permute-start(bf16[384,256]{1,0:T(8,128)(2,1)S(1)} %get-tuple-element.229), channel_id=1, source_target_pairs={{0,0},{1,2},{2,4},{3,6},{4,1},{5,3},{6,5},{7,7},{8,8},{9,10},{10,1... | collective-permute-start | bytes 589832 | tf_op jit(solution)/shard_map/ppermute | solution.py:487
  127.1 2.9 collective-permute-start.11
  131.4 4.3 collective-permute-start.14
  134.0 2.5 collective-permute-start.13
  134.0 2.5 collective-permute-start.12
  136.4 3.6 collective-permute-start.17
  164.9 52.6 %collective-permute-start.23 = (bf16[4,4,1408,128]{3,2,1,0:T(8,128)(2,1)}, bf16[4,4,1408,128]{3,2,1,0:T(8,128)(2,1)}, u32[]{:S(2)}, u32[]{:S(2)}) collective-permute-start(bf16[4,4,1408,128]{3,2,1,0:T(8,128)(2,1)} %get-tuple-element.122), channel_id=1, source_target_pairs={{0,4},{1,5},{2,6},{3,7},{4,0},{5,1},{6,2},{7,3},{8,12},{9,13},{10,... | collective-permute-start | bytes 17301512 | tf_op jit(solution)/shard_map/ppermute | solution.py:90
  193.8 22.0 %collective-permute-start.18 = (bf16[384,256]{1,0:T(8,128)(2,1)}, bf16[384,256]{1,0:T(8,128)(2,1)S(1)}, u32[]{:S(2)}, u32[]{:S(2)}) collective-permute-start(bf16[384,256]{1,0:T(8,128)(2,1)} %get-tuple-element.131), channel_id=1, source_target_pairs={{0,0},{1,4},{2,1},{3,5},{4,2},{5,6},{6,3},{7,7},{8,8},{9,12},{10,9... | collective-permute-start | bytes 589832 | tf_op jit(solution)/shard_map/ppermute | solution.py:487
  197.3 18.5 %collective-permute-start.19 = (bf16[384,256]{1,0:T(8,128)(2,1)}, bf16[384,256]{1,0:T(8,128)(2,1)S(1)}, u32[]{:S(2)}, u32[]{:S(2)}) collective-permute-start(bf16[384,256]{1,0:T(8,128)(2,1)} %get-tuple-element.132), channel_id=1, source_target_pairs={{0,5},{1,0},{2,4},{3,1},{4,7},{5,2},{6,6},{7,3},{8,13},{9,8},{10,1... | collective-permute-start | bytes 589832 | tf_op jit(solution)/shard_map/ppermute | solution.py:487
  198.9 17.0 %collective-permute-start.20 = (bf16[384,256]{1,0:T(8,128)(2,1)}, bf16[384,256]{1,0:T(8,128)(2,1)S(1)}, u32[]{:S(2)}, u32[]{:S(2)}) collective-permute-start(bf16[384,256]{1,0:T(8,128)(2,1)} %get-tuple-element.133), channel_id=1, source_target_pairs={{0,1},{1,5},{2,0},{3,4},{4,3},{5,7},{6,2},{7,6},{8,9},{9,13},{10,8... | collective-permute-start | bytes 589832 | tf_op jit(solution)/shard_map/ppermute | solution.py:487
  200.4 15.5 %collective-permute-start.21 = (bf16[384,256]{1,0:T(8,128)(2,1)}, bf16[384,256]{1,0:T(8,128)(2,1)S(1)}, u32[]{:S(2)}, u32[]{:S(2)}) collective-permute-start(bf16[384,256]{1,0:T(8,128)(2,1)} %get-tuple-element.134), channel_id=1, source_target_pairs={{0,4},{1,1},{2,5},{3,0},{4,6},{5,3},{6,7},{7,2},{8,12},{9,9},{10,1... | collective-permute-start | bytes 589832 | tf_op jit(solution)/shard_map/ppermute | solution.py:487
  215.9 10.2 %collective-permute-start.22 = (bf16[4,4,1288,128]{3,2,1,0:T(8,128)(2,1)}, bf16[4,4,1288,128]{3,2,1,0:T(8,128)(2,1)S(1)}, u32[]{:S(2)}, u32[]{:S(2)}) collective-permute-start(bf16[4,4,1288,128]{3,2,1,0:T(8,128)(2,1)} %get-tuple-element.143), channel_id=1, source_target_pairs={{0,4},{1,5},{2,6},{3,7},{4,0},{5,1},{6,2},{7,3},{8,12},{9,13},{10,... | collective-permute-start | bytes 15826952 | tf_op jit(solution)/shard_map/ppermute | solution.py:90
  222.3 39.1 %collective-permute-start.24 = (bf16[4,1408,128]{2,1,0:T(8,128)(2,1)}, bf16[4,1408,128]{2,1,0:T(8,128)(2,1)S(1)}, u32[]{:S(2)}, u32[]{:S(2)}) collective-permute-start(bf16[4,1408,128]{2,1,0:T(8,128)(2,1)} %get-tuple-element.211), channel_id=1, source_target_pairs={{0,8},{1,9},{2,10},{3,11},{4,12},{5,13},{6,14},{7,15},{8,0},{9,1},... | collective-permute-start | bytes 4325384 | tf_op jit(solution)/shard_map/ppermute | solution.py:90
  229.2 32.1 %collective-permute-start.25 = (bf16[4,1288,128]{2,1,0:T(8,128)(2,1)}, bf16[4,1288,128]{2,1,0:T(8,128)(2,1)}, u32[]{:S(2)}, u32[]{:S(2)}) collective-permute-start(bf16[4,1288,128]{2,1,0:T(8,128)(2,1)} %get-tuple-element.213), channel_id=1, source_target_pairs={{0,16},{1,17},{2,18},{3,19},{4,20},{5,21},{6,22},{7,23},{8,24},{9,... | collective-permute-start | bytes 3956744 | tf_op jit(solution)/shard_map/ppermute | solution.py:90
  261.4 32.7 %collective-permute-start.26 = (bf16[4,1408,128]{2,1,0:T(8,128)(2,1)S(1)}, bf16[4,1408,128]{2,1,0:T(8,128)(2,1)}, u32[]{:S(2)}, u32[]{:S(2)}) collective-permute-start(bf16[4,1408,128]{2,1,0:T(8,128)(2,1)S(1)} %get-tuple-element.157), channel_id=1, source_target_pairs={{0,8},{1,9},{2,10},{3,11},{4,12},{5,13},{6,14},{7,15},{8,0},{9,1},... | collective-permute-start | bytes 4325384 | tf_op jit(solution)/shard_map/ppermute | solution.py:90
  261.5 30.2 %collective-permute-start.27 = (bf16[4,1288,128]{2,1,0:T(8,128)(2,1)}, bf16[4,1288,128]{2,1,0:T(8,128)(2,1)}, u32[]{:S(2)}, u32[]{:S(2)}) collective-permute-start(bf16[4,1288,128]{2,1,0:T(8,128)(2,1)} %get-tuple-element.158), channel_id=1, source_target_pairs={{0,16},{1,17},{2,18},{3,19},{4,20},{5,21},{6,22},{7,23},{8,24},{9,... | collective-permute-start | bytes 3956744 | tf_op jit(solution)/shard_map/ppermute | solution.py:90
  294.1 12.9 %collective-permute-start.28 = (bf16[1536,1024]{1,0:T(8,128)(2,1)}, bf16[1536,1024]{1,0:T(8,128)(2,1)}, u32[]{:S(2)}, u32[]{:S(2)}) collective-permute-start(bf16[1536,1024]{1,0:T(8,128)(2,1)} %get-tuple-element.159), channel_id=1, source_target_pairs={{2,6},{3,7},{4,0},{5,1},{10,14},{11,15},{12,8},{13,9},{18,22},{19,... | collective-permute-start | bytes 9437192 | tf_op jit(solution)/shard_map/ppermute | solution.py:487
  305.5 30.2 %collective-permute-start.30 = (bf16[4,1408,128]{2,1,0:T(8,128)(2,1)}, bf16[4,1408,128]{2,1,0:T(8,128)(2,1)}, u32[]{:S(2)}, u32[]{:S(2)}) collective-permute-start(bf16[4,1408,128]{2,1,0:T(8,128)(2,1)} %fusion), channel_id=1, source_target_pairs={{0,16},{1,17},{2,18},{3,19},{4,20},{5,21},{6,22},{7,23},{8,24},{9,... | collective-permute-start | bytes 4325384 | tf_op jit(solution)/shard_map/ppermute | solution.py:90
  306.6 18.0 %collective-permute-start.31 = (bf16[4,2,72,768]{3,2,1,0:T(8,128)(2,1)}, bf16[4,2,72,768]{3,2,1,0:T(8,128)(2,1)}, u32[]{:S(2)}, u32[]{:S(2)}) collective-permute-start(bf16[4,2,72,768]{3,2,1,0:T(8,128)(2,1)} %pad_maximum_fusion.3), channel_id=1, source_target_pairs={{0,8},{1,9},{2,10},{3,11},{4,12},{5,13},{6,14},{7,15},{8,0},{9,1},... | collective-permute-start | bytes 2654216 | tf_op jit(solution)/shard_map/ppermute | solution.py:90
  311.1 27.5 %collective-permute-start.29 = (bf16[2,384,1024]{2,1,0:T(8,128)(2,1)}, bf16[2,384,1024]{2,1,0:T(8,128)(2,1)}, u32[]{:S(2)}, u32[]{:S(2)}) collective-permute-start(bf16[2,384,1024]{2,1,0:T(8,128)(2,1)} %pad_maximum_fusion), channel_id=1, source_target_pairs={{0,1},{1,0},{6,7},{7,6},{8,9},{9,8},{14,15},{15,14},{16,17},{17,16... | collective-permute-start | bytes 4718600 | tf_op jit(solution)/shard_map/ppermute | solution.py:487
  314.6 38.3 %collective-permute-start.35 = (bf16[4,1288,128]{2,1,0:T(8,128)(2,1)}, bf16[4,1288,128]{2,1,0:T(8,128)(2,1)}, u32[]{:S(2)}, u32[]{:S(2)}) collective-permute-start(bf16[4,1288,128]{2,1,0:T(8,128)(2,1)} %fusion.1), channel_id=1, source_target_pairs={{0,8},{1,9},{2,10},{3,11},{4,12},{5,13},{6,14},{7,15},{8,0},{9,1},... | collective-permute-start | bytes 3956744 | tf_op jit(solution)/shard_map/ppermute | solution.py:90
  326.8 29.1 %collective-permute-start.34 = (bf16[4,1,72,768]{3,2,1,0:T(8,128)(2,1)S(1)}, bf16[4,1,72,768]{3,2,1,0:T(8,128)(2,1)S(1)}, u32[]{:S(2)}, u32[]{:S(2)}) collective-permute-start(bf16[4,1,72,768]{3,2,1,0:T(8,128)(2,1)S(1)} %add_convert_fusion.7), channel_id=1, source_target_pairs={{0,16},{1,17},{2,18},{3,19},{4,20},{5,21},{6,22},{7,23},{8,24},{9,... | collective-permute-start | bytes 1327112 | tf_op jit(solution)/shard_map/ppermute | solution.py:90
  337.6 26.6 %collective-permute-start.33 = (bf16[2,1408,128]{2,1,0:T(8,128)(2,1)S(1)}, bf16[2,1408,128]{2,1,0:T(8,128)(2,1)S(1)}, u32[]{:S(2)}, u32[]{:S(2)}) collective-permute-start(bf16[2,1408,128]{2,1,0:T(8,128)(2,1)S(1)} %fusion.13), channel_id=1, source_target_pairs={{0,1},{1,0},{2,3},{3,2},{4,5},{5,4},{6,7},{7,6},{8,9},{9,8},{10,11... | collective-permute-start | bytes 2162696 | tf_op jit(solution)/shard_map/ppermute | solution.py:90
  340.4 36.3 %collective-permute-start.32 = (bf16[1,384,1024]{2,1,0:T(8,128)(2,1)S(1)}, bf16[1,384,1024]{2,1,0:T(8,128)(2,1)S(1)}, u32[]{:S(2)}, u32[]{:S(2)}) collective-permute-start(bf16[1,384,1024]{2,1,0:T(8,128)(2,1)S(1)} %fusion.8), channel_id=1, source_target_pairs={{0,3},{1,2},{6,5},{7,4},{8,11},{9,10},{14,13},{15,12},{16,19},{17,... | collective-permute-start | bytes 2359304 | tf_op jit(solution)/shard_map/ppermute | solution.py:487
  354.9 26.1 %collective-permute-start.37 = (bf16[2,1288,128]{2,1,0:T(8,128)(2,1)S(1)}, bf16[2,1288,128]{2,1,0:T(8,128)(2,1)S(1)}, u32[]{:S(2)}, u32[]{:S(2)}) collective-permute-start(bf16[2,1288,128]{2,1,0:T(8,128)(2,1)S(1)} %fusion.17), channel_id=1, source_target_pairs={{0,1},{1,0},{2,3},{3,2},{4,5},{5,4},{6,7},{7,6},{8,9},{9,8},{10,11... | collective-permute-start | bytes 1978376 | tf_op jit(solution)/shard_map/ppermute | solution.py:90
  356.0 41.1 %collective-permute-start.36 = (bf16[2,1,72,768]{3,2,1,0:T(8,128)(2,1)S(1)}, bf16[2,1,72,768]{3,2,1,0:T(8,128)(2,1)S(1)}, u32[]{:S(2)}, u32[]{:S(2)}) collective-permute-start(bf16[2,1,72,768]{3,2,1,0:T(8,128)(2,1)S(1)} %add_convert_fusion.8), channel_id=1, source_target_pairs={{0,2},{1,3},{2,0},{3,1},{4,6},{5,7},{6,4},{7,5},{8,10},{9,11},{10,... | collective-permute-start | bytes 663560 | tf_op jit(solution)/shard_map/ppermute | solution.py:90
  365.6 34.5 %collective-permute-start.40 = (bf16[1,1408,128]{2,1,0:T(8,128)(2,1)S(1)}, bf16[1,1408,128]{2,1,0:T(8,128)(2,1)S(1)}, u32[]{:S(2)}, u32[]{:S(2)}) collective-permute-start(bf16[1,1408,128]{2,1,0:T(8,128)(2,1)S(1)} %fusion.44), channel_id=1, source_target_pairs={{0,3},{1,2},{2,1},{3,0},{4,7},{5,6},{6,5},{7,4},{8,11},{9,10},{10,... | collective-permute-start | bytes 1081352 | tf_op jit(solution)/shard_map/ppermute | solution.py:90
  382.6 28.2 %collective-permute-start.39 = (bf16[1,1288,128]{2,1,0:T(8,128)(2,1)S(1)}, bf16[1,1288,128]{2,1,0:T(8,128)(2,1)S(1)}, u32[]{:S(2)}, u32[]{:S(2)}) collective-permute-start(bf16[1,1288,128]{2,1,0:T(8,128)(2,1)S(1)} %fusion.51), channel_id=1, source_target_pairs={{0,3},{1,2},{2,1},{3,0},{4,7},{5,6},{6,5},{7,4},{8,11},{9,10},{10,... | collective-permute-start | bytes 989192 | tf_op jit(solution)/shard_map/ppermute | solution.py:90
  397.2 15.2 %collective-permute-start.38 = (bf16[1,1,72,768]{3,2,1,0:T(8,128)(2,1)S(1)}, bf16[1,1,72,768]{3,2,1,0:T(8,128)(2,1)S(1)}, u32[]{:S(2)}, u32[]{:S(2)}) collective-permute-start(bf16[1,1,72,768]{3,2,1,0:T(8,128)(2,1)S(1)} %get-tuple-element.217), channel_id=1, source_target_pairs={{0,1},{1,0},{2,3},{3,2},{4,5},{5,4},{6,7},{7,6},{8,9},{9,8},{10,11... | collective-permute-start | bytes 331784 | tf_op jit(solution)/shard_map/ppermute | solution.py:90
  401.6 10.9 %collective-permute-start.43 = (bf16[1,1408,128]{2,1,0:T(8,128)(2,1)S(1)}, bf16[1,1408,128]{2,1,0:T(8,128)(2,1)S(1)}, u32[]{:S(2)}, u32[]{:S(2)}) collective-permute-start(bf16[1,1408,128]{2,1,0:T(8,128)(2,1)S(1)} %fusion.41), channel_id=1, source_target_pairs={{0,16},{1,17},{2,18},{3,19},{4,20},{5,21},{6,22},{7,23},{8,24},{9,... | collective-permute-start | bytes 1081352 | tf_op jit(solution)/shard_map/ppermute | solution.py:90
  412.3 9.7 %collective-permute-start.42 = (bf16[1,1288,128]{2,1,0:T(8,128)(2,1)S(1)}, bf16[1,1288,128]{2,1,0:T(8,128)(2,1)S(1)}, u32[]{:S(2)}, u32[]{:S(2)}) collective-permute-start(bf16[1,1288,128]{2,1,0:T(8,128)(2,1)S(1)} %fusion.48), channel_id=1, source_target_pairs={{0,8},{1,9},{2,10},{3,11},{4,12},{5,13},{6,14},{7,15},{8,0},{9,1},... | collective-permute-start | bytes 989192 | tf_op jit(solution)/shard_map/ppermute | solution.py:90
  412.6 24.9 %collective-permute-start.46 = (bf16[2,1408,128]{2,1,0:T(8,128)(2,1)S(1)}, bf16[2,1408,128]{2,1,0:T(8,128)(2,1)S(1)}, u32[]{:S(2)}, u32[]{:S(2)}) collective-permute-start(bf16[2,1408,128]{2,1,0:T(8,128)(2,1)S(1)} %pad_maximum_fusion.6), channel_id=1, source_target_pairs={{0,8},{1,9},{2,10},{3,11},{4,12},{5,13},{6,14},{7,15},{8,0},{9,1},... | collective-permute-start | bytes 2162696 | tf_op jit(solution)/shard_map/ppermute | solution.py:90
  414.7 8.1 %collective-permute-start.41 = (bf16[1,2,72,768]{3,2,1,0:T(8,128)(2,1)S(1)}, bf16[1,2,72,768]{3,2,1,0:T(8,128)(2,1)S(1)}, u32[]{:S(2)}, u32[]{:S(2)}) collective-permute-start(bf16[1,2,72,768]{3,2,1,0:T(8,128)(2,1)S(1)} %pad_maximum_fusion.9), channel_id=1, source_target_pairs={{0,16},{1,17},{2,18},{3,19},{4,20},{5,21},{6,22},{7,23},{8,24},{9,... | collective-permute-start | bytes 663560 | tf_op jit(solution)/shard_map/ppermute | solution.py:90
  422.1 17.3 %collective-permute-start.45 = (bf16[2,1288,128]{2,1,0:T(8,128)(2,1)S(1)}, bf16[2,1288,128]{2,1,0:T(8,128)(2,1)S(1)}, u32[]{:S(2)}, u32[]{:S(2)}) collective-permute-start(bf16[2,1288,128]{2,1,0:T(8,128)(2,1)S(1)} %pad_maximum_fusion.7), channel_id=1, source_target_pairs={{0,16},{1,17},{2,18},{3,19},{4,20},{5,21},{6,22},{7,23},{8,24},{9,... | collective-permute-start | bytes 1978376 | tf_op jit(solution)/shard_map/ppermute | solution.py:90
  424.3 22.7 %collective-permute-start.44 = (bf16[2,2,72,768]{3,2,1,0:T(8,128)(2,1)}, bf16[2,2,72,768]{3,2,1,0:T(8,128)(2,1)}, u32[]{:S(2)}, u32[]{:S(2)}) collective-permute-start(bf16[2,2,72,768]{3,2,1,0:T(8,128)(2,1)} %pad_maximum_fusion.8), channel_id=1, source_target_pairs={{0,8},{1,9},{2,10},{3,11},{4,12},{5,13},{6,14},{7,15},{8,0},{9,1},... | collective-permute-start | bytes 1327112 | tf_op jit(solution)/shard_map/ppermute | solution.py:90
  438.7 13.3 %collective-permute-start.49 = (bf16[4,1408,128]{2,1,0:T(8,128)(2,1)}, bf16[4,1408,128]{2,1,0:T(8,128)(2,1)}, u32[]{:S(2)}, u32[]{:S(2)}) collective-permute-start(bf16[4,1408,128]{2,1,0:T(8,128)(2,1)} %pad_maximum_fusion.1.mine_ref), channel_id=1, source_target_pairs={{0,4},{1,5},{2,6},{3,7},{4,0},{5,1},{6,2},{7,3},{8,12},{9,13},{10,... | collective-permute-start | bytes 4325384 | tf_op jit(solution)/shard_map/ppermute | solution.py:90
  440.7 17.2 %collective-permute-start.48 = (bf16[4,1288,128]{2,1,0:T(8,128)(2,1)}, bf16[4,1288,128]{2,1,0:T(8,128)(2,1)}, u32[]{:S(2)}, u32[]{:S(2)}) collective-permute-start(bf16[4,1288,128]{2,1,0:T(8,128)(2,1)} %pad_maximum_fusion.2.mine_ref), channel_id=1, source_target_pairs={{0,4},{1,5},{2,6},{3,7},{4,0},{5,1},{6,2},{7,3},{8,12},{9,13},{10,... | collective-permute-start | bytes 3956744 | tf_op jit(solution)/shard_map/ppermute | solution.py:90
  449.2 17.5 %collective-permute-start.47 = (bf16[4,2,72,768]{3,2,1,0:T(8,128)(2,1)}, bf16[4,2,72,768]{3,2,1,0:T(8,128)(2,1)}, u32[]{:S(2)}, u32[]{:S(2)}) collective-permute-start(bf16[4,2,72,768]{3,2,1,0:T(8,128)(2,1)} %pad_maximum_fusion.4.mine_ref), channel_id=1, source_target_pairs={{0,4},{1,5},{2,6},{3,7},{4,0},{5,1},{6,2},{7,3},{8,12},{9,13},{10,... | collective-permute-start | bytes 2654216 | tf_op jit(solution)/shard_map/ppermute | solution.py:90
  (39 other events, 493.7 us)

commit v5 on v4

--- a/solution.py
+++ b/solution.py
@@ -24,7 +24,7 @@
 KEY_TILE = 384
 ROW_TILE = 512
 KEY_UNIT = 128
-FEED_TILE = 512
+FEED_TILE = 1024
 
 
 def layer_norm(values, gain, shift):
@@ -631,26 +631,25 @@
     @pl.when(step == pl.num_programs(0) - 1)
     def _():
         grad_ref[...] = acc_ref[...].astype(jnp.bfloat16)
-        ones = jnp.ones((8, width), jnp.float32)
-        gain = jnp.zeros(gain_ref.shape, jnp.float32)
-        shift = jnp.zeros(shift_ref.shape, jnp.float32)
+        gain = jnp.zeros((acc_ref.shape[0], width), jnp.float32)
+        shift = jnp.zeros((acc_ref.shape[0], width), jnp.float32)
         for kind, weight_ref in enumerate((wq_ref, wk_ref, wv_ref)):
             cols = slice(kind * width, (kind + 1) * width)
             weight = weight_ref[...].astype(jnp.float32)
-            gain += exact_nt_dot(ones, weight * acc_ref[:, cols])
-            shift += exact_nt_dot(sum_ref[:, cols], weight)
-        gain_ref[...] = gain
-        shift_ref[...] = shift
-
-
-def exact_nt_dot(left, right):
-    return lax.dot_general(
-        left,
-        right,
-        (((1,), (1,)), ((), ())),
-        precision=lax.Precision.HIGHEST,
-        preferred_element_type=jnp.float32,
-    )
+            gain += weight * acc_ref[:, cols]
+            shift += weight * sum_ref[:1, cols]
+        gain_ref[...] = lane_sums(gain)
+        shift_ref[...] = lane_sums(shift)
+
+
+def lane_sums(value):
+    ones = jnp.ones((8, value.shape[1]), jnp.bfloat16)
+    total = jnp.zeros((8, value.shape[0]), jnp.float32)
+    for _ in range(3):
+        part = value.astype(jnp.bfloat16)
+        value = value - part.astype(jnp.float32)
+        total += nt_dot(ones, part)
+    return total
 
 
 def project_back(normed, grads, weights):

time: 482 us -> 478 us (level)
  Pallas kernels: 158 us -> 144 us
  waiting for transfers between devices: 98.6 us -> 107 us
    ppermute x32, waiting for transfers between devices: 75 us -> 83.3 us  [swapped(): return lax.ppermute(value, MESH_AXES, pairs)]
  transfers between devices with their start and end apart: 50 -> 50, of which waited for: 20 -> 22; matrix products, arithmetic and copies ran while one was open for 14% -> 14% of each run, Pallas kernels for 20% -> 18%
where the time goes in v5:
time: 478 us; the launch traced here: 470 us
  Pallas kernels  144 us (30%)
  starting transfers between devices  111 us (23%)
  waiting for transfers between devices  107 us (22%)
  other arithmetic  69.6 us (15%)
  local copies, waits for them, and re-layouts  15.9 us (3%)
  matrix products  15.3 us (3%)
  between operations  7.37 us (2%)
    ppermute x32, waiting for transfers between devices, swapped(): return lax.ppermute(value, MESH_AXES, pairs)  83.3 us
    ppermute x32, starting transfers between devices, swapped(): return lax.ppermute(value, MESH_AXES, pairs)  61.4 us
    ppermute x18, starting transfers between devices, moved(): return lax.ppermute(value, MESH_AXES, pairs)  49.5 us
    convert_element_type x15, other arithmetic, summed(): return total.astype(jnp.bfloat16)  30.2 us
    pallas_call x1, Pallas kernels, attention_backward(): pl.pallas_call(backward_kernel, out_shape=(out, out, out), grid_spec=pltp...  26 us
    pallas_call x2, Pallas kernels, weight_pieces(): pl.pallas_call(partial(weights_kernel, lefts_at, ready), grid_spec=pltpu....  25.1 us
    ppermute x18, waiting for transfers between devices, moved(): return lax.ppermute(value, MESH_AXES, pairs)  23.9 us
    pallas_call x1, Pallas kernels, feed_back(): pl.pallas_call(feed_back_kernel, grid_spec=pltpu.PrefetchScalarGridSpec(n...  18.1 us
  transfers between devices with their start and end apart: 50, of which 22 were waited for; matrix products, arithmetic and copies ran while one was open for 14% of the time, Pallas kernels for 18%

profile of v5, /device:TPU:17, one launch (start us, length us, event | category | flops | bytes accessed | tf_op | source)
XLA Modules:
  0.0 470.5 jit_solution(12066896057044020558)
XLA Ops:
  3.5 3.2 collective-permute-start.3
  8.0 4.1 collective-permute-start.2
  12.1 8.5 %collective-permute-done.3.refs_2_ = bf16[392,1024]{1,0:T(8,128)(2,1)} collective-permute-done((bf16[392,1024]{1,0:T(8,128)(2,1)S(1)}, bf16[392,1024]{1,0:T(8,128)(2,1)}, u32[]{:S(2)}, u32[]{:S(2)}) %collective-permute-start.3) | collective-permute-done | bytes 802848 | tf_op jit(solution)/shard_map/ppermute | solution.py:487
  20.6 2.2 collective-permute-start.4
  22.8 5.5 %collective-permute-done.refs_0_ = bf16[392,1024]{1,0:T(8,128)(2,1)} collective-permute-done((bf16[392,1024]{1,0:T(8,128)(2,1)S(1)}, bf16[392,1024]{1,0:T(8,128)(2,1)}, u32[]{:S(2)}, u32[]{:S(2)}) %collective-permute-start) | collective-permute-done | bytes 802848 | tf_op jit(solution)/shard_map/ppermute | solution.py:487
  32.8 6.7 %entry.2 = (bf16[1536,1024]{1,0:T(8,128)(2,1)}, bf16[1536,256]{1,0:T(8,128)(2,1)}, bf16[1536,256]{1,0:T(8,128)(2,1)}, bf16[1536,256]{1,0:T(8,128)(2,1)}) custom-call(s32[4]{0:T(128)} %add_add_fusion.5.place_ref, bf16[392,1024]{1,0:T(8,128)(2,1)} %copy-done.9, bf16[392,1024]{1,0:T(8,128)(2,1)} %collective-permute-done.2.refs_1_, ...), custom_call_target="tpu_custom_call" | custom-call | tf_op jit(solution)/shard_map/entry/pallas_call | solution.py:598
  42.9 2.2 collective-permute-start.6
  54.2 6.7 %entry.3 = (bf16[1536,1024]{1,0:T(8,128)(2,1)}, bf16[1536,256]{1,0:T(8,128)(2,1)}, bf16[1536,256]{1,0:T(8,128)(2,1)}, bf16[1536,256]{1,0:T(8,128)(2,1)}) custom-call(s32[4]{0:T(128)} %add_add_fusion.6.place_ref, bf16[392,1024]{1,0:T(8,128)(2,1)} %collective-permute-done.refs_0_, ...), custom_call_target="tpu_custom_call", output_to_operand_aliasing={{0}: (10, {}), {1}: (11, {}), {2}: (12, {}), {3}: (13, {})} | custom-call | tf_op jit(solution)/shard_map/entry/pallas_call | solution.py:598
  60.9 16.9 %attention_forward.1 = (bf16[1536,256]{1,0:T(8,128)(2,1)}, f32[4,1536]{1,0:T(4,128)}) custom-call(s32[6,2]{1,0:T(8,128)} %copy.73.range_ref, bf16[1536,256]{1,0:T(8,128)(2,1)} %get-tuple-element.147.q_ref, bf16[1536,256]{1,0:T(8,128)(2,1)} %get-tuple-element.116.k_ref, bf16[1536,256]{1,0:T(8,128)(2,1)} %get-tuple-element.117.v_ref, ...), custom_call_target="tpu_custom_call" | custom-call | tf_op jit(solution)/shard_map/attention_forward/pallas_call | solution.py:358
  83.1 5.1 %collective-permute-start.7 = (bf16[384,256]{1,0:T(8,128)(2,1)S(1)}, bf16[384,256]{1,0:T(8,128)(2,1)S(1)}, u32[]{:S(2)}, u32[]{:S(2)}) collective-permute-start(bf16[384,256]{1,0:T(8,128)(2,1)S(1)} %get-tuple-element.229), channel_id=1, source_target_pairs={{0,0},{1,2},{2,4},{3,6},{4,1},{5,3},{6,5},{7,7},{8,8},{9,10},{10,1... | collective-permute-start | bytes 589832 | tf_op jit(solution)/shard_map/ppermute | solution.py:487
  90.6 6.3 %collective-permute-done.7.refs_0_ = bf16[384,256]{1,0:T(8,128)(2,1)S(1)} collective-permute-done((bf16[384,256]{1,0:T(8,128)(2,1)S(1)}, bf16[384,256]{1,0:T(8,128)(2,1)S(1)}, u32[]{:S(2)}, u32[]{:S(2)}) %collective-permute-start.7) | collective-permute-done | bytes 196640 | tf_op jit(solution)/shard_map/ppermute | solution.py:487
  97.5 17.7 %feed_forward.1 = (bf16[384,1024]{1,0:T(8,128)(2,1)}, f32[384,1024]{1,0:T(8,128)}, bf16[384,1024]{1,0:T(8,128)(2,1)}, bf16[384,4096]{1,0:T(8,128)(2,1)}, bf16[38...) custom-call(s32[4]{0:T(128)} %get-tuple-element.259.head_ref, bf16[384,256]{1,0:T(8,128)(2,1)} %copy-done.26, ...), custom_call_target="tpu_custom_call" | custom-call | tf_op jit(solution)/shard_map/feed_forward/pallas_call | solution.py:807
  128.4 3.5 collective-permute-start.13
  142.8 2.8 fusion.31
  147.7 2.5 fusion.136
  150.1 12.6 %weight_pieces.2 = (bf16[4,4,1408,128]{3,2,1,0:T(8,128)(2,1)}, bf16[4,4,1408,128]{3,2,1,0:T(8,128)(2,1)}) custom-call(s32[4]{0:T(128)} %get-tuple-element.260.place_ref, s32[8]{0:T(128)} %stack.150.column_ref, bf16[384,4096]{1,0:T(8,128)(2,1)} %get-tuple-element.121.refs_0_, bf16[384,1024]{1,0:T(8,128)(2,1)} %get-tuple-element.120.refs_1_, ...), custom_call_target="tpu_custom_call" | custom-call | tf_op jit(solution)/shard_map/weight_pieces/pallas_call | solution.py:1029
  162.8 3.5 collective-permute-start.23
  170.1 18.1 %feed_back.1 = (bf16[384,4096]{1,0:T(8,128)(2,1)}, f32[1,4096]{1,0:T(1,128)}, f32[384,1024]{1,0:T(8,128)}, bf16[384,1024]{1,0:T(8,128)(2,1)}, f32[1,1024]{1,0:T(...) custom-call(s32[4]{0:T(128)} %get-tuple-element.259.head_ref, ...), custom_call_target="tpu_custom_call" | custom-call | tf_op jit(solution)/shard_map/feed_back/pallas_call | solution.py:890
  190.4 3.5 collective-permute-start.18
  199.9 12.5 %weight_pieces.3 = (bf16[4,4,1288,128]{3,2,1,0:T(8,128)(2,1)}, bf16[4,4,1288,128]{3,2,1,0:T(8,128)(2,1)}) custom-call(s32[4]{0:T(128)} %get-tuple-element.260.place_ref, s32[8]{0:T(128)} %stack.156.column_ref, bf16[384,1024]{1,0:T(8,128)(2,1)} %get-tuple-element.128.refs_0_, bf16[384,1024]{1,0:T(8,128)(2,1)} %get-tuple-element.129.refs_1_, ...), custom_call_target="tpu_custom_call" | custom-call | tf_op jit(solution)/shard_map/weight_pieces/pallas_call | solution.py:1029
  214.1 4.7 fusion.11
  218.9 3.8 collective-permute-done.22
  222.6 2.6 fusion.15
  226.4 26.0 %attention_backward.1 = (bf16[1536,256]{1,0:T(8,128)(2,1)}, bf16[1536,256]{1,0:T(8,128)(2,1)}, bf16[1536,256]{1,0:T(8,128)(2,1)}) custom-call(s32[6,2]{1,0:T(8,128)} %copy.73.range_ref, s32[4]{0:T(128)} %pad_add_fusion.3.row_ref, bf16[1536,256]{1,0:T(8,128)(2,1)} %get-tuple-element.147.q_ref, bf16[1536,256]{1,0:T(8,128)(2,1)} %get-tuple-element.118.ctx_ref, ...), custom_call_target="tpu_custom_call" | custom-call | tf_op jit(solution)/shard_map/attention_backward/pallas_call | solution.py:427
  252.3 3.9 collective-permute-done.25
  257.9 11.0 %project_back.1 = (bf16[1536,1024]{1,0:T(8,128)(2,1)}, bf16[1024,768]{1,0:T(8,128)(2,1)}, f32[8,1024]{1,0:T(8,128)}, f32[8,1024]{1,0:T(8,128)}) custom-call(s32[1]{0:T(128)} %bitcast.9.place_ref, bf16[1536,1024]{1,0:T(8,128)(2,1)} %get-tuple-element.127.normed_ref, bf16[1536,256]{1,0:T(8,128)(2,1)} %get-tuple-element.152.dq_ref, ...), custom_call_target="tpu_custom_call" | custom-call | tf_op jit(solution)/shard_map/project_back/pallas_call | solution.py:661
  268.9 17.2 %collective-permute-done.27 = bf16[4,1288,128]{2,1,0:T(8,128)(2,1)} collective-permute-done((bf16[4,1288,128]{2,1,0:T(8,128)(2,1)}, bf16[4,1288,128]{2,1,0:T(8,128)(2,1)}, u32[]{:S(2)}, u32[]{:S(2)}) %collective-permute-start.27) | collective-permute-done | bytes 1318944 | tf_op jit(solution)/shard_map/ppermute | solution.py:90
  286.1 2.2 collective-permute-done.26
  292.1 3.7 fusion.1
  295.8 4.0 fusion
  299.9 2.1 collective-permute-start.30
  307.6 3.3 collective-permute-start.29
  312.0 9.1 %collective-permute-done.31 = bf16[4,2,72,768]{3,2,1,0:T(8,128)(2,1)} collective-permute-done((bf16[4,2,72,768]{3,2,1,0:T(8,128)(2,1)}, bf16[4,2,72,768]{3,2,1,0:T(8,128)(2,1)}, u32[]{:S(2)}, u32[]{:S(2)}) %collective-permute-start.31) | collective-permute-done | bytes 884768 | tf_op jit(solution)/shard_map/ppermute | solution.py:90
  323.4 7.4 %collective-permute-done.30 = bf16[4,1408,128]{2,1,0:T(8,128)(2,1)} collective-permute-done((bf16[4,1408,128]{2,1,0:T(8,128)(2,1)}, bf16[4,1408,128]{2,1,0:T(8,128)(2,1)}, u32[]{:S(2)}, u32[]{:S(2)}) %collective-permute-start.30) | collective-permute-done | bytes 1441824 | tf_op jit(solution)/shard_map/ppermute | solution.py:90
  335.9 10.8 %collective-permute-start.32 = (bf16[1,384,1024]{2,1,0:T(8,128)(2,1)S(1)}, bf16[1,384,1024]{2,1,0:T(8,128)(2,1)S(1)}, u32[]{:S(2)}, u32[]{:S(2)}) collective-permute-start(bf16[1,384,1024]{2,1,0:T(8,128)(2,1)S(1)} %fusion.8), channel_id=1, source_target_pairs={{0,3},{1,2},{6,5},{7,4},{8,11},{9,10},{14,13},{15,12},{16,19},{17,... | collective-permute-start | bytes 2359304 | tf_op jit(solution)/shard_map/ppermute | solution.py:487
  346.7 2.6 collective-permute-done.35
  352.9 7.0 %collective-permute-start.36 = (bf16[2,1,72,768]{3,2,1,0:T(8,128)(2,1)S(1)}, bf16[2,1,72,768]{3,2,1,0:T(8,128)(2,1)S(1)}, u32[]{:S(2)}, u32[]{:S(2)}) collective-permute-start(bf16[2,1,72,768]{3,2,1,0:T(8,128)(2,1)S(1)} %add_convert_fusion.8), channel_id=1, source_target_pairs={{0,2},{1,3},{2,0},{3,1},{4,6},{5,7},{6,4},{7,5},{8,10},{9,11},{10,... | collective-permute-start | bytes 663560 | tf_op jit(solution)/shard_map/ppermute | solution.py:90
  361.4 10.2 %collective-permute-start.40 = (bf16[1,1408,128]{2,1,0:T(8,128)(2,1)S(1)}, bf16[1,1408,128]{2,1,0:T(8,128)(2,1)S(1)}, u32[]{:S(2)}, u32[]{:S(2)}) collective-permute-start(bf16[1,1408,128]{2,1,0:T(8,128)(2,1)S(1)} %fusion.44), channel_id=1, source_target_pairs={{0,3},{1,2},{2,1},{3,0},{4,7},{5,6},{6,5},{7,4},{8,11},{9,10},{10,... | collective-permute-start | bytes 1081352 | tf_op jit(solution)/shard_map/ppermute | solution.py:90
  371.6 2.3 fusion.6
  373.9 4.1 collective-permute-done.37
  379.5 13.0 %collective-permute-start.39 = (bf16[1,1288,128]{2,1,0:T(8,128)(2,1)S(1)}, bf16[1,1288,128]{2,1,0:T(8,128)(2,1)S(1)}, u32[]{:S(2)}, u32[]{:S(2)}) collective-permute-start(bf16[1,1288,128]{2,1,0:T(8,128)(2,1)S(1)} %fusion.51), channel_id=1, source_target_pairs={{0,3},{1,2},{2,1},{3,0},{4,7},{5,6},{6,5},{7,4},{8,11},{9,10},{10,... | collective-permute-start | bytes 989192 | tf_op jit(solution)/shard_map/ppermute | solution.py:90
  392.6 2.9 collective-permute-start.38
  397.3 9.1 %collective-permute-done.39 = bf16[1,1288,128]{2,1,0:T(8,128)(2,1)S(1)} collective-permute-done((bf16[1,1288,128]{2,1,0:T(8,128)(2,1)S(1)}, bf16[1,1288,128]{2,1,0:T(8,128)(2,1)S(1)}, u32[]{:S(2)}, u32[]{:S(2)}) %collective-permute-start.39) | collective-permute-done | bytes 329760 | tf_op jit(solution)/shard_map/ppermute | solution.py:90
  410.7 6.8 %collective-permute-done.42 = bf16[1,1288,128]{2,1,0:T(8,128)(2,1)S(1)} collective-permute-done((bf16[1,1288,128]{2,1,0:T(8,128)(2,1)S(1)}, bf16[1,1288,128]{2,1,0:T(8,128)(2,1)S(1)}, u32[]{:S(2)}, u32[]{:S(2)}) %collective-permute-start.42) | collective-permute-done | bytes 329760 | tf_op jit(solution)/shard_map/ppermute | solution.py:90
  420.4 12.6 %collective-permute-done.46 = bf16[2,1408,128]{2,1,0:T(8,128)(2,1)S(1)} collective-permute-done((bf16[2,1408,128]{2,1,0:T(8,128)(2,1)S(1)}, bf16[2,1408,128]{2,1,0:T(8,128)(2,1)S(1)}, u32[]{:S(2)}, u32[]{:S(2)}) %collective-permute-start.46) | collective-permute-done | bytes 720928 | tf_op jit(solution)/shard_map/ppermute | solution.py:90
  447.7 5.8 %spread_columns.2 = (f32[1024,1024]{1,0:T(8,128)}, f32[256,1024]{1,0:T(8,128)}, f32[128,1024]{1,0:T(8,128)}) custom-call(s32[8]{0:T(128)} %get-tuple-element.261.table_ref, bf16[4,1408,128]{2,1,0:T(8,128)(2,1)} %pad_maximum_fusion.1.mine_ref, bf16[4,1408,128]{2,1,0:T(8,128)(2,1)} %collective-permute-done.49.other_ref), custom_call_target="tpu_custom_call" | custom-call | tf_op jit(solution)/shard_map/spread_columns/pallas_call | solution.py:215
  453.5 5.6 %spread_columns.3 = (f32[256,4096]{1,0:T(8,128)}, f32[256,1024]{1,0:T(8,128)}, f32[8,1024]{1,0:T(8,128)}) custom-call(s32[8]{0:T(128)} %get-tuple-element.262.table_ref, bf16[4,1288,128]{2,1,0:T(8,128)(2,1)} %pad_maximum_fusion.2.mine_ref, bf16[4,1288,128]{2,1,0:T(8,128)(2,1)} %collective-permute-done.48.other_ref), custom_call_target="tpu_custom_call" | custom-call | tf_op jit(solution)/shard_map/spread_columns/pallas_call | solution.py:215
  464.5 4.6 spread_heads.1
  (292 shorter events, 120.8 us)
Async XLA Ops:
  3.5 17.1 %collective-permute-start.3 = (bf16[392,1024]{1,0:T(8,128)(2,1)S(1)}, bf16[392,1024]{1,0:T(8,128)(2,1)}, u32[]{:S(2)}, u32[]{:S(2)}) collective-permute-start(bf16[392,1024]{1,0:T(8,128)(2,1)S(1)} %fusion.27.refs_0_), channel_id=1, source_target_pairs={{0,1},{1,0},{6,7},{7,6},{8,9},{9,8},{14,15},{15,14},{16,17},{17,16... | collective-permute-start | bytes 2408456 | tf_op jit(solution)/shard_map/ppermute | solution.py:487
  6.7 21.6 %collective-permute-start = (bf16[392,1024]{1,0:T(8,128)(2,1)S(1)}, bf16[392,1024]{1,0:T(8,128)(2,1)}, u32[]{:S(2)}, u32[]{:S(2)}) collective-permute-start(bf16[392,1024]{1,0:T(8,128)(2,1)S(1)} %fusion.27.refs_0_), channel_id=1, source_target_pairs={{2,1},{3,0},{4,7},{5,6},{10,9},{11,8},{12,15},{13,14},{18,17},{19,... | collective-permute-start | bytes 2408456 | tf_op jit(solution)/shard_map/ppermute | solution.py:487
  8.0 24.8 %collective-permute-start.2 = (bf16[392,1024]{1,0:T(8,128)(2,1)S(1)}, bf16[392,1024]{1,0:T(8,128)(2,1)}, u32[]{:S(2)}, u32[]{:S(2)}) collective-permute-start(bf16[392,1024]{1,0:T(8,128)(2,1)S(1)} %fusion.27.refs_0_), channel_id=1, source_target_pairs={{0,4},{1,5},{6,2},{7,3},{8,12},{9,13},{14,10},{15,11},{16,20},{17,... | collective-permute-start | bytes 2408456 | tf_op jit(solution)/shard_map/ppermute | solution.py:487
  20.6 12.2 %collective-permute-start.4 = (bf16[392,1024]{1,0:T(8,128)(2,1)}, bf16[392,1024]{1,0:T(8,128)(2,1)}, u32[]{:S(2)}, u32[]{:S(2)}) collective-permute-start(bf16[392,1024]{1,0:T(8,128)(2,1)} %collective-permute-done.3.refs_2_), channel_id=1, source_target_pairs={{0,4},{1,5},{6,2},{7,3},{8,12},{9,13},{14,10},{15,11},{16,20},{17,... | collective-permute-start | bytes 2408456 | tf_op jit(solution)/shard_map/ppermute | solution.py:487
  28.3 13.2 %collective-permute-start.1 = (bf16[392,1024]{1,0:T(8,128)(2,1)}, bf16[392,1024]{1,0:T(8,128)(2,1)}, u32[]{:S(2)}, u32[]{:S(2)}) collective-permute-start(bf16[392,1024]{1,0:T(8,128)(2,1)} %collective-permute-done.refs_0_), channel_id=1, source_target_pairs={{0,1},{1,0},{6,7},{7,6},{8,9},{9,8},{14,15},{15,14},{16,17},{17,16... | collective-permute-start | bytes 2408456 | tf_op jit(solution)/shard_map/ppermute | solution.py:487
  41.5 7.6 %collective-permute-start.5 = (bf16[392,1024]{1,0:T(8,128)(2,1)}, bf16[392,1024]{1,0:T(8,128)(2,1)S(1)}, u32[]{:S(2)}, u32[]{:S(2)}) collective-permute-start(bf16[392,1024]{1,0:T(8,128)(2,1)} %collective-permute-done.1.refs_2_), channel_id=1, source_target_pairs={{0,4},{1,5},{6,2},{7,3},{8,12},{9,13},{14,10},{15,11},{16,20},{17,... | collective-permute-start | bytes 2408456 | tf_op jit(solution)/shard_map/ppermute | solution.py:487
  42.9 7.0 %collective-permute-start.6 = (bf16[392,1024]{1,0:T(8,128)(2,1)}, bf16[392,1024]{1,0:T(8,128)(2,1)}, u32[]{:S(2)}, u32[]{:S(2)}) collective-permute-start(bf16[392,1024]{1,0:T(8,128)(2,1)} %collective-permute-done.refs_0_), channel_id=1, source_target_pairs={{0,4},{1,5},{6,2},{7,3},{8,12},{9,13},{14,10},{15,11},{16,20},{17,... | collective-permute-start | bytes 2408456 | tf_op jit(solution)/shard_map/ppermute | solution.py:487
  79.0 10.8 %collective-permute-start.10 = (bf16[384,256]{1,0:T(8,128)(2,1)S(1)}, bf16[384,256]{1,0:T(8,128)(2,1)S(1)}, u32[]{:S(2)}, u32[]{:S(2)}) collective-permute-start(bf16[384,256]{1,0:T(8,128)(2,1)S(1)} %get-tuple-element.226), channel_id=1, source_target_pairs={{0,3},{1,1},{2,7},{3,5},{4,0},{5,2},{6,4},{7,6},{8,11},{9,9},{10,1... | collective-permute-start | bytes 589832 | tf_op jit(solution)/shard_map/ppermute | solution.py:487
  81.0 9.6 %collective-permute-start.9 = (bf16[384,256]{1,0:T(8,128)(2,1)S(1)}, bf16[384,256]{1,0:T(8,128)(2,1)S(1)}, u32[]{:S(2)}, u32[]{:S(2)}) collective-permute-start(bf16[384,256]{1,0:T(8,128)(2,1)S(1)} %get-tuple-element.227), channel_id=1, source_target_pairs={{0,2},{1,0},{2,6},{3,4},{4,3},{5,1},{6,7},{7,5},{8,10},{9,8},{10,1... | collective-permute-start | bytes 589832 | tf_op jit(solution)/shard_map/ppermute | solution.py:487
  82.5 8.1 %collective-permute-start.8 = (bf16[384,256]{1,0:T(8,128)(2,1)S(1)}, bf16[384,256]{1,0:T(8,128)(2,1)S(1)}, u32[]{:S(2)}, u32[]{:S(2)}) collective-permute-start(bf16[384,256]{1,0:T(8,128)(2,1)S(1)} %get-tuple-element.228), channel_id=1, source_target_pairs={{0,1},{1,3},{2,5},{3,7},{4,2},{5,0},{6,6},{7,4},{8,9},{9,11},{10,1... | collective-permute-start | bytes 589832 | tf_op jit(solution)/shard_map/ppermute | solution.py:487
  83.1 13.7 %collective-permute-start.7 = (bf16[384,256]{1,0:T(8,128)(2,1)S(1)}, bf16[384,256]{1,0:T(8,128)(2,1)S(1)}, u32[]{:S(2)}, u32[]{:S(2)}) collective-permute-start(bf16[384,256]{1,0:T(8,128)(2,1)S(1)} %get-tuple-element.229), channel_id=1, source_target_pairs={{0,0},{1,2},{2,4},{3,6},{4,1},{5,3},{6,5},{7,7},{8,8},{9,10},{10,1... | collective-permute-start | bytes 589832 | tf_op jit(solution)/shard_map/ppermute | solution.py:487
  122.3 2.9 collective-permute-start.11
  126.5 6.6 %collective-permute-start.14 = (f32[640]{0:T(1024)S(1)}, f32[640]{0:T(1024)S(1)}, u32[]{:S(2)}, u32[]{:S(2)}) collective-permute-start(f32[640]{0:T(1024)S(1)} %fusion.127), channel_id=1, source_target_pairs={{0,24},{1,25},{2,26},{3,27},{4,28},{5,29},{6,30},{7,31},{8,16},{9,... | collective-permute-start | bytes 7688 | tf_op jit(solution)/shard_map/ppermute | solution.py:90
  128.4 4.7 %collective-permute-start.13 = (f32[640]{0:T(1024)S(1)}, f32[640]{0:T(1024)S(1)}, u32[]{:S(2)}, u32[]{:S(2)}) collective-permute-start(f32[640]{0:T(1024)S(1)} %fusion.127), channel_id=1, source_target_pairs={{0,16},{1,17},{2,18},{3,19},{4,20},{5,21},{6,22},{7,23},{8,24},{9,... | collective-permute-start | bytes 7688 | tf_op jit(solution)/shard_map/ppermute | solution.py:90
  134.3 3.6 collective-permute-start.17
  136.0 2.9 collective-permute-start.15
  162.8 51.3 %collective-permute-start.23 = (bf16[4,4,1408,128]{3,2,1,0:T(8,128)(2,1)}, bf16[4,4,1408,128]{3,2,1,0:T(8,128)(2,1)}, u32[]{:S(2)}, u32[]{:S(2)}) collective-permute-start(bf16[4,4,1408,128]{3,2,1,0:T(8,128)(2,1)} %get-tuple-element.122), channel_id=1, source_target_pairs={{0,4},{1,5},{2,6},{3,7},{4,0},{5,1},{6,2},{7,3},{8,12},{9,13},{10,... | collective-permute-start | bytes 17301512 | tf_op jit(solution)/shard_map/ppermute | solution.py:90
  190.4 22.0 %collective-permute-start.18 = (bf16[384,256]{1,0:T(8,128)(2,1)}, bf16[384,256]{1,0:T(8,128)(2,1)S(1)}, u32[]{:S(2)}, u32[]{:S(2)}) collective-permute-start(bf16[384,256]{1,0:T(8,128)(2,1)} %get-tuple-element.131), channel_id=1, source_target_pairs={{0,0},{1,4},{2,1},{3,5},{4,2},{5,6},{6,3},{7,7},{8,8},{9,12},{10,9... | collective-permute-start | bytes 589832 | tf_op jit(solution)/shard_map/ppermute | solution.py:487
  193.9 18.5 %collective-permute-start.19 = (bf16[384,256]{1,0:T(8,128)(2,1)}, bf16[384,256]{1,0:T(8,128)(2,1)S(1)}, u32[]{:S(2)}, u32[]{:S(2)}) collective-permute-start(bf16[384,256]{1,0:T(8,128)(2,1)} %get-tuple-element.132), channel_id=1, source_target_pairs={{0,5},{1,0},{2,4},{3,1},{4,7},{5,2},{6,6},{7,3},{8,13},{9,8},{10,1... | collective-permute-start | bytes 589832 | tf_op jit(solution)/shard_map/ppermute | solution.py:487
  195.5 16.9 %collective-permute-start.20 = (bf16[384,256]{1,0:T(8,128)(2,1)}, bf16[384,256]{1,0:T(8,128)(2,1)S(1)}, u32[]{:S(2)}, u32[]{:S(2)}) collective-permute-start(bf16[384,256]{1,0:T(8,128)(2,1)} %get-tuple-element.133), channel_id=1, source_target_pairs={{0,1},{1,5},{2,0},{3,4},{4,3},{5,7},{6,2},{7,6},{8,9},{9,13},{10,8... | collective-permute-start | bytes 589832 | tf_op jit(solution)/shard_map/ppermute | solution.py:487
  196.9 15.5 %collective-permute-start.21 = (bf16[384,256]{1,0:T(8,128)(2,1)}, bf16[384,256]{1,0:T(8,128)(2,1)S(1)}, u32[]{:S(2)}, u32[]{:S(2)}) collective-permute-start(bf16[384,256]{1,0:T(8,128)(2,1)} %get-tuple-element.134), channel_id=1, source_target_pairs={{0,4},{1,1},{2,5},{3,0},{4,6},{5,3},{6,7},{7,2},{8,12},{9,9},{10,1... | collective-permute-start | bytes 589832 | tf_op jit(solution)/shard_map/ppermute | solution.py:487
  212.4 10.2 %collective-permute-start.22 = (bf16[4,4,1288,128]{3,2,1,0:T(8,128)(2,1)}, bf16[4,4,1288,128]{3,2,1,0:T(8,128)(2,1)S(1)}, u32[]{:S(2)}, u32[]{:S(2)}) collective-permute-start(bf16[4,4,1288,128]{3,2,1,0:T(8,128)(2,1)} %get-tuple-element.143), channel_id=1, source_target_pairs={{0,4},{1,5},{2,6},{3,7},{4,0},{5,1},{6,2},{7,3},{8,12},{9,13},{10,... | collective-permute-start | bytes 15826952 | tf_op jit(solution)/shard_map/ppermute | solution.py:90
  218.8 37.5 %collective-permute-start.24 = (bf16[4,1408,128]{2,1,0:T(8,128)(2,1)}, bf16[4,1408,128]{2,1,0:T(8,128)(2,1)S(1)}, u32[]{:S(2)}, u32[]{:S(2)}) collective-permute-start(bf16[4,1408,128]{2,1,0:T(8,128)(2,1)} %get-tuple-element.211), channel_id=1, source_target_pairs={{0,8},{1,9},{2,10},{3,11},{4,12},{5,13},{6,14},{7,15},{8,0},{9,1},... | collective-permute-start | bytes 4325384 | tf_op jit(solution)/shard_map/ppermute | solution.py:90
  225.8 30.5 %collective-permute-start.25 = (bf16[4,1288,128]{2,1,0:T(8,128)(2,1)}, bf16[4,1288,128]{2,1,0:T(8,128)(2,1)}, u32[]{:S(2)}, u32[]{:S(2)}) collective-permute-start(bf16[4,1288,128]{2,1,0:T(8,128)(2,1)} %get-tuple-element.213), channel_id=1, source_target_pairs={{0,16},{1,17},{2,18},{3,19},{4,20},{5,21},{6,22},{7,23},{8,24},{9,... | collective-permute-start | bytes 3956744 | tf_op jit(solution)/shard_map/ppermute | solution.py:90
  256.3 32.0 %collective-permute-start.26 = (bf16[4,1408,128]{2,1,0:T(8,128)(2,1)S(1)}, bf16[4,1408,128]{2,1,0:T(8,128)(2,1)}, u32[]{:S(2)}, u32[]{:S(2)}) collective-permute-start(bf16[4,1408,128]{2,1,0:T(8,128)(2,1)S(1)} %get-tuple-element.157), channel_id=1, source_target_pairs={{0,8},{1,9},{2,10},{3,11},{4,12},{5,13},{6,14},{7,15},{8,0},{9,1},... | collective-permute-start | bytes 4325384 | tf_op jit(solution)/shard_map/ppermute | solution.py:90
  256.3 29.8 %collective-permute-start.27 = (bf16[4,1288,128]{2,1,0:T(8,128)(2,1)}, bf16[4,1288,128]{2,1,0:T(8,128)(2,1)}, u32[]{:S(2)}, u32[]{:S(2)}) collective-permute-start(bf16[4,1288,128]{2,1,0:T(8,128)(2,1)} %get-tuple-element.158), channel_id=1, source_target_pairs={{0,16},{1,17},{2,18},{3,19},{4,20},{5,21},{6,22},{7,23},{8,24},{9,... | collective-permute-start | bytes 3956744 | tf_op jit(solution)/shard_map/ppermute | solution.py:90
  288.2 15.2 %collective-permute-start.28 = (bf16[1536,1024]{1,0:T(8,128)(2,1)}, bf16[1536,1024]{1,0:T(8,128)(2,1)}, u32[]{:S(2)}, u32[]{:S(2)}) collective-permute-start(bf16[1536,1024]{1,0:T(8,128)(2,1)} %get-tuple-element.159), channel_id=1, source_target_pairs={{2,6},{3,7},{4,0},{5,1},{10,14},{11,15},{12,8},{13,9},{18,22},{19,... | collective-permute-start | bytes 9437192 | tf_op jit(solution)/shard_map/ppermute | solution.py:487
  299.9 30.9 %collective-permute-start.30 = (bf16[4,1408,128]{2,1,0:T(8,128)(2,1)}, bf16[4,1408,128]{2,1,0:T(8,128)(2,1)}, u32[]{:S(2)}, u32[]{:S(2)}) collective-permute-start(bf16[4,1408,128]{2,1,0:T(8,128)(2,1)} %fusion), channel_id=1, source_target_pairs={{0,16},{1,17},{2,18},{3,19},{4,20},{5,21},{6,22},{7,23},{8,24},{9,... | collective-permute-start | bytes 4325384 | tf_op jit(solution)/shard_map/ppermute | solution.py:90
  303.1 17.9 %collective-permute-start.31 = (bf16[4,2,72,768]{3,2,1,0:T(8,128)(2,1)}, bf16[4,2,72,768]{3,2,1,0:T(8,128)(2,1)}, u32[]{:S(2)}, u32[]{:S(2)}) collective-permute-start(bf16[4,2,72,768]{3,2,1,0:T(8,128)(2,1)} %pad_maximum_fusion.3), channel_id=1, source_target_pairs={{0,8},{1,9},{2,10},{3,11},{4,12},{5,13},{6,14},{7,15},{8,0},{9,1},... | collective-permute-start | bytes 2654216 | tf_op jit(solution)/shard_map/ppermute | solution.py:90
  307.6 26.6 %collective-permute-start.29 = (bf16[2,384,1024]{2,1,0:T(8,128)(2,1)}, bf16[2,384,1024]{2,1,0:T(8,128)(2,1)}, u32[]{:S(2)}, u32[]{:S(2)}) collective-permute-start(bf16[2,384,1024]{2,1,0:T(8,128)(2,1)} %pad_maximum_fusion), channel_id=1, source_target_pairs={{0,1},{1,0},{6,7},{7,6},{8,9},{9,8},{14,15},{15,14},{16,17},{17,16... | collective-permute-start | bytes 4718600 | tf_op jit(solution)/shard_map/ppermute | solution.py:487
  311.6 37.7 %collective-permute-start.35 = (bf16[4,1288,128]{2,1,0:T(8,128)(2,1)}, bf16[4,1288,128]{2,1,0:T(8,128)(2,1)}, u32[]{:S(2)}, u32[]{:S(2)}) collective-permute-start(bf16[4,1288,128]{2,1,0:T(8,128)(2,1)} %fusion.1), channel_id=1, source_target_pairs={{0,8},{1,9},{2,10},{3,11},{4,12},{5,13},{6,14},{7,15},{8,0},{9,1},... | collective-permute-start | bytes 3956744 | tf_op jit(solution)/shard_map/ppermute | solution.py:90
  323.2 29.6 %collective-permute-start.34 = (bf16[4,1,72,768]{3,2,1,0:T(8,128)(2,1)S(1)}, bf16[4,1,72,768]{3,2,1,0:T(8,128)(2,1)S(1)}, u32[]{:S(2)}, u32[]{:S(2)}) collective-permute-start(bf16[4,1,72,768]{3,2,1,0:T(8,128)(2,1)S(1)} %add_convert_fusion.7), channel_id=1, source_target_pairs={{0,16},{1,17},{2,18},{3,19},{4,20},{5,21},{6,22},{7,23},{8,24},{9,... | collective-permute-start | bytes 1327112 | tf_op jit(solution)/shard_map/ppermute | solution.py:90
  332.7 27.2 %collective-permute-start.33 = (bf16[2,1408,128]{2,1,0:T(8,128)(2,1)S(1)}, bf16[2,1408,128]{2,1,0:T(8,128)(2,1)S(1)}, u32[]{:S(2)}, u32[]{:S(2)}) collective-permute-start(bf16[2,1408,128]{2,1,0:T(8,128)(2,1)S(1)} %fusion.13), channel_id=1, source_target_pairs={{0,1},{1,0},{2,3},{3,2},{4,5},{5,4},{6,7},{7,6},{8,9},{9,8},{10,11... | collective-permute-start | bytes 2162696 | tf_op jit(solution)/shard_map/ppermute | solution.py:90
  335.9 35.7 %collective-permute-start.32 = (bf16[1,384,1024]{2,1,0:T(8,128)(2,1)S(1)}, bf16[1,384,1024]{2,1,0:T(8,128)(2,1)S(1)}, u32[]{:S(2)}, u32[]{:S(2)}) collective-permute-start(bf16[1,384,1024]{2,1,0:T(8,128)(2,1)S(1)} %fusion.8), channel_id=1, source_target_pairs={{0,3},{1,2},{6,5},{7,4},{8,11},{9,10},{14,13},{15,12},{16,19},{17,... | collective-permute-start | bytes 2359304 | tf_op jit(solution)/shard_map/ppermute | solution.py:487
  351.3 26.6 %collective-permute-start.37 = (bf16[2,1288,128]{2,1,0:T(8,128)(2,1)S(1)}, bf16[2,1288,128]{2,1,0:T(8,128)(2,1)S(1)}, u32[]{:S(2)}, u32[]{:S(2)}) collective-permute-start(bf16[2,1288,128]{2,1,0:T(8,128)(2,1)S(1)} %fusion.17), channel_id=1, source_target_pairs={{0,1},{1,0},{2,3},{3,2},{4,5},{5,4},{6,7},{7,6},{8,9},{9,8},{10,11... | collective-permute-start | bytes 1978376 | tf_op jit(solution)/shard_map/ppermute | solution.py:90
  352.9 39.6 %collective-permute-start.36 = (bf16[2,1,72,768]{3,2,1,0:T(8,128)(2,1)S(1)}, bf16[2,1,72,768]{3,2,1,0:T(8,128)(2,1)S(1)}, u32[]{:S(2)}, u32[]{:S(2)}) collective-permute-start(bf16[2,1,72,768]{3,2,1,0:T(8,128)(2,1)S(1)} %add_convert_fusion.8), channel_id=1, source_target_pairs={{0,2},{1,3},{2,0},{3,1},{4,6},{5,7},{6,4},{7,5},{8,10},{9,11},{10,... | collective-permute-start | bytes 663560 | tf_op jit(solution)/shard_map/ppermute | solution.py:90
  361.4 34.2 %collective-permute-start.40 = (bf16[1,1408,128]{2,1,0:T(8,128)(2,1)S(1)}, bf16[1,1408,128]{2,1,0:T(8,128)(2,1)S(1)}, u32[]{:S(2)}, u32[]{:S(2)}) collective-permute-start(bf16[1,1408,128]{2,1,0:T(8,128)(2,1)S(1)} %fusion.44), channel_id=1, source_target_pairs={{0,3},{1,2},{2,1},{3,0},{4,7},{5,6},{6,5},{7,4},{8,11},{9,10},{10,... | collective-permute-start | bytes 1081352 | tf_op jit(solution)/shard_map/ppermute | solution.py:90
  379.5 26.9 %collective-permute-start.39 = (bf16[1,1288,128]{2,1,0:T(8,128)(2,1)S(1)}, bf16[1,1288,128]{2,1,0:T(8,128)(2,1)S(1)}, u32[]{:S(2)}, u32[]{:S(2)}) collective-permute-start(bf16[1,1288,128]{2,1,0:T(8,128)(2,1)S(1)} %fusion.51), channel_id=1, source_target_pairs={{0,3},{1,2},{2,1},{3,0},{4,7},{5,6},{6,5},{7,4},{8,11},{9,10},{10,... | collective-permute-start | bytes 989192 | tf_op jit(solution)/shard_map/ppermute | solution.py:90
  392.6 15.5 %collective-permute-start.38 = (bf16[1,1,72,768]{3,2,1,0:T(8,128)(2,1)S(1)}, bf16[1,1,72,768]{3,2,1,0:T(8,128)(2,1)S(1)}, u32[]{:S(2)}, u32[]{:S(2)}) collective-permute-start(bf16[1,1,72,768]{3,2,1,0:T(8,128)(2,1)S(1)} %get-tuple-element.217), channel_id=1, source_target_pairs={{0,1},{1,0},{2,3},{3,2},{4,5},{5,4},{6,7},{7,6},{8,9},{9,8},{10,11... | collective-permute-start | bytes 331784 | tf_op jit(solution)/shard_map/ppermute | solution.py:90
  397.0 11.2 %collective-permute-start.43 = (bf16[1,1408,128]{2,1,0:T(8,128)(2,1)S(1)}, bf16[1,1408,128]{2,1,0:T(8,128)(2,1)S(1)}, u32[]{:S(2)}, u32[]{:S(2)}) collective-permute-start(bf16[1,1408,128]{2,1,0:T(8,128)(2,1)S(1)} %fusion.41), channel_id=1, source_target_pairs={{0,16},{1,17},{2,18},{3,19},{4,20},{5,21},{6,22},{7,23},{8,24},{9,... | collective-permute-start | bytes 1081352 | tf_op jit(solution)/shard_map/ppermute | solution.py:90
  408.0 9.5 %collective-permute-start.42 = (bf16[1,1288,128]{2,1,0:T(8,128)(2,1)S(1)}, bf16[1,1288,128]{2,1,0:T(8,128)(2,1)S(1)}, u32[]{:S(2)}, u32[]{:S(2)}) collective-permute-start(bf16[1,1288,128]{2,1,0:T(8,128)(2,1)S(1)} %fusion.48), channel_id=1, source_target_pairs={{0,8},{1,9},{2,10},{3,11},{4,12},{5,13},{6,14},{7,15},{8,0},{9,1},... | collective-permute-start | bytes 989192 | tf_op jit(solution)/shard_map/ppermute | solution.py:90
  408.2 24.7 %collective-permute-start.46 = (bf16[2,1408,128]{2,1,0:T(8,128)(2,1)S(1)}, bf16[2,1408,128]{2,1,0:T(8,128)(2,1)S(1)}, u32[]{:S(2)}, u32[]{:S(2)}) collective-permute-start(bf16[2,1408,128]{2,1,0:T(8,128)(2,1)S(1)} %pad_maximum_fusion.6), channel_id=1, source_target_pairs={{0,8},{1,9},{2,10},{3,11},{4,12},{5,13},{6,14},{7,15},{8,0},{9,1},... | collective-permute-start | bytes 2162696 | tf_op jit(solution)/shard_map/ppermute | solution.py:90
  410.4 8.5 %collective-permute-start.41 = (bf16[1,2,72,768]{3,2,1,0:T(8,128)(2,1)S(1)}, bf16[1,2,72,768]{3,2,1,0:T(8,128)(2,1)S(1)}, u32[]{:S(2)}, u32[]{:S(2)}) collective-permute-start(bf16[1,2,72,768]{3,2,1,0:T(8,128)(2,1)S(1)} %pad_maximum_fusion.9), channel_id=1, source_target_pairs={{0,16},{1,17},{2,18},{3,19},{4,20},{5,21},{6,22},{7,23},{8,24},{9,... | collective-permute-start | bytes 663560 | tf_op jit(solution)/shard_map/ppermute | solution.py:90
  417.6 17.7 %collective-permute-start.45 = (bf16[2,1288,128]{2,1,0:T(8,128)(2,1)S(1)}, bf16[2,1288,128]{2,1,0:T(8,128)(2,1)S(1)}, u32[]{:S(2)}, u32[]{:S(2)}) collective-permute-start(bf16[2,1288,128]{2,1,0:T(8,128)(2,1)S(1)} %pad_maximum_fusion.7), channel_id=1, source_target_pairs={{0,16},{1,17},{2,18},{3,19},{4,20},{5,21},{6,22},{7,23},{8,24},{9,... | collective-permute-start | bytes 1978376 | tf_op jit(solution)/shard_map/ppermute | solution.py:90
  420.4 22.2 %collective-permute-start.44 = (bf16[2,2,72,768]{3,2,1,0:T(8,128)(2,1)}, bf16[2,2,72,768]{3,2,1,0:T(8,128)(2,1)}, u32[]{:S(2)}, u32[]{:S(2)}) collective-permute-start(bf16[2,2,72,768]{3,2,1,0:T(8,128)(2,1)} %pad_maximum_fusion.8), channel_id=1, source_target_pairs={{0,8},{1,9},{2,10},{3,11},{4,12},{5,13},{6,14},{7,15},{8,0},{9,1},... | collective-permute-start | bytes 1327112 | tf_op jit(solution)/shard_map/ppermute | solution.py:90
  434.2 13.5 %collective-permute-start.49 = (bf16[4,1408,128]{2,1,0:T(8,128)(2,1)}, bf16[4,1408,128]{2,1,0:T(8,128)(2,1)}, u32[]{:S(2)}, u32[]{:S(2)}) collective-permute-start(bf16[4,1408,128]{2,1,0:T(8,128)(2,1)} %pad_maximum_fusion.1.mine_ref), channel_id=1, source_target_pairs={{0,4},{1,5},{2,6},{3,7},{4,0},{5,1},{6,2},{7,3},{8,12},{9,13},{10,... | collective-permute-start | bytes 4325384 | tf_op jit(solution)/shard_map/ppermute | solution.py:90
  436.5 17.0 %collective-permute-start.48 = (bf16[4,1288,128]{2,1,0:T(8,128)(2,1)}, bf16[4,1288,128]{2,1,0:T(8,128)(2,1)}, u32[]{:S(2)}, u32[]{:S(2)}) collective-permute-start(bf16[4,1288,128]{2,1,0:T(8,128)(2,1)} %pad_maximum_fusion.2.mine_ref), channel_id=1, source_target_pairs={{0,4},{1,5},{2,6},{3,7},{4,0},{5,1},{6,2},{7,3},{8,12},{9,13},{10,... | collective-permute-start | bytes 3956744 | tf_op jit(solution)/shard_map/ppermute | solution.py:90
  444.6 17.7 %collective-permute-start.47 = (bf16[4,2,72,768]{3,2,1,0:T(8,128)(2,1)}, bf16[4,2,72,768]{3,2,1,0:T(8,128)(2,1)}, u32[]{:S(2)}, u32[]{:S(2)}) collective-permute-start(bf16[4,2,72,768]{3,2,1,0:T(8,128)(2,1)} %pad_maximum_fusion.4.mine_ref), channel_id=1, source_target_pairs={{0,4},{1,5},{2,6},{3,7},{4,0},{5,1},{6,2},{7,3},{8,12},{9,13},{10,... | collective-permute-start | bytes 2654216 | tf_op jit(solution)/shard_map/ppermute | solution.py:90
  (39 other events, 481.8 us)

commit v6 on v5

--- a/solution.py
+++ b/solution.py
@@ -539,7 +539,7 @@
         for mask in pair_masks():
             pieces += [(paired(piece, mask), place ^ mask) for piece, place in pieces]
         pieces = [
-            (piece, from_home(tied(piece, held) if mirrored else piece), blocks - 1 - (block ^ place) if mirrored else block ^ place)
+            (piece, from_home(tied(piece, held) if mirrored and place else piece), blocks - 1 - (block ^ place) if mirrored else block ^ place)
             for piece, place in pieces
         ]
         held = use(pieces, held)

time: 478 us -> 478 us (level)
  waiting for transfers between devices: 107 us -> 92.6 us
  starting transfers between devices: 111 us -> 125 us
    ppermute x32, starting transfers between devices: 61.4 us -> 72.7 us  [swapped(): return lax.ppermute(value, MESH_AXES, pairs)]
    ppermute x32, waiting for transfers between devices: 83.3 us -> 72.2 us  [swapped(): return lax.ppermute(value, MESH_AXES, pairs)]
  transfers between devices with their start and end apart: 50 -> 50, of which waited for: 22 -> 20; matrix products, arithmetic and copies ran while one was open for 14% -> 14% of each run, Pallas kernels for 18% -> 18%
where the time goes in v6:
time: 478 us; the launch traced here: 469 us
  Pallas kernels  144 us (30%)
  starting transfers between devices  125 us (26%)
  waiting for transfers between devices  92.6 us (19%)
  other arithmetic  69.6 us (15%)
  local copies, waits for them, and re-layouts  15.5 us (3%)
  matrix products  15.3 us (3%)
  between operations  7.36 us (2%)
    ppermute x32, starting transfers between devices, swapped(): return lax.ppermute(value, MESH_AXES, pairs)  72.7 us
    ppermute x32, waiting for transfers between devices, swapped(): return lax.ppermute(value, MESH_AXES, pairs)  72.2 us
    ppermute x18, starting transfers between devices, moved(): return lax.ppermute(value, MESH_AXES, pairs)  52.1 us
    convert_element_type x15, other arithmetic, summed(): return total.astype(jnp.bfloat16)  30.2 us
    pallas_call x1, Pallas kernels, attention_backward(): pl.pallas_call(backward_kernel, out_shape=(out, out, out), grid_spec=pltp...  26 us
    pallas_call x2, Pallas kernels, weight_pieces(): pl.pallas_call(partial(weights_kernel, lefts_at, ready), grid_spec=pltpu....  25.1 us
    ppermute x18, waiting for transfers between devices, moved(): return lax.ppermute(value, MESH_AXES, pairs)  20.4 us
    pallas_call x1, Pallas kernels, feed_back(): pl.pallas_call(feed_back_kernel, grid_spec=pltpu.PrefetchScalarGridSpec(n...  18.1 us
  transfers between devices with their start and end apart: 50, of which 20 were waited for; matrix products, arithmetic and copies ran while one was open for 14% of the time, Pallas kernels for 18%

profile of v6, /device:TPU:17, one launch (start us, length us, event | category | flops | bytes accessed | tf_op | source)
XLA Modules:
  0.0 469.4 jit_solution(10025991156352093176)
XLA Ops:
  3.5 3.2 collective-permute-start.3
  8.0 4.1 collective-permute-start.2
  12.1 8.5 %collective-permute-done.3.refs_2_ = bf16[392,1024]{1,0:T(8,128)(2,1)} collective-permute-done((bf16[392,1024]{1,0:T(8,128)(2,1)S(1)}, bf16[392,1024]{1,0:T(8,128)(2,1)}, u32[]{:S(2)}, u32[]{:S(2)}) %collective-permute-start.3) | collective-permute-done | bytes 802848 | tf_op jit(solution)/shard_map/ppermute | solution.py:487
  20.6 2.2 collective-permute-start.4
  22.8 5.5 %collective-permute-done.refs_0_ = bf16[392,1024]{1,0:T(8,128)(2,1)} collective-permute-done((bf16[392,1024]{1,0:T(8,128)(2,1)S(1)}, bf16[392,1024]{1,0:T(8,128)(2,1)}, u32[]{:S(2)}, u32[]{:S(2)}) %collective-permute-start) | collective-permute-done | bytes 802848 | tf_op jit(solution)/shard_map/ppermute | solution.py:487
  32.2 2.2 collective-permute-start.6
  35.0 6.7 %entry.2 = (bf16[1536,1024]{1,0:T(8,128)(2,1)}, bf16[1536,256]{1,0:T(8,128)(2,1)}, bf16[1536,256]{1,0:T(8,128)(2,1)}, bf16[1536,256]{1,0:T(8,128)(2,1)}) custom-call(s32[4]{0:T(128)} %add_add_fusion.5.place_ref, bf16[392,1024]{1,0:T(8,128)(2,1)} %copy-done.9, bf16[392,1024]{1,0:T(8,128)(2,1)} %collective-permute-done.2.refs_1_, ...), custom_call_target="tpu_custom_call" | custom-call | tf_op jit(solution)/shard_map/entry/pallas_call | solution.py:598
  52.2 6.7 %entry.3 = (bf16[1536,1024]{1,0:T(8,128)(2,1)}, bf16[1536,256]{1,0:T(8,128)(2,1)}, bf16[1536,256]{1,0:T(8,128)(2,1)}, bf16[1536,256]{1,0:T(8,128)(2,1)}) custom-call(s32[4]{0:T(128)} %add_add_fusion.6.place_ref, bf16[392,1024]{1,0:T(8,128)(2,1)} %collective-permute-done.refs_0_, ...), custom_call_target="tpu_custom_call", output_to_operand_aliasing={{0}: (10, {}), {1}: (11, {}), {2}: (12, {}), {3}: (13, {})} | custom-call | tf_op jit(solution)/shard_map/entry/pallas_call | solution.py:598
  58.9 16.9 %attention_forward.1 = (bf16[1536,256]{1,0:T(8,128)(2,1)}, f32[4,1536]{1,0:T(4,128)}) custom-call(s32[6,2]{1,0:T(8,128)} %copy.73.range_ref, bf16[1536,256]{1,0:T(8,128)(2,1)} %get-tuple-element.145.q_ref, bf16[1536,256]{1,0:T(8,128)(2,1)} %get-tuple-element.114.k_ref, bf16[1536,256]{1,0:T(8,128)(2,1)} %get-tuple-element.115.v_ref, ...), custom_call_target="tpu_custom_call" | custom-call | tf_op jit(solution)/shard_map/attention_forward/pallas_call | solution.py:358
  81.2 6.6 %collective-permute-start.7 = (bf16[384,256]{1,0:T(8,128)(2,1)S(1)}, bf16[384,256]{1,0:T(8,128)(2,1)S(1)}, u32[]{:S(2)}, u32[]{:S(2)}) collective-permute-start(bf16[384,256]{1,0:T(8,128)(2,1)S(1)} %get-tuple-element.227), channel_id=1, source_target_pairs={{0,0},{1,2},{2,4},{3,6},{4,1},{5,3},{6,5},{7,7},{8,8},{9,10},{10,1... | collective-permute-start | bytes 589832 | tf_op jit(solution)/shard_map/ppermute | solution.py:487
  89.1 5.7 %collective-permute-done.7.refs_0_ = bf16[384,256]{1,0:T(8,128)(2,1)S(1)} collective-permute-done((bf16[384,256]{1,0:T(8,128)(2,1)S(1)}, bf16[384,256]{1,0:T(8,128)(2,1)S(1)}, u32[]{:S(2)}, u32[]{:S(2)}) %collective-permute-start.7) | collective-permute-done | bytes 196640 | tf_op jit(solution)/shard_map/ppermute | solution.py:487
  95.5 17.7 %feed_forward.1 = (bf16[384,1024]{1,0:T(8,128)(2,1)}, f32[384,1024]{1,0:T(8,128)}, bf16[384,1024]{1,0:T(8,128)(2,1)}, bf16[384,4096]{1,0:T(8,128)(2,1)}, bf16[38...) custom-call(s32[4]{0:T(128)} %get-tuple-element.257.head_ref, bf16[384,256]{1,0:T(8,128)(2,1)} %copy-done.26, ...), custom_call_target="tpu_custom_call" | custom-call | tf_op jit(solution)/shard_map/feed_forward/pallas_call | solution.py:807
  113.2 2.1 convolution_add_fusion
  120.3 2.9 collective-permute-start.11
  125.4 5.1 %collective-permute-start.14 = (f32[640]{0:T(1024)S(1)}, f32[640]{0:T(1024)S(1)}, u32[]{:S(2)}, u32[]{:S(2)}) collective-permute-start(f32[640]{0:T(1024)S(1)} %fusion.127), channel_id=1, source_target_pairs={{0,24},{1,25},{2,26},{3,27},{4,28},{5,29},{6,30},{7,31},{8,16},{9,... | collective-permute-start | bytes 7688 | tf_op jit(solution)/shard_map/ppermute | solution.py:90
  134.3 2.2 collective-permute-start.15
  141.5 2.8 fusion.31
  146.4 2.5 fusion.136
  148.9 12.6 %weight_pieces.2 = (bf16[4,4,1408,128]{3,2,1,0:T(8,128)(2,1)}, bf16[4,4,1408,128]{3,2,1,0:T(8,128)(2,1)}) custom-call(s32[4]{0:T(128)} %get-tuple-element.258.place_ref, s32[8]{0:T(128)} %stack.150.column_ref, bf16[384,4096]{1,0:T(8,128)(2,1)} %get-tuple-element.119.refs_0_, bf16[384,1024]{1,0:T(8,128)(2,1)} %get-tuple-element.118.refs_1_, ...), custom_call_target="tpu_custom_call" | custom-call | tf_op jit(solution)/shard_map/weight_pieces/pallas_call | solution.py:1029
  161.5 3.2 collective-permute-start.23
  168.5 18.1 %feed_back.1 = (bf16[384,4096]{1,0:T(8,128)(2,1)}, f32[1,4096]{1,0:T(1,128)}, f32[384,1024]{1,0:T(8,128)}, bf16[384,1024]{1,0:T(8,128)(2,1)}, f32[1,1024]{1,0:T(...) custom-call(s32[4]{0:T(128)} %get-tuple-element.257.head_ref, ...), custom_call_target="tpu_custom_call" | custom-call | tf_op jit(solution)/shard_map/feed_back/pallas_call | solution.py:890
  188.8 3.5 collective-permute-start.18
  198.3 12.5 %weight_pieces.3 = (bf16[4,4,1288,128]{3,2,1,0:T(8,128)(2,1)}, bf16[4,4,1288,128]{3,2,1,0:T(8,128)(2,1)}) custom-call(s32[4]{0:T(128)} %get-tuple-element.258.place_ref, s32[8]{0:T(128)} %stack.156.column_ref, bf16[384,1024]{1,0:T(8,128)(2,1)} %get-tuple-element.126.refs_0_, bf16[384,1024]{1,0:T(8,128)(2,1)} %get-tuple-element.127.refs_1_, ...), custom_call_target="tpu_custom_call" | custom-call | tf_op jit(solution)/shard_map/weight_pieces/pallas_call | solution.py:1029
  212.1 4.7 fusion.11
  217.2 3.5 collective-permute-done.22
  220.7 2.6 fusion.15
  226.1 26.0 %attention_backward.1 = (bf16[1536,256]{1,0:T(8,128)(2,1)}, bf16[1536,256]{1,0:T(8,128)(2,1)}, bf16[1536,256]{1,0:T(8,128)(2,1)}) custom-call(s32[6,2]{1,0:T(8,128)} %copy.73.range_ref, s32[4]{0:T(128)} %pad_add_fusion.3.row_ref, bf16[1536,256]{1,0:T(8,128)(2,1)} %get-tuple-element.145.q_ref, bf16[1536,256]{1,0:T(8,128)(2,1)} %get-tuple-element.116.ctx_ref, ...), custom_call_target="tpu_custom_call" | custom-call | tf_op jit(solution)/shard_map/attention_backward/pallas_call | solution.py:427
  252.1 2.6 collective-permute-done.25
  256.2 11.0 %project_back.1 = (bf16[1536,1024]{1,0:T(8,128)(2,1)}, bf16[1024,768]{1,0:T(8,128)(2,1)}, f32[8,1024]{1,0:T(8,128)}, f32[8,1024]{1,0:T(8,128)}) custom-call(s32[1]{0:T(128)} %bitcast.9.place_ref, bf16[1536,1024]{1,0:T(8,128)(2,1)} %get-tuple-element.125.normed_ref, bf16[1536,256]{1,0:T(8,128)(2,1)} %get-tuple-element.150.dq_ref, ...), custom_call_target="tpu_custom_call" | custom-call | tf_op jit(solution)/shard_map/project_back/pallas_call | solution.py:661
  267.2 18.4 %collective-permute-done.27 = bf16[4,1288,128]{2,1,0:T(8,128)(2,1)} collective-permute-done((bf16[4,1288,128]{2,1,0:T(8,128)(2,1)}, bf16[4,1288,128]{2,1,0:T(8,128)(2,1)}, u32[]{:S(2)}, u32[]{:S(2)}) %collective-permute-start.27) | collective-permute-done | bytes 1318944 | tf_op jit(solution)/shard_map/ppermute | solution.py:90
  290.9 3.7 fusion.1
  294.6 4.0 fusion
  305.2 3.7 collective-permute-start.29
  310.4 7.7 %collective-permute-done.31 = bf16[4,2,72,768]{3,2,1,0:T(8,128)(2,1)} collective-permute-done((bf16[4,2,72,768]{3,2,1,0:T(8,128)(2,1)}, bf16[4,2,72,768]{3,2,1,0:T(8,128)(2,1)}, u32[]{:S(2)}, u32[]{:S(2)}) %collective-permute-start.31) | collective-permute-done | bytes 884768 | tf_op jit(solution)/shard_map/ppermute | solution.py:90
  321.0 7.4 %collective-permute-done.30 = bf16[4,1408,128]{2,1,0:T(8,128)(2,1)} collective-permute-done((bf16[4,1408,128]{2,1,0:T(8,128)(2,1)}, bf16[4,1408,128]{2,1,0:T(8,128)(2,1)}, u32[]{:S(2)}, u32[]{:S(2)}) %collective-permute-start.30) | collective-permute-done | bytes 1441824 | tf_op jit(solution)/shard_map/ppermute | solution.py:90
  334.0 11.6 %collective-permute-start.32 = (bf16[1,384,1024]{2,1,0:T(8,128)(2,1)S(1)}, bf16[1,384,1024]{2,1,0:T(8,128)(2,1)S(1)}, u32[]{:S(2)}, u32[]{:S(2)}) collective-permute-start(bf16[1,384,1024]{2,1,0:T(8,128)(2,1)S(1)} %fusion.8), channel_id=1, source_target_pairs={{0,3},{1,2},{6,5},{7,4},{8,11},{9,10},{14,13},{15,12},{16,19},{17,... | collective-permute-start | bytes 2359304 | tf_op jit(solution)/shard_map/ppermute | solution.py:487
  350.3 9.5 %collective-permute-start.36 = (bf16[2,1,72,768]{3,2,1,0:T(8,128)(2,1)S(1)}, bf16[2,1,72,768]{3,2,1,0:T(8,128)(2,1)S(1)}, u32[]{:S(2)}, u32[]{:S(2)}) collective-permute-start(bf16[2,1,72,768]{3,2,1,0:T(8,128)(2,1)S(1)} %add_convert_fusion.8), channel_id=1, source_target_pairs={{0,2},{1,3},{2,0},{3,1},{4,6},{5,7},{6,4},{7,5},{8,10},{9,11},{10,... | collective-permute-start | bytes 663560 | tf_op jit(solution)/shard_map/ppermute | solution.py:90
  361.2 10.2 %collective-permute-start.40 = (bf16[1,1408,128]{2,1,0:T(8,128)(2,1)S(1)}, bf16[1,1408,128]{2,1,0:T(8,128)(2,1)S(1)}, u32[]{:S(2)}, u32[]{:S(2)}) collective-permute-start(bf16[1,1408,128]{2,1,0:T(8,128)(2,1)S(1)} %fusion.44), channel_id=1, source_target_pairs={{0,3},{1,2},{2,1},{3,0},{4,7},{5,6},{6,5},{7,4},{8,11},{9,10},{10,... | collective-permute-start | bytes 1081352 | tf_op jit(solution)/shard_map/ppermute | solution.py:90
  371.5 2.3 fusion.6
  375.8 15.6 %collective-permute-start.39 = (bf16[1,1288,128]{2,1,0:T(8,128)(2,1)S(1)}, bf16[1,1288,128]{2,1,0:T(8,128)(2,1)S(1)}, u32[]{:S(2)}, u32[]{:S(2)}) collective-permute-start(bf16[1,1288,128]{2,1,0:T(8,128)(2,1)S(1)} %fusion.51), channel_id=1, source_target_pairs={{0,3},{1,2},{2,1},{3,0},{4,7},{5,6},{6,5},{7,4},{8,11},{9,10},{10,... | collective-permute-start | bytes 989192 | tf_op jit(solution)/shard_map/ppermute | solution.py:90
  391.5 2.9 collective-permute-start.38
  397.2 8.2 %collective-permute-done.39 = bf16[1,1288,128]{2,1,0:T(8,128)(2,1)S(1)} collective-permute-done((bf16[1,1288,128]{2,1,0:T(8,128)(2,1)S(1)}, bf16[1,1288,128]{2,1,0:T(8,128)(2,1)S(1)}, u32[]{:S(2)}, u32[]{:S(2)}) %collective-permute-start.39) | collective-permute-done | bytes 329760 | tf_op jit(solution)/shard_map/ppermute | solution.py:90
  410.5 5.8 %collective-permute-done.42 = bf16[1,1288,128]{2,1,0:T(8,128)(2,1)S(1)} collective-permute-done((bf16[1,1288,128]{2,1,0:T(8,128)(2,1)S(1)}, bf16[1,1288,128]{2,1,0:T(8,128)(2,1)S(1)}, u32[]{:S(2)}, u32[]{:S(2)}) %collective-permute-start.42) | collective-permute-done | bytes 329760 | tf_op jit(solution)/shard_map/ppermute | solution.py:90
  420.0 11.8 %collective-permute-done.46 = bf16[2,1408,128]{2,1,0:T(8,128)(2,1)S(1)} collective-permute-done((bf16[2,1408,128]{2,1,0:T(8,128)(2,1)S(1)}, bf16[2,1408,128]{2,1,0:T(8,128)(2,1)S(1)}, u32[]{:S(2)}, u32[]{:S(2)}) %collective-permute-start.46) | collective-permute-done | bytes 720928 | tf_op jit(solution)/shard_map/ppermute | solution.py:90
  441.4 2.1 pad_maximum_fusion.4.mine_ref
  446.6 5.8 %spread_columns.2 = (f32[1024,1024]{1,0:T(8,128)}, f32[256,1024]{1,0:T(8,128)}, f32[128,1024]{1,0:T(8,128)}) custom-call(s32[8]{0:T(128)} %get-tuple-element.259.table_ref, bf16[4,1408,128]{2,1,0:T(8,128)(2,1)} %pad_maximum_fusion.1.mine_ref, bf16[4,1408,128]{2,1,0:T(8,128)(2,1)} %collective-permute-done.49.other_ref), custom_call_target="tpu_custom_call" | custom-call | tf_op jit(solution)/shard_map/spread_columns/pallas_call | solution.py:215
  452.4 5.6 %spread_columns.3 = (f32[256,4096]{1,0:T(8,128)}, f32[256,1024]{1,0:T(8,128)}, f32[8,1024]{1,0:T(8,128)}) custom-call(s32[8]{0:T(128)} %get-tuple-element.260.table_ref, bf16[4,1288,128]{2,1,0:T(8,128)(2,1)} %pad_maximum_fusion.2.mine_ref, bf16[4,1288,128]{2,1,0:T(8,128)(2,1)} %collective-permute-done.48.other_ref), custom_call_target="tpu_custom_call" | custom-call | tf_op jit(solution)/shard_map/spread_columns/pallas_call | solution.py:215
  463.4 4.6 spread_heads.1
  (292 shorter events, 117.2 us)
Async XLA Ops:
  3.5 17.1 %collective-permute-start.3 = (bf16[392,1024]{1,0:T(8,128)(2,1)S(1)}, bf16[392,1024]{1,0:T(8,128)(2,1)}, u32[]{:S(2)}, u32[]{:S(2)}) collective-permute-start(bf16[392,1024]{1,0:T(8,128)(2,1)S(1)} %fusion.27.refs_0_), channel_id=1, source_target_pairs={{0,1},{1,0},{6,7},{7,6},{8,9},{9,8},{14,15},{15,14},{16,17},{17,16... | collective-permute-start | bytes 2408456 | tf_op jit(solution)/shard_map/ppermute | solution.py:487
  6.7 21.6 %collective-permute-start = (bf16[392,1024]{1,0:T(8,128)(2,1)S(1)}, bf16[392,1024]{1,0:T(8,128)(2,1)}, u32[]{:S(2)}, u32[]{:S(2)}) collective-permute-start(bf16[392,1024]{1,0:T(8,128)(2,1)S(1)} %fusion.27.refs_0_), channel_id=1, source_target_pairs={{2,1},{3,0},{4,7},{5,6},{10,9},{11,8},{12,15},{13,14},{18,17},{19,... | collective-permute-start | bytes 2408456 | tf_op jit(solution)/shard_map/ppermute | solution.py:487
  8.0 27.0 %collective-permute-start.2 = (bf16[392,1024]{1,0:T(8,128)(2,1)S(1)}, bf16[392,1024]{1,0:T(8,128)(2,1)}, u32[]{:S(2)}, u32[]{:S(2)}) collective-permute-start(bf16[392,1024]{1,0:T(8,128)(2,1)S(1)} %fusion.27.refs_0_), channel_id=1, source_target_pairs={{0,4},{1,5},{6,2},{7,3},{8,12},{9,13},{14,10},{15,11},{16,20},{17,... | collective-permute-start | bytes 2408456 | tf_op jit(solution)/shard_map/ppermute | solution.py:487
  20.6 14.3 %collective-permute-start.4 = (bf16[392,1024]{1,0:T(8,128)(2,1)}, bf16[392,1024]{1,0:T(8,128)(2,1)}, u32[]{:S(2)}, u32[]{:S(2)}) collective-permute-start(bf16[392,1024]{1,0:T(8,128)(2,1)} %collective-permute-done.3.refs_2_), channel_id=1, source_target_pairs={{0,4},{1,5},{6,2},{7,3},{8,12},{9,13},{14,10},{15,11},{16,20},{17,... | collective-permute-start | bytes 2408456 | tf_op jit(solution)/shard_map/ppermute | solution.py:487
  28.3 13.4 %collective-permute-start.1 = (bf16[392,1024]{1,0:T(8,128)(2,1)}, bf16[392,1024]{1,0:T(8,128)(2,1)}, u32[]{:S(2)}, u32[]{:S(2)}) collective-permute-start(bf16[392,1024]{1,0:T(8,128)(2,1)} %collective-permute-done.refs_0_), channel_id=1, source_target_pairs={{0,1},{1,0},{6,7},{7,6},{8,9},{9,8},{14,15},{15,14},{16,17},{17,16... | collective-permute-start | bytes 2408456 | tf_op jit(solution)/shard_map/ppermute | solution.py:487
  32.2 14.9 %collective-permute-start.6 = (bf16[392,1024]{1,0:T(8,128)(2,1)}, bf16[392,1024]{1,0:T(8,128)(2,1)}, u32[]{:S(2)}, u32[]{:S(2)}) collective-permute-start(bf16[392,1024]{1,0:T(8,128)(2,1)} %collective-permute-done.refs_0_), channel_id=1, source_target_pairs={{0,4},{1,5},{6,2},{7,3},{8,12},{9,13},{14,10},{15,11},{16,20},{17,... | collective-permute-start | bytes 2408456 | tf_op jit(solution)/shard_map/ppermute | solution.py:487
  41.7 6.2 %collective-permute-start.5 = (bf16[392,1024]{1,0:T(8,128)(2,1)}, bf16[392,1024]{1,0:T(8,128)(2,1)S(1)}, u32[]{:S(2)}, u32[]{:S(2)}) collective-permute-start(bf16[392,1024]{1,0:T(8,128)(2,1)} %collective-permute-done.1.refs_2_), channel_id=1, source_target_pairs={{0,4},{1,5},{6,2},{7,3},{8,12},{9,13},{14,10},{15,11},{16,20},{17,... | collective-permute-start | bytes 2408456 | tf_op jit(solution)/shard_map/ppermute | solution.py:487
  77.1 11.3 %collective-permute-start.10 = (bf16[384,256]{1,0:T(8,128)(2,1)S(1)}, bf16[384,256]{1,0:T(8,128)(2,1)S(1)}, u32[]{:S(2)}, u32[]{:S(2)}) collective-permute-start(bf16[384,256]{1,0:T(8,128)(2,1)S(1)} %get-tuple-element.224), channel_id=1, source_target_pairs={{0,3},{1,1},{2,7},{3,5},{4,0},{5,2},{6,4},{7,6},{8,11},{9,9},{10,1... | collective-permute-start | bytes 589832 | tf_op jit(solution)/shard_map/ppermute | solution.py:487
  79.0 10.1 %collective-permute-start.9 = (bf16[384,256]{1,0:T(8,128)(2,1)S(1)}, bf16[384,256]{1,0:T(8,128)(2,1)S(1)}, u32[]{:S(2)}, u32[]{:S(2)}) collective-permute-start(bf16[384,256]{1,0:T(8,128)(2,1)S(1)} %get-tuple-element.225), channel_id=1, source_target_pairs={{0,2},{1,0},{2,6},{3,4},{4,3},{5,1},{6,7},{7,5},{8,10},{9,8},{10,1... | collective-permute-start | bytes 589832 | tf_op jit(solution)/shard_map/ppermute | solution.py:487
  80.5 8.6 %collective-permute-start.8 = (bf16[384,256]{1,0:T(8,128)(2,1)S(1)}, bf16[384,256]{1,0:T(8,128)(2,1)S(1)}, u32[]{:S(2)}, u32[]{:S(2)}) collective-permute-start(bf16[384,256]{1,0:T(8,128)(2,1)S(1)} %get-tuple-element.226), channel_id=1, source_target_pairs={{0,1},{1,3},{2,5},{3,7},{4,2},{5,0},{6,6},{7,4},{8,9},{9,11},{10,1... | collective-permute-start | bytes 589832 | tf_op jit(solution)/shard_map/ppermute | solution.py:487
  81.2 13.6 %collective-permute-start.7 = (bf16[384,256]{1,0:T(8,128)(2,1)S(1)}, bf16[384,256]{1,0:T(8,128)(2,1)S(1)}, u32[]{:S(2)}, u32[]{:S(2)}) collective-permute-start(bf16[384,256]{1,0:T(8,128)(2,1)S(1)} %get-tuple-element.227), channel_id=1, source_target_pairs={{0,0},{1,2},{2,4},{3,6},{4,1},{5,3},{6,5},{7,7},{8,8},{9,10},{10,1... | collective-permute-start | bytes 589832 | tf_op jit(solution)/shard_map/ppermute | solution.py:487
  120.3 3.8 collective-permute-start.11
  125.4 6.7 %collective-permute-start.14 = (f32[640]{0:T(1024)S(1)}, f32[640]{0:T(1024)S(1)}, u32[]{:S(2)}, u32[]{:S(2)}) collective-permute-start(f32[640]{0:T(1024)S(1)} %fusion.127), channel_id=1, source_target_pairs={{0,24},{1,25},{2,26},{3,27},{4,28},{5,29},{6,30},{7,31},{8,16},{9,... | collective-permute-start | bytes 7688 | tf_op jit(solution)/shard_map/ppermute | solution.py:90
  130.5 2.5 collective-permute-start.13
  133.0 3.6 collective-permute-start.17
  134.3 3.3 collective-permute-start.15
  161.5 50.7 %collective-permute-start.23 = (bf16[4,4,1408,128]{3,2,1,0:T(8,128)(2,1)}, bf16[4,4,1408,128]{3,2,1,0:T(8,128)(2,1)}, u32[]{:S(2)}, u32[]{:S(2)}) collective-permute-start(bf16[4,4,1408,128]{3,2,1,0:T(8,128)(2,1)} %get-tuple-element.120), channel_id=1, source_target_pairs={{0,4},{1,5},{2,6},{3,7},{4,0},{5,1},{6,2},{7,3},{8,12},{9,13},{10,... | collective-permute-start | bytes 17301512 | tf_op jit(solution)/shard_map/ppermute | solution.py:90
  188.8 21.9 %collective-permute-start.18 = (bf16[384,256]{1,0:T(8,128)(2,1)}, bf16[384,256]{1,0:T(8,128)(2,1)S(1)}, u32[]{:S(2)}, u32[]{:S(2)}) collective-permute-start(bf16[384,256]{1,0:T(8,128)(2,1)} %get-tuple-element.129), channel_id=1, source_target_pairs={{0,0},{1,4},{2,1},{3,5},{4,2},{5,6},{6,3},{7,7},{8,8},{9,12},{10,9... | collective-permute-start | bytes 589832 | tf_op jit(solution)/shard_map/ppermute | solution.py:487
  192.3 18.5 %collective-permute-start.19 = (bf16[384,256]{1,0:T(8,128)(2,1)}, bf16[384,256]{1,0:T(8,128)(2,1)S(1)}, u32[]{:S(2)}, u32[]{:S(2)}) collective-permute-start(bf16[384,256]{1,0:T(8,128)(2,1)} %get-tuple-element.130), channel_id=1, source_target_pairs={{0,5},{1,0},{2,4},{3,1},{4,7},{5,2},{6,6},{7,3},{8,13},{9,8},{10,1... | collective-permute-start | bytes 589832 | tf_op jit(solution)/shard_map/ppermute | solution.py:487
  193.9 16.9 %collective-permute-start.20 = (bf16[384,256]{1,0:T(8,128)(2,1)}, bf16[384,256]{1,0:T(8,128)(2,1)S(1)}, u32[]{:S(2)}, u32[]{:S(2)}) collective-permute-start(bf16[384,256]{1,0:T(8,128)(2,1)} %get-tuple-element.131), channel_id=1, source_target_pairs={{0,1},{1,5},{2,0},{3,4},{4,3},{5,7},{6,2},{7,6},{8,9},{9,13},{10,8... | collective-permute-start | bytes 589832 | tf_op jit(solution)/shard_map/ppermute | solution.py:487
  195.4 15.5 %collective-permute-start.21 = (bf16[384,256]{1,0:T(8,128)(2,1)}, bf16[384,256]{1,0:T(8,128)(2,1)S(1)}, u32[]{:S(2)}, u32[]{:S(2)}) collective-permute-start(bf16[384,256]{1,0:T(8,128)(2,1)} %get-tuple-element.132), channel_id=1, source_target_pairs={{0,4},{1,1},{2,5},{3,0},{4,6},{5,3},{6,7},{7,2},{8,12},{9,9},{10,1... | collective-permute-start | bytes 589832 | tf_op jit(solution)/shard_map/ppermute | solution.py:487
  210.8 9.8 %collective-permute-start.22 = (bf16[4,4,1288,128]{3,2,1,0:T(8,128)(2,1)}, bf16[4,4,1288,128]{3,2,1,0:T(8,128)(2,1)S(1)}, u32[]{:S(2)}, u32[]{:S(2)}) collective-permute-start(bf16[4,4,1288,128]{3,2,1,0:T(8,128)(2,1)} %get-tuple-element.141), channel_id=1, source_target_pairs={{0,4},{1,5},{2,6},{3,7},{4,0},{5,1},{6,2},{7,3},{8,12},{9,13},{10,... | collective-permute-start | bytes 15826952 | tf_op jit(solution)/shard_map/ppermute | solution.py:90
  216.8 37.9 %collective-permute-start.24 = (bf16[4,1408,128]{2,1,0:T(8,128)(2,1)}, bf16[4,1408,128]{2,1,0:T(8,128)(2,1)S(1)}, u32[]{:S(2)}, u32[]{:S(2)}) collective-permute-start(bf16[4,1408,128]{2,1,0:T(8,128)(2,1)} %get-tuple-element.209), channel_id=1, source_target_pairs={{0,8},{1,9},{2,10},{3,11},{4,12},{5,13},{6,14},{7,15},{8,0},{9,1},... | collective-permute-start | bytes 4325384 | tf_op jit(solution)/shard_map/ppermute | solution.py:90
  223.8 30.9 %collective-permute-start.25 = (bf16[4,1288,128]{2,1,0:T(8,128)(2,1)}, bf16[4,1288,128]{2,1,0:T(8,128)(2,1)}, u32[]{:S(2)}, u32[]{:S(2)}) collective-permute-start(bf16[4,1288,128]{2,1,0:T(8,128)(2,1)} %get-tuple-element.211), channel_id=1, source_target_pairs={{0,16},{1,17},{2,18},{3,19},{4,20},{5,21},{6,22},{7,23},{8,24},{9,... | collective-permute-start | bytes 3956744 | tf_op jit(solution)/shard_map/ppermute | solution.py:90
  254.8 32.2 %collective-permute-start.26 = (bf16[4,1408,128]{2,1,0:T(8,128)(2,1)S(1)}, bf16[4,1408,128]{2,1,0:T(8,128)(2,1)}, u32[]{:S(2)}, u32[]{:S(2)}) collective-permute-start(bf16[4,1408,128]{2,1,0:T(8,128)(2,1)S(1)} %get-tuple-element.155), channel_id=1, source_target_pairs={{0,8},{1,9},{2,10},{3,11},{4,12},{5,13},{6,14},{7,15},{8,0},{9,1},... | collective-permute-start | bytes 4325384 | tf_op jit(solution)/shard_map/ppermute | solution.py:90
  255.8 29.8 %collective-permute-start.27 = (bf16[4,1288,128]{2,1,0:T(8,128)(2,1)}, bf16[4,1288,128]{2,1,0:T(8,128)(2,1)}, u32[]{:S(2)}, u32[]{:S(2)}) collective-permute-start(bf16[4,1288,128]{2,1,0:T(8,128)(2,1)} %get-tuple-element.156), channel_id=1, source_target_pairs={{0,16},{1,17},{2,18},{3,19},{4,20},{5,21},{6,22},{7,23},{8,24},{9,... | collective-permute-start | bytes 3956744 | tf_op jit(solution)/shard_map/ppermute | solution.py:90
  287.0 14.4 %collective-permute-start.28 = (bf16[1536,1024]{1,0:T(8,128)(2,1)}, bf16[1536,1024]{1,0:T(8,128)(2,1)}, u32[]{:S(2)}, u32[]{:S(2)}) collective-permute-start(bf16[1536,1024]{1,0:T(8,128)(2,1)} %get-tuple-element.157), channel_id=1, source_target_pairs={{2,6},{3,7},{4,0},{5,1},{10,14},{11,15},{12,8},{13,9},{18,22},{19,... | collective-permute-start | bytes 9437192 | tf_op jit(solution)/shard_map/ppermute | solution.py:487
  298.6 29.8 %collective-permute-start.30 = (bf16[4,1408,128]{2,1,0:T(8,128)(2,1)}, bf16[4,1408,128]{2,1,0:T(8,128)(2,1)}, u32[]{:S(2)}, u32[]{:S(2)}) collective-permute-start(bf16[4,1408,128]{2,1,0:T(8,128)(2,1)} %fusion), channel_id=1, source_target_pairs={{0,16},{1,17},{2,18},{3,19},{4,20},{5,21},{6,22},{7,23},{8,24},{9,... | collective-permute-start | bytes 4325384 | tf_op jit(solution)/shard_map/ppermute | solution.py:90
  300.7 17.3 %collective-permute-start.31 = (bf16[4,2,72,768]{3,2,1,0:T(8,128)(2,1)}, bf16[4,2,72,768]{3,2,1,0:T(8,128)(2,1)}, u32[]{:S(2)}, u32[]{:S(2)}) collective-permute-start(bf16[4,2,72,768]{3,2,1,0:T(8,128)(2,1)} %pad_maximum_fusion.3), channel_id=1, source_target_pairs={{0,8},{1,9},{2,10},{3,11},{4,12},{5,13},{6,14},{7,15},{8,0},{9,1},... | collective-permute-start | bytes 2654216 | tf_op jit(solution)/shard_map/ppermute | solution.py:90
  305.2 27.0 %collective-permute-start.29 = (bf16[2,384,1024]{2,1,0:T(8,128)(2,1)}, bf16[2,384,1024]{2,1,0:T(8,128)(2,1)}, u32[]{:S(2)}, u32[]{:S(2)}) collective-permute-start(bf16[2,384,1024]{2,1,0:T(8,128)(2,1)} %pad_maximum_fusion), channel_id=1, source_target_pairs={{0,1},{1,0},{6,7},{7,6},{8,9},{9,8},{14,15},{15,14},{16,17},{17,16... | collective-permute-start | bytes 4718600 | tf_op jit(solution)/shard_map/ppermute | solution.py:487
  309.5 36.8 %collective-permute-start.35 = (bf16[4,1288,128]{2,1,0:T(8,128)(2,1)}, bf16[4,1288,128]{2,1,0:T(8,128)(2,1)}, u32[]{:S(2)}, u32[]{:S(2)}) collective-permute-start(bf16[4,1288,128]{2,1,0:T(8,128)(2,1)} %fusion.1), channel_id=1, source_target_pairs={{0,8},{1,9},{2,10},{3,11},{4,12},{5,13},{6,14},{7,15},{8,0},{9,1},... | collective-permute-start | bytes 3956744 | tf_op jit(solution)/shard_map/ppermute | solution.py:90
  320.2 29.9 %collective-permute-start.34 = (bf16[4,1,72,768]{3,2,1,0:T(8,128)(2,1)S(1)}, bf16[4,1,72,768]{3,2,1,0:T(8,128)(2,1)S(1)}, u32[]{:S(2)}, u32[]{:S(2)}) collective-permute-start(bf16[4,1,72,768]{3,2,1,0:T(8,128)(2,1)S(1)} %add_convert_fusion.7), channel_id=1, source_target_pairs={{0,16},{1,17},{2,18},{3,19},{4,20},{5,21},{6,22},{7,23},{8,24},{9,... | collective-permute-start | bytes 1327112 | tf_op jit(solution)/shard_map/ppermute | solution.py:90
  330.3 29.4 %collective-permute-start.33 = (bf16[2,1408,128]{2,1,0:T(8,128)(2,1)S(1)}, bf16[2,1408,128]{2,1,0:T(8,128)(2,1)S(1)}, u32[]{:S(2)}, u32[]{:S(2)}) collective-permute-start(bf16[2,1408,128]{2,1,0:T(8,128)(2,1)S(1)} %fusion.13), channel_id=1, source_target_pairs={{0,1},{1,0},{2,3},{3,2},{4,5},{5,4},{6,7},{7,6},{8,9},{9,8},{10,11... | collective-permute-start | bytes 2162696 | tf_op jit(solution)/shard_map/ppermute | solution.py:90
  334.0 37.5 %collective-permute-start.32 = (bf16[1,384,1024]{2,1,0:T(8,128)(2,1)S(1)}, bf16[1,384,1024]{2,1,0:T(8,128)(2,1)S(1)}, u32[]{:S(2)}, u32[]{:S(2)}) collective-permute-start(bf16[1,384,1024]{2,1,0:T(8,128)(2,1)S(1)} %fusion.8), channel_id=1, source_target_pairs={{0,3},{1,2},{6,5},{7,4},{8,11},{9,10},{14,13},{15,12},{16,19},{17,... | collective-permute-start | bytes 2359304 | tf_op jit(solution)/shard_map/ppermute | solution.py:487
  348.3 26.0 %collective-permute-start.37 = (bf16[2,1288,128]{2,1,0:T(8,128)(2,1)S(1)}, bf16[2,1288,128]{2,1,0:T(8,128)(2,1)S(1)}, u32[]{:S(2)}, u32[]{:S(2)}) collective-permute-start(bf16[2,1288,128]{2,1,0:T(8,128)(2,1)S(1)} %fusion.17), channel_id=1, source_target_pairs={{0,1},{1,0},{2,3},{3,2},{4,5},{5,4},{6,7},{7,6},{8,9},{9,8},{10,11... | collective-permute-start | bytes 1978376 | tf_op jit(solution)/shard_map/ppermute | solution.py:90
  350.3 41.1 %collective-permute-start.36 = (bf16[2,1,72,768]{3,2,1,0:T(8,128)(2,1)S(1)}, bf16[2,1,72,768]{3,2,1,0:T(8,128)(2,1)S(1)}, u32[]{:S(2)}, u32[]{:S(2)}) collective-permute-start(bf16[2,1,72,768]{3,2,1,0:T(8,128)(2,1)S(1)} %add_convert_fusion.8), channel_id=1, source_target_pairs={{0,2},{1,3},{2,0},{3,1},{4,6},{5,7},{6,4},{7,5},{8,10},{9,11},{10,... | collective-permute-start | bytes 663560 | tf_op jit(solution)/shard_map/ppermute | solution.py:90
  361.2 33.2 %collective-permute-start.40 = (bf16[1,1408,128]{2,1,0:T(8,128)(2,1)S(1)}, bf16[1,1408,128]{2,1,0:T(8,128)(2,1)S(1)}, u32[]{:S(2)}, u32[]{:S(2)}) collective-permute-start(bf16[1,1408,128]{2,1,0:T(8,128)(2,1)S(1)} %fusion.44), channel_id=1, source_target_pairs={{0,3},{1,2},{2,1},{3,0},{4,7},{5,6},{6,5},{7,4},{8,11},{9,10},{10,... | collective-permute-start | bytes 1081352 | tf_op jit(solution)/shard_map/ppermute | solution.py:90
  375.8 29.5 %collective-permute-start.39 = (bf16[1,1288,128]{2,1,0:T(8,128)(2,1)S(1)}, bf16[1,1288,128]{2,1,0:T(8,128)(2,1)S(1)}, u32[]{:S(2)}, u32[]{:S(2)}) collective-permute-start(bf16[1,1288,128]{2,1,0:T(8,128)(2,1)S(1)} %fusion.51), channel_id=1, source_target_pairs={{0,3},{1,2},{2,1},{3,0},{4,7},{5,6},{6,5},{7,4},{8,11},{9,10},{10,... | collective-permute-start | bytes 989192 | tf_op jit(solution)/shard_map/ppermute | solution.py:90
  391.5 15.5 %collective-permute-start.38 = (bf16[1,1,72,768]{3,2,1,0:T(8,128)(2,1)S(1)}, bf16[1,1,72,768]{3,2,1,0:T(8,128)(2,1)S(1)}, u32[]{:S(2)}, u32[]{:S(2)}) collective-permute-start(bf16[1,1,72,768]{3,2,1,0:T(8,128)(2,1)S(1)} %get-tuple-element.215), channel_id=1, source_target_pairs={{0,1},{1,0},{2,3},{3,2},{4,5},{5,4},{6,7},{7,6},{8,9},{9,8},{10,11... | collective-permute-start | bytes 331784 | tf_op jit(solution)/shard_map/ppermute | solution.py:90
  395.9 11.2 %collective-permute-start.43 = (bf16[1,1408,128]{2,1,0:T(8,128)(2,1)S(1)}, bf16[1,1408,128]{2,1,0:T(8,128)(2,1)S(1)}, u32[]{:S(2)}, u32[]{:S(2)}) collective-permute-start(bf16[1,1408,128]{2,1,0:T(8,128)(2,1)S(1)} %fusion.41), channel_id=1, source_target_pairs={{0,16},{1,17},{2,18},{3,19},{4,20},{5,21},{6,22},{7,23},{8,24},{9,... | collective-permute-start | bytes 1081352 | tf_op jit(solution)/shard_map/ppermute | solution.py:90
  406.9 9.4 %collective-permute-start.42 = (bf16[1,1288,128]{2,1,0:T(8,128)(2,1)S(1)}, bf16[1,1288,128]{2,1,0:T(8,128)(2,1)S(1)}, u32[]{:S(2)}, u32[]{:S(2)}) collective-permute-start(bf16[1,1288,128]{2,1,0:T(8,128)(2,1)S(1)} %fusion.48), channel_id=1, source_target_pairs={{0,8},{1,9},{2,10},{3,11},{4,12},{5,13},{6,14},{7,15},{8,0},{9,1},... | collective-permute-start | bytes 989192 | tf_op jit(solution)/shard_map/ppermute | solution.py:90
  407.2 24.6 %collective-permute-start.46 = (bf16[2,1408,128]{2,1,0:T(8,128)(2,1)S(1)}, bf16[2,1408,128]{2,1,0:T(8,128)(2,1)S(1)}, u32[]{:S(2)}, u32[]{:S(2)}) collective-permute-start(bf16[2,1408,128]{2,1,0:T(8,128)(2,1)S(1)} %pad_maximum_fusion.6), channel_id=1, source_target_pairs={{0,8},{1,9},{2,10},{3,11},{4,12},{5,13},{6,14},{7,15},{8,0},{9,1},... | collective-permute-start | bytes 2162696 | tf_op jit(solution)/shard_map/ppermute | solution.py:90
  409.3 9.1 %collective-permute-start.41 = (bf16[1,2,72,768]{3,2,1,0:T(8,128)(2,1)S(1)}, bf16[1,2,72,768]{3,2,1,0:T(8,128)(2,1)S(1)}, u32[]{:S(2)}, u32[]{:S(2)}) collective-permute-start(bf16[1,2,72,768]{3,2,1,0:T(8,128)(2,1)S(1)} %pad_maximum_fusion.9), channel_id=1, source_target_pairs={{0,16},{1,17},{2,18},{3,19},{4,20},{5,21},{6,22},{7,23},{8,24},{9,... | collective-permute-start | bytes 663560 | tf_op jit(solution)/shard_map/ppermute | solution.py:90
  416.4 17.8 %collective-permute-start.45 = (bf16[2,1288,128]{2,1,0:T(8,128)(2,1)S(1)}, bf16[2,1288,128]{2,1,0:T(8,128)(2,1)S(1)}, u32[]{:S(2)}, u32[]{:S(2)}) collective-permute-start(bf16[2,1288,128]{2,1,0:T(8,128)(2,1)S(1)} %pad_maximum_fusion.7), channel_id=1, source_target_pairs={{0,16},{1,17},{2,18},{3,19},{4,20},{5,21},{6,22},{7,23},{8,24},{9,... | collective-permute-start | bytes 1978376 | tf_op jit(solution)/shard_map/ppermute | solution.py:90
  419.8 21.5 %collective-permute-start.44 = (bf16[2,2,72,768]{3,2,1,0:T(8,128)(2,1)}, bf16[2,2,72,768]{3,2,1,0:T(8,128)(2,1)}, u32[]{:S(2)}, u32[]{:S(2)}) collective-permute-start(bf16[2,2,72,768]{3,2,1,0:T(8,128)(2,1)} %pad_maximum_fusion.8), channel_id=1, source_target_pairs={{0,8},{1,9},{2,10},{3,11},{4,12},{5,13},{6,14},{7,15},{8,0},{9,1},... | collective-permute-start | bytes 1327112 | tf_op jit(solution)/shard_map/ppermute | solution.py:90
  433.0 13.6 %collective-permute-start.49 = (bf16[4,1408,128]{2,1,0:T(8,128)(2,1)}, bf16[4,1408,128]{2,1,0:T(8,128)(2,1)}, u32[]{:S(2)}, u32[]{:S(2)}) collective-permute-start(bf16[4,1408,128]{2,1,0:T(8,128)(2,1)} %pad_maximum_fusion.1.mine_ref), channel_id=1, source_target_pairs={{0,4},{1,5},{2,6},{3,7},{4,0},{5,1},{6,2},{7,3},{8,12},{9,13},{10,... | collective-permute-start | bytes 4325384 | tf_op jit(solution)/shard_map/ppermute | solution.py:90
  435.5 16.9 %collective-permute-start.48 = (bf16[4,1288,128]{2,1,0:T(8,128)(2,1)}, bf16[4,1288,128]{2,1,0:T(8,128)(2,1)}, u32[]{:S(2)}, u32[]{:S(2)}) collective-permute-start(bf16[4,1288,128]{2,1,0:T(8,128)(2,1)} %pad_maximum_fusion.2.mine_ref), channel_id=1, source_target_pairs={{0,4},{1,5},{2,6},{3,7},{4,0},{5,1},{6,2},{7,3},{8,12},{9,13},{10,... | collective-permute-start | bytes 3956744 | tf_op jit(solution)/shard_map/ppermute | solution.py:90
  443.5 17.8 %collective-permute-start.47 = (bf16[4,2,72,768]{3,2,1,0:T(8,128)(2,1)}, bf16[4,2,72,768]{3,2,1,0:T(8,128)(2,1)}, u32[]{:S(2)}, u32[]{:S(2)}) collective-permute-start(bf16[4,2,72,768]{3,2,1,0:T(8,128)(2,1)} %pad_maximum_fusion.4.mine_ref), channel_id=1, source_target_pairs={{0,4},{1,5},{2,6},{3,7},{4,0},{5,1},{6,2},{7,3},{8,12},{9,13},{10,... | collective-permute-start | bytes 2654216 | tf_op jit(solution)/shard_map/ppermute | solution.py:90
  (39 other events, 474.8 us)
